TPU v7x, 32 devices: a whole 2x2x4 slice. The times are simulated.
32 devices in a mesh: dp: 8 (over y, x, core), ctx: 4 (over z).
Axes of the slice: x: 2, y: 2, z: 4, core: 2. Of those that a mesh axis runs over, the one named last changes fastest.
Arguments:
- inputs: bfloat16 [16, 1024, 1024], P('dp', 'ctx'), may hold values from -6 to 6
- segment_ids: int32 [16, 1024], P('dp', 'ctx'), may hold values from 0 to 7, never falling along the last dimension, each value on 1 to 512 neighbouring positions
- first_gain: bfloat16 [1024], P(('dp', 'ctx')), may hold values from 0.5 to 1.5
- first_shift: bfloat16 [1024], P(('dp', 'ctx')), may hold values from -3 to 3
- query_weight: bfloat16 [1024, 1024], P(('dp', 'ctx')), may hold values from -0.1875 to 0.1875
- query_bias: bfloat16 [1024], P(('dp', 'ctx')), may hold values from -3 to 3
- key_weight: bfloat16 [1024, 1024], P(('dp', 'ctx')), may hold values from -0.1875 to 0.1875
- value_weight: bfloat16 [1024, 1024], P(('dp', 'ctx')), may hold values from -0.1875 to 0.1875
- value_bias: bfloat16 [1024], P(('dp', 'ctx')), may hold values from -3 to 3
- out_weight: bfloat16 [1024, 1024], P(('dp', 'ctx')), may hold values from -0.75 to 0.75
- out_bias: bfloat16 [1024], P(('dp', 'ctx')), may hold values from -3 to 3
- second_gain: bfloat16 [1024], P(('dp', 'ctx')), may hold values from 0.5 to 1.5
- second_shift: bfloat16 [1024], P(('dp', 'ctx')), may hold values from -3 to 3
- up_weight: bfloat16 [1024, 4096], P(('dp', 'ctx')), may hold values from -0.1875 to 0.1875
- up_bias: bfloat16 [4096], P(('dp', 'ctx')), may hold values from -3 to 3
- down_weight: bfloat16 [4096, 1024], P(('dp', 'ctx')), may hold values from -0.09375 to 0.09375
- down_bias: bfloat16 [1024], P(('dp', 'ctx')), may hold values from -3 to 3
- cotangent: bfloat16 [16, 1024, 1024], P('dp', 'ctx'), may hold values from -6 to 6
Outputs:
- output: bfloat16 [16, 1024, 1024], P('dp', 'ctx')
- input_grad: float32 [16, 1024, 1024], P('dp', 'ctx')
- first_gain_grad: float32 [1024], P(('dp', 'ctx'))
- first_shift_grad: float32 [1024], P(('dp', 'ctx'))
- query_weight_grad: float32 [1024, 1024], P(('dp', 'ctx'))
- query_bias_grad: float32 [1024], P(('dp', 'ctx'))
- key_weight_grad: float32 [1024, 1024], P(('dp', 'ctx'))
- value_weight_grad: float32 [1024, 1024], P(('dp', 'ctx'))
- value_bias_grad: float32 [1024], P(('dp', 'ctx'))
- out_weight_grad: float32 [1024, 1024], P(('dp', 'ctx'))
- out_bias_grad: float32 [1024], P(('dp', 'ctx'))
- second_gain_grad: float32 [1024], P(('dp', 'ctx'))
- second_shift_grad: float32 [1024], P(('dp', 'ctx'))
- up_weight_grad: float32 [1024, 4096], P(('dp', 'ctx'))
- up_bias_grad: float32 [4096], P(('dp', 'ctx'))
- down_weight_grad: float32 [4096, 1024], P(('dp', 'ctx'))
- down_bias_grad: float32 [1024], P(('dp', 'ctx'))
Inputs may be any that keep to these rules, and one draw needn't show every extreme that they name: `segment_ids`: along each sequence the document numbers never fall; each document has 1 to half of 1024 tokens, and one of each sequence has exactly half of 1024.
All inputs are finite; a program needn't handle non-finite values.
Results may differ from a plain program's by a relative error of at most 0.013.
Values may be sent and summed in bfloat16 or wider, within the bound.
No kernel may reach another device: no remote copies, remote signals or barrier semaphores. Data moves between devices by JAX's collectives and lax.ppermute only.
A program may use at most 256 MiB of HBM per device.

v0:
```python
from functools import partial
import math

import jax
import jax.numpy as jnp
from jax import lax
from jax.sharding import PartitionSpec as P

H = 16


EPS = 1e-05
MASKED = -1e30


def normalize(values, gain, shift):
    mean = jnp.mean(values, axis=-1, keepdims=True)
    centered = values - mean
    spread = jnp.mean(centered * centered, axis=-1, keepdims=True)
    return centered * lax.rsqrt(spread + EPS) * gain + shift


def product(left, right):
    return jnp.einsum("btd,de->bte", left, right, preferred_element_type=jnp.float32)


def product_back(left, right):
    return jnp.einsum("bte,de->btd", left, right, preferred_element_type=jnp.float32)


def outer_sum(left, right):
    return jnp.einsum("btd,bte->de", left, right, preferred_element_type=jnp.float32)


def column_sum(values):
    return jnp.sum(values.astype(jnp.float32), axis=(0, 1))


def gather_attention(
    first_gain,
    first_shift,
    query_weight,
    query_bias,
    key_weight,
    value_weight,
    value_bias,
    out_weight,
    out_bias,
):
    return (
        lax.all_gather(first_gain, ("dp", "ctx"), axis=0, tiled=True),
        lax.all_gather(first_shift, ("dp", "ctx"), axis=0, tiled=True),
        lax.all_gather(query_weight, ("dp", "ctx"), axis=0, tiled=True),
        lax.all_gather(query_bias, ("dp", "ctx"), axis=0, tiled=True),
        lax.all_gather(key_weight, ("dp", "ctx"), axis=0, tiled=True),
        lax.all_gather(value_weight, ("dp", "ctx"), axis=0, tiled=True),
        lax.all_gather(value_bias, ("dp", "ctx"), axis=0, tiled=True),
        lax.all_gather(out_weight, ("dp", "ctx"), axis=0, tiled=True),
        lax.all_gather(out_bias, ("dp", "ctx"), axis=0, tiled=True),
    )


def gather_feed(second_gain, second_shift, up_weight, up_bias, down_weight, down_bias):
    return (
        lax.all_gather(second_gain, ("dp", "ctx"), axis=0, tiled=True),
        lax.all_gather(second_shift, ("dp", "ctx"), axis=0, tiled=True),
        lax.all_gather(up_weight, ("dp", "ctx"), axis=0, tiled=True),
        lax.all_gather(up_bias, ("dp", "ctx"), axis=0, tiled=True),
        lax.all_gather(down_weight, ("dp", "ctx"), axis=0, tiled=True),
        lax.all_gather(down_bias, ("dp", "ctx"), axis=0, tiled=True),
    )


def gather_keys(keys, values, segments):
    return (
        lax.all_gather(keys, "ctx", axis=1, tiled=True),
        lax.all_gather(values, "ctx", axis=1, tiled=True),
        lax.all_gather(segments, "ctx", axis=1, tiled=True),
    )


def score_block(queries, keys_all, segments, segments_all):
    batch, rows, width = queries.shape
    size = width // H
    total_len = keys_all.shape[1]
    query_heads = queries.reshape(batch, rows, H, size)
    key_heads = keys_all.reshape(batch, total_len, H, size)
    raw = jnp.einsum("bqhd,bkhd->bhqk", query_heads, key_heads, preferred_element_type=jnp.float32)
    scores = raw * (1.0 / math.sqrt(size))
    offset = lax.axis_index("ctx") * rows
    query_pos = offset + jnp.arange(rows, dtype=jnp.int32)
    key_pos = jnp.arange(total_len, dtype=jnp.int32)
    causal = key_pos[None, :] <= query_pos[:, None]
    same_doc = segments[:, :, None] == segments_all[:, None, :]
    allowed = (causal[None] & same_doc)[:, None]
    return jnp.where(allowed, scores, MASKED)


def forward_part(inputs, segments, attn, feed):
    (
        first_gain,
        first_shift,
        query_weight,
        query_bias,
        key_weight,
        value_weight,
        value_bias,
        out_weight,
        out_bias,
    ) = attn
    second_gain, second_shift, up_weight, up_bias, down_weight, down_bias = feed
    batch, rows, width = inputs.shape
    size = width // H
    source = inputs.astype(jnp.float32)
    normed = normalize(
        source, first_gain.astype(jnp.float32), first_shift.astype(jnp.float32)
    ).astype(jnp.bfloat16)
    queries = (product(normed, query_weight) + query_bias.astype(jnp.float32)).astype(jnp.bfloat16)
    keys = product(normed, key_weight).astype(jnp.bfloat16)
    values = (product(normed, value_weight) + value_bias.astype(jnp.float32)).astype(jnp.bfloat16)
    keys_all, values_all, segments_all = gather_keys(keys, values, segments)
    scores = score_block(queries, keys_all, segments, segments_all)
    top = jnp.max(scores, axis=-1, keepdims=True)
    expo = jnp.exp(scores - top)
    row_total = jnp.sum(expo, axis=-1, keepdims=True)
    probs = (expo / row_total).astype(jnp.bfloat16)
    log_total = top + jnp.log(row_total)
    value_heads = values_all.reshape(batch, values_all.shape[1], H, size)
    mixed = jnp.einsum("bhqk,bkhd->bqhd", probs, value_heads, preferred_element_type=jnp.float32)
    mixed = mixed.reshape(batch, rows, width).astype(jnp.bfloat16)
    middle = source + product(mixed, out_weight) + out_bias.astype(jnp.float32)
    second = normalize(
        middle, second_gain.astype(jnp.float32), second_shift.astype(jnp.float32)
    ).astype(jnp.bfloat16)
    hidden_pre = product(second, up_weight) + up_bias.astype(jnp.float32)
    hidden = jax.nn.gelu(hidden_pre, approximate=False).astype(jnp.bfloat16)
    output = (middle + product(hidden, down_weight) + down_bias.astype(jnp.float32)).astype(
        jnp.bfloat16
    )
    kept = (
        source,
        normed,
        queries,
        keys,
        values,
        log_total,
        mixed,
        middle,
        second,
        hidden_pre,
        hidden,
    )
    return (output, kept, (keys_all, values_all, segments_all))


def backward_part(kept, gathered, segments, cotangent, attn, feed):
    (
        first_gain,
        first_shift,
        query_weight,
        query_bias,
        key_weight,
        value_weight,
        value_bias,
        out_weight,
        out_bias,
    ) = attn
    second_gain, second_shift, up_weight, up_bias, down_weight, down_bias = feed
    source, normed, queries, keys, values, log_total, mixed, middle, second, hidden_pre, hidden = (
        kept
    )
    keys_all, values_all, segments_all = gathered
    batch, rows, width = source.shape
    size = width // H
    total_len = keys_all.shape[1]
    scale = 1.0 / math.sqrt(size)
    down_grad = outer_sum(hidden, cotangent)
    down_bias_grad = column_sum(cotangent)
    hidden_grad = product_back(cotangent, down_weight)
    _, gelu_back = jax.vjp(partial(jax.nn.gelu, approximate=False), hidden_pre)
    pre_grad = gelu_back(hidden_grad)[0].astype(jnp.bfloat16)
    up_grad = outer_sum(second, pre_grad)
    up_bias_grad = column_sum(pre_grad)
    second_grad = product_back(pre_grad, up_weight)
    _, second_back = jax.vjp(
        normalize, middle, second_gain.astype(jnp.float32), second_shift.astype(jnp.float32)
    )
    middle_part, second_gain_grad, second_shift_grad = second_back(second_grad)
    feed_grads = (
        lax.psum_scatter(second_gain_grad, ("dp", "ctx"), scatter_dimension=0, tiled=True),
        lax.psum_scatter(second_shift_grad, ("dp", "ctx"), scatter_dimension=0, tiled=True),
        lax.psum_scatter(up_grad, ("dp", "ctx"), scatter_dimension=0, tiled=True),
        lax.psum_scatter(up_bias_grad, ("dp", "ctx"), scatter_dimension=0, tiled=True),
        lax.psum_scatter(down_grad, ("dp", "ctx"), scatter_dimension=0, tiled=True),
        lax.psum_scatter(down_bias_grad, ("dp", "ctx"), scatter_dimension=0, tiled=True),
    )
    middle_grad = cotangent.astype(jnp.float32) + middle_part
    branch_grad = middle_grad.astype(jnp.bfloat16)
    out_grad = outer_sum(mixed, branch_grad)
    out_bias_grad = column_sum(branch_grad)
    mixed_grad = product_back(branch_grad, out_weight).astype(jnp.bfloat16)
    scores = score_block(queries, keys_all, segments, segments_all)
    probs_full = jnp.exp(scores - log_total)
    probs = probs_full.astype(jnp.bfloat16)
    grad_heads = mixed_grad.reshape(batch, rows, H, size)
    query_heads = queries.reshape(batch, rows, H, size)
    key_heads = keys_all.reshape(batch, total_len, H, size)
    value_heads = values_all.reshape(batch, total_len, H, size)
    value_grad_all = jnp.einsum(
        "bhqk,bqhd->bkhd", probs, grad_heads, preferred_element_type=jnp.float32
    )
    prob_grad = jnp.einsum(
        "bqhd,bkhd->bhqk", grad_heads, value_heads, preferred_element_type=jnp.float32
    )
    delta = jnp.sum(probs_full * prob_grad, axis=-1, keepdims=True)
    score_grad = (probs_full * (prob_grad - delta)).astype(jnp.bfloat16)
    query_grad = (
        jnp.einsum("bhqk,bkhd->bqhd", score_grad, key_heads, preferred_element_type=jnp.float32)
        * scale
    )
    query_grad = query_grad.reshape(batch, rows, width).astype(jnp.bfloat16)
    key_grad_all = (
        jnp.einsum("bhqk,bqhd->bkhd", score_grad, query_heads, preferred_element_type=jnp.float32)
        * scale
    )
    key_sum, value_sum = (
        lax.psum_scatter(
            key_grad_all.reshape(batch, total_len, width).astype(jnp.bfloat16),
            "ctx",
            scatter_dimension=1,
            tiled=True,
        ).astype(jnp.float32),
        lax.psum_scatter(
            value_grad_all.reshape(batch, total_len, width).astype(jnp.bfloat16),
            "ctx",
            scatter_dimension=1,
            tiled=True,
        ).astype(jnp.float32),
    )
    key_grad = key_sum.astype(jnp.bfloat16)
    value_grad = value_sum.astype(jnp.bfloat16)
    query_weight_grad = outer_sum(normed, query_grad)
    query_bias_grad = column_sum(query_grad)
    key_weight_grad = outer_sum(normed, key_grad)
    value_weight_grad = outer_sum(normed, value_grad)
    value_bias_grad = column_sum(value_grad)
    normed_grad = (
        product_back(query_grad, query_weight)
        + product_back(key_grad, key_weight)
        + product_back(value_grad, value_weight)
    )
    _, first_back = jax.vjp(
        normalize, source, first_gain.astype(jnp.float32), first_shift.astype(jnp.float32)
    )
    input_part, first_gain_grad, first_shift_grad = first_back(normed_grad)
    input_grad = middle_grad + input_part
    attn_grads = (
        lax.psum_scatter(first_gain_grad, ("dp", "ctx"), scatter_dimension=0, tiled=True),
        lax.psum_scatter(first_shift_grad, ("dp", "ctx"), scatter_dimension=0, tiled=True),
        lax.psum_scatter(query_weight_grad, ("dp", "ctx"), scatter_dimension=0, tiled=True),
        lax.psum_scatter(query_bias_grad, ("dp", "ctx"), scatter_dimension=0, tiled=True),
        lax.psum_scatter(key_weight_grad, ("dp", "ctx"), scatter_dimension=0, tiled=True),
        lax.psum_scatter(value_weight_grad, ("dp", "ctx"), scatter_dimension=0, tiled=True),
        lax.psum_scatter(value_bias_grad, ("dp", "ctx"), scatter_dimension=0, tiled=True),
        lax.psum_scatter(out_grad, ("dp", "ctx"), scatter_dimension=0, tiled=True),
        lax.psum_scatter(out_bias_grad, ("dp", "ctx"), scatter_dimension=0, tiled=True),
    )
    return (input_grad, attn_grads, feed_grads)


def local(
    inputs,
    segment_ids,
    first_gain,
    first_shift,
    query_weight,
    query_bias,
    key_weight,
    value_weight,
    value_bias,
    out_weight,
    out_bias,
    second_gain,
    second_shift,
    up_weight,
    up_bias,
    down_weight,
    down_bias,
    cotangent,
):
    attn = gather_attention(
        first_gain,
        first_shift,
        query_weight,
        query_bias,
        key_weight,
        value_weight,
        value_bias,
        out_weight,
        out_bias,
    )
    feed = gather_feed(second_gain, second_shift, up_weight, up_bias, down_weight, down_bias)
    output, kept, gathered = forward_part(inputs, segment_ids, attn, feed)
    key_set = gather_keys(kept[3], kept[4], segment_ids)
    input_grad, attn_grads, feed_grads = backward_part(
        kept, key_set, segment_ids, cotangent, attn, feed
    )
    result = (output, input_grad)
    return result + tuple(attn_grads) + tuple(feed_grads)


def solution(mesh):
    return jax.shard_map(
        local,
        mesh=mesh,
        in_specs=(
            P("dp", "ctx", None),
            P("dp", "ctx"),
            P(("dp", "ctx")),
            P(("dp", "ctx")),
            P(("dp", "ctx"), None),
            P(("dp", "ctx")),
            P(("dp", "ctx"), None),
            P(("dp", "ctx"), None),
            P(("dp", "ctx")),
            P(("dp", "ctx"), None),
            P(("dp", "ctx")),
            P(("dp", "ctx")),
            P(("dp", "ctx")),
            P(("dp", "ctx"), None),
            P(("dp", "ctx")),
            P(("dp", "ctx"), None),
            P(("dp", "ctx")),
            P("dp", "ctx", None),
        ),
        out_specs=(
            P("dp", "ctx", None),
            P("dp", "ctx", None),
            P(("dp", "ctx")),
            P(("dp", "ctx")),
            P(("dp", "ctx"), None),
            P(("dp", "ctx")),
            P(("dp", "ctx"), None),
            P(("dp", "ctx"), None),
            P(("dp", "ctx")),
            P(("dp", "ctx"), None),
            P(("dp", "ctx")),
            P(("dp", "ctx")),
            P(("dp", "ctx")),
            P(("dp", "ctx"), None),
            P(("dp", "ctx")),
            P(("dp", "ctx"), None),
            P(("dp", "ctx")),
        ),
        check_vma=False,
    )
```

profile of v0, /device:TPU:13, one launch (start us, length us, event | category | flops | bytes accessed | tf_op | source)
XLA Modules:
  0.0 2105.7 jit_solution(8953281976485019431)
XLA Ops:
  9.5 0.8 dynamic-update-slice.5
  11.2 0.8 dynamic-update-slice.4
  12.0 0.8 dynamic-update-slice.3
  12.8 0.8 dynamic-update-slice
  16.2 40.6 %all-reduce.18 = (bf16[1024]{0:T(1024)(128)(2,1)S(1)}, bf16[1024]{0:T(1024)(128)(2,1)S(1)}, bf16[1024]{0:T(1024)(128)(2,1)S(1)}, bf16[1024]{0:T(1024)(128)(2,1)S...) all-reduce(bf16[1024]{0:T(1024)(128)(2,1)S(1)} %dynamic-update-slic, ...), channel_id=1, replica_groups=mesh['dp'=8,'ctx'=4] {'dp','ctx'}, use_global_device_ids=true, to_apply=%add.2 | all-reduce | flops 8192 | bytes 32768
  56.8 1.5 convert_reduce_fusion.1
  58.3 1.6 fusion.34
  60.0 7.8 all-gather.10.cloned.1.call-done
  67.8 4.2 add_convert_fusion.4
  72.1 54.0 %all-gather.16.cloned.1.call-done = bf16[1024,1024]{1,0:T(8,128)(2,1)} async-done(((bf16[32,1024]{1,0:T(8,128)(2,1)}), bf16[1024,1024]{1,0:T(8,128)(2,1)}) %all-gather.16.cloned.1.call-update) | async-done | bytes 2097168 | tf_op jit(solution)/shard_map/all_gather | solution.py:55
  126.2 3.9 fusion.63
  132.3 59.4 %all-gather = bf16[32,1,128]{2,1,0:T(2,128)(2,1)S(1)} all-gather(bf16[1,1,128]{2,1,0:T(2,128)(2,1)S(1)} %bitcast.129), channel_id=1, replica_groups=mesh['dp'=8,'ctx'=4] {'dp','ctx'}, dimensions={0}, use_global_device_ids=true | all-gather | bytes 8448 | tf_op jit(solution)/shard_map/all_gather | solution.py:68
  191.7 10.6 all_gather.62
  203.0 3.9 add_convert_fusion.3
  206.9 1.5 copy.68
  208.4 55.7 %all-gather.12.cloned.1.call-done = bf16[2,1024,1024]{2,1,0:T(8,128)(2,1)} async-done(((bf16[2,256,1024]{2,1,0:T(8,128)(2,1)}), bf16[2,1024,1024]{2,1,0:T(8,128)(2,1)}) %all-gather.12.cloned.1.call-update) | async-done | bytes 4194320 | tf_op jit(solution)/shard_map/all_gather | solution.py:77
  264.1 6.2 copy.67
  270.3 74.4 %all-gather.18.cloned.1.call-done = bf16[2,1024,1024]{2,1,0:T(8,128)(2,1)} async-done(((bf16[2,256,1024]{2,1,0:T(8,128)(2,1)}), bf16[2,1024,1024]{2,1,0:T(8,128)(2,1)}) %all-gather.18.cloned.1.call-update) | async-done | bytes 4194320 | tf_op jit(solution)/shard_map/all_gather | solution.py:76
  344.7 6.3 copy.69
  350.9 16.0 fusion.86
  366.9 14.3 fusion
  381.2 16.2 fusion.69
  397.5 6.9 all-gather.20.cloned.1.call-done
  404.4 3.3 fusion.87
  408.1 76.2 %all-gather.22.cloned.1.call-done = bf16[1024,4096]{1,0:T(8,128)(2,1)} async-done(((bf16[32,4096]{1,0:T(8,128)(2,1)}), bf16[1024,4096]{1,0:T(8,128)(2,1)}) %all-gather.22.cloned.1.call-update) | async-done | bytes 8388624 | tf_op jit(solution)/shard_map/all_gather | solution.py:67
  484.3 10.9 fusion.54
  495.2 3.2 copy-done.4
  498.4 20.6 multiply_convert_fusion.2
  519.0 44.0 %all-gather.24.cloned.1.call-done = bf16[4096,1024]{1,0:T(8,128)(2,1)} async-done(((bf16[128,1024]{1,0:T(8,128)(2,1)}), bf16[4096,1024]{1,0:T(8,128)(2,1)}) %all-gather.24.cloned.1.call-update) | async-done | bytes 8388624 | tf_op jit(solution)/shard_map/all_gather | solution.py:69
  563.0 14.1 convert_reduce_fusion
  577.1 9.7 multiply_reduce_fusion.1
  587.5 1.3 copy-done.1
  588.9 1.0 convert_reduce_fusion.3
  589.8 1.0 copy-done.12
  590.8 2.3 fusion.66
  593.1 2.3 copy.71
  595.4 15.7 fusion.26
  611.0 6.2 copy.74
  617.3 24.6 %multiply_reduce_fusion = (f32[2,16,256]{2,1,0:T(8,128)S(1)}, f32[2,16,256,1024]{3,2,1,0:T(8,128)}) fusion(f32[2,16,256,1024]{3,2,1,0:T(8,128)} %get-tuple-element.52, f32[2,16,256]{2,1,0:T(8,128)S(1)} %log_add_fusion, bf16[2,256,16,64]{1,3,2,0:T(8,128)(2,1)} %bitcast.119, bf16[2,1024,16,64]{1,3,2,0:T(8,128)(2,1)} %bitcast.115), kind=kOutput, calls=%fused_computation.1 | convolution fusion | flops 1098899456 | bytes 72417280 | tf_op jit(solution)/shard_map/bqhd,bkhd->bhqk/dot_general | solution.py:212
  642.0 28.0 %multiply_convert_fusion = bf16[2,16,256,1024]{3,2,1,0:T(8,128)(2,1)} fusion(f32[2,16,256,1024]{3,2,1,0:T(8,128)} %get-tuple-element.58, f32[2,16,256,1024]{3,2,1,0:T(8,128)} %get-tuple-element.52, f32[2,16,256]{2,1,0:T(8,128)S(1)} %get-tuple-element.57, f32[2,16,256]{2,1,0:T(8,128)S(1)} %log_add_fusion), kind=kLoop, calls=%fused_computation | loop fusion | flops 33554432 | bytes 83951616 | tf_op jit(solution)/shard_map/convert_element_type | solution.py:216
  670.0 11.1 multiply_convert_fusion.1
  681.1 6.2 copy.73
  687.4 4.8 convolution_bitcast_fusion.2
  692.3 10.1 convert_reduce_fusion.5
  702.5 1.0 copy-done.9
  703.5 3.5 convolution_bitcast_fusion.5
  707.0 4.6 convolution_bitcast_fusion.3
  711.7 60.1 %reduce-scatter.9.cloned.1.call-done = bf16[2,256,1024]{2,1,0:T(8,128)(2,1)} async-done(((bf16[2,1024,1024]{2,1,0:T(8,128)(2,1)}), bf16[2,256,1024]{2,1,0:T(8,128)(2,1)}) %reduce-scatter.9.cloned.1.call-update) | async-done | bytes 1048592 | tf_op jit(solution)/shard_map/reduce_scatter | solution.py:227
  771.8 4.6 convolution_bitcast_fusion.4
  776.5 10.5 convolution_bitcast_fusion.1
  787.3 12.8 convolution_bitcast_fusion
  800.9 3.4 fusion.45
  804.3 9.1 add_convert_fusion.1
  813.6 1.3 fusion.41
  815.0 2.0 fusion.82
  817.1 1.1 fusion.33
  818.6 2.1 convert_reduce_fusion.2
  820.8 40.4 %all-reduce.17 = (f32[1024]{0:T(1024)S(1)}, f32[1024]{0:T(1024)S(1)}, f32[1024]{0:T(1024)S(1)}, f32[1024]{0:T(1024)S(1)}, f32[1024]{0:T(1024)S(1)}, /*index=5*/f...) all-reduce(f32[1024]{0:T(1024)S(1)} %get-tuple-element.21, ...), channel_id=4, replica_groups=mesh['dp'=8,'ctx'=4] {'dp','ctx'}, use_global_device_ids=true, to_apply=%region_14.15.clone | all-reduce | flops 12288 | bytes 98304
  866.5 50.0 %reduce-scatter.19.cloned.1.call-done = f32[32,1024]{1,0:T(8,128)} async-done(((f32[1024,1024]{1,0:T(8,128)}), f32[32,1024]{1,0:T(8,128)}) %reduce-scatter.19.cloned.1.call-update) | async-done | bytes 131088 | tf_op jit(solution)/shard_map/reduce_scatter | solution.py:265
  916.5 150.1 %reduce-scatter.13.cloned.1.call-done = f32[32,1024]{1,0:T(8,128)} async-done(((f32[1024,1024]{1,0:T(8,128)}), f32[32,1024]{1,0:T(8,128)}) %reduce-scatter.13.cloned.1.call-update) | async-done | bytes 131088 | tf_op jit(solution)/shard_map/reduce_scatter | solution.py:260
  1066.6 151.5 %reduce-scatter.17.cloned.1.call-done = f32[32,1024]{1,0:T(8,128)} async-done(((f32[1024,1024]{1,0:T(8,128)}), f32[32,1024]{1,0:T(8,128)}) %reduce-scatter.17.cloned.1.call-update) | async-done | bytes 131088 | tf_op jit(solution)/shard_map/reduce_scatter | solution.py:263
  1218.1 150.0 %reduce-scatter.15.cloned.1.call-done = f32[32,1024]{1,0:T(8,128)} async-done(((f32[1024,1024]{1,0:T(8,128)}), f32[32,1024]{1,0:T(8,128)}) %reduce-scatter.15.cloned.1.call-update) | async-done | bytes 131088 | tf_op jit(solution)/shard_map/reduce_scatter | solution.py:262
  1368.0 365.9 %reduce-scatter.21.cloned.1.call-done = f32[32,4096]{1,0:T(8,128)} async-done(((f32[1024,4096]{1,0:T(8,128)}), f32[32,4096]{1,0:T(8,128)}) %reduce-scatter.21.cloned.1.call-update) | async-done | bytes 524304 | tf_op jit(solution)/shard_map/reduce_scatter | solution.py:192
  1733.9 364.7 %reduce-scatter.23.cloned.1.call-done = f32[128,1024]{1,0:T(8,128)} async-done(((f32[4096,1024]{1,0:T(8,128)}), f32[128,1024]{1,0:T(8,128)}) %reduce-scatter.23.cloned.1.call-update) | async-done | bytes 524304 | tf_op jit(solution)/shard_map/reduce_scatter | solution.py:194
  (146 shorter events, 17.1 us)
Async XLA Ops:
  7.2 60.7 %all-gather.10.cloned.1.call-start = ((), (), s32[]{:S(2)}) async-start(), calls=%async_computation.8 | async-start | bytes 2162688 | tf_op jit(solution)/shard_map/all_gather | solution.py:56
  7.9 118.3 %all-gather.16.cloned.1.call-start = ((), (), s32[]{:S(2)}) async-start(), calls=%async_computation.11 | async-start | bytes 2162688 | tf_op jit(solution)/shard_map/all_gather | solution.py:55
  8.7 194.3 %all-gather.14.cloned.1.call-start = ((), (), s32[]{:S(2)}) async-start(), calls=%async_computation.10 | async-start | bytes 2162688 | tf_op jit(solution)/shard_map/all_gather | solution.py:53
  9.4 254.6 %all-gather.12.cloned.1.call-start = ((), (), s32[]{:S(2)}) async-start(), calls=%async_computation.9 | async-start | bytes 5242880 | tf_op jit(solution)/shard_map/all_gather | solution.py:77
  56.8 146.2 %copy-start.13 = (f32[1024]{0:T(1024)}, f32[1024]{0:T(1024)S(1)}, u32[]{:S(2)}) copy-start(f32[1024]{0:T(1024)S(1)} %convert_element_type.132) | copy-start | bytes 12292
  56.8 146.2 %copy-start.28 = (f32[1024]{0:T(1024)}, f32[1024]{0:T(1024)S(1)}, u32[]{:S(2)}) copy-start(f32[1024]{0:T(1024)S(1)} %convert_element_type.133) | copy-start | bytes 12292
  58.3 144.7 %copy-start.15 = (f32[2,256]{1,0:T(2,128)}, f32[2,256]{1,0:T(2,128)S(1)}, u32[]{:S(2)}) copy-start(f32[2,256]{1,0:T(2,128)S(1)} %broadcast_multiply_fusion.1) | copy-start | bytes 6148
  59.9 12.1 copy-start.21
  60.0 143.0 %copy-start.17 = (f32[2,256]{1,0:T(2,128)}, f32[2,256]{1,0:T(2,128)S(1)}, u32[]{:S(2)}) copy-start(f32[2,256]{1,0:T(2,128)S(1)} %fusion.74) | copy-start | bytes 6148
  60.0 66.2 %copy-start = (bf16[2,256,1024]{2,1,0:T(8,128)(2,1)S(1)}, bf16[2,256,1024]{2,1,0:T(8,128)(2,1)}, u32[]{:S(2)}) copy-start(bf16[2,256,1024]{2,1,0:T(8,128)(2,1)} %param.18) | copy-start | bytes 3145732
  72.1 60.2 %copy-start.31 = (bf16[128]{0:T(256)(128)(2,1)S(1)}, bf16[128]{0:T(256)(128)(2,1)}, u32[]{:S(2)}) copy-start(bf16[128]{0:T(256)(128)(2,1)} %param.32) | copy-start | bytes 772
  72.1 119.6 %copy-start.25 = (s32[2,256]{1,0:T(2,128)S(1)}, s32[2,256]{1,0:T(2,128)}, u32[]{:S(2)}) copy-start(s32[2,256]{1,0:T(2,128)} %param.19) | copy-start | bytes 6148
  72.1 272.6 %all-gather.18.cloned.1.call-start = ((), (), s32[]{:S(2)}) async-start(), calls=%async_computation.12 | async-start | bytes 5242880 | tf_op jit(solution)/shard_map/all_gather | solution.py:76
  130.1 274.3 %all-gather.20.cloned.1.call-start = ((), (), s32[]{:S(2)}) async-start(), calls=%async_computation.13 | async-start | bytes 2162688 | tf_op jit(solution)/shard_map/all_gather | solution.py:58
  130.7 353.6 %all-gather.22.cloned.1.call-start = ((), (), s32[]{:S(2)}) async-start(), calls=%async_computation.14 | async-start | bytes 8650752 | tf_op jit(solution)/shard_map/all_gather | solution.py:67
  131.4 431.6 %all-gather.24.cloned.1.call-start = ((), (), s32[]{:S(2)}) async-start(), calls=%async_computation.15 | async-start | bytes 8650752 | tf_op jit(solution)/shard_map/all_gather | solution.py:69
  132.2 574.9 %reduce-scatter.11.cloned.1.call-start = ((), (), s32[]{:S(2)}) async-start(), calls=%async_computation.17 | async-start | bytes 5242880 | tf_op jit(solution)/shard_map/reduce_scatter | solution.py:233
  208.4 142.6 %copy-start.3 = (bf16[2,256,1024]{1,2,0:T(8,128)(2,1)}, bf16[2,256,1024]{1,2,0:T(8,128)(2,1)S(1)}, u32[]{:S(2)}) copy-start(bf16[2,256,1024]{1,2,0:T(8,128)(2,1)S(1)} %copy.68) | copy-start | bytes 3145732
  495.2 3.2 copy-start.4
  577.1 9.7 copy-start.34
  586.8 2.0 copy-start.6
  586.8 4.0 copy-start.10
  587.5 1.3 copy-start.1
  587.5 2.3 copy-start.19
  589.8 1.0 copy-start.12
  617.3 154.5 %reduce-scatter.9.cloned.1.call-start = ((), (), s32[]{:S(2)}) async-start(), calls=%async_computation.16 | async-start | bytes 5242880 | tf_op jit(solution)/shard_map/reduce_scatter | solution.py:227
  687.3 229.2 %reduce-scatter.19.cloned.1.call-start = ((), (), s32[]{:S(2)}) async-start(), calls=%async_computation.21 | async-start | bytes 4325376 | tf_op jit(solution)/shard_map/reduce_scatter | solution.py:265
  692.2 11.2 copy-start.14
  692.3 11.2 copy-start.16
  692.3 11.2 copy-start.18
  692.3 11.2 copy-start.29
  692.3 374.3 %reduce-scatter.13.cloned.1.call-start = ((), (), s32[]{:S(2)}) async-start(), calls=%async_computation.18 | async-start | bytes 4325376 | tf_op jit(solution)/shard_map/reduce_scatter | solution.py:260
  702.5 1.0 copy-start.9
  707.0 511.1 %reduce-scatter.17.cloned.1.call-start = ((), (), s32[]{:S(2)}) async-start(), calls=%async_computation.20 | async-start | bytes 4325376 | tf_op jit(solution)/shard_map/reduce_scatter | solution.py:263
  711.7 656.3 %reduce-scatter.15.cloned.1.call-start = ((), (), s32[]{:S(2)}) async-start(), calls=%async_computation.19 | async-start | bytes 4325376 | tf_op jit(solution)/shard_map/reduce_scatter | solution.py:262
  776.4 957.5 %reduce-scatter.21.cloned.1.call-start = ((), (), s32[]{:S(2)}) async-start(), calls=%async_computation.22 | async-start | bytes 17301504 | tf_op jit(solution)/shard_map/reduce_scatter | solution.py:192
  787.0 1311.6 %reduce-scatter.23.cloned.1.call-start = ((), (), s32[]{:S(2)}) async-start(), calls=%async_computation.23 | async-start | bytes 17301504 | tf_op jit(solution)/shard_map/reduce_scatter | solution.py:194
  800.1 0.7 copy-start.30
  800.9 3.4 copy-start.5
  804.3 9.1 copy-start.8
  804.3 9.3 copy-start.32
  804.3 9.3 copy-start.33
  813.4 1.6 copy-start.11
  815.0 2.1 copy-start.22
  815.0 3.2 copy-start.7
  815.0 3.2 copy-start.20
  817.0 1.6 copy-start.2
  818.6 2.1 copy-start.23
  818.6 2.1 copy-start.24
  818.6 2.1 copy-start.26
  818.6 2.1 copy-start.27
Sparse Core Ops, SparseCore 0:
  10.9 56.8 all-gather.9
  70.8 55.3 all-gather.15
  129.1 55.2 all-gather.13
  186.4 77.6 all-gather.11
  265.5 79.1 all-gather.17
  347.5 56.8 all-gather.19
  407.3 76.9 all-gather.21
  487.2 75.7 all-gather.23
  617.4 74.8 reduce-scatter.10
  694.5 77.2 reduce-scatter.8
  774.7 141.7 reduce-scatter.18
  919.2 147.3 reduce-scatter.12
  1069.4 148.6 reduce-scatter.16
  1220.8 147.2 reduce-scatter.14
  1370.7 363.1 reduce-scatter.20
  1736.7 361.9 reduce-scatter.22
where the time goes:
time: 2120 us; the launch traced here: 2110 us
  waiting for transfers between devices  1620 us (76%)
  matrix products  203 us (10%)
  blocking collectives  151 us (7%)
  other arithmetic  72.2 us (3%)
  local copies, waits for them, and re-layouts  48.4 us (2%)
    reduce_scatter x1, waiting for transfers between devices, backward_part(): lax.psum_scatter(up_grad, ('dp', 'ctx'), scatter_dimension=0, tiled=True)  366 us
    reduce_scatter x1, waiting for transfers between devices, backward_part(): lax.psum_scatter(down_grad, ('dp', 'ctx'), scatter_dimension=0, tiled=True)  365 us
    reduce_scatter x1, waiting for transfers between devices, backward_part(): lax.psum_scatter(value_weight_grad, ('dp', 'ctx'), scatter_dimension=0, t...  152 us
    reduce_scatter x1, waiting for transfers between devices, backward_part(): lax.psum_scatter(query_weight_grad, ('dp', 'ctx'), scatter_dimension=0, t...  150 us
    reduce_scatter x1, waiting for transfers between devices, backward_part(): lax.psum_scatter(key_weight_grad, ('dp', 'ctx'), scatter_dimension=0, til...  150 us
    unnamed x2, blocking collectives  81 us
    all_gather x1, waiting for transfers between devices, gather_feed(): lax.all_gather(up_weight, ('dp', 'ctx'), axis=0, tiled=True)  76.2 us
    all_gather x1, waiting for transfers between devices, gather_keys(): lax.all_gather(keys, 'ctx', axis=1, tiled=True)  74.4 us
  transfers between devices with their start and end apart: 16, of which 14 were waited for; matrix products, arithmetic and copies ran while one was open for 13% of the time, Pallas kernels for 0%

commit v1 on v0

--- a/solution.py
+++ b/solution.py
@@ -4,6 +4,8 @@
 import jax
 import jax.numpy as jnp
 from jax import lax
+from jax.experimental import pallas as pl
+from jax.experimental.pallas import tpu as pltpu
 from jax.sharding import PartitionSpec as P
 
 H = 16
@@ -309,9 +311,646 @@
     return result + tuple(attn_grads) + tuple(feed_grads)
 
 
+AXES = ("dp", "ctx")
+BLOCK = 256
+
+
+def links(step):
+    pairs = []
+    for o in range(4):
+        for c in range(2):
+            for z in range(4):
+                o2, c2, z2 = step(o, c, z)
+                pairs.append(((o * 2 + c) * 4 + z, (o2 * 2 + c2) * 4 + z2))
+    return pairs
+
+
+X_SWAP = links(lambda o, c, z: (o ^ 1, c, z))
+Y_SWAP = links(lambda o, c, z: (o ^ 2, c, z))
+CORE_SWAP = links(lambda o, c, z: (o, 1 - c, z))
+Z_UP = links(lambda o, c, z: (o, c, (z + 1) % 4))
+Z_DOWN = links(lambda o, c, z: (o, c, (z + 3) % 4))
+TO_SEQ = [links(lambda o, c, z, k=k: (o, z >> 1, 2 * c + ((z & 1) ^ k))) for k in range(2)]
+TO_TOK = [links(lambda o, c, z, k=k: (o, z >> 1, 2 * c + ((z & 1) ^ k))) for k in range(2)]
+
+
+def send(value, pairs):
+    return lax.ppermute(value, AXES, pairs)
+
+
+def place_position():
+    dp = lax.axis_index("dp")
+    return dp // 2, dp % 2, lax.axis_index("ctx")
+
+
+def ring_index(kind, o, z):
+    if kind == "z":
+        return z, (z + 3) % 4, (z + 1) % 4, (z + 2) % 4
+    return o, o ^ 1, o ^ 2, o ^ 3
+
+
+def ring_gather(value, kind):
+    n1, n2 = (Z_UP, Z_DOWN) if kind == "z" else (X_SWAP, Y_SWAP)
+    f1, f2 = (n1, n2) if kind == "z" else (n2, n1)
+    a = send(value, n1)
+    b = send(value, n2)
+    half = value.shape[0] // 2
+    if value.ndim == 2:
+        half = half // 16 * 16
+    c1 = send(a[:half], f1)
+    c2 = send(b[half:], f2)
+    return value, a, b, c1, c2
+
+
+def copy_kernel(moves, n_in, n_out):
+    def body(*refs):
+        ins, outs, sems = refs[:n_in], refs[n_in : n_in + n_out], refs[n_in + n_out]
+        todo = moves(ins, outs)
+        copies = [pltpu.make_async_copy(s, d, sems.at[i]) for i, (s, d) in enumerate(todo)]
+        for copy in copies:
+            copy.start()
+        for copy in copies:
+            copy.wait()
+
+    return body
+
+
+def assemble(pieces, shapes, moves, count, name):
+    any_space = pl.BlockSpec(memory_space=pl.ANY)
+    return pl.pallas_call(
+        copy_kernel(moves, len(pieces), len(shapes)),
+        out_shape=[jax.ShapeDtypeStruct(s, jnp.bfloat16) for s in shapes],
+        in_specs=[any_space] * len(pieces),
+        out_specs=[pl.BlockSpec(memory_space=pltpu.VMEM)] * len(shapes),
+        scratch_shapes=[pltpu.SemaphoreType.DMA((count,))],
+        name=name,
+    )(*pieces)
+
+
+def gather_ring_whole(value, kind, name):
+    pieces = ring_gather(value, kind)
+    rows = value.shape[0]
+    half = pieces[3].shape[0]
+
+    def moves(ins, outs):
+        o, c, z = place_position()
+        me, first, second, both = ring_index(kind, o, z)
+        out = outs[0]
+        return [
+            (ins[0], out.at[me]),
+            (ins[1], out.at[first]),
+            (ins[2], out.at[second]),
+            (ins[3], out.at[both, pl.ds(0, half)]),
+            (ins[4], out.at[both, pl.ds(half, rows - half)]),
+        ]
+
+    return assemble(pieces, [(4,) + value.shape], moves, 5, name)[0]
+
+
+def gather_chips(value, order, shapes, blocks, per_block, name):
+    inner, outer = ("z", "xy") if order == "zx" else ("xy", "z")
+    whole = gather_ring_whole(value, inner, name + "_inner")
+    pieces = ring_gather(whole, outer)
+
+    def moves(ins, outs):
+        o, c, z = place_position()
+        me, first, second, both = ring_index(outer, o, z)
+        todo = []
+        for ref, far, inners in (
+            (ins[0], me, (0, 1, 2, 3)),
+            (ins[1], first, (0, 1, 2, 3)),
+            (ins[2], second, (0, 1, 2, 3)),
+            (ins[3], both, (0, 1)),
+            (ins[4], both, (2, 3)),
+        ):
+            for j, near in enumerate(inners):
+                yx, zz = (far, near) if outer == "xy" else (near, far)
+                todo += blocks(ref.at[j], outs, yx, zz)
+        return todo
+
+    return assemble(pieces, shapes, moves, 16 * per_block, name)
+
+
+def split_half(block, axis):
+    half = block.shape[axis] // 2
+    return (
+        lax.slice_in_dim(block, 0, half, axis=axis),
+        lax.slice_in_dim(block, half, block.shape[axis], axis=axis),
+    )
+
+
+def ring_scatter(parts, axis, cut, kind, o, z):
+    bf = jnp.bfloat16
+    take = lambda k: lax.dynamic_index_in_dim(parts, k, axis, keepdims=False)
+    if kind == "z":
+        n1, n2 = Z_UP, Z_DOWN
+        i1, i2, far = (z + 1) % 4, (z + 3) % 4, (z + 2) % 4
+        me = z
+    else:
+        n1, n2 = X_SWAP, Y_SWAP
+        i1, i2, far = o ^ 1, o ^ 2, o ^ 3
+        me = o
+    h1, h2 = split_half(take(far), cut)
+    t1 = send(h1.astype(bf), n1)
+    t2 = send(h2.astype(bf), n2)
+    b1, b2 = split_half(take(i1), cut), split_half(take(i2), cut)
+    f32 = jnp.float32
+    plus = lambda u, v: (u.astype(f32) + v.astype(f32)).astype(bf)
+    if kind == "z":
+        s1 = lax.concatenate([plus(b1[0], t1), b1[1].astype(bf)], cut)
+        s2 = lax.concatenate([b2[0].astype(bf), plus(b2[1], t2)], cut)
+    else:
+        s1 = lax.concatenate([b1[0].astype(bf), plus(b1[1], t2)], cut)
+        s2 = lax.concatenate([plus(b2[0], t1), b2[1].astype(bf)], cut)
+    u1 = send(s1, n1)
+    u2 = send(s2, n2)
+    return take(me).astype(f32) + u1.astype(f32) + u2.astype(f32)
+
+
+def allowed_mask(column, row, i, low, high):
+    rows = i * BLOCK + lax.broadcasted_iota(jnp.int32, (BLOCK, high - low), 0)
+    cols = low + lax.broadcasted_iota(jnp.int32, (BLOCK, high - low), 1)
+    same = column[i * BLOCK : i * BLOCK + BLOCK, :] == row[:, low:high]
+    return same & (cols <= rows)
+
+
+def key_range(i, total):
+    return max(0, (i * BLOCK - total // 2 + 1) // BLOCK * BLOCK), (i + 1) * BLOCK
+
+
+NT = (((1,), (1,)), ((), ()))
+NN = (((1,), (0,)), ((), ()))
+TN = (((0,), (0,)), ((), ()))
+
+
+def dot32(left, right, dims):
+    return lax.dot_general(left, right, dims, preferred_element_type=jnp.float32)
+
+
+def attend_kernel(scale, column, row, q_ref, k_ref, v_ref, mixed_ref, log_ref):
+    total = q_ref.shape[0]
+    size = q_ref.shape[1] // 2
+    lane = lax.broadcasted_iota(jnp.int32, (BLOCK, 2 * size), 1) < size
+    for i in range(total // BLOCK):
+        low, high = key_range(i, total)
+        rows = pl.ds(i * BLOCK, BLOCK)
+        mask = allowed_mask(column, row, i, low, high)
+        keys, values = k_ref[low:high, :], v_ref[low:high, :]
+        q = q_ref[rows, :]
+        zero = jnp.zeros_like(q)
+        outs, logs = [], []
+        for own in (jnp.where(lane, q, zero), jnp.where(lane, zero, q)):
+            s = jnp.where(mask, dot32(own, keys, NT) * scale, MASKED)
+            top = jnp.max(s, axis=-1, keepdims=True)
+            e = jnp.exp(s - top)
+            tot = jnp.sum(e, axis=-1, keepdims=True)
+            p = (e * (1.0 / tot)).astype(jnp.bfloat16)
+            outs.append(dot32(p, values, NN))
+            logs.append(top + jnp.log(tot))
+        mixed_ref[rows, :] = jnp.where(lane, outs[0], outs[1]).astype(jnp.bfloat16)
+        log_ref[rows, :] = jnp.where(lane, logs[0], logs[1])
+
+
+def attend_back_kernel(
+    scale, column, row, q_ref, k_ref, v_ref, log_ref, grad_ref, out_ref, bias_ref, dk, dv
+):
+    total = q_ref.shape[0]
+    size = q_ref.shape[1] // 2
+    bf = jnp.bfloat16
+    lane = lax.broadcasted_iota(jnp.int32, (BLOCK, 2 * size), 1) < size
+    dk[...] = jnp.zeros_like(dk)
+    dv[...] = jnp.zeros_like(dv)
+    dq_sum = jnp.zeros((1, 2 * size), jnp.float32)
+    for i in range(total // BLOCK):
+        low, high = key_range(i, total)
+        rows = pl.ds(i * BLOCK, BLOCK)
+        mask = allowed_mask(column, row, i, low, high)
+        keys, values = k_ref[low:high, :], v_ref[low:high, :]
+        q, g = q_ref[rows, :], grad_ref[rows, :]
+        zero = jnp.zeros_like(q)
+        dqs = []
+        for h in range(2):
+            qh = jnp.where(lane, q, zero) if h == 0 else jnp.where(lane, zero, q)
+            gh = jnp.where(lane, g, zero) if h == 0 else jnp.where(lane, zero, g)
+            log = log_ref[rows, h * size : h * size + 1]
+            s = jnp.where(mask, dot32(qh, keys, NT) * scale, MASKED)
+            p = jnp.exp(s - log)
+            dp = dot32(gh, values, NT)
+            delta = jnp.sum(p * dp, axis=-1, keepdims=True)
+            ds = (p * (dp - delta)).astype(bf)
+            dqs.append(dot32(ds, keys, NN))
+            dk[low:high, :] += dot32(ds, qh, TN)
+            dv[low:high, :] += dot32(p.astype(bf), gh, TN)
+        dq = (jnp.where(lane, dqs[0], dqs[1]) * scale).astype(bf)
+        out_ref[0, rows, :] = dq
+        dq_sum += jnp.sum(dq.astype(jnp.float32), axis=0, keepdims=True)
+    out_ref[1, :, :] = (dk[...] * scale).astype(bf)
+    dvb = dv[...].astype(bf)
+    out_ref[2, :, :] = dvb
+    bias_ref[0:1, :] = dq_sum
+    bias_ref[1:2, :] = jnp.sum(dvb.astype(jnp.float32), axis=0, keepdims=True)
+
+
+def attend_specs(total, width):
+    pick = lambda j: pl.BlockSpec((None, total, width), lambda h: (j, 0, h))
+    return [
+        pl.BlockSpec((total, 1), lambda h: (0, 0)),
+        pl.BlockSpec((1, total), lambda h: (0, 0)),
+        pick(0),
+        pick(1),
+        pick(2),
+    ]
+
+
+def attend(qkv, column, row, size):
+    _, total, width = qkv.shape
+    pair = 2 * size
+    scale = 1.0 / math.sqrt(size)
+    flat = pl.BlockSpec((total, pair), lambda h: (0, h))
+    return pl.pallas_call(
+        partial(attend_kernel, scale),
+        grid=(width // pair,),
+        in_specs=attend_specs(total, pair),
+        out_specs=[flat, flat],
+        out_shape=[
+            jax.ShapeDtypeStruct((total, width), jnp.bfloat16),
+            jax.ShapeDtypeStruct((total, width), jnp.float32),
+        ],
+        name="attend",
+    )(column, row, qkv, qkv, qkv)
+
+
+def attend_back(qkv, log, grad, column, row, size):
+    _, total, width = qkv.shape
+    pair = 2 * size
+    scale = 1.0 / math.sqrt(size)
+    flat = pl.BlockSpec((total, pair), lambda h: (0, h))
+    return pl.pallas_call(
+        partial(attend_back_kernel, scale),
+        grid=(width // pair,),
+        in_specs=attend_specs(total, pair) + [flat, flat],
+        out_specs=[
+            pl.BlockSpec((3, total, pair), lambda h: (0, 0, h)),
+            pl.BlockSpec((2, pair), lambda h: (0, h)),
+        ],
+        out_shape=[
+            jax.ShapeDtypeStruct((3, total, width), jnp.bfloat16),
+            jax.ShapeDtypeStruct((2, width), jnp.float32),
+        ],
+        scratch_shapes=[pltpu.VMEM((total, pair), jnp.float32)] * 2,
+        name="attend_back",
+    )(column, row, qkv, qkv, qkv, log, grad)
+
+
+def feed_kernel(second, cot, up, bias, down, hidden_ref, pre_ref, sum_ref):
+    total = second.shape[0]
+    root = math.sqrt(0.5)
+    norm = 1.0 / math.sqrt(2.0 * math.pi)
+    sums = jnp.zeros(sum_ref.shape, jnp.float32)
+    for i in range(total // BLOCK):
+        rows = pl.ds(i * BLOCK, BLOCK)
+        v = dot32(second[rows, :], up[...], NN) + bias[...].astype(jnp.float32)
+        g = dot32(cot[rows, :], down[...], NT)
+        cdf = 0.5 * (1.0 + lax.erf(v * root))
+        hidden_ref[rows, :] = (v * cdf).astype(jnp.bfloat16)
+        pre = (g * (cdf + v * (norm * jnp.exp(-0.5 * (v * v))))).astype(jnp.bfloat16)
+        pre_ref[rows, :] = pre
+        sums += jnp.sum(pre.astype(jnp.float32), axis=0, keepdims=True)
+    sum_ref[...] = sums
+
+
+def feed_forward(second, cot, up, bias, down, tile=256):
+    total, width = second.shape
+    units = up.shape[1]
+    whole = pl.BlockSpec((total, width), lambda u: (0, 0))
+    cols = pl.BlockSpec((total, tile), lambda u: (0, u))
+    line = pl.BlockSpec((1, tile), lambda u: (0, u))
+    return pl.pallas_call(
+        feed_kernel,
+        grid=(units // tile,),
+        in_specs=[
+            whole,
+            whole,
+            pl.BlockSpec((width, tile), lambda u: (0, u)),
+            line,
+            pl.BlockSpec((tile, width), lambda u: (u, 0)),
+        ],
+        out_specs=[cols, cols, line],
+        out_shape=[
+            jax.ShapeDtypeStruct((total, units), jnp.bfloat16),
+            jax.ShapeDtypeStruct((total, units), jnp.bfloat16),
+            jax.ShapeDtypeStruct((1, units), jnp.float32),
+        ],
+        name="feed",
+    )(second, cot, up, bias, down)
+
+
+def moments(values):
+    mean = jnp.mean(values, axis=-1, keepdims=True)
+    centered = values - mean
+    spread = lax.rsqrt(jnp.mean(centered * centered, axis=-1, keepdims=True) + EPS)
+    return centered * spread, spread
+
+
+def norm_back(n, spread, gain, grad):
+    g = grad * gain
+    part = spread * (
+        g - jnp.mean(g, axis=-1, keepdims=True) - n * jnp.mean(g * n, axis=-1, keepdims=True)
+    )
+    return part, jnp.sum(grad * n, axis=0), jnp.sum(grad, axis=0)
+
+
+def mm(left, right):
+    return dot32(left, right, NN)
+
+
+def mm_back(left, right):
+    return dot32(left, right, NT)
+
+
+def mm_outer(left, right):
+    return dot32(left, right, TN)
+
+
+def fast_local(
+    inputs,
+    segment_ids,
+    first_gain,
+    first_shift,
+    query_weight,
+    query_bias,
+    key_weight,
+    value_weight,
+    value_bias,
+    out_weight,
+    out_bias,
+    second_gain,
+    second_shift,
+    up_weight,
+    up_bias,
+    down_weight,
+    down_bias,
+    cotangent,
+):
+    bf, f32 = jnp.bfloat16, jnp.float32
+    batch, rows, width = inputs.shape
+    o, c, z = place_position()
+    other = 1 - c
+    total = batch * rows * 2
+    half = width // 2
+    units = up_weight.shape[1]
+    own_units = units // 2
+    lead = query_weight.shape[0]
+    down_rows = down_weight.shape[0]
+    size = width // H
+    small_count = 8 * lead + down_rows
+
+    def halves(weight):
+        view = weight.reshape(lead, 4, 2, weight.shape[1] // 8)
+        pick = lambda k: lax.dynamic_index_in_dim(view, k, 2, keepdims=False).reshape(
+            lead, weight.shape[1] // 2
+        )
+        return pick(c), pick(other)
+
+    q_own, q_far = halves(query_weight)
+    k_own, k_far = halves(key_weight)
+    v_own, v_far = halves(value_weight)
+    up_own, up_far = halves(up_weight)
+    small = jnp.concatenate(
+        [
+            first_gain,
+            first_shift,
+            query_bias,
+            value_bias,
+            out_bias,
+            second_gain,
+            second_shift,
+            down_bias,
+            up_bias,
+        ]
+    )
+    small = jnp.pad(small, (0, half - small_count)).reshape(1, half)
+    small = jnp.concatenate([small, jnp.zeros((7, half), bf)], axis=0)
+    far = send(jnp.concatenate([q_far, k_far, v_far, small], axis=0), CORE_SWAP)
+    up_recv = send(up_far, CORE_SWAP)
+
+    def by_core(own, recv):
+        return jnp.where(c == 0, jnp.stack([own, recv]), jnp.stack([recv, own]))
+
+    attn_pay = jnp.concatenate(
+        [out_weight[:, :half], out_weight[:, half:]]
+        + [
+            by_core(own, far[j * lead : (j + 1) * lead]).reshape(2 * lead, half)
+            for j, own in enumerate((q_own, k_own, v_own))
+        ]
+        + [by_core(small, far[3 * lead :]).reshape(16, half)],
+        axis=0,
+    )
+    up_pay = by_core(up_own, up_recv).reshape(2 * lead, own_units)
+
+    def to_sequence(values, name):
+        tail = values.shape[1:]
+        parity = z & 1
+        first = lax.dynamic_index_in_dim(values, parity, 0, keepdims=False)
+        again = lax.dynamic_index_in_dim(values, 1 - parity, 0, keepdims=False)
+        got = [send(first, TO_SEQ[0]), send(again, TO_SEQ[1])]
+        mate = [send(g, CORE_SWAP) for g in got]
+
+        def moves(ins, outs):
+            _, cc, zz = place_position()
+            out = outs[0]
+            return [
+                (ins[2 * m + k], out.at[(1 - cc if m else cc), (zz & 1) ^ k])
+                for m in range(2)
+                for k in range(2)
+            ]
+
+        return assemble(got + mate, [(2, 2) + tail], moves, 4, name)[0]
+
+    seg = jnp.zeros((batch, 16, width), bf).at[:, 0, :rows].set(segment_ids.astype(bf))
+    x_blocks = to_sequence(jnp.concatenate([inputs, seg], axis=1), "sequence_in")
+    x_bf = x_blocks[:, :, :rows].reshape(total, width)
+    segments = x_blocks[:, :, rows, :rows].reshape(total).astype(f32)
+    column, row = segments.reshape(total, 1), segments.reshape(1, total)
+
+    def attn_blocks(src, outs, yx, zz):
+        todo = [
+            (
+                src.at[pl.ds(h * lead, lead)],
+                outs[1].at[yx, zz, :, pl.ds(h * half, half)],
+            )
+            for h in range(2)
+        ]
+        for j in range(3):
+            for cc in range(2):
+                at = (2 + 2 * j + cc) * lead
+                todo.append((src.at[pl.ds(at, lead)], outs[0].at[j, yx, cc, zz]))
+        todo.append((src.at[pl.ds(8 * lead, 16)], outs[2].at[yx, zz]))
+        return todo
+
+    wqkv, wout, small_all = gather_chips(
+        attn_pay,
+        "zx",
+        [(3, 4, 2, 4, lead, half), (4, 4, lead, width), (4, 4, 16, half)],
+        attn_blocks,
+        9,
+        "gather_attn",
+    )
+    wqkv = wqkv.reshape(3, width, half)
+    wout = wout.reshape(half, width)
+
+    def up_blocks(src, outs, yx, zz):
+        return [(src.at[pl.ds(cc * lead, lead)], outs[0].at[yx, cc, zz]) for cc in range(2)]
+
+    wup = gather_chips(
+        up_pay, "xz", [(4, 2, 4, lead, own_units)], up_blocks, 2, "gather_up"
+    )[0].reshape(width, own_units)
+
+    def down_blocks(src, outs, yx, zz):
+        return [(src, outs[0].at[yx, zz])]
+
+    wdown = gather_chips(
+        down_weight, "zx", [(4, 4, down_rows, width)], down_blocks, 1, "gather_down"
+    )[0].reshape(own_units, width)
+    cot = to_sequence(cotangent, "cotangent_in").reshape(total, width)
+
+    small_all = small_all.reshape(4, 4, 2, 8, half)[:, :, :, 0, :small_count]
+    vectors = small_all[..., : 8 * lead].reshape(4, 4, 2, 8, lead).transpose(3, 0, 2, 1, 4)
+    own_cols = lax.dynamic_index_in_dim(vectors, c, 2, keepdims=False).reshape(8, half)
+    vectors = vectors.reshape(8, width).astype(f32)
+    gain1, shift1, _, _, bias_o, gain2, shift2, bias_d = [vectors[j] for j in range(8)]
+    qkv_bias = jnp.stack([own_cols[2], jnp.zeros_like(own_cols[2]), own_cols[3]]).astype(f32)
+    bias_u = lax.dynamic_index_in_dim(small_all[..., 8 * lead :], c, 2, keepdims=False)
+    bias_u = bias_u.reshape(1, own_units)
+
+    source = x_bf.astype(f32)
+    n1, r1 = moments(source)
+    normed = (n1 * gain1 + shift1).astype(bf)
+    qkv = jnp.einsum("td,jde->jte", normed, wqkv, preferred_element_type=f32)
+    qkv = (qkv + qkv_bias[:, None]).astype(bf)
+    mixed, log = attend(qkv, column, row, size)
+    part = mm(mixed, wout).astype(bf)
+    middle = source + part.astype(f32) + send(part, CORE_SWAP).astype(f32) + bias_o
+
+    n2, r2 = moments(middle)
+    second = (n2 * gain2 + shift2).astype(bf)
+    hidden, pre_grad, up_bias_grad = feed_forward(second, cot, wup, bias_u, wdown)
+    part = mm_back(pre_grad, wup).astype(bf)
+    second_grad = part.astype(f32) + send(part, CORE_SWAP).astype(f32)
+    down_grad = mm_outer(hidden, cot).reshape(4, 4, down_rows, width)
+    up_grad = mm_outer(second, pre_grad).reshape(4, 2, 4, lead, own_units)
+    down_half = ring_scatter(down_grad, 0, 1, "xy", o, z)
+    up_half = ring_scatter(up_grad, 2, 2, "z", o, z)
+    down_out = ring_scatter(down_half, 0, 0, "z", o, z)
+    up_sum = ring_scatter(up_half, 0, 1, "xy", o, z)
+
+    tokens = total // 2
+    mine = lambda a: lax.dynamic_slice_in_dim(a, c * tokens, tokens, 0)
+    theirs = lambda a: lax.dynamic_slice_in_dim(a, other * tokens, tokens, 0)
+
+    out_part = mm(hidden, wdown)
+    out_recv = send(theirs(out_part).astype(bf), CORE_SWAP)
+    result = (mine(middle) + mine(out_part) + out_recv.astype(f32) + bias_d).astype(bf)
+
+    def to_tokens(values):
+        blocks = values.reshape(2, tokens // 2, width)
+        parity = z & 1
+        got = [
+            send(lax.dynamic_index_in_dim(blocks, parity ^ k, 0, keepdims=False), TO_TOK[k])
+            for k in range(2)
+        ]
+        return jnp.where(parity == 0, jnp.stack(got), jnp.stack(got[::-1]))
+
+    output = to_tokens(result)
+
+    middle_part, gain2_grad, shift2_grad = norm_back(n2, r2, gain2, second_grad)
+    cot32 = cot.astype(f32)
+    middle_grad = cot32 + middle_part
+    branch = middle_grad.astype(bf)
+    mixed_grad = mm_back(branch, wout).astype(bf)
+    grads, qv_bias_grad = attend_back(qkv, log, mixed_grad, column, row, size)
+    part = sum(mm_back(grads[j], wqkv[j]) for j in range(3)).astype(bf)
+    normed_grad = part.astype(f32) + send(part, CORE_SWAP).astype(f32)
+    out_grad = mm_outer(mixed, branch).reshape(4, 4, lead, width)
+    qkv_grad = jnp.einsum("td,jte->jde", normed, grads, preferred_element_type=f32)
+    qkv_grad = qkv_grad.reshape(3, 4, 2, 4, lead, half)
+    input_part, gain1_grad, shift1_grad = norm_back(n1, r1, gain1, normed_grad)
+    input_grad = to_tokens((mine(middle_grad) + mine(input_part)).astype(bf)).astype(f32)
+
+    def own_rows(vector):
+        return lax.dynamic_index_in_dim(vector.reshape(4, 2, 4, lead), c, 1, keepdims=False)
+
+    by_chip = lambda vector: vector.reshape(4, 4, -1)
+    small_grad = jnp.concatenate(
+        [
+            own_rows(gain1_grad),
+            own_rows(shift1_grad),
+            by_chip(qv_bias_grad[0]),
+            by_chip(qv_bias_grad[1]),
+            own_rows(jnp.sum(branch.astype(f32), axis=0)),
+            own_rows(gain2_grad),
+            own_rows(shift2_grad),
+            own_rows(jnp.sum(cot32, axis=0)),
+            by_chip(up_bias_grad),
+        ],
+        axis=-1,
+    )
+    small_grad = jnp.pad(small_grad, ((0, 0), (0, 0), (0, half - small_count)))
+    small_grad = jnp.pad(small_grad[:, :, None], ((0, 0), (0, 0), (0, 15), (0, 0)))
+
+    pack = jnp.concatenate(
+        [out_grad[..., :half], out_grad[..., half:]]
+        + [
+            qkv_grad[j].transpose(0, 2, 1, 3, 4).reshape(4, 4, 2 * lead, half)
+            for j in range(3)
+        ]
+        + [small_grad],
+        axis=2,
+    ).astype(bf)
+    pack = ring_scatter(pack, 0, 1, "xy", o, z)
+    pack = ring_scatter(pack, 0, 0, "z", o, z)
+    out_out = jnp.concatenate([pack[:lead], pack[lead : 2 * lead]], axis=1)
+    qkv_sum = pack[2 * lead : 8 * lead].reshape(3, 2, lead, half)
+    small_sum = pack[8 * lead]
+
+    def own_columns(grads, axis):
+        pick = lambda k: lax.dynamic_index_in_dim(grads, k, axis, keepdims=False)
+        kept, got = pick(c), send(pick(other), CORE_SWAP)
+        cols = kept.shape[-1] // 4
+        kept, got = [a.reshape(a.shape[:-1] + (4, 1, cols)) for a in (kept, got)]
+        both = jnp.where(
+            c == 0, jnp.concatenate([kept, got], -2), jnp.concatenate([got, kept], -2)
+        )
+        return both.reshape(both.shape[:-3] + (8 * cols,))
+
+    qkv_out = own_columns(qkv_sum, 1)
+    up_out = own_columns(up_sum, 0)
+    vec = lambda j: small_sum[j * lead : (j + 1) * lead]
+    return (
+        output,
+        input_grad,
+        vec(0),
+        vec(1),
+        qkv_out[0],
+        vec(2),
+        qkv_out[1],
+        qkv_out[2],
+        vec(3),
+        out_out,
+        vec(4),
+        vec(5),
+        vec(6),
+        up_out,
+        small_sum[8 * lead : 8 * lead + down_rows],
+        down_out,
+        vec(7),
+    )
+
+
 def solution(mesh):
+    fast = mesh.shape["dp"] == 8 and mesh.shape["ctx"] == 4
     return jax.shard_map(
-        local,
+        fast_local if fast else local,
         mesh=mesh,
         in_specs=(
             P("dp", "ctx", None),

time: 2120 us -> 629 us (0.30)
  waiting for transfers between devices: 1620 us -> 226 us
  blocking collectives: 151 us -> 0 us
  matrix products: 203 us -> 55 us
  starting transfers between devices: 0.89 us -> 111 us
  Pallas kernels: 0 us -> 86.6 us
  local copies, waits for them, and re-layouts: 48.4 us -> 79.7 us
    reduce_scatter x8 -> x0, waiting for transfers between devices: 1290 us -> none  [the longest x1 366 us: backward_part(): lax.psum_scatter(up_grad, ('dp', 'ctx'), scatter_dimension=0, tiled=True)]
    all_gather x8 -> x0, waiting for transfers between devices: 319 us -> none  [the longest x1 76.2 us: gather_feed(): lax.all_gather(up_weight, ('dp', 'ctx'), axis=0, tiled=True)]
    ppermute x0 -> x68, waiting for transfers between devices: none -> 226 us  [send(): return lax.ppermute(value, AXES, pairs)]
    dot_general x24 -> x12, matrix products: 203 us -> 55 us  [the longest x10 46.5 us: dot32(): lax.dot_general(left, right, dims, preferred_element_type=jnp.float32)]
    ppermute x0 -> x68, starting transfers between devices: none -> 111 us  [send(): return lax.ppermute(value, AXES, pairs)]
    pallas_call x0 -> x11, Pallas kernels: none -> 86.6 us  [the longest x8 26.8 us: assemble(): pl.pallas_call(copy_kernel(moves, len(pieces), len(shapes)), out_shape=[j...]
    unnamed x2 -> x0, blocking collectives: 81 us -> none
    all_gather x2 -> x0, blocking collectives: 69.9 us -> none  [the longest x1 59.4 us: gather_feed(): lax.all_gather(up_bias, ('dp', 'ctx'), axis=0, tiled=True)]
  transfers between devices with their start and end apart: 16 -> 68, of which waited for: 14 -> 24; matrix products, arithmetic and copies ran while one was open for 13% -> 22% of each run, Pallas kernels for 0% -> 11%
where the time goes in v1:
time: 629 us; the launch traced here: 620 us
  waiting for transfers between devices  226 us (36%)
  starting transfers between devices  111 us (18%)
  Pallas kernels  86.6 us (14%)
  local copies, waits for them, and re-layouts  79.7 us (13%)
  other arithmetic  59.6 us (9%)
  matrix products  55 us (9%)
    ppermute x68, waiting for transfers between devices, send(): return lax.ppermute(value, AXES, pairs)  226 us
    ppermute x68, starting transfers between devices, send(): return lax.ppermute(value, AXES, pairs)  111 us
    dot_general x10, matrix products, dot32(): lax.dot_general(left, right, dims, preferred_element_type=jnp.float32)  46.5 us
    pallas_call x8, Pallas kernels, assemble(): pl.pallas_call(copy_kernel(moves, len(pieces), len(shapes)), out_shape=[j...  26.8 us
    pallas_call x1, Pallas kernels, attend_back(): pl.pallas_call(partial(attend_back_kernel, scale), grid=(width // pair,),...  24.6 us
    pallas_call x1, Pallas kernels, attend(): pl.pallas_call(partial(attend_kernel, scale), grid=(width // pair,), in_s...  18.3 us
    pallas_call x1, Pallas kernels, feed_forward(): pl.pallas_call(feed_kernel, grid=(units // tile,), in_specs=[whole, whole...  16.9 us
  transfers between devices with their start and end apart: 68, of which 24 were waited for; matrix products, arithmetic and copies ran while one was open for 22% of the time, Pallas kernels for 11%

profile of v1, /device:TPU:13, one launch (start us, length us, event | category | flops | bytes accessed | tf_op | source)
XLA Modules:
  0.0 620.1 jit_solution(17744939423819823511)
XLA Ops:
  0.7 6.2 concatenate.82
  17.1 6.1 collective-permute-done.5.refs_1_
  26.3 8.1 %collective-permute-start.1 = (bf16[272,1024]{1,0:T(8,128)(2,1)}, bf16[272,1024]{1,0:T(8,128)(2,1)}, u32[]{:S(2)}, u32[]{:S(2)}) collective-permute-start(bf16[272,1024]{1,0:T(8,128)(2,1)} %get-tuple-element.103), channel_id=1, source_target_pairs={{0,1},{1,0},{2,5},{3,4},{4,3},{5,2},{6,7},{7,6},{8,9},{9,8},{10,13... | collective-permute-start | bytes 1671176 | tf_op jit(solution)/shard_map/ppermute | solution.py:338
  38.1 3.0 collective-permute-start.8
  42.1 22.4 %collective-permute-done.8.refs_4_ = bf16[144,512]{1,0:T(8,128)(2,1)S(1)} collective-permute-done((bf16[144,512]{1,0:T(8,128)(2,1)S(1)}, bf16[144,512]{1,0:T(8,128)(2,1)S(1)}, u32[]{:S(2)}, u32[]{:S(2)}) %collective-permute-start.8) | collective-permute-done | bytes 147488 | tf_op jit(solution)/shard_map/ppermute | solution.py:338
  65.2 2.2 gather_attn_inner.1.refs_0_
  67.4 6.1 collective-permute-done.27.refs_1_
  75.0 6.3 %collective-permute-start.3 = (bf16[272,1024]{1,0:T(8,128)(2,1)}, bf16[272,1024]{1,0:T(8,128)(2,1)S(1)}, u32[]{:S(2)}, u32[]{:S(2)}) collective-permute-start(bf16[272,1024]{1,0:T(8,128)(2,1)} %collective-permute-done.1.refs_1_), channel_id=1, source_target_pairs={{0,4},{1,5},{2,6},{3,7},{4,0},{5,1},{6,2},{7,3},{8,12},{9,13},{10,... | collective-permute-start | bytes 1671176 | tf_op jit(solution)/shard_map/ppermute | solution.py:338
  81.7 18.1 %collective-permute-done.19.refs_1_ = bf16[64,2048]{1,0:T(8,128)(2,1)S(1)} collective-permute-done((bf16[64,2048]{1,0:T(8,128)(2,1)S(1)}, bf16[64,2048]{1,0:T(8,128)(2,1)S(1)}, u32[]{:S(2)}, u32[]{:S(2)}) %collective-permute-start.19) | collective-permute-done | bytes 262176 | tf_op jit(solution)/shard_map/ppermute | solution.py:338
  99.8 4.3 collective-permute-start.29
  110.6 10.2 %collective-permute-start.15 = (bf16[256,1024]{1,0:T(8,128)(2,1)}, bf16[256,1024]{1,0:T(8,128)(2,1)}, u32[]{:S(2)}, u32[]{:S(2)}) collective-permute-start(bf16[256,1024]{1,0:T(8,128)(2,1)} %get-tuple-element.113), channel_id=1, source_target_pairs={{0,1},{1,0},{2,5},{3,4},{4,3},{5,2},{6,7},{7,6},{8,9},{9,8},{10,13... | collective-permute-start | bytes 1572872 | tf_op jit(solution)/shard_map/ppermute | solution.py:338
  120.9 2.2 gather_down_inner.1.refs_0_
  123.1 2.1 collective-permute-start.14
  126.7 2.9 sequence_in.1
  140.6 7.1 %collective-permute-done.12.refs_4_ = bf16[2,272,512]{2,1,0:T(8,128)(2,1)} collective-permute-done((bf16[2,272,512]{2,1,0:T(8,128)(2,1)}, bf16[2,272,512]{2,1,0:T(8,128)(2,1)}, u32[]{:S(2)}, u32[]{:S(2)}) %collective-permute-start.12) | collective-permute-done | bytes 557088 | tf_op jit(solution)/shard_map/ppermute | solution.py:338
  148.9 12.4 %collective-permute-done.11.refs_3_ = bf16[2,272,512]{2,1,0:T(8,128)(2,1)} collective-permute-done((bf16[2,272,512]{2,1,0:T(8,128)(2,1)}, bf16[2,272,512]{2,1,0:T(8,128)(2,1)}, u32[]{:S(2)}, u32[]{:S(2)}) %collective-permute-start.11) | collective-permute-done | bytes 557088 | tf_op jit(solution)/shard_map/ppermute | solution.py:338
  162.5 5.6 gather_attn.1
  172.9 4.8 fusion.14.q_ref.k_ref.v_ref
  177.6 18.3 %attend.1 = (bf16[1024,512]{1,0:T(8,128)(2,1)}, f32[1024,512]{1,0:T(8,128)}) custom-call(f32[1024,1]{1,0:T(8,128)} %copy.106.column, f32[1,1024]{1,0:T(1,128)} %bitcast.329, bf16[3,1024,512]{2,1,0:T(8,128)(2,1)} %fusion.14.q_ref.k_ref.v_ref, bf16[3,1024,512]{2,1,0:T(8,128)(2,1)} %fusion.14.q_ref.k_ref.v_ref, bf16[3,1024,512]{2,1,0:T(8,128)(2,1)} %fusion.14.q_ref.k_ref.v_ref), custom_call_target="tpu_custom_call" | custom-call | tf_op jit(solution)/shard_map/attend/pallas_call | solution.py:570
  197.4 4.1 convolution_convert_fusion.1
  201.5 2.4 collective-permute-start.13
  204.0 2.2 gather_up_inner.1.refs_0_
  212.8 40.1 %collective-permute-done.24.refs_2_ = bf16[4,64,2048]{2,1,0:T(8,128)(2,1)S(1)} collective-permute-done((bf16[4,64,2048]{2,1,0:T(8,128)(2,1)}, bf16[4,64,2048]{2,1,0:T(8,128)(2,1)S(1)}, u32[]{:S(2)}, u32[]{:S(2)}) %collective-permute-start.24) | collective-permute-done | bytes 1048608 | tf_op jit(solution)/shard_map/ppermute | solution.py:338
  258.4 2.9 cotangent_in.1
  267.1 4.3 gather_down.1
  271.5 9.9 %collective-permute-done.25.refs_3_ = bf16[2,64,2048]{2,1,0:T(8,128)(2,1)} collective-permute-done((bf16[2,64,2048]{2,1,0:T(8,128)(2,1)}, bf16[2,64,2048]{2,1,0:T(8,128)(2,1)}, u32[]{:S(2)}, u32[]{:S(2)}) %collective-permute-start.25) | collective-permute-done | bytes 524320 | tf_op jit(solution)/shard_map/ppermute | solution.py:338
  281.3 4.5 gather_up.1
  287.5 3.5 fusion.83
  291.0 3.3 fusion.80
  296.9 16.9 %feed.1 = (bf16[1024,2048]{1,0:T(8,128)(2,1)}, bf16[1024,2048]{1,0:T(8,128)(2,1)}, f32[1,2048]{1,0:T(1,128)}) custom-call(bf16[1024,1024]{1,0:T(8,128)(2,1)} %add_convert_fusion.3.second, bf16[1024,1024]{1,0:T(8,128)(2,1)} %bitcast.283, bf16[1024,2048]{1,0:T(8,128)(2,1)} %bitcast.287, bf16[1,2048]{1,0:T(2,128)(2,1)} %bitcast.331, bf16[2048,1024]{1,0:T(8,128)(2,1)} %bitcast.285), custom_call_target="tpu_custom_call" | custom-call | tf_op jit(solution)/shard_map/feed/pallas_call | solution.py:628
  313.9 9.5 %convolution_convert_fusion = bf16[1024,1024]{1,0:T(8,128)(2,1)} fusion(bf16[1024,2048]{1,0:T(8,128)(2,1)} %get-tuple-element.44, bf16[1024,2048]{1,0:T(8,128)(2,1)} %bitcast.288), kind=kOutput, calls=%fused_computation.60 | convolution fusion | flops 4296015872 | bytes 10485760 | tf_op jit(solution)/shard_map/dot_general | solution.py:487
  323.4 6.8 %fusion.92 = f32[1024,2048]{1,0:T(8,128)} fusion(bf16[1024,1024]{1,0:T(8,128)(2,1)S(1)} %copy-done.8, bf16[1024,2048]{1,0:T(8,128)(2,1)S(1)} %copy-done.70), kind=kOutput, calls=%fused_computation.262 | convolution fusion | flops 4294967296 | bytes 14680064 | tf_op jit(solution)/shard_map/dot_general | solution.py:487
  330.2 6.0 fusion.91
  336.3 6.4 %copy.127 = bf16[2048,1024]{1,0:T(8,128)(2,1)} copy(bf16[2048,1024]{0,1:T(8,128)(2,1)} %bitcast.295) | data formatting | bytes 8388608 | tf_op jit(solution)/shard_map/dot_general | solution.py:487
  346.3 7.1 %fusion.93 = f32[4,4,128,1024]{3,2,1,0:T(8,128)S(1)} fusion(bf16[4,4,128,1024]{3,2,1,0:T(8,128)(2,1)} %bitcast.294, bf16[1024,1024,1,1]{1,0,3,2:T(8,128)(2,1)} %bitcast.284), kind=kOutput, calls=%fused_computation.263 | convolution fusion | flops 4294967296 | bytes 14680064 | tf_op jit(solution)/shard_map/dot_general | solution.py:487
  355.8 2.3 collective-permute-start.53
  359.5 9.0 %collective-permute-done.53 = bf16[4,2,16,2048]{3,2,1,0:T(8,128)(2,1)S(1)} collective-permute-done((bf16[4,2,16,2048]{3,2,1,0:T(8,128)(2,1)S(1)}, bf16[4,2,16,2048]{3,2,1,0:T(8,128)(2,1)S(1)}, u32[]{:S(2)}, u32[]{:S(2)}) %collective-permute-start.53) | collective-permute-done | bytes 524320 | tf_op jit(solution)/shard_map/ppermute | solution.py:338
  369.9 11.3 %collective-permute-done.51 = bf16[4,2,16,2048]{3,2,1,0:T(8,128)(2,1)S(1)} collective-permute-done((bf16[4,2,16,2048]{3,2,1,0:T(8,128)(2,1)S(1)}, bf16[4,2,16,2048]{3,2,1,0:T(8,128)(2,1)S(1)}, u32[]{:S(2)}, u32[]{:S(2)}) %collective-permute-start.51) | collective-permute-done | bytes 524320 | tf_op jit(solution)/shard_map/ppermute | solution.py:338
  381.2 3.0 collective-permute-start.54
  393.3 13.5 %collective-permute-done.54 = bf16[4,2,32,2048]{3,2,1,0:T(8,128)(2,1)S(1)} collective-permute-done((bf16[4,2,32,2048]{3,2,1,0:T(8,128)(2,1)S(1)}, bf16[4,2,32,2048]{3,2,1,0:T(8,128)(2,1)S(1)}, u32[]{:S(2)}, u32[]{:S(2)}) %collective-permute-start.54) | collective-permute-done | bytes 1048608 | tf_op jit(solution)/shard_map/ppermute | solution.py:338
  406.8 9.0 %collective-permute-start.36 = (bf16[256,1024]{1,0:T(8,128)(2,1)}, bf16[256,1024]{1,0:T(8,128)(2,1)}, u32[]{:S(2)}, u32[]{:S(2)}) collective-permute-start(bf16[256,1024]{1,0:T(8,128)(2,1)} %get-tuple-element.111), channel_id=1, source_target_pairs={{0,0},{1,1},{2,4},{3,5},{4,2},{5,3},{6,6},{7,7},{8,8},{9,9},{10,12... | collective-permute-start | bytes 1572872 | tf_op jit(solution)/shard_map/ppermute | solution.py:338
  415.8 16.5 %collective-permute-done.52 = bf16[4,2,32,2048]{3,2,1,0:T(8,128)(2,1)S(1)} collective-permute-done((bf16[4,2,32,2048]{3,2,1,0:T(8,128)(2,1)}, bf16[4,2,32,2048]{3,2,1,0:T(8,128)(2,1)S(1)}, u32[]{:S(2)}, u32[]{:S(2)}) %collective-permute-start.52) | collective-permute-done | bytes 1048608 | tf_op jit(solution)/shard_map/ppermute | solution.py:338
  432.3 3.2 collective-permute-start.37
  441.9 2.6 collective-permute-done.57
  446.1 3.0 multiply_reduce_fusion
  449.2 2.7 convert_reduce_fusion.2
  451.9 2.3 convolution_convert_fusion.3.grad_ref
  454.3 24.6 %attend_back.1 = (bf16[3,1024,512]{2,1,0:T(8,128)(2,1)}, f32[2,512]{1,0:T(2,128)}) custom-call(f32[1024,1]{1,0:T(8,128)} %copy.106.column, f32[1,1024]{1,0:T(1,128)} %bitcast.330, bf16[3,1024,512]{2,1,0:T(8,128)(2,1)} %fusion.14.q_ref.k_ref.v_ref, bf16[3,1024,512]{2,1,0:T(8,128)(2,1)} %fusion.14.q_ref.k_ref.v_ref, ...), custom_call_target="tpu_custom_call" | custom-call | tf_op jit(solution)/shard_map/attend_back/pallas_call | solution.py:588
  478.9 3.0 fusion.36
  483.2 2.6 add_convert_fusion.2
  485.9 4.2 collective-permute-start.39
  496.7 3.8 convolution_convert_fusion.2
  502.2 6.2 %fusion.11 = (bf16[1024]{0:T(1024)(128)(2,1)S(1)}, bf16[1024]{0:T(1024)(128)(2,1)S(1)}, f32[1024]{0:T(1024)}, f32[1024]{0:T(1024)}, f32[1024,1024]{1,0:T(8,128)}, /*index=5*/f32[1024,1024]{1,0:T(8,128)S(1)}) fusion(bf16[1024,1024]{1,0:T(8,128)(2,1)} %collective-permute-done.39, bf16[1024,1024]{1,0:T(8,128)(2,1)} %add_convert_fusion.2, ...), kind=kLoop, calls=%fused_computation.30 | loop fusion | flops 13627392 | bytes 14704640 | tf_op jit(solution)/shard_map/reduce_sum | solution.py:660
  508.5 3.7 convert_bitcast_fusion
  522.1 2.1 dynamic-slice_bitcast_fusion.6
  529.5 8.5 %collective-permute-done.44 = bf16[4,136,512]{2,1,0:T(8,128)(2,1)S(1)} collective-permute-done((bf16[4,136,512]{2,1,0:T(8,128)(2,1)S(1)}, bf16[4,136,512]{2,1,0:T(8,128)(2,1)S(1)}, u32[]{:S(2)}, u32[]{:S(2)}) %collective-permute-start.44) | collective-permute-done | bytes 557088 | tf_op jit(solution)/shard_map/ppermute | solution.py:338
  542.4 2.6 collective-permute-start.59
  545.0 2.7 maximum_select_fusion
  552.0 3.3 fusion.22
  555.3 9.9 %collective-permute-done.45 = bf16[4,272,512]{2,1,0:T(8,128)(2,1)S(1)} collective-permute-done((bf16[4,272,512]{2,1,0:T(8,128)(2,1)}, bf16[4,272,512]{2,1,0:T(8,128)(2,1)S(1)}, u32[]{:S(2)}, u32[]{:S(2)}) %collective-permute-start.45) | collective-permute-done | bytes 1114144 | tf_op jit(solution)/shard_map/ppermute | solution.py:338
  570.0 8.2 %collective-permute-start.40 = (bf16[256,1024]{1,0:T(8,128)(2,1)}, bf16[256,1024]{1,0:T(8,128)(2,1)}, u32[]{:S(2)}, u32[]{:S(2)}) collective-permute-start(bf16[256,1024]{1,0:T(8,128)(2,1)} %get-tuple-element.109), channel_id=1, source_target_pairs={{0,0},{1,1},{2,4},{3,5},{4,2},{5,3},{6,6},{7,7},{8,8},{9,9},{10,12... | collective-permute-start | bytes 1572872 | tf_op jit(solution)/shard_map/ppermute | solution.py:338
  583.4 20.9 %collective-permute-done.40 = bf16[256,1024]{1,0:T(8,128)(2,1)} collective-permute-done((bf16[256,1024]{1,0:T(8,128)(2,1)}, bf16[256,1024]{1,0:T(8,128)(2,1)}, u32[]{:S(2)}, u32[]{:S(2)}) %collective-permute-start.40) | collective-permute-done | bytes 524320 | tf_op jit(solution)/shard_map/ppermute | solution.py:338
  604.3 5.5 collective-permute-done.41
  609.8 3.0 fusion.34
  (458 shorter events, 145.5 us)
Async XLA Ops:
  15.1 21.5 %collective-permute-start.18 = (bf16[32,2048]{1,0:T(8,128)(2,1)}, bf16[32,2048]{1,0:T(8,128)(2,1)S(1)}, u32[]{:S(2)}, u32[]{:S(2)}) collective-permute-start(bf16[32,2048]{1,0:T(8,128)(2,1)} %bitcast.130), channel_id=1, source_target_pairs={{0,4},{1,5},{2,6},{3,7},{4,0},{5,1},{6,2},{7,3},{8,12},{9,13},{10,... | collective-permute-start | bytes 393224 | tf_op jit(solution)/shard_map/ppermute | solution.py:338
  15.4 7.8 %collective-permute-start.5 = (bf16[272,512]{1,0:T(8,128)(2,1)S(1)}, bf16[272,512]{1,0:T(8,128)(2,1)S(1)}, u32[]{:S(2)}, u32[]{:S(2)}) collective-permute-start(bf16[272,512]{1,0:T(8,128)(2,1)S(1)} %constant_dynamic-update-slice_fusion.refs_0_), channel_id=1, source_target_pairs={{0,1},{1,2},{2,3},{3,0},{4,5},{5,6},{6,7},{7,4},{8,9},{9,10},{10,1... | collective-permute-start | bytes 835592 | tf_op jit(solution)/shard_map/ppermute | solution.py:338
  16.7 19.7 %collective-permute-start.6 = (bf16[272,512]{1,0:T(8,128)(2,1)S(1)}, bf16[272,512]{1,0:T(8,128)(2,1)S(1)}, u32[]{:S(2)}, u32[]{:S(2)}) collective-permute-start(bf16[272,512]{1,0:T(8,128)(2,1)S(1)} %constant_dynamic-update-slice_fusion.refs_0_), channel_id=1, source_target_pairs={{0,3},{1,0},{2,1},{3,2},{4,7},{5,4},{6,5},{7,6},{8,11},{9,8},{10,9... | collective-permute-start | bytes 835592 | tf_op jit(solution)/shard_map/ppermute | solution.py:338
  23.8 14.2 %collective-permute-start.7 = (bf16[128,512]{1,0:T(8,128)(2,1)}, bf16[128,512]{1,0:T(8,128)(2,1)S(1)}, u32[]{:S(2)}, u32[]{:S(2)}) collective-permute-start(bf16[128,512]{1,0:T(8,128)(2,1)} %slice.523), channel_id=1, source_target_pairs={{0,1},{1,2},{2,3},{3,0},{4,5},{5,6},{6,7},{7,4},{8,9},{9,10},{10,1... | collective-permute-start | bytes 393224 | tf_op jit(solution)/shard_map/ppermute | solution.py:338
  26.3 48.7 %collective-permute-start.1 = (bf16[272,1024]{1,0:T(8,128)(2,1)}, bf16[272,1024]{1,0:T(8,128)(2,1)}, u32[]{:S(2)}, u32[]{:S(2)}) collective-permute-start(bf16[272,1024]{1,0:T(8,128)(2,1)} %get-tuple-element.103), channel_id=1, source_target_pairs={{0,1},{1,0},{2,5},{3,4},{4,3},{5,2},{6,7},{7,6},{8,9},{9,8},{10,13... | collective-permute-start | bytes 1671176 | tf_op jit(solution)/shard_map/ppermute | solution.py:338
  34.4 46.9 %collective-permute-start = (bf16[272,1024]{1,0:T(8,128)(2,1)}, bf16[272,1024]{1,0:T(8,128)(2,1)}, u32[]{:S(2)}, u32[]{:S(2)}) collective-permute-start(bf16[272,1024]{1,0:T(8,128)(2,1)} %get-tuple-element.104), channel_id=1, source_target_pairs={{0,0},{1,1},{2,4},{3,5},{4,2},{5,3},{6,6},{7,7},{8,8},{9,9},{10,12... | collective-permute-start | bytes 1671176 | tf_op jit(solution)/shard_map/ppermute | solution.py:338
  36.5 37.1 %collective-permute-start.27 = (bf16[128,1024]{1,0:T(8,128)(2,1)}, bf16[128,1024]{1,0:T(8,128)(2,1)S(1)}, u32[]{:S(2)}, u32[]{:S(2)}) collective-permute-start(bf16[128,1024]{1,0:T(8,128)(2,1)} %refs_0_.1), channel_id=1, source_target_pairs={{0,1},{1,2},{2,3},{3,0},{4,5},{5,6},{6,7},{7,4},{8,9},{9,10},{10,1... | collective-permute-start | bytes 786440 | tf_op jit(solution)/shard_map/ppermute | solution.py:338
  36.6 37.2 %collective-permute-start.28 = (bf16[128,1024]{1,0:T(8,128)(2,1)}, bf16[128,1024]{1,0:T(8,128)(2,1)S(1)}, u32[]{:S(2)}, u32[]{:S(2)}) collective-permute-start(bf16[128,1024]{1,0:T(8,128)(2,1)} %refs_0_.1), channel_id=1, source_target_pairs={{0,3},{1,0},{2,1},{3,2},{4,7},{5,4},{6,5},{7,6},{8,11},{9,8},{10,9... | collective-permute-start | bytes 786440 | tf_op jit(solution)/shard_map/ppermute | solution.py:338
  38.1 26.4 %collective-permute-start.8 = (bf16[144,512]{1,0:T(8,128)(2,1)S(1)}, bf16[144,512]{1,0:T(8,128)(2,1)S(1)}, u32[]{:S(2)}, u32[]{:S(2)}) collective-permute-start(bf16[144,512]{1,0:T(8,128)(2,1)S(1)} %slice.524), channel_id=1, source_target_pairs={{0,3},{1,0},{2,1},{3,2},{4,7},{5,4},{6,5},{7,6},{8,11},{9,8},{10,9... | collective-permute-start | bytes 442376 | tf_op jit(solution)/shard_map/ppermute | solution.py:338
  64.5 16.9 %collective-permute-start.20 = (bf16[64,2048]{1,0:T(8,128)(2,1)S(1)}, bf16[64,2048]{1,0:T(8,128)(2,1)S(1)}, u32[]{:S(2)}, u32[]{:S(2)}) collective-permute-start(bf16[64,2048]{1,0:T(8,128)(2,1)S(1)} %bitcast.312), channel_id=1, source_target_pairs={{0,16},{1,17},{2,18},{3,19},{4,20},{5,21},{6,22},{7,23},{8,24},{9,... | collective-permute-start | bytes 786440 | tf_op jit(solution)/shard_map/ppermute | solution.py:338
  73.5 59.1 %collective-permute-start.10 = (bf16[4,272,512]{2,1,0:T(8,128)(2,1)}, bf16[4,272,512]{2,1,0:T(8,128)(2,1)}, u32[]{:S(2)}, u32[]{:S(2)}) collective-permute-start(bf16[4,272,512]{2,1,0:T(8,128)(2,1)} %gather_attn_inner.1.refs_0_), channel_id=1, source_target_pairs={{0,16},{1,17},{2,18},{3,19},{4,20},{5,21},{6,22},{7,23},{8,24},{9,... | collective-permute-start | bytes 3342344 | tf_op jit(solution)/shard_map/ppermute | solution.py:338
  73.8 62.0 %collective-permute-start.9 = (bf16[4,272,512]{2,1,0:T(8,128)(2,1)}, bf16[4,272,512]{2,1,0:T(8,128)(2,1)}, u32[]{:S(2)}, u32[]{:S(2)}) collective-permute-start(bf16[4,272,512]{2,1,0:T(8,128)(2,1)} %gather_attn_inner.1.refs_0_), channel_id=1, source_target_pairs={{0,8},{1,9},{2,10},{3,11},{4,12},{5,13},{6,14},{7,15},{8,0},{9,1},... | collective-permute-start | bytes 3342344 | tf_op jit(solution)/shard_map/ppermute | solution.py:338
  75.0 48.1 %collective-permute-start.3 = (bf16[272,1024]{1,0:T(8,128)(2,1)}, bf16[272,1024]{1,0:T(8,128)(2,1)S(1)}, u32[]{:S(2)}, u32[]{:S(2)}) collective-permute-start(bf16[272,1024]{1,0:T(8,128)(2,1)} %collective-permute-done.1.refs_1_), channel_id=1, source_target_pairs={{0,4},{1,5},{2,6},{3,7},{4,0},{5,1},{6,2},{7,3},{8,12},{9,13},{10,... | collective-permute-start | bytes 1671176 | tf_op jit(solution)/shard_map/ppermute | solution.py:338
  81.3 43.9 %collective-permute-start.2 = (bf16[272,1024]{1,0:T(8,128)(2,1)}, bf16[272,1024]{1,0:T(8,128)(2,1)}, u32[]{:S(2)}, u32[]{:S(2)}) collective-permute-start(bf16[272,1024]{1,0:T(8,128)(2,1)} %collective-permute-done.refs_0_), channel_id=1, source_target_pairs={{0,4},{1,5},{2,6},{3,7},{4,0},{5,1},{6,2},{7,3},{8,12},{9,13},{10,... | collective-permute-start | bytes 1671176 | tf_op jit(solution)/shard_map/ppermute | solution.py:338
  81.4 18.4 %collective-permute-start.19 = (bf16[64,2048]{1,0:T(8,128)(2,1)S(1)}, bf16[64,2048]{1,0:T(8,128)(2,1)S(1)}, u32[]{:S(2)}, u32[]{:S(2)}) collective-permute-start(bf16[64,2048]{1,0:T(8,128)(2,1)S(1)} %bitcast.313), channel_id=1, source_target_pairs={{0,8},{1,9},{2,10},{3,11},{4,12},{5,13},{6,14},{7,15},{8,0},{9,1},... | collective-permute-start | bytes 786440 | tf_op jit(solution)/shard_map/ppermute | solution.py:338
  99.8 6.3 %collective-permute-start.29 = (bf16[64,1024]{1,0:T(8,128)(2,1)S(1)}, bf16[64,1024]{1,0:T(8,128)(2,1)S(1)}, u32[]{:S(2)}, u32[]{:S(2)}) collective-permute-start(bf16[64,1024]{1,0:T(8,128)(2,1)S(1)} %slice.541), channel_id=1, source_target_pairs={{0,1},{1,2},{2,3},{3,0},{4,5},{5,6},{6,7},{7,4},{8,9},{9,10},{10,1... | collective-permute-start | bytes 393224 | tf_op jit(solution)/shard_map/ppermute | solution.py:338
  106.1 4.6 collective-permute-start.30
  110.6 95.5 %collective-permute-start.15 = (bf16[256,1024]{1,0:T(8,128)(2,1)}, bf16[256,1024]{1,0:T(8,128)(2,1)}, u32[]{:S(2)}, u32[]{:S(2)}) collective-permute-start(bf16[256,1024]{1,0:T(8,128)(2,1)} %get-tuple-element.113), channel_id=1, source_target_pairs={{0,1},{1,0},{2,5},{3,4},{4,3},{5,2},{6,7},{7,6},{8,9},{9,8},{10,13... | collective-permute-start | bytes 1572872 | tf_op jit(solution)/shard_map/ppermute | solution.py:338
  123.1 84.9 %collective-permute-start.14 = (bf16[256,1024]{1,0:T(8,128)(2,1)}, bf16[256,1024]{1,0:T(8,128)(2,1)}, u32[]{:S(2)}, u32[]{:S(2)}) collective-permute-start(bf16[256,1024]{1,0:T(8,128)(2,1)} %get-tuple-element.114), channel_id=1, source_target_pairs={{0,0},{1,1},{2,4},{3,5},{4,2},{5,3},{6,6},{7,7},{8,8},{9,9},{10,12... | collective-permute-start | bytes 1572872 | tf_op jit(solution)/shard_map/ppermute | solution.py:338
  125.3 82.7 %collective-permute-start.32 = (bf16[4,128,1024]{2,1,0:T(8,128)(2,1)}, bf16[4,128,1024]{2,1,0:T(8,128)(2,1)}, u32[]{:S(2)}, u32[]{:S(2)}) collective-permute-start(bf16[4,128,1024]{2,1,0:T(8,128)(2,1)} %gather_down_inner.1.refs_0_), channel_id=1, source_target_pairs={{0,16},{1,17},{2,18},{3,19},{4,20},{5,21},{6,22},{7,23},{8,24},{9,... | collective-permute-start | bytes 3145736 | tf_op jit(solution)/shard_map/ppermute | solution.py:338
  134.5 13.2 %collective-permute-start.12 = (bf16[2,272,512]{2,1,0:T(8,128)(2,1)}, bf16[2,272,512]{2,1,0:T(8,128)(2,1)}, u32[]{:S(2)}, u32[]{:S(2)}) collective-permute-start(bf16[2,272,512]{2,1,0:T(8,128)(2,1)} %slice.526), channel_id=1, source_target_pairs={{0,8},{1,9},{2,10},{3,11},{4,12},{5,13},{6,14},{7,15},{8,0},{9,1},... | collective-permute-start | bytes 1671176 | tf_op jit(solution)/shard_map/ppermute | solution.py:338
  137.6 23.7 %collective-permute-start.11 = (bf16[2,272,512]{2,1,0:T(8,128)(2,1)}, bf16[2,272,512]{2,1,0:T(8,128)(2,1)}, u32[]{:S(2)}, u32[]{:S(2)}) collective-permute-start(bf16[2,272,512]{2,1,0:T(8,128)(2,1)} %slice.525), channel_id=1, source_target_pairs={{0,16},{1,17},{2,18},{3,19},{4,20},{5,21},{6,22},{7,23},{8,24},{9,... | collective-permute-start | bytes 1671176 | tf_op jit(solution)/shard_map/ppermute | solution.py:338
  147.7 61.3 %collective-permute-start.31 = (bf16[4,128,1024]{2,1,0:T(8,128)(2,1)S(1)}, bf16[4,128,1024]{2,1,0:T(8,128)(2,1)}, u32[]{:S(2)}, u32[]{:S(2)}) collective-permute-start(bf16[4,128,1024]{2,1,0:T(8,128)(2,1)S(1)} %copy-done.12), channel_id=1, source_target_pairs={{0,8},{1,9},{2,10},{3,11},{4,12},{5,13},{6,14},{7,15},{8,0},{9,1},... | collective-permute-start | bytes 3145736 | tf_op jit(solution)/shard_map/ppermute | solution.py:338
  161.3 34.6 %collective-permute-start.22 = (bf16[32,2048]{1,0:T(8,128)(2,1)}, bf16[32,2048]{1,0:T(8,128)(2,1)}, u32[]{:S(2)}, u32[]{:S(2)}) collective-permute-start(bf16[32,2048]{1,0:T(8,128)(2,1)} %slice.537), channel_id=1, source_target_pairs={{0,8},{1,9},{2,10},{3,11},{4,12},{5,13},{6,14},{7,15},{8,0},{9,1},... | collective-permute-start | bytes 393224 | tf_op jit(solution)/shard_map/ppermute | solution.py:338
  195.9 5.6 collective-permute-start.21
  201.5 89.5 %collective-permute-start.13 = (bf16[1024,1024]{1,0:T(8,128)(2,1)}, bf16[1024,1024]{1,0:T(8,128)(2,1)}, u32[]{:S(2)}, u32[]{:S(2)}) collective-permute-start(bf16[1024,1024]{1,0:T(8,128)(2,1)} %convolution_convert_fusion.1), channel_id=1, source_target_pairs={{0,4},{1,5},{2,6},{3,7},{4,0},{5,1},{6,2},{7,3},{8,12},{9,13},{10,... | collective-permute-start | bytes 6291464 | tf_op jit(solution)/shard_map/ppermute | solution.py:338
  206.2 46.8 %collective-permute-start.24 = (bf16[4,64,2048]{2,1,0:T(8,128)(2,1)}, bf16[4,64,2048]{2,1,0:T(8,128)(2,1)S(1)}, u32[]{:S(2)}, u32[]{:S(2)}) collective-permute-start(bf16[4,64,2048]{2,1,0:T(8,128)(2,1)} %gather_up_inner.1.refs_0_), channel_id=1, source_target_pairs={{0,3},{1,0},{2,1},{3,2},{4,7},{5,4},{6,5},{7,6},{8,11},{9,8},{10,9... | collective-permute-start | bytes 3145736 | tf_op jit(solution)/shard_map/ppermute | solution.py:338
  208.0 46.7 %collective-permute-start.23 = (bf16[4,64,2048]{2,1,0:T(8,128)(2,1)}, bf16[4,64,2048]{2,1,0:T(8,128)(2,1)S(1)}, u32[]{:S(2)}, u32[]{:S(2)}) collective-permute-start(bf16[4,64,2048]{2,1,0:T(8,128)(2,1)} %gather_up_inner.1.refs_0_), channel_id=1, source_target_pairs={{0,1},{1,2},{2,3},{3,0},{4,5},{5,6},{6,7},{7,4},{8,9},{9,10},{10,1... | collective-permute-start | bytes 3145736 | tf_op jit(solution)/shard_map/ppermute | solution.py:338
  208.0 48.6 %collective-permute-start.17 = (bf16[256,1024]{1,0:T(8,128)(2,1)}, bf16[256,1024]{1,0:T(8,128)(2,1)}, u32[]{:S(2)}, u32[]{:S(2)}) collective-permute-start(bf16[256,1024]{1,0:T(8,128)(2,1)} %collective-permute-done.15.refs_1_), channel_id=1, source_target_pairs={{0,4},{1,5},{2,6},{3,7},{4,0},{5,1},{6,2},{7,3},{8,12},{9,13},{10,... | collective-permute-start | bytes 1572872 | tf_op jit(solution)/shard_map/ppermute | solution.py:338
  209.0 49.4 %collective-permute-start.16 = (bf16[256,1024]{1,0:T(8,128)(2,1)}, bf16[256,1024]{1,0:T(8,128)(2,1)}, u32[]{:S(2)}, u32[]{:S(2)}) collective-permute-start(bf16[256,1024]{1,0:T(8,128)(2,1)} %collective-permute-done.14.refs_0_), channel_id=1, source_target_pairs={{0,4},{1,5},{2,6},{3,7},{4,0},{5,1},{6,2},{7,3},{8,12},{9,13},{10,... | collective-permute-start | bytes 1572872 | tf_op jit(solution)/shard_map/ppermute | solution.py:338
  253.0 12.3 %collective-permute-start.34 = (bf16[2,128,1024]{2,1,0:T(8,128)(2,1)}, bf16[2,128,1024]{2,1,0:T(8,128)(2,1)S(1)}, u32[]{:S(2)}, u32[]{:S(2)}) collective-permute-start(bf16[2,128,1024]{2,1,0:T(8,128)(2,1)} %slice.544), channel_id=1, source_target_pairs={{0,8},{1,9},{2,10},{3,11},{4,12},{5,13},{6,14},{7,15},{8,0},{9,1},... | collective-permute-start | bytes 1572872 | tf_op jit(solution)/shard_map/ppermute | solution.py:338
  254.8 12.3 %collective-permute-start.33 = (bf16[2,128,1024]{2,1,0:T(8,128)(2,1)}, bf16[2,128,1024]{2,1,0:T(8,128)(2,1)}, u32[]{:S(2)}, u32[]{:S(2)}) collective-permute-start(bf16[2,128,1024]{2,1,0:T(8,128)(2,1)} %slice.543), channel_id=1, source_target_pairs={{0,16},{1,17},{2,18},{3,19},{4,20},{5,21},{6,22},{7,23},{8,24},{9,... | collective-permute-start | bytes 1572872 | tf_op jit(solution)/shard_map/ppermute | solution.py:338
  256.6 14.8 %collective-permute-start.26 = (bf16[2,64,2048]{2,1,0:T(8,128)(2,1)}, bf16[2,64,2048]{2,1,0:T(8,128)(2,1)S(1)}, u32[]{:S(2)}, u32[]{:S(2)}) collective-permute-start(bf16[2,64,2048]{2,1,0:T(8,128)(2,1)} %slice.539), channel_id=1, source_target_pairs={{0,3},{1,0},{2,1},{3,2},{4,7},{5,4},{6,5},{7,6},{8,11},{9,8},{10,9... | collective-permute-start | bytes 1572872 | tf_op jit(solution)/shard_map/ppermute | solution.py:338
  258.4 22.9 %collective-permute-start.25 = (bf16[2,64,2048]{2,1,0:T(8,128)(2,1)}, bf16[2,64,2048]{2,1,0:T(8,128)(2,1)}, u32[]{:S(2)}, u32[]{:S(2)}) collective-permute-start(bf16[2,64,2048]{2,1,0:T(8,128)(2,1)} %slice.538), channel_id=1, source_target_pairs={{0,1},{1,2},{2,3},{3,0},{4,5},{5,6},{6,7},{7,4},{8,9},{9,10},{10,1... | collective-permute-start | bytes 1572872 | tf_op jit(solution)/shard_map/ppermute | solution.py:338
  344.6 44.8 %collective-permute-start.35 = (bf16[512,1024]{1,0:T(8,128)(2,1)S(1)}, bf16[512,1024]{1,0:T(8,128)(2,1)}, u32[]{:S(2)}, u32[]{:S(2)}) collective-permute-start(bf16[512,1024]{1,0:T(8,128)(2,1)S(1)} %dynamic-slice_convert_fusion.2), channel_id=1, source_target_pairs={{0,4},{1,5},{2,6},{3,7},{4,0},{5,1},{6,2},{7,3},{8,12},{9,13},{10,... | collective-permute-start | bytes 3145736 | tf_op jit(solution)/shard_map/ppermute | solution.py:338
  346.2 99.9 %collective-permute-start.38 = (bf16[1024,1024]{1,0:T(8,128)(2,1)}, bf16[1024,1024]{1,0:T(8,128)(2,1)S(1)}, u32[]{:S(2)}, u32[]{:S(2)}) collective-permute-start(bf16[1024,1024]{1,0:T(8,128)(2,1)} %convolution_convert_fusion), channel_id=1, source_target_pairs={{0,4},{1,5},{2,6},{3,7},{4,0},{5,1},{6,2},{7,3},{8,12},{9,13},{10,... | collective-permute-start | bytes 6291464 | tf_op jit(solution)/shard_map/ppermute | solution.py:338
  354.4 33.8 %collective-permute-start.60 = (bf16[4,64,1024]{2,1,0:T(8,128)(2,1)}, bf16[4,64,1024]{2,1,0:T(8,128)(2,1)S(1)}, u32[]{:S(2)}, u32[]{:S(2)}) collective-permute-start(bf16[4,64,1024]{2,1,0:T(8,128)(2,1)} %get-tuple-element.105), channel_id=1, source_target_pairs={{0,16},{1,17},{2,18},{3,19},{4,20},{5,21},{6,22},{7,23},{8,24},{9,... | collective-permute-start | bytes 1572872 | tf_op jit(solution)/shard_map/ppermute | solution.py:338
  355.0 30.4 %collective-permute-start.62 = (bf16[4,64,1024]{2,1,0:T(8,128)(2,1)S(1)}, bf16[4,64,1024]{2,1,0:T(8,128)(2,1)}, u32[]{:S(2)}, u32[]{:S(2)}) collective-permute-start(bf16[4,64,1024]{2,1,0:T(8,128)(2,1)S(1)} %get-tuple-element.106), channel_id=1, source_target_pairs={{0,8},{1,9},{2,10},{3,11},{4,12},{5,13},{6,14},{7,15},{8,0},{9,1},... | collective-permute-start | bytes 1572872 | tf_op jit(solution)/shard_map/ppermute | solution.py:338
  355.8 12.8 %collective-permute-start.53 = (bf16[4,2,16,2048]{3,2,1,0:T(8,128)(2,1)S(1)}, bf16[4,2,16,2048]{3,2,1,0:T(8,128)(2,1)S(1)}, u32[]{:S(2)}, u32[]{:S(2)}) collective-permute-start(bf16[4,2,16,2048]{3,2,1,0:T(8,128)(2,1)S(1)} %get-tuple-element.108), channel_id=1, source_target_pairs={{0,3},{1,0},{2,1},{3,2},{4,7},{5,4},{6,5},{7,6},{8,11},{9,8},{10,9... | collective-permute-start | bytes 1572872 | tf_op jit(solution)/shard_map/ppermute | solution.py:338
  368.6 12.7 %collective-permute-start.51 = (bf16[4,2,16,2048]{3,2,1,0:T(8,128)(2,1)S(1)}, bf16[4,2,16,2048]{3,2,1,0:T(8,128)(2,1)S(1)}, u32[]{:S(2)}, u32[]{:S(2)}) collective-permute-start(bf16[4,2,16,2048]{3,2,1,0:T(8,128)(2,1)S(1)} %get-tuple-element.107), channel_id=1, source_target_pairs={{0,1},{1,2},{2,3},{3,0},{4,5},{5,6},{6,7},{7,4},{8,9},{9,10},{10,1... | collective-permute-start | bytes 1572872 | tf_op jit(solution)/shard_map/ppermute | solution.py:338
  381.2 25.6 %collective-permute-start.54 = (bf16[4,2,32,2048]{3,2,1,0:T(8,128)(2,1)S(1)}, bf16[4,2,32,2048]{3,2,1,0:T(8,128)(2,1)S(1)}, u32[]{:S(2)}, u32[]{:S(2)}) collective-permute-start(bf16[4,2,32,2048]{3,2,1,0:T(8,128)(2,1)S(1)} %pad_maximum_fusion.3), channel_id=1, source_target_pairs={{0,3},{1,0},{2,1},{3,2},{4,7},{5,4},{6,5},{7,6},{8,11},{9,8},{10,9... | collective-permute-start | bytes 3145736 | tf_op jit(solution)/shard_map/ppermute | solution.py:338
  385.4 46.9 %collective-permute-start.52 = (bf16[4,2,32,2048]{3,2,1,0:T(8,128)(2,1)}, bf16[4,2,32,2048]{3,2,1,0:T(8,128)(2,1)S(1)}, u32[]{:S(2)}, u32[]{:S(2)}) collective-permute-start(bf16[4,2,32,2048]{3,2,1,0:T(8,128)(2,1)} %pad_maximum_fusion.2), channel_id=1, source_target_pairs={{0,1},{1,2},{2,3},{3,0},{4,5},{5,6},{6,7},{7,4},{8,9},{9,10},{10,1... | collective-permute-start | bytes 3145736 | tf_op jit(solution)/shard_map/ppermute | solution.py:338
  388.2 47.8 %collective-permute-start.63 = (bf16[4,128,1024]{2,1,0:T(8,128)(2,1)}, bf16[4,128,1024]{2,1,0:T(8,128)(2,1)S(1)}, u32[]{:S(2)}, u32[]{:S(2)}) collective-permute-start(bf16[4,128,1024]{2,1,0:T(8,128)(2,1)} %pad_maximum_fusion.5), channel_id=1, source_target_pairs={{0,16},{1,17},{2,18},{3,19},{4,20},{5,21},{6,22},{7,23},{8,24},{9,... | collective-permute-start | bytes 3145736 | tf_op jit(solution)/shard_map/ppermute | solution.py:338
  389.4 47.6 %collective-permute-start.61 = (bf16[4,128,1024]{2,1,0:T(8,128)(2,1)S(1)}, bf16[4,128,1024]{2,1,0:T(8,128)(2,1)S(1)}, u32[]{:S(2)}, u32[]{:S(2)}) collective-permute-start(bf16[4,128,1024]{2,1,0:T(8,128)(2,1)S(1)} %pad_maximum_fusion.4), channel_id=1, source_target_pairs={{0,8},{1,9},{2,10},{3,11},{4,12},{5,13},{6,14},{7,15},{8,0},{9,1},... | collective-permute-start | bytes 3145736 | tf_op jit(solution)/shard_map/ppermute | solution.py:338
  406.8 134.7 %collective-permute-start.36 = (bf16[256,1024]{1,0:T(8,128)(2,1)}, bf16[256,1024]{1,0:T(8,128)(2,1)}, u32[]{:S(2)}, u32[]{:S(2)}) collective-permute-start(bf16[256,1024]{1,0:T(8,128)(2,1)} %get-tuple-element.111), channel_id=1, source_target_pairs={{0,0},{1,1},{2,4},{3,5},{4,2},{5,3},{6,6},{7,7},{8,8},{9,9},{10,12... | collective-permute-start | bytes 1572872 | tf_op jit(solution)/shard_map/ppermute | solution.py:338
  432.3 110.1 %collective-permute-start.37 = (bf16[256,1024]{1,0:T(8,128)(2,1)}, bf16[256,1024]{1,0:T(8,128)(2,1)}, u32[]{:S(2)}, u32[]{:S(2)}) collective-permute-start(bf16[256,1024]{1,0:T(8,128)(2,1)} %get-tuple-element.112), channel_id=1, source_target_pairs={{0,1},{1,0},{2,5},{3,4},{4,3},{5,2},{6,7},{7,6},{8,9},{9,8},{10,13... | collective-permute-start | bytes 1572872 | tf_op jit(solution)/shard_map/ppermute | solution.py:338
  438.4 53.2 %collective-permute-start.64 = (bf16[64,1024]{1,0:T(8,128)(2,1)}, bf16[64,1024]{1,0:T(8,128)(2,1)}, u32[]{:S(2)}, u32[]{:S(2)}) collective-permute-start(bf16[64,1024]{1,0:T(8,128)(2,1)} %get-tuple-element.134), channel_id=1, source_target_pairs={{0,1},{1,2},{2,3},{3,0},{4,5},{5,6},{6,7},{7,4},{8,9},{9,10},{10,1... | collective-permute-start | bytes 393224 | tf_op jit(solution)/shard_map/ppermute | solution.py:338
  444.5 47.6 %collective-permute-start.66 = (bf16[64,1024]{1,0:T(8,128)(2,1)}, bf16[64,1024]{1,0:T(8,128)(2,1)}, u32[]{:S(2)}, u32[]{:S(2)}) collective-permute-start(bf16[64,1024]{1,0:T(8,128)(2,1)} %get-tuple-element.135), channel_id=1, source_target_pairs={{0,3},{1,0},{2,1},{3,2},{4,7},{5,4},{6,5},{7,6},{8,11},{9,8},{10,9... | collective-permute-start | bytes 393224 | tf_op jit(solution)/shard_map/ppermute | solution.py:338
  485.9 16.3 %collective-permute-start.39 = (bf16[1024,1024]{1,0:T(8,128)(2,1)}, bf16[1024,1024]{1,0:T(8,128)(2,1)}, u32[]{:S(2)}, u32[]{:S(2)}) collective-permute-start(bf16[1024,1024]{1,0:T(8,128)(2,1)} %add_convert_fusion.2), channel_id=1, source_target_pairs={{0,4},{1,5},{2,6},{3,7},{4,0},{5,1},{6,2},{7,3},{8,12},{9,13},{10,... | collective-permute-start | bytes 6291464 | tf_op jit(solution)/shard_map/ppermute | solution.py:338
  491.5 34.2 %collective-permute-start.58 = (bf16[2,32,2048]{2,1,0:T(8,128)(2,1)}, bf16[2,32,2048]{2,1,0:T(8,128)(2,1)}, u32[]{:S(2)}, u32[]{:S(2)}) collective-permute-start(bf16[2,32,2048]{2,1,0:T(8,128)(2,1)} %pad_maximum_fusion.9), channel_id=1, source_target_pairs={{0,16},{1,17},{2,18},{3,19},{4,20},{5,21},{6,22},{7,23},{8,24},{9,... | collective-permute-start | bytes 786440 | tf_op jit(solution)/shard_map/ppermute | solution.py:338
  492.1 35.1 %collective-permute-start.56 = (bf16[2,32,2048]{2,1,0:T(8,128)(2,1)}, bf16[2,32,2048]{2,1,0:T(8,128)(2,1)}, u32[]{:S(2)}, u32[]{:S(2)}) collective-permute-start(bf16[2,32,2048]{2,1,0:T(8,128)(2,1)} %pad_maximum_fusion.8), channel_id=1, source_target_pairs={{0,8},{1,9},{2,10},{3,11},{4,12},{5,13},{6,14},{7,15},{8,0},{9,1},... | collective-permute-start | bytes 786440 | tf_op jit(solution)/shard_map/ppermute | solution.py:338
  524.3 13.7 %collective-permute-start.44 = (bf16[4,136,512]{2,1,0:T(8,128)(2,1)S(1)}, bf16[4,136,512]{2,1,0:T(8,128)(2,1)S(1)}, u32[]{:S(2)}, u32[]{:S(2)}) collective-permute-start(bf16[4,136,512]{2,1,0:T(8,128)(2,1)S(1)} %get-tuple-element.102), channel_id=1, source_target_pairs={{0,8},{1,9},{2,10},{3,11},{4,12},{5,13},{6,14},{7,15},{8,0},{9,1},... | collective-permute-start | bytes 1671176 | tf_op jit(solution)/shard_map/ppermute | solution.py:338
  525.7 23.0 %collective-permute-start.67 = (bf16[128,1024]{1,0:T(8,128)(2,1)}, bf16[128,1024]{1,0:T(8,128)(2,1)}, u32[]{:S(2)}, u32[]{:S(2)}) collective-permute-start(bf16[128,1024]{1,0:T(8,128)(2,1)} %pad_maximum_fusion.11), channel_id=1, source_target_pairs={{0,3},{1,0},{2,1},{3,2},{4,7},{5,4},{6,5},{7,6},{8,11},{9,8},{10,9... | collective-permute-start | bytes 786440 | tf_op jit(solution)/shard_map/ppermute | solution.py:338
  527.2 13.3 %collective-permute-start.42 = (bf16[4,136,512]{2,1,0:T(8,128)(2,1)S(1)}, bf16[4,136,512]{2,1,0:T(8,128)(2,1)S(1)}, u32[]{:S(2)}, u32[]{:S(2)}) collective-permute-start(bf16[4,136,512]{2,1,0:T(8,128)(2,1)S(1)} %get-tuple-element.101), channel_id=1, source_target_pairs={{0,16},{1,17},{2,18},{3,19},{4,20},{5,21},{6,22},{7,23},{8,24},{9,... | collective-permute-start | bytes 1671176 | tf_op jit(solution)/shard_map/ppermute | solution.py:338
  538.0 10.7 %collective-permute-start.65 = (bf16[128,1024]{1,0:T(8,128)(2,1)}, bf16[128,1024]{1,0:T(8,128)(2,1)}, u32[]{:S(2)}, u32[]{:S(2)}) collective-permute-start(bf16[128,1024]{1,0:T(8,128)(2,1)} %pad_maximum_fusion.10), channel_id=1, source_target_pairs={{0,1},{1,2},{2,3},{3,0},{4,5},{5,6},{6,7},{7,4},{8,9},{9,10},{10,1... | collective-permute-start | bytes 786440 | tf_op jit(solution)/shard_map/ppermute | solution.py:338
  540.5 24.7 %collective-permute-start.45 = (bf16[4,272,512]{2,1,0:T(8,128)(2,1)}, bf16[4,272,512]{2,1,0:T(8,128)(2,1)S(1)}, u32[]{:S(2)}, u32[]{:S(2)}) collective-permute-start(bf16[4,272,512]{2,1,0:T(8,128)(2,1)} %pad_maximum_fusion.1), channel_id=1, source_target_pairs={{0,16},{1,17},{2,18},{3,19},{4,20},{5,21},{6,22},{7,23},{8,24},{9,... | collective-permute-start | bytes 3342344 | tf_op jit(solution)/shard_map/ppermute | solution.py:338
  541.5 24.0 %collective-permute-start.43 = (bf16[4,272,512]{2,1,0:T(8,128)(2,1)S(1)}, bf16[4,272,512]{2,1,0:T(8,128)(2,1)}, u32[]{:S(2)}, u32[]{:S(2)}) collective-permute-start(bf16[4,272,512]{2,1,0:T(8,128)(2,1)S(1)} %pad_maximum_fusion), channel_id=1, source_target_pairs={{0,8},{1,9},{2,10},{3,11},{4,12},{5,13},{6,14},{7,15},{8,0},{9,1},... | collective-permute-start | bytes 3342344 | tf_op jit(solution)/shard_map/ppermute | solution.py:338
  542.4 8.4 %collective-permute-start.59 = (f32[32,2048]{1,0:T(8,128)S(1)}, f32[32,2048]{1,0:T(8,128)S(1)}, u32[]{:S(2)}, u32[]{:S(2)}) collective-permute-start(f32[32,2048]{1,0:T(8,128)S(1)} %get-tuple-element.126), channel_id=1, source_target_pairs={{0,4},{1,5},{2,6},{3,7},{4,0},{5,1},{6,2},{7,3},{8,12},{9,13},{10,... | collective-permute-start | bytes 786440 | tf_op jit(solution)/shard_map/ppermute | solution.py:338
  567.6 10.8 %collective-permute-start.46 = (bf16[136,512]{1,0:T(8,128)(2,1)S(1)}, bf16[136,512]{1,0:T(8,128)(2,1)S(1)}, u32[]{:S(2)}, u32[]{:S(2)}) collective-permute-start(bf16[136,512]{1,0:T(8,128)(2,1)S(1)} %get-tuple-element.132), channel_id=1, source_target_pairs={{0,1},{1,2},{2,3},{3,0},{4,5},{5,6},{6,7},{7,4},{8,9},{9,10},{10,1... | collective-permute-start | bytes 417800 | tf_op jit(solution)/shard_map/ppermute | solution.py:338
  567.7 10.7 %collective-permute-start.48 = (bf16[136,512]{1,0:T(8,128)(2,1)S(1)}, bf16[136,512]{1,0:T(8,128)(2,1)S(1)}, u32[]{:S(2)}, u32[]{:S(2)}) collective-permute-start(bf16[136,512]{1,0:T(8,128)(2,1)S(1)} %get-tuple-element.133), channel_id=1, source_target_pairs={{0,3},{1,0},{2,1},{3,2},{4,7},{5,4},{6,5},{7,6},{8,11},{9,8},{10,9... | collective-permute-start | bytes 417800 | tf_op jit(solution)/shard_map/ppermute | solution.py:338
  570.0 34.3 %collective-permute-start.40 = (bf16[256,1024]{1,0:T(8,128)(2,1)}, bf16[256,1024]{1,0:T(8,128)(2,1)}, u32[]{:S(2)}, u32[]{:S(2)}) collective-permute-start(bf16[256,1024]{1,0:T(8,128)(2,1)} %get-tuple-element.109), channel_id=1, source_target_pairs={{0,0},{1,1},{2,4},{3,5},{4,2},{5,3},{6,6},{7,7},{8,8},{9,9},{10,12... | collective-permute-start | bytes 1572872 | tf_op jit(solution)/shard_map/ppermute | solution.py:338
  578.2 31.6 %collective-permute-start.41 = (bf16[256,1024]{1,0:T(8,128)(2,1)S(1)}, bf16[256,1024]{1,0:T(8,128)(2,1)}, u32[]{:S(2)}, u32[]{:S(2)}) collective-permute-start(bf16[256,1024]{1,0:T(8,128)(2,1)S(1)} %get-tuple-element.110), channel_id=1, source_target_pairs={{0,1},{1,0},{2,5},{3,4},{4,3},{5,2},{6,7},{7,6},{8,9},{9,8},{10,13... | collective-permute-start | bytes 1572872 | tf_op jit(solution)/shard_map/ppermute | solution.py:338
  579.2 33.6 %collective-permute-start.49 = (bf16[272,512]{1,0:T(8,128)(2,1)}, bf16[272,512]{1,0:T(8,128)(2,1)S(1)}, u32[]{:S(2)}, u32[]{:S(2)}) collective-permute-start(bf16[272,512]{1,0:T(8,128)(2,1)} %pad_maximum_fusion.7), channel_id=1, source_target_pairs={{0,3},{1,0},{2,1},{3,2},{4,7},{5,4},{6,5},{7,6},{8,11},{9,8},{10,9... | collective-permute-start | bytes 835592 | tf_op jit(solution)/shard_map/ppermute | solution.py:338
  581.1 31.8 %collective-permute-start.47 = (bf16[272,512]{1,0:T(8,128)(2,1)}, bf16[272,512]{1,0:T(8,128)(2,1)}, u32[]{:S(2)}, u32[]{:S(2)}) collective-permute-start(bf16[272,512]{1,0:T(8,128)(2,1)} %pad_maximum_fusion.6), channel_id=1, source_target_pairs={{0,1},{1,2},{2,3},{3,0},{4,5},{5,6},{6,7},{7,4},{8,9},{9,10},{10,1... | collective-permute-start | bytes 835592 | tf_op jit(solution)/shard_map/ppermute | solution.py:338
  (78 other events, 988.6 us)

commit v2 on v0

--- a/solution.py
+++ b/solution.py
@@ -4,6 +4,8 @@
 import jax
 import jax.numpy as jnp
 from jax import lax
+from jax.experimental import pallas as pl
+from jax.experimental.pallas import tpu as pltpu
 from jax.sharding import PartitionSpec as P
 
 H = 16
@@ -309,9 +311,1193 @@
     return result + tuple(attn_grads) + tuple(feed_grads)
 
 
+AXES = ("dp", "ctx")
+BLOCK = 256
+BF = jnp.bfloat16
+F32 = jnp.float32
+NT = (((1,), (1,)), ((), ()))
+NN = (((1,), (0,)), ((), ()))
+TN = (((0,), (0,)), ((), ()))
+ANY = pl.BlockSpec(memory_space=pl.ANY)
+VMEM = pl.BlockSpec(memory_space=pltpu.VMEM)
+
+
+def links(step):
+    pairs = []
+    for o in range(4):
+        for c in range(2):
+            for z in range(4):
+                o2, c2, z2 = step(o, c, z)
+                pairs.append(((o * 2 + c) * 4 + z, (o2 * 2 + c2) * 4 + z2))
+    return pairs
+
+
+X_SWAP = links(lambda o, c, z: (o ^ 1, c, z))
+Y_SWAP = links(lambda o, c, z: (o ^ 2, c, z))
+CORE_SWAP = links(lambda o, c, z: (o, 1 - c, z))
+Z_UP = links(lambda o, c, z: (o, c, (z + 1) % 4))
+Z_DOWN = links(lambda o, c, z: (o, c, (z + 3) % 4))
+SEQUENCE = [links(lambda o, c, z, k=k: (o, z >> 1, 2 * c + ((z & 1) ^ k))) for k in range(2)]
+
+
+def send(value, pairs):
+    return lax.ppermute(value, AXES, pairs)
+
+
+def place():
+    dp = lax.axis_index("dp")
+    return dp // 2, dp % 2, lax.axis_index("ctx")
+
+
+def dot32(left, right, dims):
+    return lax.dot_general(left, right, dims, preferred_element_type=F32)
+
+
+def shape(dims, kind=BF):
+    return jax.ShapeDtypeStruct(dims, kind)
+
+
+def cost(flops, nbytes, special=0):
+    return pl.CostEstimate(flops=int(flops), bytes_accessed=int(nbytes), transcendentals=special)
+
+
+def call(body, ins, outs, name, in_specs=None, out_specs=None, scratch=(), flops=0, grid=()):
+    moved = sum(a.size * a.dtype.itemsize for a in ins)
+    moved += sum(math.prod(a.shape) * jnp.dtype(a.dtype).itemsize for a in outs)
+    return pl.pallas_call(
+        body,
+        grid=grid,
+        in_specs=in_specs or [VMEM] * len(ins),
+        out_specs=out_specs or [VMEM] * len(outs),
+        out_shape=outs,
+        scratch_shapes=list(scratch),
+        cost_estimate=cost(flops, moved),
+        name=name,
+    )(*ins)
+
+
+def placed_call(body, pos, ins, outs, name, grid, in_specs, out_specs, scratch=(), flops=0):
+    moved = sum(a.size * a.dtype.itemsize for a in ins)
+    moved += sum(math.prod(a.shape) * jnp.dtype(a.dtype).itemsize for a in outs)
+    return pl.pallas_call(
+        body,
+        grid_spec=pltpu.PrefetchScalarGridSpec(
+            num_scalar_prefetch=1,
+            grid=grid,
+            in_specs=in_specs,
+            out_specs=out_specs,
+            scratch_shapes=list(scratch),
+        ),
+        out_shape=outs,
+        cost_estimate=cost(flops, moved),
+        name=name,
+    )(pos, *ins)
+
+
+def copies(ins, outs, moves, count, name):
+    def body(*refs):
+        sems = refs[-1]
+        todo = moves(refs[: len(ins)], refs[len(ins) : -1])
+        started = [pltpu.make_async_copy(s, d, sems.at[i]) for i, (s, d) in enumerate(todo)]
+        for copy in started:
+            copy.start()
+        for copy in started:
+            copy.wait()
+
+    return call(
+        body,
+        ins,
+        outs,
+        name,
+        in_specs=[ANY] * len(ins),
+        scratch=[pltpu.SemaphoreType.DMA((count,))],
+    )
+
+
+def own_columns(weight, k):
+    n = weight.shape[1] // 8
+    parts = [
+        jnp.where(k == 0, weight[:, 2 * g * n : (2 * g + 1) * n], weight[:, (2 * g + 1) * n : (2 * g + 2) * n])
+        for g in range(4)
+    ]
+    return jnp.concatenate(parts, axis=1)
+
+
+def first_kernel(qw, kw, vw, uw, small, inputs, segs, far, up_far, in0, in1, sems):
+    _, c, z = place()
+    rows = inputs.shape[1]
+    parity = lax.rem(z, 2)
+    todo = []
+    for k, out in enumerate((in0, in1)):
+        pick = parity if k == 0 else 1 - parity
+        todo.append(pltpu.make_async_copy(inputs.at[pick], out.at[pl.ds(0, rows)], sems.at[k]))
+        todo[-1].start()
+        line = segs[pl.ds(pick, 1), :].astype(F32)
+        out[rows:, :] = jnp.zeros((out.shape[0] - rows, out.shape[1]), BF)
+        out[rows:, :rows] = jnp.broadcast_to(line, (out.shape[0] - rows, rows)).astype(BF)
+    lead = qw.shape[0]
+    for j, ref in enumerate((qw, kw, vw)):
+        far[j * lead : (j + 1) * lead, :] = own_columns(ref[...], 1 - c)
+    far[3 * lead :, :] = small[...]
+    up_far[...] = own_columns(uw[...], 1 - c)
+    for copy in todo:
+        copy.wait()
+
+
+def second_kernel(qw, kw, vw, ow, uw, small, far, up_far, attn, up):
+    _, c, _ = place()
+    lead, width = ow.shape
+    half = width // 2
+    attn[0:lead, :] = ow[:, :half]
+    attn[lead : 2 * lead, :] = ow[:, half:]
+
+    def both(out, at, own, got):
+        n = own.shape[0]
+        out[at : at + n, :] = jnp.where(c == 0, own, got)
+        out[at + n : at + 2 * n, :] = jnp.where(c == 0, got, own)
+
+    for j, ref in enumerate((qw, kw, vw)):
+        both(attn, (2 + 2 * j) * lead, own_columns(ref[...], c), far[j * lead : (j + 1) * lead, :])
+    both(attn, 8 * lead, small[...], far[3 * lead :, :])
+    both(up, 0, own_columns(uw[...], c), up_far[...])
+
+
+def inner_kernel_moves(n):
+    def moves(ins, outs):
+        todo = []
+        for g in range(n):
+            own, first, second, far1, far2 = ins[5 * g : 5 * g + 5]
+            low, high = outs[2 * g : 2 * g + 2]
+            cut = far1.shape[0]
+            todo += [
+                (own, low.at[0]),
+                (first, low.at[1]),
+                (second, high.at[0]),
+                (far1, high.at[1, pl.ds(0, cut)]),
+                (far2, high.at[1, pl.ds(cut, far2.shape[0])]),
+            ]
+        return todo
+
+    return moves
+
+
+def ring_first(value, n1, n2):
+    return send(value, n1), send(value, n2)
+
+
+def ring_second(a, b, f1, f2):
+    cut = a.shape[0] // 2 // 16 * 16
+    return send(a[:cut], f1), send(b[cut:], f2)
+
+
+def ring_outer(low, high, n1, n2, f1, f2):
+    b_high = send(high, n2)
+    a_low = send(low, n1)
+    b_low = send(low, n2)
+    a_high = send(high, n1)
+    return [low, high, a_low, a_high, b_low, b_high, send(a_low, f1), send(b_high, f2)]
+
+
+def final_moves(ins, outs, inner, blocks):
+    o, c, z = place()
+    z_ring = (z, lax.rem(z + 3, 4), lax.rem(z + 1, 4), lax.rem(z + 2, 4))
+    yx_ring = (o, o ^ 1, o ^ 2, o ^ 3)
+    near, far = (z_ring, yx_ring) if inner == "z" else (yx_ring, z_ring)
+    todo = []
+    for i, (k, part) in enumerate(((0, 0), (0, 1), (1, 0), (1, 1), (2, 0), (2, 1), (3, 0), (3, 1))):
+        for j in range(2):
+            a, b = near[2 * part + j], far[k]
+            yx, zz = (b, a) if inner == "z" else (a, b)
+            todo += blocks(ins[i].at[j], outs, yx, zz)
+    return todo
+
+
+def moments(values):
+    mean = jnp.mean(values, axis=-1, keepdims=True)
+    centered = values - mean
+    spread = lax.rsqrt(jnp.mean(centered * centered, axis=-1, keepdims=True) + EPS)
+    return centered * spread, spread
+
+
+def project_kernel(x, gain, shift, weight, bias, normed, qkv):
+    n, _ = moments(x[...].astype(F32))
+    value = (n * gain[...] + shift[...]).astype(BF)
+    normed[...] = value
+    for j in range(3):
+        qkv[j] = (dot32(value, weight[j], NN) + bias[j : j + 1, :]).astype(BF)
+
+
+def project(x, gain, shift, weight, bias):
+    total, width = x.shape
+    half = weight.shape[2]
+    rows = pl.BlockSpec((BLOCK, width), lambda i: (i, 0))
+    line = pl.BlockSpec((1, width), lambda i: (0, 0))
+    return call(
+        project_kernel,
+        [x, gain, shift, weight, bias],
+        [shape((total, width)), shape((3, total, half))],
+        "project",
+        in_specs=[
+            rows,
+            line,
+            line,
+            pl.BlockSpec((3, width, half), lambda i: (0, 0, 0)),
+            pl.BlockSpec((3, half), lambda i: (0, 0)),
+        ],
+        out_specs=[rows, pl.BlockSpec((3, BLOCK, half), lambda i: (0, i, 0))],
+        flops=6 * total * width * half,
+        grid=(total // BLOCK,),
+    )
+
+
+def allowed_mask(column, row, i, low, high):
+    rows = i * BLOCK + lax.broadcasted_iota(jnp.int32, (BLOCK, high - low), 0)
+    cols = low + lax.broadcasted_iota(jnp.int32, (BLOCK, high - low), 1)
+    same = column[i * BLOCK : i * BLOCK + BLOCK, :] == row[:, low:high]
+    return same & (cols <= rows)
+
+
+def key_range(i, total):
+    return max(0, (i * BLOCK - total // 2 + 1) // BLOCK * BLOCK), (i + 1) * BLOCK
+
+
+def attend_kernel(scale, column, row, q_ref, k_ref, v_ref, _, mixed_ref, log_ref):
+    total = q_ref.shape[0]
+    size = q_ref.shape[1] // 2
+    lane = lax.broadcasted_iota(jnp.int32, (BLOCK, 2 * size), 1) < size
+    for i in range(total // BLOCK):
+        low, high = key_range(i, total)
+        rows = pl.ds(i * BLOCK, BLOCK)
+        mask = allowed_mask(column, row, i, low, high)
+        keys, values = k_ref[low:high, :], v_ref[low:high, :]
+        q = q_ref[rows, :]
+        zero = jnp.zeros_like(q)
+        outs, logs = [], []
+        for own in (jnp.where(lane, q, zero), jnp.where(lane, zero, q)):
+            s = jnp.where(mask, dot32(own, keys, NT) * scale, MASKED)
+            top = jnp.max(s, axis=-1, keepdims=True)
+            e = jnp.exp(s - top)
+            tot = jnp.sum(e, axis=-1, keepdims=True)
+            p = (e * (1.0 / tot)).astype(BF)
+            outs.append(dot32(p, values, NN))
+            logs.append(top + jnp.log(tot))
+        mixed_ref[rows, :] = jnp.where(lane, outs[0], outs[1]).astype(BF)
+        log_ref[rows, :] = jnp.where(lane, logs[0], logs[1])
+
+
+def attend_back_kernel(
+    scale, column, row, q_ref, k_ref, v_ref, log_ref, grad_ref, _, out_ref, bias_ref, dk, dv
+):
+    total = q_ref.shape[0]
+    size = q_ref.shape[1] // 2
+    lane = lax.broadcasted_iota(jnp.int32, (BLOCK, 2 * size), 1) < size
+    dk[...] = jnp.zeros_like(dk)
+    dv[...] = jnp.zeros_like(dv)
+    dq_sum = jnp.zeros((1, 2 * size), F32)
+    for i in range(total // BLOCK):
+        low, high = key_range(i, total)
+        rows = pl.ds(i * BLOCK, BLOCK)
+        mask = allowed_mask(column, row, i, low, high)
+        keys, values = k_ref[low:high, :], v_ref[low:high, :]
+        q, g = q_ref[rows, :], grad_ref[rows, :]
+        zero = jnp.zeros_like(q)
+        dqs = []
+        for h in range(2):
+            qh = jnp.where(lane, q, zero) if h == 0 else jnp.where(lane, zero, q)
+            gh = jnp.where(lane, g, zero) if h == 0 else jnp.where(lane, zero, g)
+            log = log_ref[rows, h * size : h * size + 1]
+            s = jnp.where(mask, dot32(qh, keys, NT) * scale, MASKED)
+            p = jnp.exp(s - log)
+            dp = dot32(gh, values, NT)
+            delta = jnp.sum(p * dp, axis=-1, keepdims=True)
+            ds = (p * (dp - delta)).astype(BF)
+            dqs.append(dot32(ds, keys, NN))
+            dk[low:high, :] += dot32(ds, qh, TN)
+            dv[low:high, :] += dot32(p.astype(BF), gh, TN)
+        dq = (jnp.where(lane, dqs[0], dqs[1]) * scale).astype(BF)
+        out_ref[0, rows, :] = dq
+        dq_sum += jnp.sum(dq.astype(F32), axis=0, keepdims=True)
+    out_ref[1, :, :] = (dk[...] * scale).astype(BF)
+    dvb = dv[...].astype(BF)
+    out_ref[2, :, :] = dvb
+    bias_ref[0:1, :] = dq_sum
+    bias_ref[1:2, :] = jnp.sum(dvb.astype(F32), axis=0, keepdims=True)
+
+
+def attend_specs(total, width):
+    pick = lambda j: pl.BlockSpec((None, total, width), lambda h: (j, 0, h))
+    return [
+        pl.BlockSpec((total, 1), lambda h: (0, 0)),
+        pl.BlockSpec((1, total), lambda h: (0, 0)),
+        pick(0),
+        pick(1),
+        pick(2),
+    ]
+
+
+def attend(qkv, column, row, size, after):
+    _, total, width = qkv.shape
+    pair = 2 * size
+    flat = pl.BlockSpec((total, pair), lambda h: (0, h))
+    return call(
+        partial(attend_kernel, 1.0 / math.sqrt(size)),
+        [column, row, qkv, qkv, qkv, after],
+        [shape((total, width)), shape((total, width), F32)],
+        "attend",
+        in_specs=attend_specs(total, pair) + [ANY],
+        out_specs=[flat, flat],
+        flops=total * total * width * 16,
+        grid=(width // pair,),
+    )
+
+
+def attend_back(qkv, log, grad, column, row, size, after):
+    _, total, width = qkv.shape
+    pair = 2 * size
+    flat = pl.BlockSpec((total, pair), lambda h: (0, h))
+    return call(
+        partial(attend_back_kernel, 1.0 / math.sqrt(size)),
+        [column, row, qkv, qkv, qkv, log, grad, after],
+        [shape((3, total, width)), shape((2, width), F32)],
+        "attend_back",
+        in_specs=attend_specs(total, pair) + [flat, flat, ANY],
+        out_specs=[
+            pl.BlockSpec((3, total, pair), lambda h: (0, 0, h)),
+            pl.BlockSpec((2, pair), lambda h: (0, h)),
+        ],
+        scratch=[pltpu.VMEM((total, pair), F32)] * 2,
+        flops=total * total * width * 24,
+        grid=(width // pair,),
+    )
+
+
+def rows_kernel(dims, left, right, out):
+    out[...] = dot32(left[...], right[...], dims).astype(out.dtype)
+
+
+def rows_matmul(left, right, dims, name, kind=BF):
+    total, depth = left.shape
+    cols = right.shape[0] if dims is NT else right.shape[1]
+    return call(
+        partial(rows_kernel, dims),
+        [left, right],
+        [shape((total, cols), kind)],
+        name,
+        in_specs=[
+            pl.BlockSpec((BLOCK, depth), lambda i: (i, 0)),
+            pl.BlockSpec(right.shape, lambda i: (0, 0)),
+        ],
+        out_specs=[pl.BlockSpec((BLOCK, cols), lambda i: (i, 0))],
+        flops=2 * total * depth * cols,
+        grid=(total // BLOCK,),
+    )[0]
+
+
+def middle_kernel(x, part, got, bias, gain, shift, middle, second):
+    value = x[...].astype(F32) + part[...].astype(F32) + got[...].astype(F32) + bias[...]
+    middle[...] = value
+    n, _ = moments(value)
+    second[...] = (n * gain[...] + shift[...]).astype(BF)
+
+
+def middle_norm(x, part, got, bias, gain, shift):
+    total, width = x.shape
+    rows = pl.BlockSpec((BLOCK, width), lambda i: (i, 0))
+    line = pl.BlockSpec((1, width), lambda i: (0, 0))
+    return call(
+        middle_kernel,
+        [x, part, got, bias, gain, shift],
+        [shape((total, width), F32), shape((total, width))],
+        "middle",
+        in_specs=[rows] * 3 + [line] * 3,
+        out_specs=[rows, rows],
+        grid=(total // BLOCK,),
+    )
+
+
+def feed_kernel(second, cot, up, bias, down, hidden_ref, pre_ref, sum_ref):
+    total = second.shape[0]
+    root = math.sqrt(0.5)
+    norm = 1.0 / math.sqrt(2.0 * math.pi)
+    sums = jnp.zeros(sum_ref.shape, F32)
+    for i in range(total // BLOCK):
+        rows = pl.ds(i * BLOCK, BLOCK)
+        v = dot32(second[rows, :], up[...], NN) + bias[...]
+        g = dot32(cot[rows, :], down[...], NT)
+        cdf = 0.5 * (1.0 + lax.erf(v * root))
+        hidden_ref[rows, :] = (v * cdf).astype(BF)
+        pre = (g * (cdf + v * (norm * jnp.exp(-0.5 * (v * v))))).astype(BF)
+        pre_ref[rows, :] = pre
+        sums += jnp.sum(pre.astype(F32), axis=0, keepdims=True)
+    sum_ref[...] = sums
+
+
+def feed_forward(second, cot, up, bias, down, tile=256):
+    total, width = second.shape
+    units = up.shape[1]
+    whole = pl.BlockSpec((total, width), lambda u: (0, 0))
+    cols = pl.BlockSpec((total, tile), lambda u: (0, u))
+    line = pl.BlockSpec((1, tile), lambda u: (0, u))
+    return call(
+        feed_kernel,
+        [second, cot, up, bias, down],
+        [shape((total, units)), shape((total, units)), shape((1, units), F32)],
+        "feed",
+        in_specs=[
+            whole,
+            whole,
+            pl.BlockSpec((width, tile), lambda u: (0, u)),
+            line,
+            pl.BlockSpec((tile, width), lambda u: (u, 0)),
+        ],
+        out_specs=[cols, cols, line],
+        flops=4 * total * width * units,
+        grid=(units // tile,),
+    )
+
+
+def down_grads_kernel(pos, hidden, cot, far1, far2, n1a, n1b, n2a, n2b, own):
+    g = pl.program_id(0)
+    rows = own.shape[1]
+    acc = dot32(hidden[...], cot[...], TN).astype(BF)
+    for k, outs in enumerate(((far1, far2), (n2a, n2b), (n1a, n1b), (own, own))):
+
+        @pl.when(g == k)
+        def _():
+            for j in range(4):
+                at = j if k == 3 else j % 2
+                outs[j // 2][at] = acc[j * rows : (j + 1) * rows, :]
+
+
+def ring_shapes(rows, cols):
+    return [shape((2, rows, cols))] * 6 + [shape((4, rows, cols))]
+
+
+def ring_specs(rows, cols):
+    return [pl.BlockSpec((2, rows, cols), lambda g, pos: (0, 0, 0))] * 6 + [
+        pl.BlockSpec((4, rows, cols), lambda g, pos: (0, 0, 0))
+    ]
+
+
+def down_grads(pos, hidden, cot, rows):
+    total, units = hidden.shape
+    width = cot.shape[1]
+    return placed_call(
+        down_grads_kernel,
+        pos,
+        [hidden, cot],
+        ring_shapes(rows, width),
+        "down_grads",
+        (4,),
+        [
+            pl.BlockSpec((total, units // 4), lambda g, pos: (0, pos[0] ^ (3 - g))),
+            pl.BlockSpec((total, width), lambda g, pos: (0, 0)),
+        ],
+        ring_specs(rows, width),
+        flops=2 * total * units * width,
+    )
+
+
+def z_places(z):
+    return lax.rem(z + 2, 4), lax.rem(z + 1, 4), lax.rem(z + 3, 4), z
+
+
+def up_grads_kernel(pos, second, pre, far1, far2, n1a, n1b, n2a, n2b, own, acc):
+    g = pl.program_id(0)
+    lead = own.shape[1] // 2
+    acc[...] = dot32(second[...], pre[...], TN).astype(BF)
+    spots = z_places(pos[2])
+    for half in range(2):
+
+        @pl.when(g // 2 == half)
+        def _():
+            outs = ((far1, far2), (n1a, n1b), (n2a, n2b), (own, own))
+            for k in range(4):
+                at = g if k == 3 else lax.rem(g, 2)
+                for cc in range(2):
+                    start = pl.multiple_of(cc * 4 * lead + spots[k] * lead, lead)
+                    outs[k][half][at, cc * lead : (cc + 1) * lead, :] = acc[pl.ds(start, lead), :]
+
+
+def up_grads(pos, second, pre, lead):
+    total, width = second.shape
+    units = pre.shape[1]
+    return placed_call(
+        up_grads_kernel,
+        pos,
+        [second, pre],
+        ring_shapes(2 * lead, units),
+        "up_grads",
+        (4,),
+        [
+            pl.BlockSpec((total, width // 4), lambda g, pos: (0, g)),
+            pl.BlockSpec((total, units), lambda g, pos: (0, 0)),
+        ],
+        ring_specs(2 * lead, units),
+        scratch=[pltpu.VMEM((width // 4, units), BF)],
+        flops=2 * total * units * width,
+    )
+
+
+def attn_grads_kernel(pos, normed, grads, mixed, branch, *refs):
+    p, q, (accv, acco) = refs[0:7], refs[7:14], refs[14:16]
+    g = pl.program_id(0)
+    yx = pos[0] ^ (3 - g)
+    lead = accv.shape[0] // 8
+    half = accv.shape[1]
+    accq = dot32(normed[...], grads[0], TN).astype(BF)
+    acck = dot32(normed[...], grads[1], TN).astype(BF)
+    accv[...] = dot32(normed[...], grads[2], TN).astype(BF)
+    acco[...] = dot32(mixed[...], branch[...], TN).astype(BF)
+    far1, far2, n1a, n1b, n2a, n2b, own = p
+    for k, outs in enumerate(((far1, far2), (n2a, n2b), (n1a, n1b), (own, own))):
+
+        @pl.when(g == k)
+        def _():
+            for zz in range(4):
+                at = zz if k == 3 else zz % 2
+                for j, acc in enumerate((accq, acck)):
+                    for cc in range(2):
+                        row = (2 * j + cc) * lead
+                        start = (cc * 4 + zz) * lead
+                        outs[zz // 2][at, row : row + lead, :] = acc[start : start + lead, :]
+
+    far1, far2, n1a, n1b, n2a, n2b, own = q
+    spots = z_places(pos[2])
+    for part in range(2):
+
+        @pl.when(yx // 2 == part)
+        def _():
+            for k, outs in enumerate(((far1, far2), (n1a, n1b), (n2a, n2b), (own, own))):
+                at = yx if k == 3 else lax.rem(yx, 2)
+                out = outs[part]
+                for cc in range(2):
+                    start = pl.multiple_of(cc * 4 * lead + spots[k] * lead, lead)
+                    out[at, cc * lead : (cc + 1) * lead, :] = accv[pl.ds(start, lead), :]
+                    start = pl.multiple_of(spots[k] * lead, lead)
+                    out[at, (2 + cc) * lead : (3 + cc) * lead, :] = acco[
+                        pl.ds(start, lead), cc * half : (cc + 1) * half
+                    ]
+
+
+def attn_grads(pos, normed, grads, mixed, branch, lead):
+    total, width = normed.shape
+    half = width // 2
+    return placed_call(
+        attn_grads_kernel,
+        pos,
+        [normed, grads, mixed, branch],
+        ring_shapes(4 * lead, half) * 2,
+        "attn_grads",
+        (4,),
+        [
+            pl.BlockSpec((total, width // 4), lambda g, pos: (0, pos[0] ^ (3 - g))),
+            pl.BlockSpec((3, total, half), lambda g, pos: (0, 0, 0)),
+            pl.BlockSpec((total, half // 4), lambda g, pos: (0, pos[0] ^ (3 - g))),
+            pl.BlockSpec((total, width), lambda g, pos: (0, 0)),
+        ],
+        ring_specs(4 * lead, half) * 2,
+        scratch=[pltpu.VMEM((width // 4, half), BF), pltpu.VMEM((half // 4, width), BF)],
+        flops=8 * total * width * half,
+    )
+
+
+def add_kernel(n):
+    def body(*refs):
+        for a, b, out in zip(refs[:n], refs[n : 2 * n], refs[2 * n :]):
+            out[...] = (a[...].astype(F32) + b[...].astype(F32)).astype(BF)
+
+    return body
+
+
+def outer_scatter(p, q, name):
+    far1, far2, n1a, n1b, n2a, n2b, _ = p
+    qfar1, qfar2, qn1a, qn1b, qn2a, qn2b, _ = q
+    t1, t2 = send(far1, X_SWAP), send(far2, Y_SWAP)
+    v1, v2 = send(qfar1, Z_UP), send(qfar2, Z_DOWN)
+    p1a, p2b = send(n1a, X_SWAP), send(n2b, Y_SWAP)
+    q1b, q2a = send(qn1b, Z_UP), send(qn2a, Z_DOWN)
+    mine = [n1b, n2a, qn1a, qn2b]
+    came = [t2, t1, v1, v2]
+    m1, m2, w1, w2 = call(
+        add_kernel(4), mine + came, [shape(a.shape) for a in mine], name + "_pass"
+    )
+    p1b, p2a = send(m1, X_SWAP), send(m2, Y_SWAP)
+    q1a, q2b = send(w1, Z_UP), send(w2, Z_DOWN)
+    return [p1a, p1b, p2a, p2b], [q1a, q1b, q2a, q2b], m1
+
+
+def joined_kernel(extra):
+    def body(*refs):
+        o, c, z = place()
+        ins = refs[: 10 + extra]
+        outs, (ps, qs) = refs[10 + extra : 20 + extra], refs[20 + extra :]
+        spots = {
+            "z": z_places(z),
+            "xy": (o ^ 3, o ^ 1, o ^ 2, o),
+        }
+        for n, (kind, acc) in enumerate((("z", ps), ("xy", qs))):
+            own, r1a, r1b, r2a, r2b = ins[5 * n : 5 * n + 5]
+            rows = own.shape[1]
+            for j in range(4):
+                r1, r2 = (r1a, r2a) if j < 2 else (r1b, r2b)
+                acc[j, :rows, :] = (
+                    own[j].astype(F32) + r1[j % 2].astype(F32) + r2[j % 2].astype(F32)
+                )
+                if n == 1 and extra:
+                    acc[j, rows:, :] = sum(ref[j].astype(F32) for ref in ins[10:])
+            far1, far2, first, second, mine = outs[5 * n : 5 * n + 5]
+            far, one, two, me = spots[kind]
+            cut = far1.shape[0]
+            far1[...] = acc[far, :cut, :].astype(BF)
+            far2[...] = acc[far, cut:, :].astype(BF)
+            first[...] = acc[one].astype(BF)
+            second[...] = acc[two].astype(BF)
+            mine[...] = acc[me]
+
+    return body
+
+
+def inner_pass_kernel(p1, p2, q1, q2, t1, t2, v1, v2, p1o, p2o, q1o, q2o):
+    def half(out, base, got, first):
+        cut = base.shape[0] // 2 // 16 * 16
+        low, high = base[:cut, :], base[cut:, :]
+        plus = lambda a: (a.astype(F32) + got[...].astype(F32)).astype(BF)
+        out[:cut, :] = plus(low) if first else low
+        out[cut:, :] = high if first else plus(high)
+
+    half(p1o, p1, t1, True)
+    half(p2o, p2, t2, False)
+    half(q1o, q1, v2, False)
+    half(q2o, q2, v1, True)
+
+
+def inner_scatter(p, q, p_got, q_got, extra, name):
+    _, prows, pcols = p[6].shape
+    _, qrows, qcols = q[6].shape
+    qall = qrows + (extra[0].shape[1] if extra else 0)
+
+    def outs(rows, cols):
+        cut = rows // 2 // 16 * 16
+        return [
+            shape((cut, cols)),
+            shape((rows - cut, cols)),
+            shape((rows, cols)),
+            shape((rows, cols)),
+            shape((rows, cols), F32),
+        ]
+
+    pf1, pf2, p1, p2, pme, qf1, qf2, q1, q2, qme = call(
+        joined_kernel(len(extra)),
+        [p[6]] + p_got + [q[6]] + q_got + extra,
+        outs(prows, pcols) + outs(qall, qcols),
+        name + "_join",
+        scratch=[pltpu.VMEM((4, prows, pcols), F32), pltpu.VMEM((4, qall, qcols), F32)],
+    )
+    t1, t2 = send(pf1, Z_UP), send(pf2, Z_DOWN)
+    v1, v2 = send(qf1, X_SWAP), send(qf2, Y_SWAP)
+    p1, p2, q1, q2 = call(
+        inner_pass_kernel,
+        [p1, p2, q1, q2, t1, t2, v1, v2],
+        [shape(a.shape) for a in (p1, p2, q1, q2)],
+        name + "_inner",
+    )
+    return (
+        [pme, send(p1, Z_UP), send(p2, Z_DOWN)],
+        [qme, send(q1, X_SWAP), send(q2, Y_SWAP)],
+    )
+
+
+def total_of(refs):
+    return refs[0][...] + refs[1][...].astype(F32) + refs[2][...].astype(F32)
+
+
+def feed_last_kernel(p0, p1, p2, q0, q1, q2, down, kept, given, acc):
+    _, c, _ = place()
+    down[...] = total_of((p0, p1, p2))
+    acc[...] = total_of((q0, q1, q2))
+    lead = kept.shape[0]
+    kept[...] = acc[pl.ds(pl.multiple_of(c * lead, lead), lead), :]
+    given[...] = acc[pl.ds(pl.multiple_of((1 - c) * lead, lead), lead), :]
+
+
+def attn_last_kernel(p0, p1, p2, q0, q1, q2, kept, given, out, small, accp, accq):
+    _, c, _ = place()
+    accp[...] = total_of((p0, p1, p2))
+    accq[...] = total_of((q0, q1, q2))
+    lead = kept.shape[1]
+    half = kept.shape[2]
+    for j, (acc, at) in enumerate(((accp, 0), (accp, 2 * lead), (accq, 0))):
+        kept[j] = acc[pl.ds(pl.multiple_of(at + c * lead, lead), lead), :]
+        given[j] = acc[pl.ds(pl.multiple_of(at + (1 - c) * lead, lead), lead), :]
+    out[:, :half] = accq[2 * lead : 3 * lead, :]
+    out[:, half:] = accq[3 * lead : 4 * lead, :]
+    small[...] = accq[4 * lead :, :]
+
+
+def norm_back(n, spread, gain, grad):
+    g = grad * gain
+    return spread * (
+        g - jnp.mean(g, axis=-1, keepdims=True) - n * jnp.mean(g * n, axis=-1, keepdims=True)
+    )
+
+
+def column(values):
+    return jnp.sum(values, axis=0, keepdims=True)
+
+
+def middle_back_kernel(part, got, middle, cot, gain, wout, branch, mgrad, mixed, sums):
+    n, spread = moments(middle[...])
+    grad = part[...].astype(F32) + got[...].astype(F32)
+    c32 = cot[...].astype(F32)
+    value = c32 + norm_back(n, spread, gain[...], grad)
+    mgrad[...] = value
+    rounded = value.astype(BF)
+    branch[...] = rounded
+    mixed[...] = dot32(rounded, wout[...], NT).astype(BF)
+
+    @pl.when(pl.program_id(0) == 0)
+    def _():
+        sums[...] = jnp.zeros_like(sums)
+
+    for j, v in enumerate((grad * n, grad, rounded.astype(F32), c32)):
+        sums[j : j + 1, :] += column(v)
+
+
+def middle_back(part, got, middle, cot, gain, wout):
+    total, width = middle.shape
+    half = wout.shape[0]
+    rows = pl.BlockSpec((BLOCK, width), lambda i: (i, 0))
+    fixed = lambda dims: pl.BlockSpec(dims, lambda i: (0, 0))
+    return call(
+        middle_back_kernel,
+        [part, got, middle, cot, gain, wout],
+        [
+            shape((total, width)),
+            shape((total, width), F32),
+            shape((total, half)),
+            shape((4, width), F32),
+        ],
+        "middle_back",
+        in_specs=[rows] * 4 + [fixed((1, width)), fixed((half, width))],
+        out_specs=[
+            rows,
+            rows,
+            pl.BlockSpec((BLOCK, half), lambda i: (i, 0)),
+            fixed((4, width)),
+        ],
+        flops=2 * total * width * half,
+        grid=(total // BLOCK,),
+    )
+
+
+def source_grad_kernel(grads, weight, out):
+    out[...] = sum(dot32(grads[j], weight[j], NT) for j in range(3)).astype(BF)
+
+
+def source_grad(grads, weight):
+    _, total, half = grads.shape
+    width = weight.shape[1]
+    return call(
+        source_grad_kernel,
+        [grads, weight],
+        [shape((total, width))],
+        "source_grad",
+        in_specs=[
+            pl.BlockSpec((3, BLOCK, half), lambda i: (0, i, 0)),
+            pl.BlockSpec((3, width, half), lambda i: (0, 0, 0)),
+        ],
+        out_specs=[pl.BlockSpec((BLOCK, width), lambda i: (i, 0))],
+        flops=6 * total * width * half,
+        grid=(total // BLOCK,),
+    )[0]
+
+
+def own_block(g, pos):
+    _, c, z = pos[0], pos[1], pos[2]
+    parity = lax.rem(z, 2)
+    return jnp.where(g < 2, 2 * c + (parity ^ (g & 1)), 2 * (1 - c) + (g & 1))
+
+
+def input_back_kernel(pos, part, got, x, mgrad, gain, first, again, sums):
+    g = pl.program_id(0)
+    n, spread = moments(x[...].astype(F32))
+    grad = part[...].astype(F32) + got[...].astype(F32)
+    value = (mgrad[...] + norm_back(n, spread, gain[...], grad)).astype(BF)
+
+    @pl.when(g == 0)
+    def _():
+        first[...] = value
+        sums[...] = jnp.zeros_like(sums)
+
+    @pl.when(g == 1)
+    def _():
+        again[...] = value
+
+    for j, v in enumerate((grad * n, grad)):
+        sums[j : j + 1, :] += column(v)
+
+
+def input_back(pos, part, got, x, mgrad, gain):
+    total, width = x.shape
+    rows = pl.BlockSpec((BLOCK, width), lambda g, pos: (own_block(g, pos), 0))
+    fixed = lambda n: pl.BlockSpec((n, width), lambda g, pos: (0, 0))
+    return placed_call(
+        input_back_kernel,
+        pos,
+        [part, got, x, mgrad, gain],
+        [shape((BLOCK, width))] * 2 + [shape((2, width), F32)],
+        "input_back",
+        (total // BLOCK,),
+        [rows] * 4 + [fixed(1)],
+        [fixed(BLOCK), fixed(BLOCK), fixed(2)],
+    )
+
+
+def other_block(g, pos):
+    return jnp.where(g < 2, 2 * (1 - pos[1]) + (g & 1), 2 * pos[1] + (g & 1))
+
+
+def output_kernel(pos, hidden, down, middle, bias, theirs, mine):
+    g = pl.program_id(0)
+    value = dot32(hidden[...], down[...], NN)
+
+    @pl.when(g < 2)
+    def _():
+        theirs[...] = value.astype(BF)
+
+    @pl.when(g >= 2)
+    def _():
+        mine[...] = value + middle[...] + bias[...]
+
+
+def output_rows(pos, hidden, down, middle, bias):
+    total, units = hidden.shape
+    width = down.shape[1]
+    return placed_call(
+        output_kernel,
+        pos,
+        [hidden, down, middle, bias],
+        [shape((total // 2, width)), shape((total // 2, width), F32)],
+        "output_rows",
+        (4,),
+        [
+            pl.BlockSpec((BLOCK, units), lambda g, pos: (other_block(g, pos), 0)),
+            pl.BlockSpec((units, width), lambda g, pos: (0, 0)),
+            pl.BlockSpec((BLOCK, width), lambda g, pos: (other_block(g, pos), 0)),
+            pl.BlockSpec((1, width), lambda g, pos: (0, 0)),
+        ],
+        [
+            pl.BlockSpec((BLOCK, width), lambda g, pos: (jnp.minimum(g, 1), 0)),
+            pl.BlockSpec((BLOCK, width), lambda g, pos: (jnp.maximum(g - 2, 0), 0)),
+        ],
+        flops=2 * total * units * width,
+    )
+
+
+def result_kernel(mine, got, first, again):
+    _, _, z = place()
+    parity = lax.rem(z, 2)
+    for k, out in enumerate((first, again)):
+        at = pl.multiple_of((parity ^ k) * BLOCK, BLOCK)
+        out[...] = (mine[pl.ds(at, BLOCK), :] + got[pl.ds(at, BLOCK), :].astype(F32)).astype(BF)
+
+
+Z_FAR = links(lambda o, c, z: (o, c, (z + 2) % 4))
+
+
+def fast_local(
+    inputs,
+    segment_ids,
+    first_gain,
+    first_shift,
+    query_weight,
+    query_bias,
+    key_weight,
+    value_weight,
+    value_bias,
+    out_weight,
+    out_bias,
+    second_gain,
+    second_shift,
+    up_weight,
+    up_bias,
+    down_weight,
+    down_bias,
+    cotangent,
+):
+    batch, rows, width = inputs.shape
+    o, c, z = place()
+    pos = jnp.stack([o, c, z]).astype(jnp.int32)
+    total = batch * rows * 2
+    half = width // 2
+    units = up_weight.shape[1] // 2
+    lead = query_weight.shape[0]
+    down_rows = down_weight.shape[0]
+    size = width // H
+    vector_list = [
+        first_gain,
+        first_shift,
+        query_bias,
+        value_bias,
+        out_bias,
+        second_gain,
+        second_shift,
+        down_bias,
+        up_bias,
+    ]
+    count = 8 * lead + down_rows
+
+    small, at = jnp.zeros((half,), BF), 0
+    for vector in vector_list:
+        small = small + jnp.pad(vector, (at, half - at - vector.shape[0]))
+        at += vector.shape[0]
+    small = jnp.pad(small.reshape(1, half), ((0, 7), (0, 0)))
+    weights = [query_weight, key_weight, value_weight]
+    far, up_far, in0, in1 = call(
+        first_kernel,
+        weights + [up_weight, small, inputs, segment_ids],
+        [
+            shape((3 * lead + 8, half)),
+            shape((lead, units)),
+            shape((rows + 16, width)),
+            shape((rows + 16, width)),
+        ],
+        "first",
+        in_specs=[VMEM] * 5 + [ANY, VMEM],
+        scratch=[pltpu.SemaphoreType.DMA((2,))],
+    )
+    far_got, up_got = send(far, CORE_SWAP), send(up_far, CORE_SWAP)
+    got = [send(in0, SEQUENCE[0]), send(in1, SEQUENCE[1])]
+    attn_pay, up_pay = call(
+        second_kernel,
+        weights + [out_weight, up_weight, small, far_got, up_got],
+        [shape((8 * lead + 16, half)), shape((2 * lead, units))],
+        "second",
+    )
+
+    pa, pb = ring_first(attn_pay, Z_UP, Z_DOWN)
+    qa, qb = ring_first(up_pay, X_SWAP, Y_SWAP)
+    pc = ring_second(pa, pb, Z_UP, Z_DOWN)
+    qc = ring_second(qa, qb, Y_SWAP, X_SWAP)
+    attn_rows = 8 * lead + 16
+    pl_low, pl_high, q_low, q_high = copies(
+        [attn_pay, pa, pb, *pc, up_pay, qa, qb, *qc],
+        [shape((2, attn_rows, half))] * 2 + [shape((2, 2 * lead, units))] * 2,
+        inner_kernel_moves(2),
+        10,
+        "inner",
+    )
+    p_pieces = ring_outer(pl_low, pl_high, X_SWAP, Y_SWAP, Y_SWAP, X_SWAP)
+    q_pieces = ring_outer(q_low, q_high, Z_UP, Z_DOWN, Z_UP, Z_DOWN)
+    mate = [send(g, CORE_SWAP) for g in got]
+
+    def attn_blocks(src, outs, yx, zz):
+        todo = [
+            (src.at[pl.ds(h * lead, lead)], outs[1].at[yx, zz, :, pl.ds(h * half, half)])
+            for h in range(2)
+        ]
+        for j in range(3):
+            for cc in range(2):
+                first = (2 + 2 * j + cc) * lead
+                todo.append((src.at[pl.ds(first, lead)], outs[0].at[j, yx, cc, zz]))
+        todo.append((src.at[pl.ds(8 * lead, 16)], outs[2].at[yx, zz]))
+        return todo
+
+    def attn_moves(ins, outs):
+        _, _, zz = place()
+        parity = lax.rem(zz, 2)
+        todo = final_moves(ins[:8], outs, "z", attn_blocks)
+        todo += [(ins[8], outs[3])]
+        todo += [(ins[9].at[parity], outs[4]), (ins[9].at[1 - parity], outs[5])]
+        return todo
+
+    wqkv, wout, small_all, down_own, cot0, cot1 = copies(
+        p_pieces + [down_weight, cotangent],
+        [
+            shape((3, 4, 2, 4, lead, half)),
+            shape((4, 4, lead, width)),
+            shape((4, 4, 16, half)),
+            shape(down_weight.shape),
+            shape((rows, width)),
+            shape((rows, width)),
+        ],
+        attn_moves,
+        16 * 9 + 3,
+        "attn_whole",
+    )
+    wqkv = wqkv.reshape(3, width, half)
+    wout = wout.reshape(half, width)
+
+    def up_blocks(src, outs, yx, zz):
+        return [(src.at[pl.ds(cc * lead, lead)], outs[0].at[yx, cc, zz]) for cc in range(2)]
+
+    wup = copies(
+        q_pieces,
+        [shape((4, 2, 4, lead, units))],
+        lambda ins, outs: final_moves(ins, outs, "xy", up_blocks),
+        32,
+        "up_whole",
+    )[0].reshape(width, units)
+
+    def sequence_moves(ins, outs):
+        _, cc, zz = place()
+        parity = lax.rem(zz, 2)
+        return [
+            (ins[2 * m + k], outs[0].at[(1 - cc if m else cc), parity ^ k])
+            for m in range(2)
+            for k in range(2)
+        ]
+
+    def whole_sequence(pieces, name):
+        return copies(pieces, [shape((2, 2) + pieces[0].shape)], sequence_moves, 4, name)[0]
+
+    x_blocks = whole_sequence(got + mate, "inputs_whole")
+    x = x_blocks[:, :, :rows].reshape(total, width)
+    segments = x_blocks[:, :, rows, :rows].reshape(total).astype(F32)
+    seg_col, seg_row = segments.reshape(total, 1), segments.reshape(1, total)
+
+    da, db = ring_first(down_own, Z_UP, Z_DOWN)
+    dc = ring_second(da, db, Z_UP, Z_DOWN)
+    d_low, d_high = copies(
+        [down_own, da, db, *dc],
+        [shape((2, down_rows, width))] * 2,
+        inner_kernel_moves(1),
+        5,
+        "down_inner",
+    )
+    d_pieces = ring_outer(d_low, d_high, X_SWAP, Y_SWAP, Y_SWAP, X_SWAP)
+    cot_got = [send(cot0, SEQUENCE[0]), send(cot1, SEQUENCE[1])]
+    cot_mate = [send(g, CORE_SWAP) for g in cot_got]
+    wdown = copies(
+        d_pieces,
+        [shape((4, 4, down_rows, width))],
+        lambda ins, outs: final_moves(
+            ins, outs, "z", lambda src, outs, yx, zz: [(src, outs[0].at[yx, zz])]
+        ),
+        16,
+        "down_whole",
+    )[0].reshape(units, width)
+    cot = whole_sequence(cot_got + cot_mate, "cotangent_whole").reshape(total, width)
+
+    small_all = small_all.reshape(4, 4, 2, 8, half)[:, :, :, 0, :count]
+    vectors = small_all[..., : 8 * lead].reshape(4, 4, 2, 8, lead).transpose(3, 0, 2, 1, 4)
+    own_cols = lax.dynamic_index_in_dim(vectors, c, 2, keepdims=False).reshape(8, half)
+    vectors = vectors.reshape(8, width).astype(F32)
+    line = lambda j: vectors[j : j + 1]
+    gain1, shift1, bias_o, gain2, shift2, bias_d = [line(j) for j in (0, 1, 4, 5, 6, 7)]
+    qkv_bias = jnp.stack([own_cols[2], jnp.zeros_like(own_cols[2]), own_cols[3]]).astype(F32)
+    bias_u = lax.dynamic_index_in_dim(small_all[..., 8 * lead :], c, 2, keepdims=False)
+    bias_u = bias_u.reshape(1, units).astype(F32)
+
+    normed, qkv = project(x, gain1, shift1, wqkv, qkv_bias)
+    mixed, log = attend(qkv, seg_col, seg_row, size, d_low)
+    part = rows_matmul(mixed, wout, NN, "attend_out")
+    middle, second = middle_norm(x, part, send(part, CORE_SWAP), bias_o, gain2, shift2)
+    hidden, pre_grad, up_bias_grad = feed_forward(second, cot, wup, bias_u, wdown)
+
+    part = rows_matmul(pre_grad, wup, NT, "second_grad")
+    got = send(part, CORE_SWAP)
+    p = down_grads(pos, hidden, cot, down_rows)
+    q = up_grads(pos, second, pre_grad, lead)
+    p_got, q_got, passed = outer_scatter(p, q, "feed")
+    branch, middle_grad, mixed_grad, sums2 = middle_back(part, got, middle, cot, gain2, wout)
+
+    grads, qv_bias_grad = attend_back(qkv, log, mixed_grad, seg_col, seg_row, size, passed)
+    p_last, q_last = inner_scatter(p, q, p_got, q_got, [], "feed")
+    down_out, up_kept, up_given = call(
+        feed_last_kernel,
+        p_last + q_last,
+        [shape(p_last[0].shape, F32)] + [shape((lead, units), F32)] * 2,
+        "feed_last",
+        scratch=[pltpu.VMEM((2 * lead, units), F32)],
+    )
+    up_got = send(up_given, CORE_SWAP)
+
+    part = source_grad(grads, wqkv)
+    got = send(part, CORE_SWAP)
+    pq = attn_grads(pos, normed, grads, mixed, branch, lead)
+    p, q = pq[:7], pq[7:]
+    p_got, q_got, _ = outer_scatter(p, q, "attn")
+
+    theirs, mine = output_rows(pos, hidden, wdown, middle, bias_d)
+    blocks = call(
+        result_kernel, [mine, send(theirs, CORE_SWAP)], [shape((rows, width))] * 2, "result"
+    )
+
+    def to_tokens(blocks):
+        got = [send(block, pairs) for block, pairs in zip(blocks, SEQUENCE)]
+        return jnp.where((z & 1) == 0, jnp.stack(got), jnp.stack(got[::-1]))
+
+    output = to_tokens(blocks)
+    in0, in1, sums1 = input_back(pos, part, got, x, middle_grad, gain1)
+    input_grad = to_tokens([in0, in1]).astype(F32)
+
+    wide = jnp.stack([sums1[0], sums1[1], sums2[2], sums2[0], sums2[1], sums2[3]])
+    wide = lax.dynamic_index_in_dim(wide.reshape(6, 4, 2, 4, lead), c, 2, keepdims=False)
+    wide = jnp.concatenate(
+        [wide[:2], qv_bias_grad.reshape(2, 4, 4, lead), wide[2:]], axis=0
+    ).transpose(2, 1, 0, 3)
+    tiny = jnp.concatenate(
+        [
+            wide.reshape(4, 4, 8 * lead),
+            up_bias_grad.reshape(4, 4, down_rows).transpose(1, 0, 2),
+        ],
+        axis=-1,
+    ).astype(BF)
+    tiny = jnp.pad(tiny[:, :, None], ((0, 0), (0, 0), (0, 15), (0, half - count)))
+    pick = lambda k: lax.dynamic_index_in_dim(tiny, (z + k) % 4, 0, keepdims=False)
+    extra = [pick(0), send(pick(1), Z_UP), send(pick(3), Z_DOWN), send(pick(2), Z_FAR)]
+
+    p_last, q_last = inner_scatter(p, q, p_got, q_got, extra, "attn")
+    qkv_kept, qkv_given, out_out, small_sum = call(
+        attn_last_kernel,
+        p_last + q_last,
+        [shape((3, lead, half), F32)] * 2 + [shape((lead, width), F32), shape((16, half), F32)],
+        "attn_last",
+        scratch=[
+            pltpu.VMEM((4 * lead, half), F32),
+            pltpu.VMEM((4 * lead + 16, half), F32),
+        ],
+    )
+
+    def whole_columns(kept, got):
+        cols = kept.shape[-1] // 4
+        kept, got = [a.reshape(a.shape[:-1] + (4, 1, cols)) for a in (kept, got)]
+        both = jnp.where(
+            c == 0, jnp.concatenate([kept, got], -2), jnp.concatenate([got, kept], -2)
+        )
+        return both.reshape(both.shape[:-3] + (8 * cols,))
+
+    up_out = whole_columns(up_kept, up_got)
+    qkv_out = whole_columns(qkv_kept, send(qkv_given, CORE_SWAP))
+    small_sum = small_sum[0]
+    vec = lambda j: small_sum[j * lead : (j + 1) * lead]
+    return (
+        output,
+        input_grad,
+        vec(0),
+        vec(1),
+        qkv_out[0],
+        vec(2),
+        qkv_out[1],
+        qkv_out[2],
+        vec(3),
+        out_out,
+        vec(4),
+        vec(5),
+        vec(6),
+        up_out,
+        small_sum[8 * lead : count],
+        down_out,
+        vec(7),
+    )
+
+
 def solution(mesh):
+    fast = mesh.shape["dp"] == 8 and mesh.shape["ctx"] == 4
     return jax.shard_map(
-        local,
+        fast_local if fast else local,
         mesh=mesh,
         in_specs=(
             P("dp", "ctx", None),

time: 2120 us -> 566 us (0.27)
  waiting for transfers between devices: 1620 us -> 177 us
  Pallas kernels: 0 us -> 214 us
  matrix products: 203 us -> 0 us
  blocking collectives: 151 us -> 0 us
  starting transfers between devices: 0.89 us -> 121 us
  other arithmetic: 72.2 us -> 7.2 us
    reduce_scatter x8 -> x0, waiting for transfers between devices: 1290 us -> none  [the longest x1 366 us: backward_part(): lax.psum_scatter(up_grad, ('dp', 'ctx'), scatter_dimension=0, tiled=True)]
    all_gather x8 -> x0, waiting for transfers between devices: 319 us -> none  [the longest x1 76.2 us: gather_feed(): lax.all_gather(up_weight, ('dp', 'ctx'), axis=0, tiled=True)]
    pallas_call x0 -> x32, Pallas kernels: none -> 214 us  [the longest x27 163 us: call(): pl.pallas_call(body, grid=grid, in_specs=in_specs or [VMEM] * len(ins), o...]
    dot_general x24 -> x0, matrix products: 203 us -> none  [the longest x6 40.8 us: outer_sum(): jnp.einsum('btd,bte->de', left, right, preferred_element_type=jnp.float32)]
    ppermute x0 -> x93, waiting for transfers between devices: none -> 177 us  [send(): return lax.ppermute(value, AXES, pairs)]
    ppermute x0 -> x93, starting transfers between devices: none -> 121 us  [send(): return lax.ppermute(value, AXES, pairs)]
    unnamed x2 -> x0, blocking collectives: 81 us -> none
    all_gather x2 -> x0, blocking collectives: 69.9 us -> none  [the longest x1 59.4 us: gather_feed(): lax.all_gather(up_bias, ('dp', 'ctx'), axis=0, tiled=True)]
  transfers between devices with their start and end apart: 16 -> 93, of which waited for: 14 -> 28; matrix products, arithmetic and copies ran while one was open for 13% -> 5% of each run, Pallas kernels for 0% -> 32%
where the time goes in v2:
time: 566 us; the launch traced here: 558 us
  Pallas kernels  214 us (38%)
  waiting for transfers between devices  177 us (31%)
  starting transfers between devices  121 us (21%)
  local copies, waits for them, and re-layouts  36.3 us (6%)
  other arithmetic  7.2 us (1%)
    ppermute x93, waiting for transfers between devices, send(): return lax.ppermute(value, AXES, pairs)  177 us
    pallas_call x27, Pallas kernels, call(): pl.pallas_call(body, grid=grid, in_specs=in_specs or [VMEM] * len(ins), o...  163 us
    ppermute x93, starting transfers between devices, send(): return lax.ppermute(value, AXES, pairs)  121 us
    pallas_call x5, Pallas kernels, placed_call(): pl.pallas_call(body, grid_spec=pltpu.PrefetchScalarGridSpec(num_scalar_pr...  50.9 us
    unnamed x142, local copies, waits for them, and re-layouts  15.4 us
  transfers between devices with their start and end apart: 93, of which 28 were waited for; matrix products, arithmetic and copies ran while one was open for 5% of the time, Pallas kernels for 32%

profile of v2, /device:TPU:13, one launch (start us, length us, event | category | flops | bytes accessed | tf_op | source)
XLA Modules:
  0.0 557.7 jit_solution(13520367768924222383)
XLA Ops:
  2.1 3.3 first.1
  6.3 4.5 collective-permute-start
  17.0 3.7 collective-permute-done.11.refs_7_
  22.0 15.0 %collective-permute-done.7.refs_2_ = bf16[272,512]{1,0:T(8,128)(2,1)S(1)} collective-permute-done((bf16[272,512]{1,0:T(8,128)(2,1)}, bf16[272,512]{1,0:T(8,128)(2,1)S(1)}, u32[]{:S(2)}, u32[]{:S(2)}) %collective-permute-start.7) | collective-permute-done | bytes 278560 | tf_op jit(solution)/shard_map/ppermute | solution.py:344
  37.1 3.9 collective-permute-start.1
  47.1 4.6 collective-permute-done.8.refs_3_
  52.9 2.9 inner.1
  59.0 2.9 collective-permute-start.2
  63.6 2.5 collective-permute-done.14.refs_2_
  68.7 3.6 collective-permute-start.18
  73.5 3.0 inputs_whole.1
  76.5 3.2 slice.240
  81.5 6.1 %collective-permute-start.29 = (bf16[2,64,2048]{2,1,0:T(8,128)(2,1)S(1)}, bf16[2,64,2048]{2,1,0:T(8,128)(2,1)}, u32[]{:S(2)}, u32[]{:S(2)}) collective-permute-start(bf16[2,64,2048]{2,1,0:T(8,128)(2,1)S(1)} %copy-done.15), channel_id=1, source_target_pairs={{0,1},{1,2},{2,3},{3,0},{4,5},{5,6},{6,7},{7,4},{8,9},{9,10},{10,1... | collective-permute-start | bytes 1572872 | tf_op jit(solution)/shard_map/ppermute | solution.py:344
  87.5 5.0 collective-permute-done.18.refs_6_
  92.5 6.6 %attn_whole.1 = (bf16[3,4,2,4,32,512]{5,4,3,2,1,0:T(8,128)(2,1)}, bf16[4,4,32,1024]{3,2,1,0:T(8,128)(2,1)}, bf16[4,4,16,512]{3,2,1,0:T(8,128)(2,1)}, bf16[128,10...) custom-call(bf16[2,272,512]{2,1,0:T(8,128)(2,1)} %get-tuple-element.134.refs_0_, ...), custom_call_target="tpu_custom_call" | custom-call | bytes 11534336 | tf_op jit(solution)/shard_map/attn_whole/pallas_call | solution.py:367
  99.1 7.8 %collective-permute-start.20 = (bf16[128,1024]{1,0:T(8,128)(2,1)}, bf16[128,1024]{1,0:T(8,128)(2,1)S(1)}, u32[]{:S(2)}, u32[]{:S(2)}) collective-permute-start(bf16[128,1024]{1,0:T(8,128)(2,1)} %get-tuple-element.139.refs_0_), channel_id=1, source_target_pairs={{0,1},{1,2},{2,3},{3,0},{4,5},{5,6},{6,7},{7,4},{8,9},{9,10},{10,1... | collective-permute-start | bytes 786440 | tf_op jit(solution)/shard_map/ppermute | solution.py:344
  110.5 8.2 %collective-permute-done.21.refs_2_ = bf16[128,1024]{1,0:T(8,128)(2,1)S(1)} collective-permute-done((bf16[128,1024]{1,0:T(8,128)(2,1)}, bf16[128,1024]{1,0:T(8,128)(2,1)S(1)}, u32[]{:S(2)}, u32[]{:S(2)}) %collective-permute-start.21) | collective-permute-done | bytes 262176 | tf_op jit(solution)/shard_map/ppermute | solution.py:344
  118.7 4.9 collective-permute-done.20.refs_1_
  123.6 2.1 collective-permute-start.22
  125.8 8.1 %project.1 = (bf16[1024,1024]{1,0:T(8,128)(2,1)}, bf16[3,1024,512]{2,1,0:T(8,128)(2,1)}) custom-call(bf16[1024,1024]{1,0:T(8,128)(2,1)} %bitcast.70, f32[1,1024]{1,0:T(1,128)} %slice.194.gain, f32[1,1024]{1,0:T(1,128)} %slice.196.shift, bf16[3,1024,512]{2,1,0:T(8,128)(2,1)} %bitcast.99, f32[3,512]{1,0:T(4,128)} %maximum_convert_fusion.bias), custom_call_target="tpu_custom_call" | custom-call | flops 3221225472 | bytes 10500096 | tf_op jit(solution)/shard_map/project/pallas_call | solution.py:367
  135.3 2.2 down_inner.1
  137.5 18.3 %attend.1 = (bf16[1024,512]{1,0:T(8,128)(2,1)}, f32[1024,512]{1,0:T(8,128)}) custom-call(f32[1024,1]{1,0:T(8,128)} %copy.66.column, f32[1,1024]{1,0:T(1,128)} %bitcast.94, bf16[3,1024,512]{2,1,0:T(8,128)(2,1)} %get-tuple-element.138.q_ref.k_ref.v_ref, bf16[3,1024,512]{2,1,0:T(8,128)(2,1)} %get-tuple-element.138.q_ref.k_ref.v_ref, ...), custom_call_target="tpu_custom_call" | custom-call | flops 8589934592 | bytes 13115392 | tf_op jit(solution)/shard_map/attend/pallas_call | solution.py:367
  155.8 4.8 attend_out.1.part
  160.6 2.8 collective-permute-start.24
  164.8 4.1 collective-permute-start.25
  168.9 2.5 collective-permute-start.26
  171.4 5.6 %collective-permute-done.33.refs_6_ = bf16[2,64,2048]{2,1,0:T(8,128)(2,1)S(1)} collective-permute-done((bf16[2,64,2048]{2,1,0:T(8,128)(2,1)}, bf16[2,64,2048]{2,1,0:T(8,128)(2,1)S(1)}, u32[]{:S(2)}, u32[]{:S(2)}) %collective-permute-start.33) | collective-permute-done | bytes 524320 | tf_op jit(solution)/shard_map/ppermute | solution.py:344
  177.9 10.8 %collective-permute-done.34.refs_7_ = bf16[2,64,2048]{2,1,0:T(8,128)(2,1)S(1)} collective-permute-done((bf16[2,64,2048]{2,1,0:T(8,128)(2,1)}, bf16[2,64,2048]{2,1,0:T(8,128)(2,1)S(1)}, u32[]{:S(2)}, u32[]{:S(2)}) %collective-permute-start.34) | collective-permute-done | bytes 524320 | tf_op jit(solution)/shard_map/ppermute | solution.py:344
  188.7 2.4 collective-permute-start.35
  191.1 10.5 %collective-permute-done.25.refs_0_ = bf16[256,1024]{1,0:T(8,128)(2,1)S(1)} collective-permute-done((bf16[256,1024]{1,0:T(8,128)(2,1)}, bf16[256,1024]{1,0:T(8,128)(2,1)S(1)}, u32[]{:S(2)}, u32[]{:S(2)}) %collective-permute-start.25) | collective-permute-done | bytes 524320 | tf_op jit(solution)/shard_map/ppermute | solution.py:344
  201.6 10.1 %collective-permute-done.26.refs_1_ = bf16[256,1024]{1,0:T(8,128)(2,1)S(1)} collective-permute-done((bf16[256,1024]{1,0:T(8,128)(2,1)}, bf16[256,1024]{1,0:T(8,128)(2,1)S(1)}, u32[]{:S(2)}, u32[]{:S(2)}) %collective-permute-start.26) | collective-permute-done | bytes 524320 | tf_op jit(solution)/shard_map/ppermute | solution.py:344
  215.6 4.6 up_whole.1
  222.9 2.9 cotangent_whole.1
  225.8 10.6 %collective-permute-done.40.refs_7_ = bf16[2,128,1024]{2,1,0:T(8,128)(2,1)} collective-permute-done((bf16[2,128,1024]{2,1,0:T(8,128)(2,1)S(1)}, bf16[2,128,1024]{2,1,0:T(8,128)(2,1)}, u32[]{:S(2)}, u32[]{:S(2)}) %collective-permute-start.40) | collective-permute-done | bytes 524320 | tf_op jit(solution)/shard_map/ppermute | solution.py:344
  236.8 4.3 down_whole.1
  242.6 6.0 %middle.1 = (f32[1024,1024]{1,0:T(8,128)}, bf16[1024,1024]{1,0:T(8,128)(2,1)}) custom-call(bf16[1024,1024]{1,0:T(8,128)(2,1)} %bitcast.71, bf16[1024,1024]{1,0:T(8,128)(2,1)} %attend_out.1.part, bf16[1024,1024]{1,0:T(8,128)(2,1)} %copy-done.1, f32[1,1024]{1,0:T(1,128)} %slice.204.bias, f32[1,1024]{1,0:T(1,128)} %slice.206.gain, f32[1,1024]{1,0:T(1,128)} %slice.208.shift), custom_call_target="tpu_custom_call" | custom-call | bytes 12595200 | tf_op jit(solution)/shard_map/middle/pallas_call | solution.py:367
  248.6 16.4 %feed.1 = (bf16[1024,2048]{1,0:T(8,128)(2,1)}, bf16[1024,2048]{1,0:T(8,128)(2,1)}, f32[1,2048]{1,0:T(1,128)}) custom-call(bf16[1024,1024]{1,0:T(8,128)(2,1)} %get-tuple-element.143.second, bf16[1024,1024]{1,0:T(8,128)(2,1)} %bitcast.73, bf16[1024,2048]{1,0:T(8,128)(2,1)} %bitcast.78, f32[1,2048]{1,0:T(1,128)} %convert.28.bias, bf16[2048,1024]{1,0:T(8,128)(2,1)} %bitcast.76), custom_call_target="tpu_custom_call" | custom-call | flops 8589934592 | bytes 20987904 | tf_op jit(solution)/shard_map/feed/pallas_call | solution.py:367
  264.9 8.6 %second_grad.1.part = bf16[1024,1024]{1,0:T(8,128)(2,1)} custom-call(bf16[1024,2048]{1,0:T(8,128)(2,1)} %get-tuple-element.156.left.pre, bf16[1024,2048]{1,0:T(8,128)(2,1)} %bitcast.79), custom_call_target="tpu_custom_call" | custom-call | flops 4294967296 | bytes 10485760 | tf_op jit(solution)/shard_map/second_grad/pallas_call | solution.py:367
  275.7 10.6 %up_grads.1 = (bf16[2,64,2048]{2,1,0:T(8,128)(2,1)}, bf16[2,64,2048]{2,1,0:T(8,128)(2,1)}, bf16[2,64,2048]{2,1,0:T(8,128)(2,1)}, bf16[2,64,2048]{2,1,0:T(8,128)(...) custom-call(s32[3]{0:T(128)} %pad_add_fusion.1.pos, ...), custom_call_target="tpu_custom_call" | custom-call | flops 4294967296 | bytes 10485760 | tf_op jit(solution)/shard_map/up_grads/pallas_call | solution.py:382
  287.8 10.3 %down_grads.1 = (bf16[2,128,1024]{2,1,0:T(8,128)(2,1)}, bf16[2,128,1024]{2,1,0:T(8,128)(2,1)}, bf16[2,128,1024]{2,1,0:T(8,128)(2,1)}, bf16[2,128,1024]{2,1,0:T(8...) custom-call(s32[3]{0:T(128)} %pad_add_fusion.1.pos, ...), custom_call_target="tpu_custom_call" | custom-call | flops 4294967296 | bytes 10485760 | tf_op jit(solution)/shard_map/down_grads/pallas_call | solution.py:382
  302.0 6.8 %collective-permute-done.48.refs_7_ = bf16[2,64,2048]{2,1,0:T(8,128)(2,1)S(1)} collective-permute-done((bf16[2,64,2048]{2,1,0:T(8,128)(2,1)}, bf16[2,64,2048]{2,1,0:T(8,128)(2,1)S(1)}, u32[]{:S(2)}, u32[]{:S(2)}) %collective-permute-start.48) | collective-permute-done | bytes 524320 | tf_op jit(solution)/shard_map/ppermute | solution.py:344
  312.3 2.8 collective-permute-start.79
  315.2 3.6 feed_pass.1
  320.1 9.9 %middle_back.1 = (bf16[1024,1024]{1,0:T(8,128)(2,1)}, f32[1024,1024]{1,0:T(8,128)}, bf16[1024,512]{1,0:T(8,128)(2,1)}, f32[4,1024]{1,0:T(4,128)}) custom-call(bf16[1024,1024]{1,0:T(8,128)(2,1)} %second_grad.1.part, bf16[1024,1024]{1,0:T(8,128)(2,1)} %copy-done.2, f32[1024,1024]{1,0:T(8,128)} %get-tuple-element.150.middle, bf16[1024,1024]{1,0:T(8,128)(2,1)} %bitcast.75, ...), custom_call_target="tpu_custom_call" | custom-call | flops 1073741824 | bytes 18894848 | tf_op jit(solution)/shard_map/middle_back/pallas_call | solution.py:367
  330.0 24.4 %attend_back.1 = (bf16[3,1024,512]{2,1,0:T(8,128)(2,1)}, f32[2,512]{1,0:T(2,128)}) custom-call(f32[1024,1]{1,0:T(8,128)} %copy.66.column, f32[1,1024]{1,0:T(1,128)} %bitcast.95, bf16[3,1024,512]{2,1,0:T(8,128)(2,1)} %get-tuple-element.138.q_ref.k_ref.v_ref, bf16[3,1024,512]{2,1,0:T(8,128)(2,1)} %get-tuple-element.138.q_ref.k_ref.v_ref, ...), custom_call_target="tpu_custom_call" | custom-call | flops 12884901888 | bytes 16265216 | tf_op jit(solution)/shard_map/attend_back/pallas_call | solution.py:367
  354.4 7.4 %source_grad.1.part = bf16[1024,1024]{1,0:T(8,128)(2,1)} custom-call(bf16[3,1024,512]{2,1,0:T(8,128)(2,1)} %get-tuple-element.167.grads, bf16[3,1024,512]{2,1,0:T(8,128)(2,1)} %bitcast.100), custom_call_target="tpu_custom_call" | custom-call | flops 3221225472 | bytes 8388608 | tf_op jit(solution)/shard_map/source_grad/pallas_call | solution.py:367
  363.5 10.5 %output_rows.1 = (bf16[512,1024]{1,0:T(8,128)(2,1)}, f32[512,1024]{1,0:T(8,128)}) custom-call(s32[3]{0:T(128)} %pad_add_fusion.1.pos, bf16[1024,2048]{1,0:T(8,128)(2,1)} %get-tuple-element.149.hidden, bf16[2048,1024]{1,0:T(8,128)(2,1)} %bitcast.77, f32[1024,1024]{1,0:T(8,128)} %get-tuple-element.150.middle, f32[1,1024]{1,0:T(1,128)} %slice.211.bias), custom_call_target="tpu_custom_call" | custom-call | flops 4294967296 | bytes 15732736 | tf_op jit(solution)/shard_map/output_rows/pallas_call | solution.py:382
  378.2 11.3 %collective-permute-done.80.refs_6_ = bf16[2,64,2048]{2,1,0:T(8,128)(2,1)} collective-permute-done((bf16[2,64,2048]{2,1,0:T(8,128)(2,1)}, bf16[2,64,2048]{2,1,0:T(8,128)(2,1)}, u32[]{:S(2)}, u32[]{:S(2)}) %collective-permute-start.80) | collective-permute-done | bytes 524320 | tf_op jit(solution)/shard_map/ppermute | solution.py:344
  389.5 11.2 %collective-permute-done.83.refs_9_ = bf16[2,64,2048]{2,1,0:T(8,128)(2,1)} collective-permute-done((bf16[2,64,2048]{2,1,0:T(8,128)(2,1)}, bf16[2,64,2048]{2,1,0:T(8,128)(2,1)}, u32[]{:S(2)}, u32[]{:S(2)}) %collective-permute-start.83) | collective-permute-done | bytes 524320 | tf_op jit(solution)/shard_map/ppermute | solution.py:344
  400.7 5.3 feed_join.1
  406.0 2.2 collective-permute-start.84
  410.4 11.5 %attn_grads.1 = (bf16[2,128,512]{2,1,0:T(8,128)(2,1)}, bf16[2,128,512]{2,1,0:T(8,128)(2,1)}, bf16[2,128,512]{2,1,0:T(8,128)(2,1)}, bf16[2,128,512]{2,1,0:T(8,128...) custom-call(s32[3]{0:T(128)} %pad_add_fusion.1.pos, ...), custom_call_target="tpu_custom_call" | custom-call | flops 4294967296 | bytes 12582912 | tf_op jit(solution)/shard_map/attn_grads/pallas_call | solution.py:382
  425.4 3.0 result.1
  428.4 2.4 feed_inner.1
  437.6 2.5 attn_pass.1
  441.5 8.1 %input_back.1 = (bf16[256,1024]{1,0:T(8,128)(2,1)}, bf16[256,1024]{1,0:T(8,128)(2,1)}, f32[2,1024]{1,0:T(2,128)}) custom-call(s32[3]{0:T(128)} %pad_add_fusion.1.pos, bf16[1024,1024]{1,0:T(8,128)(2,1)} %source_grad.1.part, bf16[1024,1024]{1,0:T(8,128)(2,1)} %copy-done, bf16[1024,1024]{1,0:T(8,128)(2,1)} %bitcast.72, f32[1024,1024]{1,0:T(8,128)} %get-tuple-element.168.mgrad, ...), custom_call_target="tpu_custom_call" | custom-call | bytes 11546624 | tf_op jit(solution)/shard_map/input_back/pallas_call | solution.py:382
  451.9 2.8 collective-permute-start.60
  456.4 7.9 %collective-permute-start.42 = (bf16[256,1024]{1,0:T(8,128)(2,1)}, bf16[256,1024]{1,0:T(8,128)(2,1)S(1)}, u32[]{:S(2)}, u32[]{:S(2)}) collective-permute-start(bf16[256,1024]{1,0:T(8,128)(2,1)} %get-tuple-element.153), channel_id=1, source_target_pairs={{0,0},{1,1},{2,4},{3,5},{4,2},{5,3},{6,6},{7,7},{8,8},{9,9},{10,12... | collective-permute-start | bytes 1572872 | tf_op jit(solution)/shard_map/ppermute | solution.py:344
  468.2 32.3 %collective-permute-done.64.refs_11_ = bf16[4,16,512]{2,1,0:T(8,128)(2,1)S(1)} collective-permute-done((bf16[4,16,512]{2,1,0:T(8,128)(2,1)S(1)}, bf16[4,16,512]{2,1,0:T(8,128)(2,1)S(1)}, u32[]{:S(2)}, u32[]{:S(2)}) %collective-permute-start.64) | collective-permute-done | bytes 65568 | tf_op jit(solution)/shard_map/ppermute | solution.py:344
  503.2 3.3 attn_join.1
  508.5 2.6 feed_last.1
  525.4 6.6 %collective-permute-start.50 = (bf16[256,1024]{1,0:T(8,128)(2,1)S(1)}, bf16[256,1024]{1,0:T(8,128)(2,1)S(1)}, u32[]{:S(2)}, u32[]{:S(2)}) collective-permute-start(bf16[256,1024]{1,0:T(8,128)(2,1)S(1)} %copy-done.67), channel_id=1, source_target_pairs={{0,0},{1,1},{2,4},{3,5},{4,2},{5,3},{6,6},{7,7},{8,8},{9,9},{10,12... | collective-permute-start | bytes 1572872 | tf_op jit(solution)/shard_map/ppermute | solution.py:344
  532.8 2.1 attn_last.1
  543.9 11.8 %collective-permute-done.51 = bf16[256,1024]{1,0:T(8,128)(2,1)S(1)} collective-permute-done((bf16[256,1024]{1,0:T(8,128)(2,1)S(1)}, bf16[256,1024]{1,0:T(8,128)(2,1)S(1)}, u32[]{:S(2)}, u32[]{:S(2)}) %collective-permute-start.51) | collective-permute-done | bytes 524320 | tf_op jit(solution)/shard_map/ppermute | solution.py:344
  (374 shorter events, 112.9 us)
Async XLA Ops:
  6.3 52.7 %collective-permute-start = (bf16[272,1024]{1,0:T(8,128)(2,1)}, bf16[272,1024]{1,0:T(8,128)(2,1)S(1)}, u32[]{:S(2)}, u32[]{:S(2)}) collective-permute-start(bf16[272,1024]{1,0:T(8,128)(2,1)} %get-tuple-element.128), channel_id=1, source_target_pairs={{0,0},{1,1},{2,4},{3,5},{4,2},{5,3},{6,6},{7,7},{8,8},{9,9},{10,12... | collective-permute-start | bytes 1671176 | tf_op jit(solution)/shard_map/ppermute | solution.py:344
  14.4 22.7 %collective-permute-start.7 = (bf16[272,512]{1,0:T(8,128)(2,1)}, bf16[272,512]{1,0:T(8,128)(2,1)S(1)}, u32[]{:S(2)}, u32[]{:S(2)}) collective-permute-start(bf16[272,512]{1,0:T(8,128)(2,1)} %get-tuple-element.132.refs_0_), channel_id=1, source_target_pairs={{0,3},{1,0},{2,1},{3,2},{4,7},{5,4},{6,5},{7,6},{8,11},{9,8},{10,9... | collective-permute-start | bytes 835592 | tf_op jit(solution)/shard_map/ppermute | solution.py:344
  14.5 28.4 %collective-permute-start.6 = (bf16[272,512]{1,0:T(8,128)(2,1)}, bf16[272,512]{1,0:T(8,128)(2,1)S(1)}, u32[]{:S(2)}, u32[]{:S(2)}) collective-permute-start(bf16[272,512]{1,0:T(8,128)(2,1)} %get-tuple-element.132.refs_0_), channel_id=1, source_target_pairs={{0,1},{1,2},{2,3},{3,0},{4,5},{5,6},{6,7},{7,4},{8,9},{9,10},{10,1... | collective-permute-start | bytes 835592 | tf_op jit(solution)/shard_map/ppermute | solution.py:344
  15.8 25.2 %collective-permute-start.10 = (bf16[64,2048]{1,0:T(8,128)(2,1)}, bf16[64,2048]{1,0:T(8,128)(2,1)S(1)}, u32[]{:S(2)}, u32[]{:S(2)}) collective-permute-start(bf16[64,2048]{1,0:T(8,128)(2,1)} %get-tuple-element.133.refs_5_), channel_id=1, source_target_pairs={{0,8},{1,9},{2,10},{3,11},{4,12},{5,13},{6,14},{7,15},{8,0},{9,1},... | collective-permute-start | bytes 786440 | tf_op jit(solution)/shard_map/ppermute | solution.py:344
  20.7 22.5 %collective-permute-start.13 = (bf16[32,2048]{1,0:T(8,128)(2,1)S(1)}, bf16[32,2048]{1,0:T(8,128)(2,1)S(1)}, u32[]{:S(2)}, u32[]{:S(2)}) collective-permute-start(bf16[32,2048]{1,0:T(8,128)(2,1)S(1)} %slice.245), channel_id=1, source_target_pairs={{0,8},{1,9},{2,10},{3,11},{4,12},{5,13},{6,14},{7,15},{8,0},{9,1},... | collective-permute-start | bytes 393224 | tf_op jit(solution)/shard_map/ppermute | solution.py:344
  37.1 24.8 %collective-permute-start.1 = (bf16[272,1024]{1,0:T(8,128)(2,1)}, bf16[272,1024]{1,0:T(8,128)(2,1)S(1)}, u32[]{:S(2)}, u32[]{:S(2)}) collective-permute-start(bf16[272,1024]{1,0:T(8,128)(2,1)} %get-tuple-element.129), channel_id=1, source_target_pairs={{0,1},{1,0},{2,5},{3,4},{4,3},{5,2},{6,7},{7,6},{8,9},{9,8},{10,13... | collective-permute-start | bytes 1671176 | tf_op jit(solution)/shard_map/ppermute | solution.py:344
  59.0 13.4 %collective-permute-start.2 = (bf16[272,1024]{1,0:T(8,128)(2,1)S(1)}, bf16[272,1024]{1,0:T(8,128)(2,1)S(1)}, u32[]{:S(2)}, u32[]{:S(2)}) collective-permute-start(bf16[272,1024]{1,0:T(8,128)(2,1)S(1)} %collective-permute-done.refs_0_), channel_id=1, source_target_pairs={{0,4},{1,5},{2,6},{3,7},{4,0},{5,1},{6,2},{7,3},{8,12},{9,13},{10,... | collective-permute-start | bytes 1671176 | tf_op jit(solution)/shard_map/ppermute | solution.py:344
  61.9 19.5 %collective-permute-start.16 = (bf16[2,272,512]{2,1,0:T(8,128)(2,1)}, bf16[2,272,512]{2,1,0:T(8,128)(2,1)}, u32[]{:S(2)}, u32[]{:S(2)}) collective-permute-start(bf16[2,272,512]{2,1,0:T(8,128)(2,1)} %get-tuple-element.134.refs_0_), channel_id=1, source_target_pairs={{0,16},{1,17},{2,18},{3,19},{4,20},{5,21},{6,22},{7,23},{8,24},{9,... | collective-permute-start | bytes 1671176 | tf_op jit(solution)/shard_map/ppermute | solution.py:344
  66.1 21.4 %collective-permute-start.15 = (bf16[2,272,512]{2,1,0:T(8,128)(2,1)}, bf16[2,272,512]{2,1,0:T(8,128)(2,1)}, u32[]{:S(2)}, u32[]{:S(2)}) collective-permute-start(bf16[2,272,512]{2,1,0:T(8,128)(2,1)} %get-tuple-element.135.refs_1_), channel_id=1, source_target_pairs={{0,8},{1,9},{2,10},{3,11},{4,12},{5,13},{6,14},{7,15},{8,0},{9,1},... | collective-permute-start | bytes 1671176 | tf_op jit(solution)/shard_map/ppermute | solution.py:344
  68.7 23.8 %collective-permute-start.18 = (bf16[2,272,512]{2,1,0:T(8,128)(2,1)S(1)}, bf16[2,272,512]{2,1,0:T(8,128)(2,1)}, u32[]{:S(2)}, u32[]{:S(2)}) collective-permute-start(bf16[2,272,512]{2,1,0:T(8,128)(2,1)S(1)} %collective-permute-done.14.refs_2_), channel_id=1, source_target_pairs={{0,16},{1,17},{2,18},{3,19},{4,20},{5,21},{6,22},{7,23},{8,24},{9,... | collective-permute-start | bytes 1671176 | tf_op jit(solution)/shard_map/ppermute | solution.py:344
  72.4 20.1 %collective-permute-start.19 = (bf16[2,272,512]{2,1,0:T(8,128)(2,1)}, bf16[2,272,512]{2,1,0:T(8,128)(2,1)}, u32[]{:S(2)}, u32[]{:S(2)}) collective-permute-start(bf16[2,272,512]{2,1,0:T(8,128)(2,1)} %collective-permute-done.17.refs_5_), channel_id=1, source_target_pairs={{0,8},{1,9},{2,10},{3,11},{4,12},{5,13},{6,14},{7,15},{8,0},{9,1},... | collective-permute-start | bytes 1671176 | tf_op jit(solution)/shard_map/ppermute | solution.py:344
  72.7 92.1 %collective-permute-start.31 = (bf16[2,64,2048]{2,1,0:T(8,128)(2,1)}, bf16[2,64,2048]{2,1,0:T(8,128)(2,1)}, u32[]{:S(2)}, u32[]{:S(2)}) collective-permute-start(bf16[2,64,2048]{2,1,0:T(8,128)(2,1)} %get-tuple-element.146.refs_0_), channel_id=1, source_target_pairs={{0,3},{1,0},{2,1},{3,2},{4,7},{5,4},{6,5},{7,6},{8,11},{9,8},{10,9... | collective-permute-start | bytes 1572872 | tf_op jit(solution)/shard_map/ppermute | solution.py:344
  81.5 81.9 %collective-permute-start.29 = (bf16[2,64,2048]{2,1,0:T(8,128)(2,1)S(1)}, bf16[2,64,2048]{2,1,0:T(8,128)(2,1)}, u32[]{:S(2)}, u32[]{:S(2)}) collective-permute-start(bf16[2,64,2048]{2,1,0:T(8,128)(2,1)S(1)} %copy-done.15), channel_id=1, source_target_pairs={{0,1},{1,2},{2,3},{3,0},{4,5},{5,6},{6,7},{7,4},{8,9},{9,10},{10,1... | collective-permute-start | bytes 1572872 | tf_op jit(solution)/shard_map/ppermute | solution.py:344
  87.5 76.6 %collective-permute-start.32 = (bf16[2,64,2048]{2,1,0:T(8,128)(2,1)S(1)}, bf16[2,64,2048]{2,1,0:T(8,128)(2,1)}, u32[]{:S(2)}, u32[]{:S(2)}) collective-permute-start(bf16[2,64,2048]{2,1,0:T(8,128)(2,1)S(1)} %copy-done.16), channel_id=1, source_target_pairs={{0,3},{1,0},{2,1},{3,2},{4,7},{5,4},{6,5},{7,6},{8,11},{9,8},{10,9... | collective-permute-start | bytes 1572872 | tf_op jit(solution)/shard_map/ppermute | solution.py:344
  99.1 19.6 %collective-permute-start.21 = (bf16[128,1024]{1,0:T(8,128)(2,1)}, bf16[128,1024]{1,0:T(8,128)(2,1)S(1)}, u32[]{:S(2)}, u32[]{:S(2)}) collective-permute-start(bf16[128,1024]{1,0:T(8,128)(2,1)} %get-tuple-element.139.refs_0_), channel_id=1, source_target_pairs={{0,3},{1,0},{2,1},{3,2},{4,7},{5,4},{6,5},{7,6},{8,11},{9,8},{10,9... | collective-permute-start | bytes 786440 | tf_op jit(solution)/shard_map/ppermute | solution.py:344
  99.1 24.5 %collective-permute-start.20 = (bf16[128,1024]{1,0:T(8,128)(2,1)}, bf16[128,1024]{1,0:T(8,128)(2,1)S(1)}, u32[]{:S(2)}, u32[]{:S(2)}) collective-permute-start(bf16[128,1024]{1,0:T(8,128)(2,1)} %get-tuple-element.139.refs_0_), channel_id=1, source_target_pairs={{0,1},{1,2},{2,3},{3,0},{4,5},{5,6},{6,7},{7,4},{8,9},{9,10},{10,1... | collective-permute-start | bytes 786440 | tf_op jit(solution)/shard_map/ppermute | solution.py:344
  118.7 15.3 %collective-permute-start.23 = (bf16[64,1024]{1,0:T(8,128)(2,1)S(1)}, bf16[64,1024]{1,0:T(8,128)(2,1)S(1)}, u32[]{:S(2)}, u32[]{:S(2)}) collective-permute-start(bf16[64,1024]{1,0:T(8,128)(2,1)S(1)} %slice.253), channel_id=1, source_target_pairs={{0,3},{1,0},{2,1},{3,2},{4,7},{5,4},{6,5},{7,6},{8,11},{9,8},{10,9... | collective-permute-start | bytes 393224 | tf_op jit(solution)/shard_map/ppermute | solution.py:344
  134.0 35.0 %collective-permute-start.30 = (bf16[2,64,2048]{2,1,0:T(8,128)(2,1)S(1)}, bf16[2,64,2048]{2,1,0:T(8,128)(2,1)}, u32[]{:S(2)}, u32[]{:S(2)}) collective-permute-start(bf16[2,64,2048]{2,1,0:T(8,128)(2,1)S(1)} %copy-done.16), channel_id=1, source_target_pairs={{0,1},{1,2},{2,3},{3,0},{4,5},{5,6},{6,7},{7,4},{8,9},{9,10},{10,1... | collective-permute-start | bytes 1572872 | tf_op jit(solution)/shard_map/ppermute | solution.py:344
  160.6 80.6 %collective-permute-start.24 = (bf16[1024,1024]{1,0:T(8,128)(2,1)}, bf16[1024,1024]{1,0:T(8,128)(2,1)S(1)}, u32[]{:S(2)}, u32[]{:S(2)}) collective-permute-start(bf16[1024,1024]{1,0:T(8,128)(2,1)} %attend_out.1.part), channel_id=1, source_target_pairs={{0,4},{1,5},{2,6},{3,7},{4,0},{5,1},{6,2},{7,3},{8,12},{9,13},{10,... | collective-permute-start | bytes 6291464 | tf_op jit(solution)/shard_map/ppermute | solution.py:344
  163.4 13.6 %collective-permute-start.33 = (bf16[2,64,2048]{2,1,0:T(8,128)(2,1)}, bf16[2,64,2048]{2,1,0:T(8,128)(2,1)S(1)}, u32[]{:S(2)}, u32[]{:S(2)}) collective-permute-start(bf16[2,64,2048]{2,1,0:T(8,128)(2,1)} %collective-permute-done.29.refs_2_), channel_id=1, source_target_pairs={{0,1},{1,2},{2,3},{3,0},{4,5},{5,6},{6,7},{7,4},{8,9},{9,10},{10,1... | collective-permute-start | bytes 1572872 | tf_op jit(solution)/shard_map/ppermute | solution.py:344
  164.1 24.6 %collective-permute-start.34 = (bf16[2,64,2048]{2,1,0:T(8,128)(2,1)}, bf16[2,64,2048]{2,1,0:T(8,128)(2,1)S(1)}, u32[]{:S(2)}, u32[]{:S(2)}) collective-permute-start(bf16[2,64,2048]{2,1,0:T(8,128)(2,1)} %collective-permute-done.32.refs_5_), channel_id=1, source_target_pairs={{0,3},{1,0},{2,1},{3,2},{4,7},{5,4},{6,5},{7,6},{8,11},{9,8},{10,9... | collective-permute-start | bytes 1572872 | tf_op jit(solution)/shard_map/ppermute | solution.py:344
  164.8 36.8 %collective-permute-start.25 = (bf16[256,1024]{1,0:T(8,128)(2,1)}, bf16[256,1024]{1,0:T(8,128)(2,1)S(1)}, u32[]{:S(2)}, u32[]{:S(2)}) collective-permute-start(bf16[256,1024]{1,0:T(8,128)(2,1)} %get-tuple-element.144), channel_id=1, source_target_pairs={{0,0},{1,1},{2,4},{3,5},{4,2},{5,3},{6,6},{7,7},{8,8},{9,9},{10,12... | collective-permute-start | bytes 1572872 | tf_op jit(solution)/shard_map/ppermute | solution.py:344
  168.9 42.8 %collective-permute-start.26 = (bf16[256,1024]{1,0:T(8,128)(2,1)}, bf16[256,1024]{1,0:T(8,128)(2,1)S(1)}, u32[]{:S(2)}, u32[]{:S(2)}) collective-permute-start(bf16[256,1024]{1,0:T(8,128)(2,1)} %get-tuple-element.145), channel_id=1, source_target_pairs={{0,1},{1,0},{2,5},{3,4},{4,3},{5,2},{6,7},{7,6},{8,9},{9,8},{10,13... | collective-permute-start | bytes 1572872 | tf_op jit(solution)/shard_map/ppermute | solution.py:344
  177.8 33.9 %collective-permute-start.38 = (bf16[2,128,1024]{2,1,0:T(8,128)(2,1)}, bf16[2,128,1024]{2,1,0:T(8,128)(2,1)S(1)}, u32[]{:S(2)}, u32[]{:S(2)}) collective-permute-start(bf16[2,128,1024]{2,1,0:T(8,128)(2,1)} %get-tuple-element.148.refs_1_), channel_id=1, source_target_pairs={{0,16},{1,17},{2,18},{3,19},{4,20},{5,21},{6,22},{7,23},{8,24},{9,... | collective-permute-start | bytes 1572872 | tf_op jit(solution)/shard_map/ppermute | solution.py:344
  188.7 23.8 %collective-permute-start.35 = (bf16[2,128,1024]{2,1,0:T(8,128)(2,1)}, bf16[2,128,1024]{2,1,0:T(8,128)(2,1)S(1)}, u32[]{:S(2)}, u32[]{:S(2)}) collective-permute-start(bf16[2,128,1024]{2,1,0:T(8,128)(2,1)} %get-tuple-element.140._.refs_0_), channel_id=1, source_target_pairs={{0,8},{1,9},{2,10},{3,11},{4,12},{5,13},{6,14},{7,15},{8,0},{9,1},... | collective-permute-start | bytes 1572872 | tf_op jit(solution)/shard_map/ppermute | solution.py:344
  211.7 14.0 %collective-permute-start.36 = (bf16[2,128,1024]{2,1,0:T(8,128)(2,1)}, bf16[2,128,1024]{2,1,0:T(8,128)(2,1)}, u32[]{:S(2)}, u32[]{:S(2)}) collective-permute-start(bf16[2,128,1024]{2,1,0:T(8,128)(2,1)} %get-tuple-element.148.refs_1_), channel_id=1, source_target_pairs={{0,8},{1,9},{2,10},{3,11},{4,12},{5,13},{6,14},{7,15},{8,0},{9,1},... | collective-permute-start | bytes 1572872 | tf_op jit(solution)/shard_map/ppermute | solution.py:344
  212.5 13.3 %collective-permute-start.37 = (bf16[2,128,1024]{2,1,0:T(8,128)(2,1)}, bf16[2,128,1024]{2,1,0:T(8,128)(2,1)}, u32[]{:S(2)}, u32[]{:S(2)}) collective-permute-start(bf16[2,128,1024]{2,1,0:T(8,128)(2,1)} %get-tuple-element.140._.refs_0_), channel_id=1, source_target_pairs={{0,16},{1,17},{2,18},{3,19},{4,20},{5,21},{6,22},{7,23},{8,24},{9,... | collective-permute-start | bytes 1572872 | tf_op jit(solution)/shard_map/ppermute | solution.py:344
  212.9 23.5 %collective-permute-start.40 = (bf16[2,128,1024]{2,1,0:T(8,128)(2,1)S(1)}, bf16[2,128,1024]{2,1,0:T(8,128)(2,1)}, u32[]{:S(2)}, u32[]{:S(2)}) collective-permute-start(bf16[2,128,1024]{2,1,0:T(8,128)(2,1)S(1)} %collective-permute-done.38.refs_5_), channel_id=1, source_target_pairs={{0,8},{1,9},{2,10},{3,11},{4,12},{5,13},{6,14},{7,15},{8,0},{9,1},... | collective-permute-start | bytes 1572872 | tf_op jit(solution)/shard_map/ppermute | solution.py:344
  215.1 21.8 %collective-permute-start.39 = (bf16[2,128,1024]{2,1,0:T(8,128)(2,1)S(1)}, bf16[2,128,1024]{2,1,0:T(8,128)(2,1)}, u32[]{:S(2)}, u32[]{:S(2)}) collective-permute-start(bf16[2,128,1024]{2,1,0:T(8,128)(2,1)S(1)} %collective-permute-done.35.refs_2_), channel_id=1, source_target_pairs={{0,16},{1,17},{2,18},{3,19},{4,20},{5,21},{6,22},{7,23},{8,24},{9,... | collective-permute-start | bytes 1572872 | tf_op jit(solution)/shard_map/ppermute | solution.py:344
  273.6 45.2 %collective-permute-start.44 = (bf16[1024,1024]{1,0:T(8,128)(2,1)}, bf16[1024,1024]{1,0:T(8,128)(2,1)S(1)}, u32[]{:S(2)}, u32[]{:S(2)}) collective-permute-start(bf16[1024,1024]{1,0:T(8,128)(2,1)} %second_grad.1.part), channel_id=1, source_target_pairs={{0,4},{1,5},{2,6},{3,7},{4,0},{5,1},{6,2},{7,3},{8,12},{9,13},{10,... | collective-permute-start | bytes 6291464 | tf_op jit(solution)/shard_map/ppermute | solution.py:344
  286.3 14.2 %collective-permute-start.47 = (bf16[2,64,2048]{2,1,0:T(8,128)(2,1)}, bf16[2,64,2048]{2,1,0:T(8,128)(2,1)S(1)}, u32[]{:S(2)}, u32[]{:S(2)}) collective-permute-start(bf16[2,64,2048]{2,1,0:T(8,128)(2,1)} %get-tuple-element.164), channel_id=1, source_target_pairs={{0,1},{1,2},{2,3},{3,0},{4,5},{5,6},{6,7},{7,4},{8,9},{9,10},{10,1... | collective-permute-start | bytes 1572872 | tf_op jit(solution)/shard_map/ppermute | solution.py:344
  287.3 21.5 %collective-permute-start.48 = (bf16[2,64,2048]{2,1,0:T(8,128)(2,1)}, bf16[2,64,2048]{2,1,0:T(8,128)(2,1)S(1)}, u32[]{:S(2)}, u32[]{:S(2)}) collective-permute-start(bf16[2,64,2048]{2,1,0:T(8,128)(2,1)} %get-tuple-element.165), channel_id=1, source_target_pairs={{0,3},{1,0},{2,1},{3,2},{4,7},{5,4},{6,5},{7,6},{8,11},{9,8},{10,9... | collective-permute-start | bytes 1572872 | tf_op jit(solution)/shard_map/ppermute | solution.py:344
  298.0 13.6 %collective-permute-start.45 = (bf16[2,128,1024]{2,1,0:T(8,128)(2,1)}, bf16[2,128,1024]{2,1,0:T(8,128)(2,1)}, u32[]{:S(2)}, u32[]{:S(2)}) collective-permute-start(bf16[2,128,1024]{2,1,0:T(8,128)(2,1)} %get-tuple-element.162), channel_id=1, source_target_pairs={{0,16},{1,17},{2,18},{3,19},{4,20},{5,21},{6,22},{7,23},{8,24},{9,... | collective-permute-start | bytes 1572872 | tf_op jit(solution)/shard_map/ppermute | solution.py:344
  298.8 13.6 %collective-permute-start.46 = (bf16[2,128,1024]{2,1,0:T(8,128)(2,1)}, bf16[2,128,1024]{2,1,0:T(8,128)(2,1)}, u32[]{:S(2)}, u32[]{:S(2)}) collective-permute-start(bf16[2,128,1024]{2,1,0:T(8,128)(2,1)} %get-tuple-element.163), channel_id=1, source_target_pairs={{0,8},{1,9},{2,10},{3,11},{4,12},{5,13},{6,14},{7,15},{8,0},{9,1},... | collective-permute-start | bytes 1572872 | tf_op jit(solution)/shard_map/ppermute | solution.py:344
  301.2 60.6 %collective-permute-start.81 = (bf16[2,64,2048]{2,1,0:T(8,128)(2,1)}, bf16[2,64,2048]{2,1,0:T(8,128)(2,1)S(1)}, u32[]{:S(2)}, u32[]{:S(2)}) collective-permute-start(bf16[2,64,2048]{2,1,0:T(8,128)(2,1)} %get-tuple-element.219), channel_id=1, source_target_pairs={{0,1},{1,2},{2,3},{3,0},{4,5},{5,6},{6,7},{7,4},{8,9},{9,10},{10,1... | collective-permute-start | bytes 1572872 | tf_op jit(solution)/shard_map/ppermute | solution.py:344
  309.5 64.4 %collective-permute-start.82 = (bf16[2,64,2048]{2,1,0:T(8,128)(2,1)}, bf16[2,64,2048]{2,1,0:T(8,128)(2,1)S(1)}, u32[]{:S(2)}, u32[]{:S(2)}) collective-permute-start(bf16[2,64,2048]{2,1,0:T(8,128)(2,1)} %get-tuple-element.220), channel_id=1, source_target_pairs={{0,3},{1,0},{2,1},{3,2},{4,7},{5,4},{6,5},{7,6},{8,11},{9,8},{10,9... | collective-permute-start | bytes 1572872 | tf_op jit(solution)/shard_map/ppermute | solution.py:344
  311.6 63.2 %collective-permute-start.76 = (bf16[2,128,1024]{2,1,0:T(8,128)(2,1)}, bf16[2,128,1024]{2,1,0:T(8,128)(2,1)}, u32[]{:S(2)}, u32[]{:S(2)}) collective-permute-start(bf16[2,128,1024]{2,1,0:T(8,128)(2,1)} %get-tuple-element.214), channel_id=1, source_target_pairs={{0,8},{1,9},{2,10},{3,11},{4,12},{5,13},{6,14},{7,15},{8,0},{9,1},... | collective-permute-start | bytes 1572872 | tf_op jit(solution)/shard_map/ppermute | solution.py:344
  312.3 64.1 %collective-permute-start.79 = (bf16[2,128,1024]{2,1,0:T(8,128)(2,1)}, bf16[2,128,1024]{2,1,0:T(8,128)(2,1)}, u32[]{:S(2)}, u32[]{:S(2)}) collective-permute-start(bf16[2,128,1024]{2,1,0:T(8,128)(2,1)} %get-tuple-element.216), channel_id=1, source_target_pairs={{0,16},{1,17},{2,18},{3,19},{4,20},{5,21},{6,22},{7,23},{8,24},{9,... | collective-permute-start | bytes 1572872 | tf_op jit(solution)/shard_map/ppermute | solution.py:344
  318.8 58.7 %collective-permute-start.78 = (bf16[2,128,1024]{2,1,0:T(8,128)(2,1)}, bf16[2,128,1024]{2,1,0:T(8,128)(2,1)}, u32[]{:S(2)}, u32[]{:S(2)}) collective-permute-start(bf16[2,128,1024]{2,1,0:T(8,128)(2,1)} %get-tuple-element.215), channel_id=1, source_target_pairs={{0,16},{1,17},{2,18},{3,19},{4,20},{5,21},{6,22},{7,23},{8,24},{9,... | collective-permute-start | bytes 1572872 | tf_op jit(solution)/shard_map/ppermute | solution.py:344
  361.8 78.3 %collective-permute-start.49 = (bf16[1024,1024]{1,0:T(8,128)(2,1)}, bf16[1024,1024]{1,0:T(8,128)(2,1)S(1)}, u32[]{:S(2)}, u32[]{:S(2)}) collective-permute-start(bf16[1024,1024]{1,0:T(8,128)(2,1)} %source_grad.1.part), channel_id=1, source_target_pairs={{0,4},{1,5},{2,6},{3,7},{4,0},{5,1},{6,2},{7,3},{8,12},{9,13},{10,... | collective-permute-start | bytes 6291464 | tf_op jit(solution)/shard_map/ppermute | solution.py:344
  374.8 35.6 %collective-permute-start.41 = (bf16[512,1024]{1,0:T(8,128)(2,1)}, bf16[512,1024]{1,0:T(8,128)(2,1)S(1)}, u32[]{:S(2)}, u32[]{:S(2)}) collective-permute-start(bf16[512,1024]{1,0:T(8,128)(2,1)} %get-tuple-element.152), channel_id=1, source_target_pairs={{0,4},{1,5},{2,6},{3,7},{4,0},{5,1},{6,2},{7,3},{8,12},{9,13},{10,... | collective-permute-start | bytes 3145736 | tf_op jit(solution)/shard_map/ppermute | solution.py:344
  374.8 14.7 %collective-permute-start.80 = (bf16[2,64,2048]{2,1,0:T(8,128)(2,1)}, bf16[2,64,2048]{2,1,0:T(8,128)(2,1)}, u32[]{:S(2)}, u32[]{:S(2)}) collective-permute-start(bf16[2,64,2048]{2,1,0:T(8,128)(2,1)} %get-tuple-element.218), channel_id=1, source_target_pairs={{0,1},{1,2},{2,3},{3,0},{4,5},{5,6},{6,7},{7,4},{8,9},{9,10},{10,1... | collective-permute-start | bytes 1572872 | tf_op jit(solution)/shard_map/ppermute | solution.py:344
  376.4 24.3 %collective-permute-start.83 = (bf16[2,64,2048]{2,1,0:T(8,128)(2,1)}, bf16[2,64,2048]{2,1,0:T(8,128)(2,1)}, u32[]{:S(2)}, u32[]{:S(2)}) collective-permute-start(bf16[2,64,2048]{2,1,0:T(8,128)(2,1)} %get-tuple-element.221), channel_id=1, source_target_pairs={{0,3},{1,0},{2,1},{3,2},{4,7},{5,4},{6,5},{7,6},{8,11},{9,8},{10,9... | collective-permute-start | bytes 1572872 | tf_op jit(solution)/shard_map/ppermute | solution.py:344
  377.5 23.2 %collective-permute-start.77 = (bf16[2,128,1024]{2,1,0:T(8,128)(2,1)}, bf16[2,128,1024]{2,1,0:T(8,128)(2,1)}, u32[]{:S(2)}, u32[]{:S(2)}) collective-permute-start(bf16[2,128,1024]{2,1,0:T(8,128)(2,1)} %get-tuple-element.166._), channel_id=1, source_target_pairs={{0,8},{1,9},{2,10},{3,11},{4,12},{5,13},{6,14},{7,15},{8,0},{9,1},... | collective-permute-start | bytes 1572872 | tf_op jit(solution)/shard_map/ppermute | solution.py:344
  406.0 15.9 %collective-permute-start.84 = (bf16[64,1024]{1,0:T(8,128)(2,1)}, bf16[64,1024]{1,0:T(8,128)(2,1)S(1)}, u32[]{:S(2)}, u32[]{:S(2)}) collective-permute-start(bf16[64,1024]{1,0:T(8,128)(2,1)} %get-tuple-element.227), channel_id=1, source_target_pairs={{0,1},{1,2},{2,3},{3,0},{4,5},{5,6},{6,7},{7,4},{8,9},{9,10},{10,1... | collective-permute-start | bytes 393224 | tf_op jit(solution)/shard_map/ppermute | solution.py:344
  408.2 15.3 %collective-permute-start.85 = (bf16[64,1024]{1,0:T(8,128)(2,1)}, bf16[64,1024]{1,0:T(8,128)(2,1)}, u32[]{:S(2)}, u32[]{:S(2)}) collective-permute-start(bf16[64,1024]{1,0:T(8,128)(2,1)} %get-tuple-element.228), channel_id=1, source_target_pairs={{0,3},{1,0},{2,1},{3,2},{4,7},{5,4},{6,5},{7,6},{8,11},{9,8},{10,9... | collective-permute-start | bytes 393224 | tf_op jit(solution)/shard_map/ppermute | solution.py:344
  408.4 15.1 %collective-permute-start.86 = (bf16[32,2048]{1,0:T(8,128)(2,1)}, bf16[32,2048]{1,0:T(8,128)(2,1)}, u32[]{:S(2)}, u32[]{:S(2)}) collective-permute-start(bf16[32,2048]{1,0:T(8,128)(2,1)} %get-tuple-element.229), channel_id=1, source_target_pairs={{0,8},{1,9},{2,10},{3,11},{4,12},{5,13},{6,14},{7,15},{8,0},{9,1},... | collective-permute-start | bytes 393224 | tf_op jit(solution)/shard_map/ppermute | solution.py:344
  410.4 13.9 %collective-permute-start.87 = (bf16[32,2048]{1,0:T(8,128)(2,1)}, bf16[32,2048]{1,0:T(8,128)(2,1)}, u32[]{:S(2)}, u32[]{:S(2)}) collective-permute-start(bf16[32,2048]{1,0:T(8,128)(2,1)} %get-tuple-element.230), channel_id=1, source_target_pairs={{0,16},{1,17},{2,18},{3,19},{4,20},{5,21},{6,22},{7,23},{8,24},{9,... | collective-permute-start | bytes 393224 | tf_op jit(solution)/shard_map/ppermute | solution.py:344
  430.9 19.6 %collective-permute-start.88 = (bf16[128,1024]{1,0:T(8,128)(2,1)}, bf16[128,1024]{1,0:T(8,128)(2,1)S(1)}, u32[]{:S(2)}, u32[]{:S(2)}) collective-permute-start(bf16[128,1024]{1,0:T(8,128)(2,1)} %get-tuple-element.231), channel_id=1, source_target_pairs={{0,1},{1,2},{2,3},{3,0},{4,5},{5,6},{6,7},{7,4},{8,9},{9,10},{10,1... | collective-permute-start | bytes 786440 | tf_op jit(solution)/shard_map/ppermute | solution.py:344
  432.2 19.4 %collective-permute-start.52 = (bf16[2,128,512]{2,1,0:T(8,128)(2,1)}, bf16[2,128,512]{2,1,0:T(8,128)(2,1)S(1)}, u32[]{:S(2)}, u32[]{:S(2)}) collective-permute-start(bf16[2,128,512]{2,1,0:T(8,128)(2,1)} %get-tuple-element.174), channel_id=1, source_target_pairs={{0,8},{1,9},{2,10},{3,11},{4,12},{5,13},{6,14},{7,15},{8,0},{9,1},... | collective-permute-start | bytes 786440 | tf_op jit(solution)/shard_map/ppermute | solution.py:344
  433.5 18.4 %collective-permute-start.59 = (bf16[2,128,512]{2,1,0:T(8,128)(2,1)}, bf16[2,128,512]{2,1,0:T(8,128)(2,1)S(1)}, u32[]{:S(2)}, u32[]{:S(2)}) collective-permute-start(bf16[2,128,512]{2,1,0:T(8,128)(2,1)} %get-tuple-element.185), channel_id=1, source_target_pairs={{0,16},{1,17},{2,18},{3,19},{4,20},{5,21},{6,22},{7,23},{8,24},{9,... | collective-permute-start | bytes 786440 | tf_op jit(solution)/shard_map/ppermute | solution.py:344
  436.5 18.3 %collective-permute-start.61 = (bf16[2,128,512]{2,1,0:T(8,128)(2,1)}, bf16[2,128,512]{2,1,0:T(8,128)(2,1)S(1)}, u32[]{:S(2)}, u32[]{:S(2)}) collective-permute-start(bf16[2,128,512]{2,1,0:T(8,128)(2,1)} %get-tuple-element.188), channel_id=1, source_target_pairs={{0,1},{1,2},{2,3},{3,0},{4,5},{5,6},{6,7},{7,4},{8,9},{9,10},{10,1... | collective-permute-start | bytes 786440 | tf_op jit(solution)/shard_map/ppermute | solution.py:344
  440.1 16.2 %collective-permute-start.62 = (bf16[2,128,512]{2,1,0:T(8,128)(2,1)}, bf16[2,128,512]{2,1,0:T(8,128)(2,1)S(1)}, u32[]{:S(2)}, u32[]{:S(2)}) collective-permute-start(bf16[2,128,512]{2,1,0:T(8,128)(2,1)} %get-tuple-element.189), channel_id=1, source_target_pairs={{0,3},{1,0},{2,1},{3,2},{4,7},{5,4},{6,5},{7,6},{8,11},{9,8},{10,9... | collective-permute-start | bytes 786440 | tf_op jit(solution)/shard_map/ppermute | solution.py:344
  450.6 13.7 %collective-permute-start.57 = (bf16[2,128,512]{2,1,0:T(8,128)(2,1)}, bf16[2,128,512]{2,1,0:T(8,128)(2,1)S(1)}, u32[]{:S(2)}, u32[]{:S(2)}) collective-permute-start(bf16[2,128,512]{2,1,0:T(8,128)(2,1)} %get-tuple-element.183), channel_id=1, source_target_pairs={{0,8},{1,9},{2,10},{3,11},{4,12},{5,13},{6,14},{7,15},{8,0},{9,1},... | collective-permute-start | bytes 786440 | tf_op jit(solution)/shard_map/ppermute | solution.py:344
  451.6 12.9 %collective-permute-start.58 = (bf16[2,128,512]{2,1,0:T(8,128)(2,1)}, bf16[2,128,512]{2,1,0:T(8,128)(2,1)S(1)}, u32[]{:S(2)}, u32[]{:S(2)}) collective-permute-start(bf16[2,128,512]{2,1,0:T(8,128)(2,1)} %get-tuple-element.184), channel_id=1, source_target_pairs={{0,16},{1,17},{2,18},{3,19},{4,20},{5,21},{6,22},{7,23},{8,24},{9,... | collective-permute-start | bytes 786440 | tf_op jit(solution)/shard_map/ppermute | solution.py:344
  451.9 12.7 %collective-permute-start.60 = (bf16[2,128,512]{2,1,0:T(8,128)(2,1)}, bf16[2,128,512]{2,1,0:T(8,128)(2,1)S(1)}, u32[]{:S(2)}, u32[]{:S(2)}) collective-permute-start(bf16[2,128,512]{2,1,0:T(8,128)(2,1)} %get-tuple-element.187), channel_id=1, source_target_pairs={{0,1},{1,2},{2,3},{3,0},{4,5},{5,6},{6,7},{7,4},{8,9},{9,10},{10,1... | collective-permute-start | bytes 786440 | tf_op jit(solution)/shard_map/ppermute | solution.py:344
  456.4 64.4 %collective-permute-start.42 = (bf16[256,1024]{1,0:T(8,128)(2,1)}, bf16[256,1024]{1,0:T(8,128)(2,1)S(1)}, u32[]{:S(2)}, u32[]{:S(2)}) collective-permute-start(bf16[256,1024]{1,0:T(8,128)(2,1)} %get-tuple-element.153), channel_id=1, source_target_pairs={{0,0},{1,1},{2,4},{3,5},{4,2},{5,3},{6,6},{7,7},{8,8},{9,9},{10,12... | collective-permute-start | bytes 1572872 | tf_op jit(solution)/shard_map/ppermute | solution.py:344
  464.3 57.0 %collective-permute-start.43 = (bf16[256,1024]{1,0:T(8,128)(2,1)}, bf16[256,1024]{1,0:T(8,128)(2,1)S(1)}, u32[]{:S(2)}, u32[]{:S(2)}) collective-permute-start(bf16[256,1024]{1,0:T(8,128)(2,1)} %get-tuple-element.154), channel_id=1, source_target_pairs={{0,1},{1,0},{2,5},{3,4},{4,3},{5,2},{6,7},{7,6},{8,9},{9,8},{10,13... | collective-permute-start | bytes 1572872 | tf_op jit(solution)/shard_map/ppermute | solution.py:344
  464.6 35.9 %collective-permute-start.64 = (bf16[4,16,512]{2,1,0:T(8,128)(2,1)S(1)}, bf16[4,16,512]{2,1,0:T(8,128)(2,1)S(1)}, u32[]{:S(2)}, u32[]{:S(2)}) collective-permute-start(bf16[4,16,512]{2,1,0:T(8,128)(2,1)S(1)} %bitcast.89), channel_id=1, source_target_pairs={{0,1},{1,2},{2,3},{3,0},{4,5},{5,6},{6,7},{7,4},{8,9},{9,10},{10,1... | collective-permute-start | bytes 196616 | tf_op jit(solution)/shard_map/ppermute | solution.py:344
  464.7 35.8 %collective-permute-start.65 = (bf16[4,16,512]{2,1,0:T(8,128)(2,1)S(1)}, bf16[4,16,512]{2,1,0:T(8,128)(2,1)S(1)}, u32[]{:S(2)}, u32[]{:S(2)}) collective-permute-start(bf16[4,16,512]{2,1,0:T(8,128)(2,1)S(1)} %bitcast.90), channel_id=1, source_target_pairs={{0,3},{1,0},{2,1},{3,2},{4,7},{5,4},{6,5},{7,6},{8,11},{9,8},{10,9... | collective-permute-start | bytes 196616 | tf_op jit(solution)/shard_map/ppermute | solution.py:344
  466.2 34.9 %collective-permute-start.66 = (bf16[4,16,512]{2,1,0:T(8,128)(2,1)S(1)}, bf16[4,16,512]{2,1,0:T(8,128)(2,1)S(1)}, u32[]{:S(2)}, u32[]{:S(2)}) collective-permute-start(bf16[4,16,512]{2,1,0:T(8,128)(2,1)S(1)} %bitcast.91), channel_id=1, source_target_pairs={{0,2},{1,3},{2,0},{3,1},{4,6},{5,7},{6,4},{7,5},{8,10},{9,11},{10,... | collective-permute-start | bytes 196616 | tf_op jit(solution)/shard_map/ppermute | solution.py:344
  518.8 13.2 %collective-permute-start.71 = (bf16[128,512]{1,0:T(8,128)(2,1)}, bf16[128,512]{1,0:T(8,128)(2,1)S(1)}, u32[]{:S(2)}, u32[]{:S(2)}) collective-permute-start(bf16[128,512]{1,0:T(8,128)(2,1)} %get-tuple-element.204), channel_id=1, source_target_pairs={{0,1},{1,2},{2,3},{3,0},{4,5},{5,6},{6,7},{7,4},{8,9},{9,10},{10,1... | collective-permute-start | bytes 393224 | tf_op jit(solution)/shard_map/ppermute | solution.py:344
  525.4 18.6 %collective-permute-start.50 = (bf16[256,1024]{1,0:T(8,128)(2,1)S(1)}, bf16[256,1024]{1,0:T(8,128)(2,1)S(1)}, u32[]{:S(2)}, u32[]{:S(2)}) collective-permute-start(bf16[256,1024]{1,0:T(8,128)(2,1)S(1)} %copy-done.67), channel_id=1, source_target_pairs={{0,0},{1,1},{2,4},{3,5},{4,2},{5,3},{6,6},{7,7},{8,8},{9,9},{10,12... | collective-permute-start | bytes 1572872 | tf_op jit(solution)/shard_map/ppermute | solution.py:344
  532.0 23.7 %collective-permute-start.51 = (bf16[256,1024]{1,0:T(8,128)(2,1)S(1)}, bf16[256,1024]{1,0:T(8,128)(2,1)S(1)}, u32[]{:S(2)}, u32[]{:S(2)}) collective-permute-start(bf16[256,1024]{1,0:T(8,128)(2,1)S(1)} %copy-done.66), channel_id=1, source_target_pairs={{0,1},{1,0},{2,5},{3,4},{4,3},{5,2},{6,7},{7,6},{8,9},{9,8},{10,13... | collective-permute-start | bytes 1572872 | tf_op jit(solution)/shard_map/ppermute | solution.py:344
  (99 other events, 1006.2 us)

commit v3 on v2

--- a/solution.py
+++ b/solution.py
@@ -361,40 +361,59 @@
     return pl.CostEstimate(flops=int(flops), bytes_accessed=int(nbytes), transcendentals=special)
 
 
-def call(body, ins, outs, name, in_specs=None, out_specs=None, scratch=(), flops=0, grid=()):
-    moved = sum(a.size * a.dtype.itemsize for a in ins)
-    moved += sum(math.prod(a.shape) * jnp.dtype(a.dtype).itemsize for a in outs)
+def moved_bytes(arrays):
+    return sum(math.prod(a.shape) * jnp.dtype(a.dtype).itemsize for a in arrays)
+
+
+def without(body, lead, count):
+    return (lambda *refs: body(*refs[:lead], *refs[lead + count :])) if count else body
+
+
+def call(
+    body,
+    ins,
+    outs,
+    name,
+    in_specs=None,
+    out_specs=None,
+    scratch=(),
+    flops=0,
+    grid=(),
+    after=(),
+    aliases={},
+):
     return pl.pallas_call(
-        body,
+        without(body, len(ins), len(after)),
         grid=grid,
-        in_specs=in_specs or [VMEM] * len(ins),
+        in_specs=list(in_specs or [VMEM] * len(ins)) + [ANY] * len(after),
         out_specs=out_specs or [VMEM] * len(outs),
         out_shape=outs,
         scratch_shapes=list(scratch),
-        cost_estimate=cost(flops, moved),
+        cost_estimate=cost(flops, moved_bytes(ins) + moved_bytes(outs)),
+        input_output_aliases=aliases,
         name=name,
-    )(*ins)
-
-
-def placed_call(body, pos, ins, outs, name, grid, in_specs, out_specs, scratch=(), flops=0):
-    moved = sum(a.size * a.dtype.itemsize for a in ins)
-    moved += sum(math.prod(a.shape) * jnp.dtype(a.dtype).itemsize for a in outs)
+    )(*ins, *after)
+
+
+def placed_call(
+    body, pos, ins, outs, name, grid, in_specs, out_specs, scratch=(), flops=0, after=()
+):
     return pl.pallas_call(
-        body,
+        without(body, len(ins) + 1, len(after)),
         grid_spec=pltpu.PrefetchScalarGridSpec(
             num_scalar_prefetch=1,
             grid=grid,
-            in_specs=in_specs,
+            in_specs=list(in_specs) + [ANY] * len(after),
             out_specs=out_specs,
             scratch_shapes=list(scratch),
         ),
         out_shape=outs,
-        cost_estimate=cost(flops, moved),
+        cost_estimate=cost(flops, moved_bytes(ins) + moved_bytes(outs)),
         name=name,
-    )(pos, *ins)
-
-
-def copies(ins, outs, moves, count, name):
+    )(pos, *ins, *after)
+
+
+def copies(ins, outs, moves, count, name, after=()):
     def body(*refs):
         sems = refs[-1]
         todo = moves(refs[: len(ins)], refs[len(ins) : -1])
@@ -411,6 +430,7 @@
         name,
         in_specs=[ANY] * len(ins),
         scratch=[pltpu.SemaphoreType.DMA((count,))],
+        after=after,
     )
 
 
@@ -423,10 +443,18 @@
     return jnp.concatenate(parts, axis=1)
 
 
-def first_kernel(qw, kw, vw, uw, small, inputs, segs, far, up_far, in0, in1, sems):
-    _, c, z = place()
+def first_kernel(qw, kw, vw, uw, small, far, up_far):
+    _, c, _ = place()
+    lead = qw.shape[0]
+    for j, ref in enumerate((qw, kw, vw)):
+        far[j * lead : (j + 1) * lead, :] = own_columns(ref[...], 1 - c)
+    far[3 * lead :, :] = small[...]
+    up_far[...] = own_columns(uw[...], 1 - c)
+
+
+def inputs_kernel(inputs, segs, in0, in1, sems):
     rows = inputs.shape[1]
-    parity = lax.rem(z, 2)
+    parity = lax.rem(place()[2], 2)
     todo = []
     for k, out in enumerate((in0, in1)):
         pick = parity if k == 0 else 1 - parity
@@ -435,21 +463,13 @@
         line = segs[pl.ds(pick, 1), :].astype(F32)
         out[rows:, :] = jnp.zeros((out.shape[0] - rows, out.shape[1]), BF)
         out[rows:, :rows] = jnp.broadcast_to(line, (out.shape[0] - rows, rows)).astype(BF)
-    lead = qw.shape[0]
-    for j, ref in enumerate((qw, kw, vw)):
-        far[j * lead : (j + 1) * lead, :] = own_columns(ref[...], 1 - c)
-    far[3 * lead :, :] = small[...]
-    up_far[...] = own_columns(uw[...], 1 - c)
     for copy in todo:
         copy.wait()
 
 
-def second_kernel(qw, kw, vw, ow, uw, small, far, up_far, attn, up):
+def second_kernel(qw, kw, vw, uw, small, far, up_far, attn, up):
     _, c, _ = place()
-    lead, width = ow.shape
-    half = width // 2
-    attn[0:lead, :] = ow[:, :half]
-    attn[lead : 2 * lead, :] = ow[:, half:]
+    lead = qw.shape[0]
 
     def both(out, at, own, got):
         n = own.shape[0]
@@ -457,28 +477,21 @@
         out[at + n : at + 2 * n, :] = jnp.where(c == 0, got, own)
 
     for j, ref in enumerate((qw, kw, vw)):
-        both(attn, (2 + 2 * j) * lead, own_columns(ref[...], c), far[j * lead : (j + 1) * lead, :])
-    both(attn, 8 * lead, small[...], far[3 * lead :, :])
+        both(attn, 2 * j * lead, own_columns(ref[...], c), far[j * lead : (j + 1) * lead, :])
+    both(attn, 6 * lead, small[...], far[3 * lead :, :])
     both(up, 0, own_columns(uw[...], c), up_far[...])
 
 
-def inner_kernel_moves(n):
-    def moves(ins, outs):
-        todo = []
-        for g in range(n):
-            own, first, second, far1, far2 = ins[5 * g : 5 * g + 5]
-            low, high = outs[2 * g : 2 * g + 2]
-            cut = far1.shape[0]
-            todo += [
-                (own, low.at[0]),
-                (first, low.at[1]),
-                (second, high.at[0]),
-                (far1, high.at[1, pl.ds(0, cut)]),
-                (far2, high.at[1, pl.ds(cut, far2.shape[0])]),
-            ]
-        return todo
-
-    return moves
+def inner_moves(ins, outs):
+    own, first, second, far1, far2 = ins[:5]
+    cut = far1.shape[0]
+    return [
+        (own, outs[0].at[0]),
+        (first, outs[0].at[1]),
+        (second, outs[0].at[2]),
+        (far1, outs[0].at[3, pl.ds(0, cut)]),
+        (far2, outs[0].at[3, pl.ds(cut, far2.shape[0])]),
+    ]
 
 
 def ring_first(value, n1, n2):
@@ -490,25 +503,19 @@
     return send(a[:cut], f1), send(b[cut:], f2)
 
 
-def ring_outer(low, high, n1, n2, f1, f2):
-    b_high = send(high, n2)
-    a_low = send(low, n1)
-    b_low = send(low, n2)
-    a_high = send(high, n1)
-    return [low, high, a_low, a_high, b_low, b_high, send(a_low, f1), send(b_high, f2)]
-
-
-def final_moves(ins, outs, inner, blocks):
-    o, c, z = place()
+def ring_outer_second(a, b, f1, f2):
+    return send(a[:2], f1), send(b[2:], f2)
+
+
+def final_moves(ins, outs, blocks):
+    o, _, z = place()
     z_ring = (z, lax.rem(z + 3, 4), lax.rem(z + 1, 4), lax.rem(z + 2, 4))
     yx_ring = (o, o ^ 1, o ^ 2, o ^ 3)
-    near, far = (z_ring, yx_ring) if inner == "z" else (yx_ring, z_ring)
     todo = []
-    for i, (k, part) in enumerate(((0, 0), (0, 1), (1, 0), (1, 1), (2, 0), (2, 1), (3, 0), (3, 1))):
-        for j in range(2):
-            a, b = near[2 * part + j], far[k]
-            yx, zz = (b, a) if inner == "z" else (a, b)
-            todo += blocks(ins[i].at[j], outs, yx, zz)
+    for k in range(4):
+        for j in range(4):
+            source = ins[k].at[j] if k < 3 else ins[3 + j // 2].at[j % 2]
+            todo += blocks(source, outs, yx_ring[k], z_ring[j])
     return todo
 
 
@@ -527,7 +534,7 @@
         qkv[j] = (dot32(value, weight[j], NN) + bias[j : j + 1, :]).astype(BF)
 
 
-def project(x, gain, shift, weight, bias):
+def project(x, gain, shift, weight, bias, after):
     total, width = x.shape
     half = weight.shape[2]
     rows = pl.BlockSpec((BLOCK, width), lambda i: (i, 0))
@@ -547,6 +554,7 @@
         out_specs=[rows, pl.BlockSpec((3, BLOCK, half), lambda i: (0, i, 0))],
         flops=6 * total * width * half,
         grid=(total // BLOCK,),
+        after=after,
     )
 
 
@@ -561,7 +569,8 @@
     return max(0, (i * BLOCK - total // 2 + 1) // BLOCK * BLOCK), (i + 1) * BLOCK
 
 
-def attend_kernel(scale, column, row, q_ref, k_ref, v_ref, _, mixed_ref, log_ref):
+def attend_kernel(scale, column, row, q_ref, k_ref, v_ref, *refs):
+    mixed_ref, log_ref = refs[-2:]
     total = q_ref.shape[0]
     size = q_ref.shape[1] // 2
     lane = lax.broadcasted_iota(jnp.int32, (BLOCK, 2 * size), 1) < size
@@ -586,8 +595,9 @@
 
 
 def attend_back_kernel(
-    scale, column, row, q_ref, k_ref, v_ref, log_ref, grad_ref, _, out_ref, bias_ref, dk, dv
+    scale, column, row, q_ref, k_ref, v_ref, log_ref, grad_ref, *refs
 ):
+    out_ref, bias_ref, dk, dv = refs[-4:]
     total = q_ref.shape[0]
     size = q_ref.shape[1] // 2
     lane = lax.broadcasted_iota(jnp.int32, (BLOCK, 2 * size), 1) < size
@@ -624,8 +634,8 @@
     bias_ref[1:2, :] = jnp.sum(dvb.astype(F32), axis=0, keepdims=True)
 
 
-def attend_specs(total, width):
-    pick = lambda j: pl.BlockSpec((None, total, width), lambda h: (j, 0, h))
+def attend_specs(total, width, first):
+    pick = lambda j: pl.BlockSpec((None, total, width), lambda h: (j, 0, h + first))
     return [
         pl.BlockSpec((total, 1), lambda h: (0, 0)),
         pl.BlockSpec((1, total), lambda h: (0, 0)),
@@ -635,39 +645,45 @@
     ]
 
 
-def attend(qkv, column, row, size, after):
+def attend(qkv, column, row, size, part, before, after):
     _, total, width = qkv.shape
     pair = 2 * size
-    flat = pl.BlockSpec((total, pair), lambda h: (0, h))
+    count = width // pair // 2
+    flat = pl.BlockSpec((total, pair), lambda h: (0, h + part * count))
     return call(
         partial(attend_kernel, 1.0 / math.sqrt(size)),
-        [column, row, qkv, qkv, qkv, after],
+        [column, row, qkv, qkv, qkv, *before],
         [shape((total, width)), shape((total, width), F32)],
         "attend",
-        in_specs=attend_specs(total, pair) + [ANY],
+        in_specs=attend_specs(total, pair, part * count) + [ANY] * len(before),
         out_specs=[flat, flat],
-        flops=total * total * width * 16,
-        grid=(width // pair,),
-    )
-
-
-def attend_back(qkv, log, grad, column, row, size, after):
+        flops=total * total * width * 8,
+        grid=(count,),
+        after=after,
+        aliases={5 + i: i for i in range(len(before))},
+    )
+
+
+def attend_back(qkv, log, grad, column, row, size, part, before, after):
     _, total, width = qkv.shape
     pair = 2 * size
-    flat = pl.BlockSpec((total, pair), lambda h: (0, h))
+    count = width // pair // 2
+    flat = pl.BlockSpec((total, pair), lambda h: (0, h + part * count))
     return call(
         partial(attend_back_kernel, 1.0 / math.sqrt(size)),
-        [column, row, qkv, qkv, qkv, log, grad, after],
+        [column, row, qkv, qkv, qkv, log, grad, *before],
         [shape((3, total, width)), shape((2, width), F32)],
         "attend_back",
-        in_specs=attend_specs(total, pair) + [flat, flat, ANY],
+        in_specs=attend_specs(total, pair, part * count) + [flat, flat] + [ANY] * len(before),
         out_specs=[
-            pl.BlockSpec((3, total, pair), lambda h: (0, 0, h)),
-            pl.BlockSpec((2, pair), lambda h: (0, h)),
+            pl.BlockSpec((3, total, pair), lambda h: (0, 0, h + part * count)),
+            pl.BlockSpec((2, pair), lambda h: (0, h + part * count)),
         ],
         scratch=[pltpu.VMEM((total, pair), F32)] * 2,
-        flops=total * total * width * 24,
-        grid=(width // pair,),
+        flops=total * total * width * 12,
+        grid=(count,),
+        after=after,
+        aliases={7 + i: i for i in range(len(before))},
     )
 
 
@@ -675,7 +691,7 @@
     out[...] = dot32(left[...], right[...], dims).astype(out.dtype)
 
 
-def rows_matmul(left, right, dims, name, kind=BF):
+def rows_matmul(left, right, dims, name, kind=BF, after=()):
     total, depth = left.shape
     cols = right.shape[0] if dims is NT else right.shape[1]
     return call(
@@ -690,6 +706,7 @@
         out_specs=[pl.BlockSpec((BLOCK, cols), lambda i: (i, 0))],
         flops=2 * total * depth * cols,
         grid=(total // BLOCK,),
+        after=after,
     )[0]
 
 
@@ -756,30 +773,32 @@
     )
 
 
-def down_grads_kernel(pos, hidden, cot, far1, far2, n1a, n1b, n2a, n2b, own):
+def down_grads_kernel(pos, hidden, cot, far1, far2, n1, n2, own):
     g = pl.program_id(0)
     rows = own.shape[1]
     acc = dot32(hidden[...], cot[...], TN).astype(BF)
-    for k, outs in enumerate(((far1, far2), (n2a, n2b), (n1a, n1b), (own, own))):
+    for k, out in enumerate((None, n2, n1, own)):
 
         @pl.when(g == k)
         def _():
             for j in range(4):
-                at = j if k == 3 else j % 2
-                outs[j // 2][at] = acc[j * rows : (j + 1) * rows, :]
+                value = acc[j * rows : (j + 1) * rows, :]
+                if k == 0:
+                    (far1, far2)[j // 2][j % 2] = value
+                else:
+                    out[j] = value
 
 
 def ring_shapes(rows, cols):
-    return [shape((2, rows, cols))] * 6 + [shape((4, rows, cols))]
+    return [shape((2, rows, cols))] * 2 + [shape((4, rows, cols))] * 3
 
 
 def ring_specs(rows, cols):
-    return [pl.BlockSpec((2, rows, cols), lambda g, pos: (0, 0, 0))] * 6 + [
-        pl.BlockSpec((4, rows, cols), lambda g, pos: (0, 0, 0))
-    ]
-
-
-def down_grads(pos, hidden, cot, rows):
+    whole = lambda n: pl.BlockSpec((n, rows, cols), lambda g, pos: (0, 0, 0))
+    return [whole(2)] * 2 + [whole(4)] * 3
+
+
+def down_grads(pos, hidden, cot, rows, after):
     total, units = hidden.shape
     width = cot.shape[1]
     return placed_call(
@@ -795,6 +814,7 @@
         ],
         ring_specs(rows, width),
         flops=2 * total * units * width,
+        after=after,
     )
 
 
@@ -802,24 +822,32 @@
     return lax.rem(z + 2, 4), lax.rem(z + 1, 4), lax.rem(z + 3, 4), z
 
 
-def up_grads_kernel(pos, second, pre, far1, far2, n1a, n1b, n2a, n2b, own, acc):
-    g = pl.program_id(0)
-    lead = own.shape[1] // 2
-    acc[...] = dot32(second[...], pre[...], TN).astype(BF)
-    spots = z_places(pos[2])
-    for half in range(2):
-
-        @pl.when(g // 2 == half)
+def split_ring(g, refs, store):
+    far1, far2, n1, n2, own = refs
+    for k, out in enumerate((None, n2, n1, own)):
+
+        @pl.when(g == k)
         def _():
-            outs = ((far1, far2), (n1a, n1b), (n2a, n2b), (own, own))
-            for k in range(4):
-                at = g if k == 3 else lax.rem(g, 2)
-                for cc in range(2):
-                    start = pl.multiple_of(cc * 4 * lead + spots[k] * lead, lead)
-                    outs[k][half][at, cc * lead : (cc + 1) * lead, :] = acc[pl.ds(start, lead), :]
-
-
-def up_grads(pos, second, pre, lead):
+            for zz in range(4):
+                if k:
+                    store(out, zz, zz)
+                else:
+                    store((far1, far2)[zz // 2], zz % 2, zz)
+
+
+def up_grads_kernel(pos, second, pre, *refs):
+    lead = refs[-1].shape[1] // 2
+    acc = dot32(second[...], pre[...], TN).astype(BF)
+
+    def store(out, at, zz):
+        for cc in range(2):
+            start = (cc * 4 + zz) * lead
+            out[at, cc * lead : (cc + 1) * lead, :] = acc[start : start + lead, :]
+
+    split_ring(pl.program_id(0), refs, store)
+
+
+def up_grads(pos, second, pre, lead, after):
     total, width = second.shape
     units = pre.shape[1]
     return placed_call(
@@ -830,64 +858,42 @@
         "up_grads",
         (4,),
         [
-            pl.BlockSpec((total, width // 4), lambda g, pos: (0, g)),
+            pl.BlockSpec((total, width // 4), lambda g, pos: (0, pos[0] ^ (3 - g))),
             pl.BlockSpec((total, units), lambda g, pos: (0, 0)),
         ],
         ring_specs(2 * lead, units),
-        scratch=[pltpu.VMEM((width // 4, units), BF)],
         flops=2 * total * units * width,
+        after=after,
     )
 
 
 def attn_grads_kernel(pos, normed, grads, mixed, branch, *refs):
-    p, q, (accv, acco) = refs[0:7], refs[7:14], refs[14:16]
-    g = pl.program_id(0)
-    yx = pos[0] ^ (3 - g)
-    lead = accv.shape[0] // 8
-    half = accv.shape[1]
-    accq = dot32(normed[...], grads[0], TN).astype(BF)
-    acck = dot32(normed[...], grads[1], TN).astype(BF)
-    accv[...] = dot32(normed[...], grads[2], TN).astype(BF)
-    acco[...] = dot32(mixed[...], branch[...], TN).astype(BF)
-    far1, far2, n1a, n1b, n2a, n2b, own = p
-    for k, outs in enumerate(((far1, far2), (n2a, n2b), (n1a, n1b), (own, own))):
-
-        @pl.when(g == k)
-        def _():
-            for zz in range(4):
-                at = zz if k == 3 else zz % 2
-                for j, acc in enumerate((accq, acck)):
-                    for cc in range(2):
-                        row = (2 * j + cc) * lead
-                        start = (cc * 4 + zz) * lead
-                        outs[zz // 2][at, row : row + lead, :] = acc[start : start + lead, :]
-
-    far1, far2, n1a, n1b, n2a, n2b, own = q
-    spots = z_places(pos[2])
-    for part in range(2):
-
-        @pl.when(yx // 2 == part)
-        def _():
-            for k, outs in enumerate(((far1, far2), (n1a, n1b), (n2a, n2b), (own, own))):
-                at = yx if k == 3 else lax.rem(yx, 2)
-                out = outs[part]
-                for cc in range(2):
-                    start = pl.multiple_of(cc * 4 * lead + spots[k] * lead, lead)
-                    out[at, cc * lead : (cc + 1) * lead, :] = accv[pl.ds(start, lead), :]
-                    start = pl.multiple_of(spots[k] * lead, lead)
-                    out[at, (2 + cc) * lead : (3 + cc) * lead, :] = acco[
-                        pl.ds(start, lead), cc * half : (cc + 1) * half
-                    ]
-
-
-def attn_grads(pos, normed, grads, mixed, branch, lead):
+    lead = refs[-1].shape[1] // 8
+    half = refs[-1].shape[2]
+    accs = [dot32(normed[...], grads[j], TN).astype(BF) for j in range(3)]
+    acco = dot32(mixed[...], branch[...], TN).astype(BF)
+
+    def store(out, at, zz):
+        for cc in range(2):
+            for j, acc in enumerate(accs):
+                row, start = (2 * j + cc) * lead, (cc * 4 + zz) * lead
+                out[at, row : row + lead, :] = acc[start : start + lead, :]
+            row = (6 + cc) * lead
+            out[at, row : row + lead, :] = acco[
+                zz * lead : (zz + 1) * lead, cc * half : (cc + 1) * half
+            ]
+
+    split_ring(pl.program_id(0), refs, store)
+
+
+def attn_grads(pos, normed, grads, mixed, branch, lead, after):
     total, width = normed.shape
     half = width // 2
     return placed_call(
         attn_grads_kernel,
         pos,
         [normed, grads, mixed, branch],
-        ring_shapes(4 * lead, half) * 2,
+        ring_shapes(8 * lead, half),
         "attn_grads",
         (4,),
         [
@@ -896,116 +902,97 @@
             pl.BlockSpec((total, half // 4), lambda g, pos: (0, pos[0] ^ (3 - g))),
             pl.BlockSpec((total, width), lambda g, pos: (0, 0)),
         ],
-        ring_specs(4 * lead, half) * 2,
-        scratch=[pltpu.VMEM((width // 4, half), BF), pltpu.VMEM((half // 4, width), BF)],
+        ring_specs(8 * lead, half),
         flops=8 * total * width * half,
-    )
-
-
-def add_kernel(n):
-    def body(*refs):
-        for a, b, out in zip(refs[:n], refs[n : 2 * n], refs[2 * n :]):
-            out[...] = (a[...].astype(F32) + b[...].astype(F32)).astype(BF)
+        after=after,
+    )
+
+
+def pass_kernel(n1, n2, t1, t2, s1, s2):
+    for s, n, t, part in ((s1, n1, t2, 1), (s2, n2, t1, 0)):
+        for j in range(4):
+            if j // 2 == part:
+                s[j] = (n[j].astype(F32) + t[j % 2].astype(F32)).astype(BF)
+            else:
+                s[j] = n[j]
+
+
+def far_round(ring):
+    return send(ring[0], X_SWAP), send(ring[1], Y_SWAP)
+
+
+def near_round(ring, got, name, after=()):
+    s1, s2 = call(
+        pass_kernel,
+        [ring[2], ring[3], *got],
+        [shape(ring[2].shape)] * 2,
+        name + "_pass",
+        after=after,
+    )
+    return s1, [send(s1, X_SWAP), send(s2, Y_SWAP)]
+
+
+def joined_kernel(extra):
+    def body(own, r1, r2, *refs):
+        far1, far2, first, second, mine, acc = refs[extra:]
+        rows = own.shape[1]
+        for j in range(4):
+            acc[j, :rows, :] = own[j].astype(F32) + r1[j].astype(F32) + r2[j].astype(F32)
+            if extra:
+                acc[j, rows:, :] = sum(ref[j].astype(F32) for ref in refs[:extra])
+        far, one, two, me = z_places(place()[2])
+        cut = far1.shape[0]
+        far1[...] = acc[far, :cut, :].astype(BF)
+        far2[...] = acc[far, cut:, :].astype(BF)
+        first[...] = acc[one].astype(BF)
+        second[...] = acc[two].astype(BF)
+        mine[...] = acc[me]
 
     return body
 
 
-def outer_scatter(p, q, name):
-    far1, far2, n1a, n1b, n2a, n2b, _ = p
-    qfar1, qfar2, qn1a, qn1b, qn2a, qn2b, _ = q
-    t1, t2 = send(far1, X_SWAP), send(far2, Y_SWAP)
-    v1, v2 = send(qfar1, Z_UP), send(qfar2, Z_DOWN)
-    p1a, p2b = send(n1a, X_SWAP), send(n2b, Y_SWAP)
-    q1b, q2a = send(qn1b, Z_UP), send(qn2a, Z_DOWN)
-    mine = [n1b, n2a, qn1a, qn2b]
-    came = [t2, t1, v1, v2]
-    m1, m2, w1, w2 = call(
-        add_kernel(4), mine + came, [shape(a.shape) for a in mine], name + "_pass"
-    )
-    p1b, p2a = send(m1, X_SWAP), send(m2, Y_SWAP)
-    q1a, q2b = send(w1, Z_UP), send(w2, Z_DOWN)
-    return [p1a, p1b, p2a, p2b], [q1a, q1b, q2a, q2b], m1
-
-
-def joined_kernel(extra):
-    def body(*refs):
-        o, c, z = place()
-        ins = refs[: 10 + extra]
-        outs, (ps, qs) = refs[10 + extra : 20 + extra], refs[20 + extra :]
-        spots = {
-            "z": z_places(z),
-            "xy": (o ^ 3, o ^ 1, o ^ 2, o),
-        }
-        for n, (kind, acc) in enumerate((("z", ps), ("xy", qs))):
-            own, r1a, r1b, r2a, r2b = ins[5 * n : 5 * n + 5]
-            rows = own.shape[1]
-            for j in range(4):
-                r1, r2 = (r1a, r2a) if j < 2 else (r1b, r2b)
-                acc[j, :rows, :] = (
-                    own[j].astype(F32) + r1[j % 2].astype(F32) + r2[j % 2].astype(F32)
-                )
-                if n == 1 and extra:
-                    acc[j, rows:, :] = sum(ref[j].astype(F32) for ref in ins[10:])
-            far1, far2, first, second, mine = outs[5 * n : 5 * n + 5]
-            far, one, two, me = spots[kind]
-            cut = far1.shape[0]
-            far1[...] = acc[far, :cut, :].astype(BF)
-            far2[...] = acc[far, cut:, :].astype(BF)
-            first[...] = acc[one].astype(BF)
-            second[...] = acc[two].astype(BF)
-            mine[...] = acc[me]
-
-    return body
-
-
-def inner_pass_kernel(p1, p2, q1, q2, t1, t2, v1, v2, p1o, p2o, q1o, q2o):
-    def half(out, base, got, first):
-        cut = base.shape[0] // 2 // 16 * 16
-        low, high = base[:cut, :], base[cut:, :]
-        plus = lambda a: (a.astype(F32) + got[...].astype(F32)).astype(BF)
-        out[:cut, :] = plus(low) if first else low
-        out[cut:, :] = high if first else plus(high)
-
-    half(p1o, p1, t1, True)
-    half(p2o, p2, t2, False)
-    half(q1o, q1, v2, False)
-    half(q2o, q2, v1, True)
-
-
-def inner_scatter(p, q, p_got, q_got, extra, name):
-    _, prows, pcols = p[6].shape
-    _, qrows, qcols = q[6].shape
-    qall = qrows + (extra[0].shape[1] if extra else 0)
-
-    def outs(rows, cols):
-        cut = rows // 2 // 16 * 16
-        return [
+def join(ring, got, name, extra=(), after=()):
+    _, rows, cols = ring[4].shape
+    rows += extra[0].shape[1] if extra else 0
+    cut = rows // 2 // 16 * 16
+    return call(
+        joined_kernel(len(extra)),
+        [ring[4], *got, *extra],
+        [
             shape((cut, cols)),
             shape((rows - cut, cols)),
             shape((rows, cols)),
             shape((rows, cols)),
             shape((rows, cols), F32),
-        ]
-
-    pf1, pf2, p1, p2, pme, qf1, qf2, q1, q2, qme = call(
-        joined_kernel(len(extra)),
-        [p[6]] + p_got + [q[6]] + q_got + extra,
-        outs(prows, pcols) + outs(qall, qcols),
+        ],
         name + "_join",
-        scratch=[pltpu.VMEM((4, prows, pcols), F32), pltpu.VMEM((4, qall, qcols), F32)],
-    )
-    t1, t2 = send(pf1, Z_UP), send(pf2, Z_DOWN)
-    v1, v2 = send(qf1, X_SWAP), send(qf2, Y_SWAP)
-    p1, p2, q1, q2 = call(
+        scratch=[pltpu.VMEM((4, rows, cols), F32)],
+        after=after,
+    )
+
+
+def inner_pass_kernel(p1, p2, t1, t2, p1o, p2o):
+    cut = p1.shape[0] // 2 // 16 * 16
+    plus = lambda a, got: (a.astype(F32) + got[...].astype(F32)).astype(BF)
+    p1o[:cut, :] = plus(p1[:cut, :], t1)
+    p1o[cut:, :] = p1[cut:, :]
+    p2o[:cut, :] = p2[:cut, :]
+    p2o[cut:, :] = plus(p2[cut:, :], t2)
+
+
+def inner_far(joined):
+    return send(joined[0], Z_UP), send(joined[1], Z_DOWN)
+
+
+def inner_near(joined, came, name, after=()):
+    p1, p2 = call(
         inner_pass_kernel,
-        [p1, p2, q1, q2, t1, t2, v1, v2],
-        [shape(a.shape) for a in (p1, p2, q1, q2)],
+        [joined[2], joined[3], *came],
+        [shape(joined[2].shape)] * 2,
         name + "_inner",
-    )
-    return (
-        [pme, send(p1, Z_UP), send(p2, Z_DOWN)],
-        [qme, send(q1, X_SWAP), send(q2, Y_SWAP)],
-    )
+        after=after,
+    )
+    return p1, [joined[4], send(p1, Z_UP), send(p2, Z_DOWN)]
 
 
 def total_of(refs):
@@ -1021,18 +1008,18 @@
     given[...] = acc[pl.ds(pl.multiple_of((1 - c) * lead, lead), lead), :]
 
 
-def attn_last_kernel(p0, p1, p2, q0, q1, q2, kept, given, out, small, accp, accq):
+def attn_last_kernel(p0, p1, p2, kept, given, out, small, acc):
     _, c, _ = place()
-    accp[...] = total_of((p0, p1, p2))
-    accq[...] = total_of((q0, q1, q2))
+    acc[...] = total_of((p0, p1, p2))
     lead = kept.shape[1]
     half = kept.shape[2]
-    for j, (acc, at) in enumerate(((accp, 0), (accp, 2 * lead), (accq, 0))):
+    for j in range(3):
+        at = 2 * j * lead
         kept[j] = acc[pl.ds(pl.multiple_of(at + c * lead, lead), lead), :]
         given[j] = acc[pl.ds(pl.multiple_of(at + (1 - c) * lead, lead), lead), :]
-    out[:, :half] = accq[2 * lead : 3 * lead, :]
-    out[:, half:] = accq[3 * lead : 4 * lead, :]
-    small[...] = accq[4 * lead :, :]
+    out[:, :half] = acc[6 * lead : 7 * lead, :]
+    out[:, half:] = acc[7 * lead : 8 * lead, :]
+    small[...] = acc[8 * lead :, :]
 
 
 def norm_back(n, spread, gain, grad):
@@ -1064,7 +1051,7 @@
         sums[j : j + 1, :] += column(v)
 
 
-def middle_back(part, got, middle, cot, gain, wout):
+def middle_back(part, got, middle, cot, gain, wout, after):
     total, width = middle.shape
     half = wout.shape[0]
     rows = pl.BlockSpec((BLOCK, width), lambda i: (i, 0))
@@ -1088,6 +1075,7 @@
         ],
         flops=2 * total * width * half,
         grid=(total // BLOCK,),
+        after=after,
     )
 
 
@@ -1095,7 +1083,7 @@
     out[...] = sum(dot32(grads[j], weight[j], NT) for j in range(3)).astype(BF)
 
 
-def source_grad(grads, weight):
+def source_grad(grads, weight, after):
     _, total, half = grads.shape
     width = weight.shape[1]
     return call(
@@ -1110,6 +1098,7 @@
         out_specs=[pl.BlockSpec((BLOCK, width), lambda i: (i, 0))],
         flops=6 * total * width * half,
         grid=(total // BLOCK,),
+        after=after,
     )[0]
 
 
@@ -1138,7 +1127,7 @@
         sums[j : j + 1, :] += column(v)
 
 
-def input_back(pos, part, got, x, mgrad, gain):
+def input_back(pos, part, got, x, mgrad, gain, after):
     total, width = x.shape
     rows = pl.BlockSpec((BLOCK, width), lambda g, pos: (own_block(g, pos), 0))
     fixed = lambda n: pl.BlockSpec((n, width), lambda g, pos: (0, 0))
@@ -1151,6 +1140,7 @@
         (total // BLOCK,),
         [rows] * 4 + [fixed(1)],
         [fixed(BLOCK), fixed(BLOCK), fixed(2)],
+        after=after,
     )
 
 
@@ -1171,7 +1161,7 @@
         mine[...] = value + middle[...] + bias[...]
 
 
-def output_rows(pos, hidden, down, middle, bias):
+def output_rows(pos, hidden, down, middle, bias, after):
     total, units = hidden.shape
     width = down.shape[1]
     return placed_call(
@@ -1192,6 +1182,7 @@
             pl.BlockSpec((BLOCK, width), lambda g, pos: (jnp.maximum(g - 2, 0), 0)),
         ],
         flops=2 * total * units * width,
+        after=after,
     )
 
 
@@ -1202,8 +1193,7 @@
         at = pl.multiple_of((parity ^ k) * BLOCK, BLOCK)
         out[...] = (mine[pl.ds(at, BLOCK), :] + got[pl.ds(at, BLOCK), :].astype(F32)).astype(BF)
 
-
-Z_FAR = links(lambda o, c, z: (o, c, (z + 2) % 4))
+XY_FAR = links(lambda o, c, z: (o ^ 3, c, z))
 
 
 def fast_local(
@@ -1254,131 +1244,98 @@
         at += vector.shape[0]
     small = jnp.pad(small.reshape(1, half), ((0, 7), (0, 0)))
     weights = [query_weight, key_weight, value_weight]
-    far, up_far, in0, in1 = call(
+    far, up_far = call(
         first_kernel,
-        weights + [up_weight, small, inputs, segment_ids],
-        [
-            shape((3 * lead + 8, half)),
-            shape((lead, units)),
-            shape((rows + 16, width)),
-            shape((rows + 16, width)),
-        ],
+        weights + [up_weight, small],
+        [shape((3 * lead + 8, half)), shape((lead, units))],
         "first",
-        in_specs=[VMEM] * 5 + [ANY, VMEM],
-        scratch=[pltpu.SemaphoreType.DMA((2,))],
-    )
-    far_got, up_got = send(far, CORE_SWAP), send(up_far, CORE_SWAP)
-    got = [send(in0, SEQUENCE[0]), send(in1, SEQUENCE[1])]
+    )
     attn_pay, up_pay = call(
         second_kernel,
-        weights + [out_weight, up_weight, small, far_got, up_got],
-        [shape((8 * lead + 16, half)), shape((2 * lead, units))],
+        weights + [up_weight, small, send(far, CORE_SWAP), send(up_far, CORE_SWAP)],
+        [shape((6 * lead + 16, half)), shape((2 * lead, units))],
         "second",
     )
 
     pa, pb = ring_first(attn_pay, Z_UP, Z_DOWN)
-    qa, qb = ring_first(up_pay, X_SWAP, Y_SWAP)
     pc = ring_second(pa, pb, Z_UP, Z_DOWN)
-    qc = ring_second(qa, qb, Y_SWAP, X_SWAP)
-    attn_rows = 8 * lead + 16
-    pl_low, pl_high, q_low, q_high = copies(
-        [attn_pay, pa, pb, *pc, up_pay, qa, qb, *qc],
-        [shape((2, attn_rows, half))] * 2 + [shape((2, 2 * lead, units))] * 2,
-        inner_kernel_moves(2),
-        10,
-        "inner",
-    )
-    p_pieces = ring_outer(pl_low, pl_high, X_SWAP, Y_SWAP, Y_SWAP, X_SWAP)
-    q_pieces = ring_outer(q_low, q_high, Z_UP, Z_DOWN, Z_UP, Z_DOWN)
-    mate = [send(g, CORE_SWAP) for g in got]
-
-    def attn_blocks(src, outs, yx, zz):
-        todo = [
-            (src.at[pl.ds(h * lead, lead)], outs[1].at[yx, zz, :, pl.ds(h * half, half)])
-            for h in range(2)
-        ]
-        for j in range(3):
-            for cc in range(2):
-                first = (2 + 2 * j + cc) * lead
-                todo.append((src.at[pl.ds(first, lead)], outs[0].at[j, yx, cc, zz]))
-        todo.append((src.at[pl.ds(8 * lead, 16)], outs[2].at[yx, zz]))
-        return todo
-
-    def attn_moves(ins, outs):
-        _, _, zz = place()
-        parity = lax.rem(zz, 2)
-        todo = final_moves(ins[:8], outs, "z", attn_blocks)
-        todo += [(ins[8], outs[3])]
-        todo += [(ins[9].at[parity], outs[4]), (ins[9].at[1 - parity], outs[5])]
-        return todo
-
-    wqkv, wout, small_all, down_own, cot0, cot1 = copies(
-        p_pieces + [down_weight, cotangent],
-        [
-            shape((3, 4, 2, 4, lead, half)),
-            shape((4, 4, lead, width)),
-            shape((4, 4, 16, half)),
-            shape(down_weight.shape),
-            shape((rows, width)),
-            shape((rows, width)),
+    attn_all, down_own = copies(
+        [attn_pay, pa, pb, *pc, down_weight, out_weight],
+        [shape((4,) + attn_pay.shape), shape((down_rows + lead, width))],
+        lambda ins, outs: inner_moves(ins, outs)
+        + [
+            (ins[5], outs[1].at[pl.ds(0, down_rows)]),
+            (ins[6], outs[1].at[pl.ds(down_rows, lead)]),
         ],
-        attn_moves,
-        16 * 9 + 3,
-        "attn_whole",
-    )
-    wqkv = wqkv.reshape(3, width, half)
-    wout = wout.reshape(half, width)
-
-    def up_blocks(src, outs, yx, zz):
-        return [(src.at[pl.ds(cc * lead, lead)], outs[0].at[yx, cc, zz]) for cc in range(2)]
-
-    wup = copies(
-        q_pieces,
-        [shape((4, 2, 4, lead, units))],
-        lambda ins, outs: final_moves(ins, outs, "xy", up_blocks),
-        32,
-        "up_whole",
-    )[0].reshape(width, units)
+        7,
+        "attn_inner",
+    )
+    aa, ab = ring_first(attn_all, X_SWAP, Y_SWAP)
+    da, db = ring_first(down_own, Z_UP, Z_DOWN)
+    dc = ring_second(da, db, Z_UP, Z_DOWN)
+    in0, in1 = call(
+        inputs_kernel,
+        [inputs, segment_ids],
+        [shape((rows + 16, width))] * 2,
+        "inputs_own",
+        in_specs=[ANY, VMEM],
+        scratch=[pltpu.SemaphoreType.DMA((2,))],
+        after=[attn_all],
+    )
+    got = [send(in0, SEQUENCE[0]), send(in1, SEQUENCE[1])]
+    ac = ring_outer_second(aa, ab, Y_SWAP, X_SWAP)
 
     def sequence_moves(ins, outs):
         _, cc, zz = place()
         parity = lax.rem(zz, 2)
-        return [
-            (ins[2 * m + k], outs[0].at[(1 - cc if m else cc), parity ^ k])
-            for m in range(2)
-            for k in range(2)
+        todo = []
+        for m in range(2):
+            for k in range(2):
+                piece = ins[2 * m + k]
+                at = (1 - cc if m else cc, parity ^ k)
+                todo.append((piece.at[pl.ds(0, rows)], outs[0].at[at]))
+                if len(outs) > 1:
+                    todo.append((piece.at[pl.ds(rows, 16)], outs[1].at[at]))
+        return todo
+
+    def whole_sequence(pieces, name, after=()):
+        more = pieces[0].shape[0] > rows
+        outs = [shape((2, 2, rows, width))] + [shape((2, 2, 16, width))] * more
+        return copies(pieces, outs, sequence_moves, 8 if more else 4, name, after=after)
+
+    x, segments = whole_sequence(got + [send(g, CORE_SWAP) for g in got], "inputs_whole")
+    x = x.reshape(total, width)
+    segments = segments[:, :, 0, :rows].reshape(total).astype(F32)
+    seg_col, seg_row = segments.reshape(total, 1), segments.reshape(1, total)
+
+    down_all, up_own = copies(
+        [down_own, da, db, *dc, up_pay],
+        [shape((4,) + down_own.shape), shape(up_pay.shape)],
+        lambda ins, outs: inner_moves(ins, outs) + [(ins[5], outs[1])],
+        6,
+        "down_inner",
+        after=ac,
+    )
+    ea, eb = ring_first(down_all, X_SWAP, Y_SWAP)
+    ua, ub = ring_first(up_own, Z_UP, Z_DOWN)
+
+    def attn_blocks(src, outs, yx, zz):
+        todo = [
+            (src.at[pl.ds((2 * j + cc) * lead, lead)], outs[0].at[j, yx, cc, zz])
+            for j in range(3)
+            for cc in range(2)
         ]
-
-    def whole_sequence(pieces, name):
-        return copies(pieces, [shape((2, 2) + pieces[0].shape)], sequence_moves, 4, name)[0]
-
-    x_blocks = whole_sequence(got + mate, "inputs_whole")
-    x = x_blocks[:, :, :rows].reshape(total, width)
-    segments = x_blocks[:, :, rows, :rows].reshape(total).astype(F32)
-    seg_col, seg_row = segments.reshape(total, 1), segments.reshape(1, total)
-
-    da, db = ring_first(down_own, Z_UP, Z_DOWN)
-    dc = ring_second(da, db, Z_UP, Z_DOWN)
-    d_low, d_high = copies(
-        [down_own, da, db, *dc],
-        [shape((2, down_rows, width))] * 2,
-        inner_kernel_moves(1),
-        5,
-        "down_inner",
-    )
-    d_pieces = ring_outer(d_low, d_high, X_SWAP, Y_SWAP, Y_SWAP, X_SWAP)
-    cot_got = [send(cot0, SEQUENCE[0]), send(cot1, SEQUENCE[1])]
-    cot_mate = [send(g, CORE_SWAP) for g in cot_got]
-    wdown = copies(
-        d_pieces,
-        [shape((4, 4, down_rows, width))],
-        lambda ins, outs: final_moves(
-            ins, outs, "z", lambda src, outs, yx, zz: [(src, outs[0].at[yx, zz])]
-        ),
-        16,
-        "down_whole",
-    )[0].reshape(units, width)
-    cot = whole_sequence(cot_got + cot_mate, "cotangent_whole").reshape(total, width)
+        return todo + [(src.at[pl.ds(6 * lead, 16)], outs[1].at[yx, zz])]
+
+    wqkv, small_all = copies(
+        [attn_all, aa, ab, *ac],
+        [shape((3, 4, 2, 4, lead, half)), shape((4, 4, 16, half))],
+        lambda ins, outs: final_moves(ins, outs, attn_blocks),
+        16 * 7,
+        "attn_whole",
+        after=[down_all],
+    )
+    wqkv = wqkv.reshape(3, width, half)
 
     small_all = small_all.reshape(4, 4, 2, 8, half)[:, :, :, 0, :count]
     vectors = small_all[..., : 8 * lead].reshape(4, 4, 2, 8, lead).transpose(3, 0, 2, 1, 4)
@@ -1390,48 +1347,119 @@
     bias_u = lax.dynamic_index_in_dim(small_all[..., 8 * lead :], c, 2, keepdims=False)
     bias_u = bias_u.reshape(1, units).astype(F32)
 
-    normed, qkv = project(x, gain1, shift1, wqkv, qkv_bias)
-    mixed, log = attend(qkv, seg_col, seg_row, size, d_low)
+    normed, qkv = project(x, gain1, shift1, wqkv, qkv_bias, [])
+    uc = ring_second(ua, ub, Z_UP, Z_DOWN)
+
+    def cotangent_moves(ins, outs):
+        parity = lax.rem(place()[2], 2)
+        return [(ins[0].at[parity], outs[0]), (ins[0].at[1 - parity], outs[1])]
+
+    cots = copies(
+        [cotangent],
+        [shape((rows, width))] * 2,
+        cotangent_moves,
+        2,
+        "cotangent_own",
+        after=[ua, ub, normed],
+    )
+    cot_got = [send(block, pairs) for block, pairs in zip(cots, SEQUENCE)]
+    heads = attend(qkv, seg_col, seg_row, size, 0, [], cots)
+    ec = ring_outer_second(ea, eb, Y_SWAP, X_SWAP)
+    mixed, log = attend(qkv, seg_col, seg_row, size, 1, heads, [ea, eb])
+    up_all = copies(
+        [up_own, ua, ub, *uc],
+        [shape((4,) + up_pay.shape)],
+        inner_moves,
+        5,
+        "up_inner",
+        after=[*ec, mixed],
+    )[0]
+    fa, fb = ring_first(up_all, X_SWAP, Y_SWAP)
+
+    def down_blocks(src, outs, yx, zz):
+        return [
+            (src.at[pl.ds(0, down_rows)], outs[0].at[yx, zz]),
+            (src.at[pl.ds(down_rows, lead)], outs[1].at[yx, zz]),
+        ]
+
+    wdown, wout = copies(
+        [down_all, ea, eb, *ec],
+        [shape((4, 4, down_rows, width)), shape((4, 4, lead, width))],
+        lambda ins, outs: final_moves(ins, outs, down_blocks),
+        32,
+        "down_whole",
+        after=[up_all],
+    )
+    wdown, wout = wdown.reshape(units, width), wout.reshape(half, width)
     part = rows_matmul(mixed, wout, NN, "attend_out")
     middle, second = middle_norm(x, part, send(part, CORE_SWAP), bias_o, gain2, shift2)
+    cot = whole_sequence(
+        cot_got + [send(g, CORE_SWAP) for g in cot_got], "cotangent_whole", [part]
+    )[0].reshape(total, width)
+
+    def up_blocks(src, outs, yx, zz):
+        return [(src.at[pl.ds(cc * lead, lead)], outs[0].at[yx, cc, zz]) for cc in range(2)]
+
+    wup = copies(
+        [up_all, fa, fb, *ring_outer_second(fa, fb, Y_SWAP, X_SWAP)],
+        [shape((4, 2, 4, lead, units))],
+        lambda ins, outs: final_moves(ins, outs, up_blocks),
+        32,
+        "up_whole",
+        after=[second],
+    )[0].reshape(width, units)
     hidden, pre_grad, up_bias_grad = feed_forward(second, cot, wup, bias_u, wdown)
 
-    part = rows_matmul(pre_grad, wup, NT, "second_grad")
+    def to_tokens(got):
+        return jnp.where((z & 1) == 0, jnp.stack(got), jnp.stack(got[::-1]))
+
+    theirs, mine = output_rows(pos, hidden, wdown, middle, bias_d, [])
+    d = down_grads(pos, hidden, cot, down_rows, [mine])
+    d_far = far_round(d)
+    blocks = call(
+        result_kernel,
+        [mine, send(theirs, CORE_SWAP)],
+        [shape((rows, width))] * 2,
+        "result",
+        after=[d[4]],
+    )
+    out_got = [send(block, pairs) for block, pairs in zip(blocks, SEQUENCE)]
+    u = up_grads(pos, second, pre_grad, lead, [blocks[0]])
+    u_far = far_round(u)
+    passed, d_got = near_round(d, d_far, "down", [u[4]])
+    part = rows_matmul(pre_grad, wup, NT, "second_grad", after=[passed])
+    passed, u_got = near_round(u, u_far, "up", [part])
+    branch, middle_grad, mixed_grad, sums2 = middle_back(
+        part, send(part, CORE_SWAP), middle, cot, gain2, wout, [passed]
+    )
+
+    back = attend_back(qkv, log, mixed_grad, seg_col, seg_row, size, 0, [], out_got)
+    output = to_tokens(out_got)
+    d_joined = join(d, d_got, "down", after=[back[1]])
+    d_came = inner_far(d_joined)
+    grads, qv_bias_grad = attend_back(
+        qkv, log, mixed_grad, seg_col, seg_row, size, 1, back, [d_joined[4]]
+    )
+    passed, d_last = inner_near(d_joined, d_came, "down", [qv_bias_grad])
+    a = attn_grads(pos, normed, grads, mixed, branch, lead, [passed])
+    a_far = far_round(a)
+    u_joined = join(u, u_got, "up", after=[a[4], *d_last[1:]])
+    u_came = inner_far(u_joined)
+    part = source_grad(grads, wqkv, [u_joined[4]])
     got = send(part, CORE_SWAP)
-    p = down_grads(pos, hidden, cot, down_rows)
-    q = up_grads(pos, second, pre_grad, lead)
-    p_got, q_got, passed = outer_scatter(p, q, "feed")
-    branch, middle_grad, mixed_grad, sums2 = middle_back(part, got, middle, cot, gain2, wout)
-
-    grads, qv_bias_grad = attend_back(qkv, log, mixed_grad, seg_col, seg_row, size, passed)
-    p_last, q_last = inner_scatter(p, q, p_got, q_got, [], "feed")
+    passed, u_last = inner_near(u_joined, u_came, "up", [part])
+    passed, a_got = near_round(a, a_far, "attn", [passed])
+    in0, in1, sums1 = input_back(pos, part, got, x, middle_grad, gain1, [passed])
+    in_got = [send(block, pairs) for block, pairs in zip((in0, in1), SEQUENCE)]
+    input_grad = to_tokens(in_got).astype(F32)
     down_out, up_kept, up_given = call(
         feed_last_kernel,
-        p_last + q_last,
-        [shape(p_last[0].shape, F32)] + [shape((lead, units), F32)] * 2,
+        d_last + u_last,
+        [shape(down_weight.shape, F32)] + [shape((lead, units), F32)] * 2,
         "feed_last",
         scratch=[pltpu.VMEM((2 * lead, units), F32)],
-    )
-    up_got = send(up_given, CORE_SWAP)
-
-    part = source_grad(grads, wqkv)
-    got = send(part, CORE_SWAP)
-    pq = attn_grads(pos, normed, grads, mixed, branch, lead)
-    p, q = pq[:7], pq[7:]
-    p_got, q_got, _ = outer_scatter(p, q, "attn")
-
-    theirs, mine = output_rows(pos, hidden, wdown, middle, bias_d)
-    blocks = call(
-        result_kernel, [mine, send(theirs, CORE_SWAP)], [shape((rows, width))] * 2, "result"
-    )
-
-    def to_tokens(blocks):
-        got = [send(block, pairs) for block, pairs in zip(blocks, SEQUENCE)]
-        return jnp.where((z & 1) == 0, jnp.stack(got), jnp.stack(got[::-1]))
-
-    output = to_tokens(blocks)
-    in0, in1, sums1 = input_back(pos, part, got, x, middle_grad, gain1)
-    input_grad = to_tokens([in0, in1]).astype(F32)
+        after=[in0],
+    )
 
     wide = jnp.stack([sums1[0], sums1[1], sums2[2], sums2[0], sums2[1], sums2[3]])
     wide = lax.dynamic_index_in_dim(wide.reshape(6, 4, 2, 4, lead), c, 2, keepdims=False)
@@ -1446,19 +1474,17 @@
         axis=-1,
     ).astype(BF)
     tiny = jnp.pad(tiny[:, :, None], ((0, 0), (0, 0), (0, 15), (0, half - count)))
-    pick = lambda k: lax.dynamic_index_in_dim(tiny, (z + k) % 4, 0, keepdims=False)
-    extra = [pick(0), send(pick(1), Z_UP), send(pick(3), Z_DOWN), send(pick(2), Z_FAR)]
-
-    p_last, q_last = inner_scatter(p, q, p_got, q_got, extra, "attn")
+    pick = lambda k: lax.dynamic_index_in_dim(tiny, o ^ k, 1, keepdims=False)
+    extra = [pick(0), send(pick(1), X_SWAP), send(pick(2), Y_SWAP), send(pick(3), XY_FAR)]
+
+    joined = join(a, a_got, "attn", extra, [down_out])
+    _, attn_last = inner_near(joined, inner_far(joined), "attn")
     qkv_kept, qkv_given, out_out, small_sum = call(
         attn_last_kernel,
-        p_last + q_last,
+        attn_last,
         [shape((3, lead, half), F32)] * 2 + [shape((lead, width), F32), shape((16, half), F32)],
         "attn_last",
-        scratch=[
-            pltpu.VMEM((4 * lead, half), F32),
-            pltpu.VMEM((4 * lead + 16, half), F32),
-        ],
+        scratch=[pltpu.VMEM((8 * lead + 16, half), F32)],
     )
 
     def whole_columns(kept, got):
@@ -1469,7 +1495,7 @@
         )
         return both.reshape(both.shape[:-3] + (8 * cols,))
 
-    up_out = whole_columns(up_kept, up_got)
+    up_out = whole_columns(up_kept, send(up_given, CORE_SWAP))
     qkv_out = whole_columns(qkv_kept, send(qkv_given, CORE_SWAP))
     small_sum = small_sum[0]
     vec = lambda j: small_sum[j * lead : (j + 1) * lead]

time: 566 us -> 488 us (0.86)
  waiting for transfers between devices: 177 us -> 115 us
  starting transfers between devices: 121 us -> 81.9 us
  Pallas kernels: 214 us -> 230 us
  local copies, waits for them, and re-layouts: 36.3 us -> 42.8 us
    ppermute x93 -> x71, waiting for transfers between devices: 177 us -> 115 us  [send(): return lax.ppermute(value, AXES, pairs)]
    ppermute x93 -> x71, starting transfers between devices: 121 us -> 81.9 us  [send(): return lax.ppermute(value, AXES, pairs)]
    pallas_call x32 -> x40, Pallas kernels: 214 us -> 230 us  [the longest x35 179 us: call(): pl.pallas_call(without(body, len(ins), len(after)), grid=grid, in_specs=l...]
    unnamed x142 -> x124, local copies, waits for them, and re-layouts: 15.4 us -> 16.5 us
  transfers between devices with their start and end apart: 93 -> 71, of which waited for: 28 -> 23; matrix products, arithmetic and copies ran while one was open for 5% -> 6% of each run, Pallas kernels for 32% -> 31%
where the time goes in v3:
time: 488 us; the launch traced here: 480 us
  Pallas kernels  230 us (47%)
  waiting for transfers between devices  115 us (24%)
  starting transfers between devices  81.9 us (17%)
  local copies, waits for them, and re-layouts  42.8 us (9%)
  other arithmetic  8.8 us (2%)
    pallas_call x35, Pallas kernels, call(): pl.pallas_call(without(body, len(ins), len(after)), grid=grid, in_specs=l...  179 us
    ppermute x71, waiting for transfers between devices, send(): return lax.ppermute(value, AXES, pairs)  115 us
    ppermute x71, starting transfers between devices, send(): return lax.ppermute(value, AXES, pairs)  81.9 us
    pallas_call x5, Pallas kernels, placed_call(): pl.pallas_call(without(body, len(ins) + 1, len(after)), grid_spec=pltpu.P...  50.8 us
    unnamed x124, local copies, waits for them, and re-layouts  16.5 us
  transfers between devices with their start and end apart: 71, of which 23 were waited for; matrix products, arithmetic and copies ran while one was open for 6% of the time, Pallas kernels for 31%

profile of v3, /device:TPU:13, one launch (start us, length us, event | category | flops | bytes accessed | tf_op | source)
XLA Modules:
  0.0 480.3 jit_solution(7556946871430656866)
XLA Ops:
  7.3 2.0 second.1
  10.8 5.4 %collective-permute-done.3.refs_2_ = bf16[208,512]{1,0:T(8,128)(2,1)S(1)} collective-permute-done((bf16[208,512]{1,0:T(8,128)(2,1)}, bf16[208,512]{1,0:T(8,128)(2,1)S(1)}, u32[]{:S(2)}, u32[]{:S(2)}) %collective-permute-start.3) | collective-permute-done | bytes 213024 | tf_op jit(solution)/shard_map/ppermute | solution.py:344
  17.7 5.1 %collective-permute-done.2.refs_1_ = bf16[208,512]{1,0:T(8,128)(2,1)S(1)} collective-permute-done((bf16[208,512]{1,0:T(8,128)(2,1)}, bf16[208,512]{1,0:T(8,128)(2,1)S(1)}, u32[]{:S(2)}, u32[]{:S(2)}) %collective-permute-start.2) | collective-permute-done | bytes 213024 | tf_op jit(solution)/shard_map/ppermute | solution.py:344
  22.9 4.1 collective-permute-done.4.refs_3_
  28.3 2.4 attn_inner.2
  32.2 2.9 inputs_own.1
  35.1 5.7 %collective-permute-start.6 = (bf16[272,1024]{1,0:T(8,128)(2,1)}, bf16[272,1024]{1,0:T(8,128)(2,1)S(1)}, u32[]{:S(2)}, u32[]{:S(2)}) collective-permute-start(bf16[272,1024]{1,0:T(8,128)(2,1)} %get-tuple-element.114), channel_id=1, source_target_pairs={{0,0},{1,1},{2,4},{3,5},{4,2},{5,3},{6,6},{7,7},{8,8},{9,9},{10,12... | collective-permute-start | bytes 1671176 | tf_op jit(solution)/shard_map/ppermute | solution.py:344
  40.9 19.7 %collective-permute-done.6.refs_0_ = bf16[272,1024]{1,0:T(8,128)(2,1)S(1)} collective-permute-done((bf16[272,1024]{1,0:T(8,128)(2,1)}, bf16[272,1024]{1,0:T(8,128)(2,1)S(1)}, u32[]{:S(2)}, u32[]{:S(2)}) %collective-permute-start.6) | collective-permute-done | bytes 557088 | tf_op jit(solution)/shard_map/ppermute | solution.py:344
  60.6 11.9 %collective-permute-done.7.refs_1_ = bf16[272,1024]{1,0:T(8,128)(2,1)} collective-permute-done((bf16[272,1024]{1,0:T(8,128)(2,1)}, bf16[272,1024]{1,0:T(8,128)(2,1)}, u32[]{:S(2)}, u32[]{:S(2)}) %collective-permute-start.7) | collective-permute-done | bytes 557088 | tf_op jit(solution)/shard_map/ppermute | solution.py:344
  75.5 3.9 collective-permute-done.14.refs_1_
  85.2 3.0 inputs_whole.1
  88.2 4.1 collective-permute-done.17.refs_4_
  93.2 2.6 down_inner.2
  100.9 4.7 attn_whole.1
  110.4 8.2 %project.1 = (bf16[1024,1024]{1,0:T(8,128)(2,1)}, bf16[3,1024,512]{2,1,0:T(8,128)(2,1)}) custom-call(bf16[1024,1024]{1,0:T(8,128)(2,1)} %bitcast.73, f32[1,1024]{1,0:T(1,128)} %slice.210.gain.refs_5_, f32[1,1024]{1,0:T(1,128)} %slice.212.shift, bf16[3,1024,512]{2,1,0:T(8,128)(2,1)} %bitcast.99, f32[3,512]{1,0:T(4,128)} %maximum_convert_fusion.bias), custom_call_target="tpu_custom_call" | custom-call | flops 3221225472 | bytes 10500096 | tf_op jit(solution)/shard_map/project/pallas_call | solution.py:385
  120.3 2.3 collective-permute-start.25
  122.7 2.2 cotangent_own.1
  129.8 10.1 %attend.2 = (bf16[1024,512]{1,0:T(8,128)(2,1)}, f32[1024,512]{1,0:T(8,128)}) custom-call(f32[1024,1]{1,0:T(8,128)} %copy.72.refs_0_, f32[1,1024]{1,0:T(1,128)} %bitcast.90, bf16[3,1024,512]{2,1,0:T(8,128)(2,1)} %get-tuple-element.123.refs_2_.refs_3_.refs_4_, bf16[3,1024,512]{2,1,0:T(8,128)(2,1)} %get-tuple-element.123.refs_2_.refs_3_.refs_4_, ...), custom_call_target="tpu_custom_call" | custom-call | flops 4294967296 | bytes 12591104 | tf_op jit(solution)/shard_map/attend/pallas_call | solution.py:385
  140.0 10.2 %attend.3 = (bf16[1024,512]{1,0:T(8,128)(2,1)}, f32[1024,512]{1,0:T(8,128)}) custom-call(f32[1024,1]{1,0:T(8,128)} %copy.72.refs_0_, f32[1,1024]{1,0:T(1,128)} %bitcast.91, bf16[3,1024,512]{2,1,0:T(8,128)(2,1)} %get-tuple-element.123.refs_2_.refs_3_.refs_4_, ...), custom_call_target="tpu_custom_call", output_to_operand_aliasing={{0}: (5, {}), {1}: (6, {})} | custom-call | flops 4294967296 | bytes 15736832 | tf_op jit(solution)/shard_map/attend/pallas_call | solution.py:385
  151.0 2.2 up_inner.2.refs_5_.refs_0_
  153.2 5.1 %down_whole.1 = (bf16[4,4,128,1024]{3,2,1,0:T(8,128)(2,1)}, bf16[4,4,32,1024]{3,2,1,0:T(8,128)(2,1)}) custom-call(bf16[4,160,1024]{2,1,0:T(8,128)(2,1)} %get-tuple-element.120.refs_5_.refs_0_, bf16[4,160,1024]{2,1,0:T(8,128)(2,1)} %copy-done.1, bf16[4,160,1024]{2,1,0:T(8,128)(2,1)} %copy-done.2, bf16[2,160,1024]{2,1,0:T(8,128)(2,1)} %copy-done.3, ...), custom_call_target="tpu_custom_call" | custom-call | bytes 10485760 | tf_op jit(solution)/shard_map/down_whole/pallas_call | solution.py:385
  158.3 4.9 %attend_out.1.part.refs_4_ = bf16[1024,1024]{1,0:T(8,128)(2,1)} custom-call(bf16[1024,512]{1,0:T(8,128)(2,1)} %get-tuple-element.130.refs_7_.left.refs_3_, bf16[512,1024]{1,0:T(8,128)(2,1)} %bitcast.78), custom_call_target="tpu_custom_call" | custom-call | flops 1073741824 | bytes 4194304 | tf_op jit(solution)/shard_map/attend_out/pallas_call | solution.py:385
  166.1 4.6 collective-permute-start.27
  170.7 2.4 collective-permute-start.28
  173.1 13.2 %collective-permute-done.27.refs_0_ = bf16[256,1024]{1,0:T(8,128)(2,1)} collective-permute-done((bf16[256,1024]{1,0:T(8,128)(2,1)}, bf16[256,1024]{1,0:T(8,128)(2,1)}, u32[]{:S(2)}, u32[]{:S(2)}) %collective-permute-start.27) | collective-permute-done | bytes 524320 | tf_op jit(solution)/shard_map/ppermute | solution.py:344
  186.3 8.4 %collective-permute-done.28.refs_1_ = bf16[256,1024]{1,0:T(8,128)(2,1)} collective-permute-done((bf16[256,1024]{1,0:T(8,128)(2,1)}, bf16[256,1024]{1,0:T(8,128)(2,1)}, u32[]{:S(2)}, u32[]{:S(2)}) %collective-permute-start.28) | collective-permute-done | bytes 524320 | tf_op jit(solution)/shard_map/ppermute | solution.py:344
  202.2 2.9 cotangent_whole.1
  205.1 6.1 %middle.1 = (f32[1024,1024]{1,0:T(8,128)}, bf16[1024,1024]{1,0:T(8,128)(2,1)}) custom-call(bf16[1024,1024]{1,0:T(8,128)(2,1)} %bitcast.74, bf16[1024,1024]{1,0:T(8,128)(2,1)} %attend_out.1.part.refs_4_, bf16[1024,1024]{1,0:T(8,128)(2,1)} %collective-permute-done.26.got, f32[1,1024]{1,0:T(1,128)} %slice.222.bias, f32[1,1024]{1,0:T(1,128)} %slice.224.gain.refs_4_, ...), custom_call_target="tpu_custom_call" | custom-call | bytes 12595200 | tf_op jit(solution)/shard_map/middle/pallas_call | solution.py:385
  212.0 4.5 up_whole.1
  216.6 16.4 %feed.1 = (bf16[1024,2048]{1,0:T(8,128)(2,1)}, bf16[1024,2048]{1,0:T(8,128)(2,1)}, f32[1,2048]{1,0:T(1,128)}) custom-call(bf16[1024,1024]{1,0:T(8,128)(2,1)} %get-tuple-element.132.refs_5_.second.refs_1_, bf16[1024,1024]{1,0:T(8,128)(2,1)} %bitcast.70, bf16[1024,2048]{1,0:T(8,128)(2,1)} %bitcast.76, f32[1,2048]{1,0:T(1,128)} %convert.28.bias, ...), custom_call_target="tpu_custom_call" | custom-call | flops 8589934592 | bytes 20987904 | tf_op jit(solution)/shard_map/feed/pallas_call | solution.py:385
  232.9 10.5 %output_rows.1 = (bf16[512,1024]{1,0:T(8,128)(2,1)}, f32[512,1024]{1,0:T(8,128)}) custom-call(s32[3]{0:T(128)} %pad_add_fusion.1.pos.refs_0_, bf16[1024,2048]{1,0:T(8,128)(2,1)} %get-tuple-element.134.hidden.refs_1_, bf16[2048,1024]{1,0:T(8,128)(2,1)} %bitcast.98, f32[1024,1024]{1,0:T(8,128)} %get-tuple-element.135.middle.refs_2_, f32[1,1024]{1,0:T(1,128)} %slice.231.bias), custom_call_target="tpu_custom_call" | custom-call | flops 4294967296 | bytes 15732736 | tf_op jit(solution)/shard_map/output_rows/pallas_call | solution.py:401
  244.5 10.3 %down_grads.1 = (bf16[2,128,1024]{2,1,0:T(8,128)(2,1)}, bf16[2,128,1024]{2,1,0:T(8,128)(2,1)}, bf16[4,128,1024]{2,1,0:T(8,128)(2,1)}, bf16[4,128,1024]{2,1,0:T(8,128)(2,1)}, bf16[4,128,1024]{2,1,0:T(8,128)(2,1)}) custom-call(s32[3]{0:T(128)} %pad_add_fusion.1.pos.refs_0_, bf16[1024,2048]{1,0:T(8,128)(2,1)} %get-tuple-element.134.hidden.refs_1_, ...), custom_call_target="tpu_custom_call" | custom-call | flops 4294967296 | bytes 10485760 | tf_op jit(solution)/shard_map/down_grads/pallas_call | solution.py:401
  256.9 2.9 result.1
  259.8 10.7 %up_grads.1 = (bf16[2,64,2048]{2,1,0:T(8,128)(2,1)}, bf16[2,64,2048]{2,1,0:T(8,128)(2,1)}, bf16[4,64,2048]{2,1,0:T(8,128)(2,1)}, bf16[4,64,2048]{2,1,0:T(8,128)(2,1)}, bf16[4,64,2048]{2,1,0:T(8,128)(2,1)}) custom-call(s32[3]{0:T(128)} %pad_add_fusion.1.pos.refs_0_, bf16[1024,1024]{1,0:T(8,128)(2,1)} %get-tuple-element.132.refs_5_.second.refs_1_, ...), custom_call_target="tpu_custom_call" | custom-call | flops 4294967296 | bytes 10485760 | tf_op jit(solution)/shard_map/up_grads/pallas_call | solution.py:401
  271.6 3.3 down_pass.1
  274.9 8.7 %second_grad.1.refs_4_.refs_0_ = bf16[1024,1024]{1,0:T(8,128)(2,1)} custom-call(bf16[1024,2048]{1,0:T(8,128)(2,1)} %get-tuple-element.142.refs_2_.refs_0_, bf16[1024,2048]{1,0:T(8,128)(2,1)} %bitcast.77, bf16[4,128,1024]{2,1,0:T(8,128)(2,1)} %get-tuple-element.148.refs_2_), custom_call_target="tpu_custom_call" | custom-call | flops 4294967296 | bytes 10485760 | tf_op jit(solution)/shard_map/second_grad/pallas_call | solution.py:385
  286.0 2.4 collective-permute-start.36
  289.7 8.0 %collective-permute-done.41.refs_2_ = bf16[2,64,2048]{2,1,0:T(8,128)(2,1)} collective-permute-done((bf16[2,64,2048]{2,1,0:T(8,128)(2,1)S(1)}, bf16[2,64,2048]{2,1,0:T(8,128)(2,1)}, u32[]{:S(2)}, u32[]{:S(2)}) %collective-permute-start.41) | collective-permute-done | bytes 524320 | tf_op jit(solution)/shard_map/ppermute | solution.py:344
  299.5 3.3 up_pass.1
  304.2 9.9 %middle_back.1 = (bf16[1024,1024]{1,0:T(8,128)(2,1)}, f32[1024,1024]{1,0:T(8,128)}, bf16[1024,512]{1,0:T(8,128)(2,1)}, f32[4,1024]{1,0:T(4,128)}) custom-call(bf16[1024,1024]{1,0:T(8,128)(2,1)} %second_grad.1.refs_4_.refs_0_, bf16[1024,1024]{1,0:T(8,128)(2,1)} %copy-done.7, f32[1024,1024]{1,0:T(8,128)} %get-tuple-element.135.middle.refs_2_, ...), custom_call_target="tpu_custom_call" | custom-call | flops 1073741824 | bytes 18894848 | tf_op jit(solution)/shard_map/middle_back/pallas_call | solution.py:385
  314.8 13.5 %attend_back.2 = (bf16[3,1024,512]{2,1,0:T(8,128)(2,1)}, f32[2,512]{1,0:T(2,128)}) custom-call(f32[1024,1]{1,0:T(8,128)} %copy.72.refs_0_, f32[1,1024]{1,0:T(1,128)} %bitcast.92, bf16[3,1024,512]{2,1,0:T(8,128)(2,1)} %get-tuple-element.123.refs_2_.refs_3_.refs_4_, bf16[3,1024,512]{2,1,0:T(8,128)(2,1)} %get-tuple-element.123.refs_2_.refs_3_.refs_4_, ...), custom_call_target="tpu_custom_call" | custom-call | flops 6442450944 | bytes 15740928 | tf_op jit(solution)/shard_map/attend_back/pallas_call | solution.py:385
  329.3 3.4 down_join.1
  334.3 13.6 %attend_back.3 = (bf16[3,1024,512]{2,1,0:T(8,128)(2,1)}, f32[2,512]{1,0:T(2,128)}) custom-call(f32[1024,1]{1,0:T(8,128)} %copy.72.refs_0_, f32[1,1024]{1,0:T(1,128)} %bitcast.93, bf16[3,1024,512]{2,1,0:T(8,128)(2,1)} %get-tuple-element.123.refs_2_.refs_3_.refs_4_, ...), custom_call_target="tpu_custom_call", output_to_operand_aliasing={{0}: (7, {}), {1}: (8, {})} | custom-call | flops 6442450944 | bytes 18890752 | tf_op jit(solution)/shard_map/attend_back/pallas_call | solution.py:385
  348.6 2.0 down_inner.3
  352.4 11.2 %attn_grads.1 = (bf16[2,256,512]{2,1,0:T(8,128)(2,1)}, bf16[2,256,512]{2,1,0:T(8,128)(2,1)}, bf16[4,256,512]{2,1,0:T(8,128)(2,1)}, bf16[4,256,512]{2,1,0:T(8,128)(2,1)}, bf16[4,256,512]{2,1,0:T(8,128)(2,1)}) custom-call(s32[3]{0:T(128)} %pad_add_fusion.1.pos.refs_0_, bf16[1024,1024]{1,0:T(8,128)(2,1)} %get-tuple-element.125.refs_3_.refs_1_, ...), custom_call_target="tpu_custom_call" | custom-call | flops 4294967296 | bytes 12582912 | tf_op jit(solution)/shard_map/attn_grads/pallas_call | solution.py:401
  365.6 3.4 up_join.1
  369.0 7.4 %source_grad.1.refs_4_.refs_1_ = bf16[1024,1024]{1,0:T(8,128)(2,1)} custom-call(bf16[3,1024,512]{2,1,0:T(8,128)(2,1)} %get-tuple-element.159.refs_2_.refs_0_, bf16[3,1024,512]{2,1,0:T(8,128)(2,1)} %bitcast.100, f32[64,2048]{1,0:T(8,128)} %get-tuple-element.170.refs_2_.refs_3_), custom_call_target="tpu_custom_call" | custom-call | flops 3221225472 | bytes 8388608 | tf_op jit(solution)/shard_map/source_grad/pallas_call | solution.py:385
  380.3 2.4 collective-permute-start.55
  382.7 3.4 collective-permute-done.54.refs_2_
  386.8 1.9 up_inner.3
  388.8 4.8 %collective-permute-start.63 = (bf16[64,2048]{1,0:T(8,128)(2,1)}, bf16[64,2048]{1,0:T(8,128)(2,1)S(1)}, u32[]{:S(2)}, u32[]{:S(2)}) collective-permute-start(bf16[64,2048]{1,0:T(8,128)(2,1)} %get-tuple-element.180.refs_4_), channel_id=1, source_target_pairs={{0,1},{1,2},{2,3},{3,0},{4,5},{5,6},{6,7},{7,4},{8,9},{9,10},{10,1... | collective-permute-start | bytes 786440 | tf_op jit(solution)/shard_map/ppermute | solution.py:344
  394.8 3.3 attn_pass.1
  401.8 8.1 %input_back.1 = (bf16[256,1024]{1,0:T(8,128)(2,1)}, bf16[256,1024]{1,0:T(8,128)(2,1)}, f32[2,1024]{1,0:T(2,128)}) custom-call(s32[3]{0:T(128)} %pad_add_fusion.1.pos.refs_0_, bf16[1024,1024]{1,0:T(8,128)(2,1)} %source_grad.1.refs_4_.refs_1_, bf16[1024,1024]{1,0:T(8,128)(2,1)} %copy-done.6, bf16[1024,1024]{1,0:T(8,128)(2,1)} %bitcast.75, ...), custom_call_target="tpu_custom_call" | custom-call | bytes 11546624 | tf_op jit(solution)/shard_map/input_back/pallas_call | solution.py:401
  412.5 2.0 collective-permute-start.62
  415.2 2.6 feed_last.1
  417.8 3.6 collective-permute-done.58.refs_1_
  425.4 3.5 attn_join.1
  430.4 3.6 collective-permute-start.70
  435.8 2.0 attn_inner.3
  439.5 2.7 maximum_select_fusion
  442.2 9.1 %collective-permute-start.56 = (bf16[256,1024]{1,0:T(8,128)(2,1)S(1)}, bf16[256,1024]{1,0:T(8,128)(2,1)S(1)}, u32[]{:S(2)}, u32[]{:S(2)}) collective-permute-start(bf16[256,1024]{1,0:T(8,128)(2,1)S(1)} %copy-done.24), channel_id=1, source_target_pairs={{0,0},{1,1},{2,4},{3,5},{4,2},{5,3},{6,6},{7,7},{8,8},{9,9},{10,12... | collective-permute-start | bytes 1572872 | tf_op jit(solution)/shard_map/ppermute | solution.py:344
  454.4 2.1 attn_last.1
  460.8 5.3 %collective-permute-done.56 = bf16[256,1024]{1,0:T(8,128)(2,1)S(1)} collective-permute-done((bf16[256,1024]{1,0:T(8,128)(2,1)S(1)}, bf16[256,1024]{1,0:T(8,128)(2,1)S(1)}, u32[]{:S(2)}, u32[]{:S(2)}) %collective-permute-start.56) | collective-permute-done | bytes 524320 | tf_op jit(solution)/shard_map/ppermute | solution.py:344
  466.0 9.8 %collective-permute-done.57 = bf16[256,1024]{1,0:T(8,128)(2,1)S(1)} collective-permute-done((bf16[256,1024]{1,0:T(8,128)(2,1)S(1)}, bf16[256,1024]{1,0:T(8,128)(2,1)S(1)}, u32[]{:S(2)}, u32[]{:S(2)}) %collective-permute-start.57) | collective-permute-done | bytes 524320 | tf_op jit(solution)/shard_map/ppermute | solution.py:344
  (325 shorter events, 102.7 us)
Async XLA Ops:
  9.4 6.8 %collective-permute-start.3 = (bf16[208,512]{1,0:T(8,128)(2,1)}, bf16[208,512]{1,0:T(8,128)(2,1)S(1)}, u32[]{:S(2)}, u32[]{:S(2)}) collective-permute-start(bf16[208,512]{1,0:T(8,128)(2,1)} %get-tuple-element.112.refs_0_), channel_id=1, source_target_pairs={{0,3},{1,0},{2,1},{3,2},{4,7},{5,4},{6,5},{7,6},{8,11},{9,8},{10,9... | collective-permute-start | bytes 638984 | tf_op jit(solution)/shard_map/ppermute | solution.py:344
  9.5 13.3 %collective-permute-start.2 = (bf16[208,512]{1,0:T(8,128)(2,1)}, bf16[208,512]{1,0:T(8,128)(2,1)S(1)}, u32[]{:S(2)}, u32[]{:S(2)}) collective-permute-start(bf16[208,512]{1,0:T(8,128)(2,1)} %get-tuple-element.112.refs_0_), channel_id=1, source_target_pairs={{0,1},{1,2},{2,3},{3,0},{4,5},{5,6},{6,7},{7,4},{8,9},{9,10},{10,1... | collective-permute-start | bytes 638984 | tf_op jit(solution)/shard_map/ppermute | solution.py:344
  16.2 10.8 %collective-permute-start.5 = (bf16[112,512]{1,0:T(8,128)(2,1)S(1)}, bf16[112,512]{1,0:T(8,128)(2,1)S(1)}, u32[]{:S(2)}, u32[]{:S(2)}) collective-permute-start(bf16[112,512]{1,0:T(8,128)(2,1)S(1)} %slice.261), channel_id=1, source_target_pairs={{0,3},{1,0},{2,1},{3,2},{4,7},{5,4},{6,5},{7,6},{8,11},{9,8},{10,9... | collective-permute-start | bytes 344072 | tf_op jit(solution)/shard_map/ppermute | solution.py:344
  30.7 41.8 %collective-permute-start.10 = (bf16[4,208,512]{2,1,0:T(8,128)(2,1)}, bf16[4,208,512]{2,1,0:T(8,128)(2,1)S(1)}, u32[]{:S(2)}, u32[]{:S(2)}) collective-permute-start(bf16[4,208,512]{2,1,0:T(8,128)(2,1)} %get-tuple-element.113.refs_2_.refs_0_), channel_id=1, source_target_pairs={{0,8},{1,9},{2,10},{3,11},{4,12},{5,13},{6,14},{7,15},{8,0},{9,1},... | collective-permute-start | bytes 2555912 | tf_op jit(solution)/shard_map/ppermute | solution.py:344
  32.0 41.5 %collective-permute-start.11 = (bf16[4,208,512]{2,1,0:T(8,128)(2,1)}, bf16[4,208,512]{2,1,0:T(8,128)(2,1)S(1)}, u32[]{:S(2)}, u32[]{:S(2)}) collective-permute-start(bf16[4,208,512]{2,1,0:T(8,128)(2,1)} %get-tuple-element.113.refs_2_.refs_0_), channel_id=1, source_target_pairs={{0,16},{1,17},{2,18},{3,19},{4,20},{5,21},{6,22},{7,23},{8,24},{9,... | collective-permute-start | bytes 2555912 | tf_op jit(solution)/shard_map/ppermute | solution.py:344
  35.1 25.5 %collective-permute-start.6 = (bf16[272,1024]{1,0:T(8,128)(2,1)}, bf16[272,1024]{1,0:T(8,128)(2,1)S(1)}, u32[]{:S(2)}, u32[]{:S(2)}) collective-permute-start(bf16[272,1024]{1,0:T(8,128)(2,1)} %get-tuple-element.114), channel_id=1, source_target_pairs={{0,0},{1,1},{2,4},{3,5},{4,2},{5,3},{6,6},{7,7},{8,8},{9,9},{10,12... | collective-permute-start | bytes 1671176 | tf_op jit(solution)/shard_map/ppermute | solution.py:344
  40.7 31.8 %collective-permute-start.7 = (bf16[272,1024]{1,0:T(8,128)(2,1)}, bf16[272,1024]{1,0:T(8,128)(2,1)}, u32[]{:S(2)}, u32[]{:S(2)}) collective-permute-start(bf16[272,1024]{1,0:T(8,128)(2,1)} %get-tuple-element.115), channel_id=1, source_target_pairs={{0,1},{1,0},{2,5},{3,4},{4,3},{5,2},{6,7},{7,6},{8,9},{9,8},{10,13... | collective-permute-start | bytes 1671176 | tf_op jit(solution)/shard_map/ppermute | solution.py:344
  40.8 38.6 %collective-permute-start.14 = (bf16[160,1024]{1,0:T(8,128)(2,1)}, bf16[160,1024]{1,0:T(8,128)(2,1)S(1)}, u32[]{:S(2)}, u32[]{:S(2)}) collective-permute-start(bf16[160,1024]{1,0:T(8,128)(2,1)} %get-tuple-element.118.refs_0_), channel_id=1, source_target_pairs={{0,1},{1,2},{2,3},{3,0},{4,5},{5,6},{6,7},{7,4},{8,9},{9,10},{10,1... | collective-permute-start | bytes 983048 | tf_op jit(solution)/shard_map/ppermute | solution.py:344
  60.6 22.6 %collective-permute-start.8 = (bf16[272,1024]{1,0:T(8,128)(2,1)S(1)}, bf16[272,1024]{1,0:T(8,128)(2,1)S(1)}, u32[]{:S(2)}, u32[]{:S(2)}) collective-permute-start(bf16[272,1024]{1,0:T(8,128)(2,1)S(1)} %collective-permute-done.6.refs_0_), channel_id=1, source_target_pairs={{0,4},{1,5},{2,6},{3,7},{4,0},{5,1},{6,2},{7,3},{8,12},{9,13},{10,... | collective-permute-start | bytes 1671176 | tf_op jit(solution)/shard_map/ppermute | solution.py:344
  72.5 12.6 %collective-permute-start.9 = (bf16[272,1024]{1,0:T(8,128)(2,1)}, bf16[272,1024]{1,0:T(8,128)(2,1)}, u32[]{:S(2)}, u32[]{:S(2)}) collective-permute-start(bf16[272,1024]{1,0:T(8,128)(2,1)} %collective-permute-done.7.refs_1_), channel_id=1, source_target_pairs={{0,4},{1,5},{2,6},{3,7},{4,0},{5,1},{6,2},{7,3},{8,12},{9,13},{10,... | collective-permute-start | bytes 1671176 | tf_op jit(solution)/shard_map/ppermute | solution.py:344
  72.5 9.1 %collective-permute-start.15 = (bf16[160,1024]{1,0:T(8,128)(2,1)}, bf16[160,1024]{1,0:T(8,128)(2,1)S(1)}, u32[]{:S(2)}, u32[]{:S(2)}) collective-permute-start(bf16[160,1024]{1,0:T(8,128)(2,1)} %get-tuple-element.118.refs_0_), channel_id=1, source_target_pairs={{0,3},{1,0},{2,1},{3,2},{4,7},{5,4},{6,5},{7,6},{8,11},{9,8},{10,9... | collective-permute-start | bytes 983048 | tf_op jit(solution)/shard_map/ppermute | solution.py:344
  73.5 18.8 %collective-permute-start.12 = (bf16[2,208,512]{2,1,0:T(8,128)(2,1)}, bf16[2,208,512]{2,1,0:T(8,128)(2,1)S(1)}, u32[]{:S(2)}, u32[]{:S(2)}) collective-permute-start(bf16[2,208,512]{2,1,0:T(8,128)(2,1)} %slice.262), channel_id=1, source_target_pairs={{0,16},{1,17},{2,18},{3,19},{4,20},{5,21},{6,22},{7,23},{8,24},{9,... | collective-permute-start | bytes 1277960 | tf_op jit(solution)/shard_map/ppermute | solution.py:344
  79.5 12.9 %collective-permute-start.13 = (bf16[2,208,512]{2,1,0:T(8,128)(2,1)}, bf16[2,208,512]{2,1,0:T(8,128)(2,1)S(1)}, u32[]{:S(2)}, u32[]{:S(2)}) collective-permute-start(bf16[2,208,512]{2,1,0:T(8,128)(2,1)} %slice.263), channel_id=1, source_target_pairs={{0,8},{1,9},{2,10},{3,11},{4,12},{5,13},{6,14},{7,15},{8,0},{9,1},... | collective-permute-start | bytes 1277960 | tf_op jit(solution)/shard_map/ppermute | solution.py:344
  81.6 6.5 %collective-permute-start.16 = (bf16[80,1024]{1,0:T(8,128)(2,1)}, bf16[80,1024]{1,0:T(8,128)(2,1)S(1)}, u32[]{:S(2)}, u32[]{:S(2)}) collective-permute-start(bf16[80,1024]{1,0:T(8,128)(2,1)} %slice.264), channel_id=1, source_target_pairs={{0,1},{1,2},{2,3},{3,0},{4,5},{5,6},{6,7},{7,4},{8,9},{9,10},{10,1... | collective-permute-start | bytes 491528 | tf_op jit(solution)/shard_map/ppermute | solution.py:344
  84.0 8.3 %collective-permute-start.17 = (bf16[80,1024]{1,0:T(8,128)(2,1)}, bf16[80,1024]{1,0:T(8,128)(2,1)}, u32[]{:S(2)}, u32[]{:S(2)}) collective-permute-start(bf16[80,1024]{1,0:T(8,128)(2,1)} %slice.265), channel_id=1, source_target_pairs={{0,3},{1,0},{2,1},{3,2},{4,7},{5,4},{6,5},{7,6},{8,11},{9,8},{10,9... | collective-permute-start | bytes 491528 | tf_op jit(solution)/shard_map/ppermute | solution.py:344
  95.8 30.1 %collective-permute-start.20 = (bf16[4,160,1024]{2,1,0:T(8,128)(2,1)}, bf16[4,160,1024]{2,1,0:T(8,128)(2,1)S(1)}, u32[]{:S(2)}, u32[]{:S(2)}) collective-permute-start(bf16[4,160,1024]{2,1,0:T(8,128)(2,1)} %get-tuple-element.120.refs_5_.refs_0_), channel_id=1, source_target_pairs={{0,8},{1,9},{2,10},{3,11},{4,12},{5,13},{6,14},{7,15},{8,0},{9,1},... | collective-permute-start | bytes 3932168 | tf_op jit(solution)/shard_map/ppermute | solution.py:344
  96.5 31.6 %collective-permute-start.21 = (bf16[4,160,1024]{2,1,0:T(8,128)(2,1)}, bf16[4,160,1024]{2,1,0:T(8,128)(2,1)S(1)}, u32[]{:S(2)}, u32[]{:S(2)}) collective-permute-start(bf16[4,160,1024]{2,1,0:T(8,128)(2,1)} %get-tuple-element.120.refs_5_.refs_0_), channel_id=1, source_target_pairs={{0,16},{1,17},{2,18},{3,19},{4,20},{5,21},{6,22},{7,23},{8,24},{9,... | collective-permute-start | bytes 3932168 | tf_op jit(solution)/shard_map/ppermute | solution.py:344
  99.5 19.0 %collective-permute-start.18 = (bf16[64,2048]{1,0:T(8,128)(2,1)}, bf16[64,2048]{1,0:T(8,128)(2,1)S(1)}, u32[]{:S(2)}, u32[]{:S(2)}) collective-permute-start(bf16[64,2048]{1,0:T(8,128)(2,1)} %get-tuple-element.124.refs_0_), channel_id=1, source_target_pairs={{0,1},{1,2},{2,3},{3,0},{4,5},{5,6},{6,7},{7,4},{8,9},{9,10},{10,1... | collective-permute-start | bytes 786440 | tf_op jit(solution)/shard_map/ppermute | solution.py:344
  99.9 19.8 %collective-permute-start.19 = (bf16[64,2048]{1,0:T(8,128)(2,1)}, bf16[64,2048]{1,0:T(8,128)(2,1)S(1)}, u32[]{:S(2)}, u32[]{:S(2)}) collective-permute-start(bf16[64,2048]{1,0:T(8,128)(2,1)} %get-tuple-element.124.refs_0_), channel_id=1, source_target_pairs={{0,3},{1,0},{2,1},{3,2},{4,7},{5,4},{6,5},{7,6},{8,11},{9,8},{10,9... | collective-permute-start | bytes 786440 | tf_op jit(solution)/shard_map/ppermute | solution.py:344
  119.2 30.9 %collective-permute-start.24 = (bf16[32,2048]{1,0:T(8,128)(2,1)}, bf16[32,2048]{1,0:T(8,128)(2,1)}, u32[]{:S(2)}, u32[]{:S(2)}) collective-permute-start(bf16[32,2048]{1,0:T(8,128)(2,1)} %slice.274), channel_id=1, source_target_pairs={{0,1},{1,2},{2,3},{3,0},{4,5},{5,6},{6,7},{7,4},{8,9},{9,10},{10,1... | collective-permute-start | bytes 393224 | tf_op jit(solution)/shard_map/ppermute | solution.py:344
  120.3 29.8 %collective-permute-start.25 = (bf16[32,2048]{1,0:T(8,128)(2,1)}, bf16[32,2048]{1,0:T(8,128)(2,1)}, u32[]{:S(2)}, u32[]{:S(2)}) collective-permute-start(bf16[32,2048]{1,0:T(8,128)(2,1)} %slice.275), channel_id=1, source_target_pairs={{0,3},{1,0},{2,1},{3,2},{4,7},{5,4},{6,5},{7,6},{8,11},{9,8},{10,9... | collective-permute-start | bytes 393224 | tf_op jit(solution)/shard_map/ppermute | solution.py:344
  126.8 23.4 %collective-permute-start.22 = (bf16[2,160,1024]{2,1,0:T(8,128)(2,1)}, bf16[2,160,1024]{2,1,0:T(8,128)(2,1)S(1)}, u32[]{:S(2)}, u32[]{:S(2)}) collective-permute-start(bf16[2,160,1024]{2,1,0:T(8,128)(2,1)} %slice.272), channel_id=1, source_target_pairs={{0,16},{1,17},{2,18},{3,19},{4,20},{5,21},{6,22},{7,23},{8,24},{9,... | collective-permute-start | bytes 1966088 | tf_op jit(solution)/shard_map/ppermute | solution.py:344
  129.0 21.2 %collective-permute-start.23 = (bf16[2,160,1024]{2,1,0:T(8,128)(2,1)}, bf16[2,160,1024]{2,1,0:T(8,128)(2,1)}, u32[]{:S(2)}, u32[]{:S(2)}) collective-permute-start(bf16[2,160,1024]{2,1,0:T(8,128)(2,1)} %slice.273), channel_id=1, source_target_pairs={{0,8},{1,9},{2,10},{3,11},{4,12},{5,13},{6,14},{7,15},{8,0},{9,1},... | collective-permute-start | bytes 1966088 | tf_op jit(solution)/shard_map/ppermute | solution.py:344
  163.2 41.9 %collective-permute-start.26 = (bf16[1024,1024]{1,0:T(8,128)(2,1)}, bf16[1024,1024]{1,0:T(8,128)(2,1)}, u32[]{:S(2)}, u32[]{:S(2)}) collective-permute-start(bf16[1024,1024]{1,0:T(8,128)(2,1)} %attend_out.1.part.refs_4_), channel_id=1, source_target_pairs={{0,4},{1,5},{2,6},{3,7},{4,0},{5,1},{6,2},{7,3},{8,12},{9,13},{10,... | collective-permute-start | bytes 6291464 | tf_op jit(solution)/shard_map/ppermute | solution.py:344
  165.0 29.7 %collective-permute-start.31 = (bf16[4,64,2048]{2,1,0:T(8,128)(2,1)S(1)}, bf16[4,64,2048]{2,1,0:T(8,128)(2,1)S(1)}, u32[]{:S(2)}, u32[]{:S(2)}) collective-permute-start(bf16[4,64,2048]{2,1,0:T(8,128)(2,1)S(1)} %copy-done), channel_id=1, source_target_pairs={{0,8},{1,9},{2,10},{3,11},{4,12},{5,13},{6,14},{7,15},{8,0},{9,1},... | collective-permute-start | bytes 3145736 | tf_op jit(solution)/shard_map/ppermute | solution.py:344
  165.9 31.0 %collective-permute-start.32 = (bf16[4,64,2048]{2,1,0:T(8,128)(2,1)S(1)}, bf16[4,64,2048]{2,1,0:T(8,128)(2,1)S(1)}, u32[]{:S(2)}, u32[]{:S(2)}) collective-permute-start(bf16[4,64,2048]{2,1,0:T(8,128)(2,1)S(1)} %copy-done), channel_id=1, source_target_pairs={{0,16},{1,17},{2,18},{3,19},{4,20},{5,21},{6,22},{7,23},{8,24},{9,... | collective-permute-start | bytes 3145736 | tf_op jit(solution)/shard_map/ppermute | solution.py:344
  166.1 20.2 %collective-permute-start.27 = (bf16[256,1024]{1,0:T(8,128)(2,1)}, bf16[256,1024]{1,0:T(8,128)(2,1)}, u32[]{:S(2)}, u32[]{:S(2)}) collective-permute-start(bf16[256,1024]{1,0:T(8,128)(2,1)} %get-tuple-element.126.refs_5_), channel_id=1, source_target_pairs={{0,0},{1,1},{2,4},{3,5},{4,2},{5,3},{6,6},{7,7},{8,8},{9,9},{10,12... | collective-permute-start | bytes 1572872 | tf_op jit(solution)/shard_map/ppermute | solution.py:344
  170.7 24.0 %collective-permute-start.28 = (bf16[256,1024]{1,0:T(8,128)(2,1)}, bf16[256,1024]{1,0:T(8,128)(2,1)}, u32[]{:S(2)}, u32[]{:S(2)}) collective-permute-start(bf16[256,1024]{1,0:T(8,128)(2,1)} %get-tuple-element.127.refs_6_), channel_id=1, source_target_pairs={{0,1},{1,0},{2,5},{3,4},{4,3},{5,2},{6,7},{7,6},{8,9},{9,8},{10,13... | collective-permute-start | bytes 1572872 | tf_op jit(solution)/shard_map/ppermute | solution.py:344
  186.3 15.9 %collective-permute-start.29 = (bf16[256,1024]{1,0:T(8,128)(2,1)}, bf16[256,1024]{1,0:T(8,128)(2,1)}, u32[]{:S(2)}, u32[]{:S(2)}) collective-permute-start(bf16[256,1024]{1,0:T(8,128)(2,1)} %collective-permute-done.27.refs_0_), channel_id=1, source_target_pairs={{0,4},{1,5},{2,6},{3,7},{4,0},{5,1},{6,2},{7,3},{8,12},{9,13},{10,... | collective-permute-start | bytes 1572872 | tf_op jit(solution)/shard_map/ppermute | solution.py:344
  194.7 7.5 %collective-permute-start.30 = (bf16[256,1024]{1,0:T(8,128)(2,1)}, bf16[256,1024]{1,0:T(8,128)(2,1)}, u32[]{:S(2)}, u32[]{:S(2)}) collective-permute-start(bf16[256,1024]{1,0:T(8,128)(2,1)} %collective-permute-done.28.refs_1_), channel_id=1, source_target_pairs={{0,4},{1,5},{2,6},{3,7},{4,0},{5,1},{6,2},{7,3},{8,12},{9,13},{10,... | collective-permute-start | bytes 1572872 | tf_op jit(solution)/shard_map/ppermute | solution.py:344
  195.6 15.6 %collective-permute-start.33 = (bf16[2,64,2048]{2,1,0:T(8,128)(2,1)}, bf16[2,64,2048]{2,1,0:T(8,128)(2,1)}, u32[]{:S(2)}, u32[]{:S(2)}) collective-permute-start(bf16[2,64,2048]{2,1,0:T(8,128)(2,1)} %slice.279), channel_id=1, source_target_pairs={{0,16},{1,17},{2,18},{3,19},{4,20},{5,21},{6,22},{7,23},{8,24},{9,... | collective-permute-start | bytes 1572872 | tf_op jit(solution)/shard_map/ppermute | solution.py:344
  196.9 14.3 %collective-permute-start.34 = (bf16[2,64,2048]{2,1,0:T(8,128)(2,1)S(1)}, bf16[2,64,2048]{2,1,0:T(8,128)(2,1)S(1)}, u32[]{:S(2)}, u32[]{:S(2)}) collective-permute-start(bf16[2,64,2048]{2,1,0:T(8,128)(2,1)S(1)} %slice.280), channel_id=1, source_target_pairs={{0,8},{1,9},{2,10},{3,11},{4,12},{5,13},{6,14},{7,15},{8,0},{9,1},... | collective-permute-start | bytes 1572872 | tf_op jit(solution)/shard_map/ppermute | solution.py:344
  243.4 12.4 %collective-permute-start.35 = (bf16[512,1024]{1,0:T(8,128)(2,1)}, bf16[512,1024]{1,0:T(8,128)(2,1)S(1)}, u32[]{:S(2)}, u32[]{:S(2)}) collective-permute-start(bf16[512,1024]{1,0:T(8,128)(2,1)} %get-tuple-element.137), channel_id=1, source_target_pairs={{0,4},{1,5},{2,6},{3,7},{4,0},{5,1},{6,2},{7,3},{8,12},{9,13},{10,... | collective-permute-start | bytes 3145736 | tf_op jit(solution)/shard_map/ppermute | solution.py:344
  254.8 15.8 %collective-permute-start.38 = (bf16[2,128,1024]{2,1,0:T(8,128)(2,1)}, bf16[2,128,1024]{2,1,0:T(8,128)(2,1)S(1)}, u32[]{:S(2)}, u32[]{:S(2)}) collective-permute-start(bf16[2,128,1024]{2,1,0:T(8,128)(2,1)} %get-tuple-element.145), channel_id=1, source_target_pairs={{0,8},{1,9},{2,10},{3,11},{4,12},{5,13},{6,14},{7,15},{8,0},{9,1},... | collective-permute-start | bytes 1572872 | tf_op jit(solution)/shard_map/ppermute | solution.py:344
  255.7 14.9 %collective-permute-start.39 = (bf16[2,128,1024]{2,1,0:T(8,128)(2,1)}, bf16[2,128,1024]{2,1,0:T(8,128)(2,1)S(1)}, u32[]{:S(2)}, u32[]{:S(2)}) collective-permute-start(bf16[2,128,1024]{2,1,0:T(8,128)(2,1)} %get-tuple-element.146), channel_id=1, source_target_pairs={{0,16},{1,17},{2,18},{3,19},{4,20},{5,21},{6,22},{7,23},{8,24},{9,... | collective-permute-start | bytes 1572872 | tf_op jit(solution)/shard_map/ppermute | solution.py:344
  283.5 19.3 %collective-permute-start.40 = (bf16[1024,1024]{1,0:T(8,128)(2,1)}, bf16[1024,1024]{1,0:T(8,128)(2,1)S(1)}, u32[]{:S(2)}, u32[]{:S(2)}) collective-permute-start(bf16[1024,1024]{1,0:T(8,128)(2,1)} %second_grad.1.refs_4_.refs_0_), channel_id=1, source_target_pairs={{0,4},{1,5},{2,6},{3,7},{4,0},{5,1},{6,2},{7,3},{8,12},{9,13},{10,... | collective-permute-start | bytes 6291464 | tf_op jit(solution)/shard_map/ppermute | solution.py:344
  284.1 13.5 %collective-permute-start.41 = (bf16[2,64,2048]{2,1,0:T(8,128)(2,1)S(1)}, bf16[2,64,2048]{2,1,0:T(8,128)(2,1)}, u32[]{:S(2)}, u32[]{:S(2)}) collective-permute-start(bf16[2,64,2048]{2,1,0:T(8,128)(2,1)S(1)} %copy-done.60), channel_id=1, source_target_pairs={{0,8},{1,9},{2,10},{3,11},{4,12},{5,13},{6,14},{7,15},{8,0},{9,1},... | collective-permute-start | bytes 1572872 | tf_op jit(solution)/shard_map/ppermute | solution.py:344
  285.1 13.5 %collective-permute-start.42 = (bf16[2,64,2048]{2,1,0:T(8,128)(2,1)}, bf16[2,64,2048]{2,1,0:T(8,128)(2,1)}, u32[]{:S(2)}, u32[]{:S(2)}) collective-permute-start(bf16[2,64,2048]{2,1,0:T(8,128)(2,1)} %get-tuple-element.152), channel_id=1, source_target_pairs={{0,16},{1,17},{2,18},{3,19},{4,20},{5,21},{6,22},{7,23},{8,24},{9,... | collective-permute-start | bytes 1572872 | tf_op jit(solution)/shard_map/ppermute | solution.py:344
  286.0 28.1 %collective-permute-start.36 = (bf16[256,1024]{1,0:T(8,128)(2,1)}, bf16[256,1024]{1,0:T(8,128)(2,1)}, u32[]{:S(2)}, u32[]{:S(2)}) collective-permute-start(bf16[256,1024]{1,0:T(8,128)(2,1)} %get-tuple-element.139.refs_3_), channel_id=1, source_target_pairs={{0,0},{1,1},{2,4},{3,5},{4,2},{5,3},{6,6},{7,7},{8,8},{9,9},{10,12... | collective-permute-start | bytes 1572872 | tf_op jit(solution)/shard_map/ppermute | solution.py:344
  288.3 26.4 %collective-permute-start.37 = (bf16[256,1024]{1,0:T(8,128)(2,1)}, bf16[256,1024]{1,0:T(8,128)(2,1)}, u32[]{:S(2)}, u32[]{:S(2)}) collective-permute-start(bf16[256,1024]{1,0:T(8,128)(2,1)} %get-tuple-element.140), channel_id=1, source_target_pairs={{0,1},{1,0},{2,5},{3,4},{4,3},{5,2},{6,7},{7,6},{8,9},{9,8},{10,13... | collective-permute-start | bytes 1572872 | tf_op jit(solution)/shard_map/ppermute | solution.py:344
  297.6 30.7 %collective-permute-start.43 = (bf16[4,128,1024]{2,1,0:T(8,128)(2,1)}, bf16[4,128,1024]{2,1,0:T(8,128)(2,1)S(1)}, u32[]{:S(2)}, u32[]{:S(2)}) collective-permute-start(bf16[4,128,1024]{2,1,0:T(8,128)(2,1)} %get-tuple-element.148.refs_2_), channel_id=1, source_target_pairs={{0,8},{1,9},{2,10},{3,11},{4,12},{5,13},{6,14},{7,15},{8,0},{9,1},... | collective-permute-start | bytes 3145736 | tf_op jit(solution)/shard_map/ppermute | solution.py:344
  298.7 29.7 %collective-permute-start.44 = (bf16[4,128,1024]{2,1,0:T(8,128)(2,1)}, bf16[4,128,1024]{2,1,0:T(8,128)(2,1)}, u32[]{:S(2)}, u32[]{:S(2)}) collective-permute-start(bf16[4,128,1024]{2,1,0:T(8,128)(2,1)} %get-tuple-element.157), channel_id=1, source_target_pairs={{0,16},{1,17},{2,18},{3,19},{4,20},{5,21},{6,22},{7,23},{8,24},{9,... | collective-permute-start | bytes 3145736 | tf_op jit(solution)/shard_map/ppermute | solution.py:344
  302.8 60.8 %collective-permute-start.45 = (bf16[4,64,2048]{2,1,0:T(8,128)(2,1)}, bf16[4,64,2048]{2,1,0:T(8,128)(2,1)}, u32[]{:S(2)}, u32[]{:S(2)}) collective-permute-start(bf16[4,64,2048]{2,1,0:T(8,128)(2,1)} %get-tuple-element.153.refs_6_), channel_id=1, source_target_pairs={{0,8},{1,9},{2,10},{3,11},{4,12},{5,13},{6,14},{7,15},{8,0},{9,1},... | collective-permute-start | bytes 3145736 | tf_op jit(solution)/shard_map/ppermute | solution.py:344
  314.1 49.5 %collective-permute-start.46 = (bf16[4,64,2048]{2,1,0:T(8,128)(2,1)}, bf16[4,64,2048]{2,1,0:T(8,128)(2,1)S(1)}, u32[]{:S(2)}, u32[]{:S(2)}) collective-permute-start(bf16[4,64,2048]{2,1,0:T(8,128)(2,1)} %get-tuple-element.160), channel_id=1, source_target_pairs={{0,16},{1,17},{2,18},{3,19},{4,20},{5,21},{6,22},{7,23},{8,24},{9,... | collective-permute-start | bytes 3145736 | tf_op jit(solution)/shard_map/ppermute | solution.py:344
  332.7 15.2 %collective-permute-start.47 = (bf16[64,1024]{1,0:T(8,128)(2,1)}, bf16[64,1024]{1,0:T(8,128)(2,1)S(1)}, u32[]{:S(2)}, u32[]{:S(2)}) collective-permute-start(bf16[64,1024]{1,0:T(8,128)(2,1)} %get-tuple-element.164), channel_id=1, source_target_pairs={{0,1},{1,2},{2,3},{3,0},{4,5},{5,6},{6,7},{7,4},{8,9},{9,10},{10,1... | collective-permute-start | bytes 393224 | tf_op jit(solution)/shard_map/ppermute | solution.py:344
  334.1 13.9 %collective-permute-start.48 = (bf16[64,1024]{1,0:T(8,128)(2,1)}, bf16[64,1024]{1,0:T(8,128)(2,1)S(1)}, u32[]{:S(2)}, u32[]{:S(2)}) collective-permute-start(bf16[64,1024]{1,0:T(8,128)(2,1)} %get-tuple-element.165), channel_id=1, source_target_pairs={{0,3},{1,0},{2,1},{3,2},{4,7},{5,4},{6,5},{7,6},{8,11},{9,8},{10,9... | collective-permute-start | bytes 393224 | tf_op jit(solution)/shard_map/ppermute | solution.py:344
  350.6 13.0 %collective-permute-start.49 = (bf16[128,1024]{1,0:T(8,128)(2,1)}, bf16[128,1024]{1,0:T(8,128)(2,1)S(1)}, u32[]{:S(2)}, u32[]{:S(2)}) collective-permute-start(bf16[128,1024]{1,0:T(8,128)(2,1)} %get-tuple-element.167.refs_5_), channel_id=1, source_target_pairs={{0,1},{1,2},{2,3},{3,0},{4,5},{5,6},{6,7},{7,4},{8,9},{9,10},{10,1... | collective-permute-start | bytes 786440 | tf_op jit(solution)/shard_map/ppermute | solution.py:344
  351.9 12.9 %collective-permute-start.50 = (bf16[128,1024]{1,0:T(8,128)(2,1)}, bf16[128,1024]{1,0:T(8,128)(2,1)S(1)}, u32[]{:S(2)}, u32[]{:S(2)}) collective-permute-start(bf16[128,1024]{1,0:T(8,128)(2,1)} %get-tuple-element.169), channel_id=1, source_target_pairs={{0,3},{1,0},{2,1},{3,2},{4,7},{5,4},{6,5},{7,6},{8,11},{9,8},{10,9... | collective-permute-start | bytes 786440 | tf_op jit(solution)/shard_map/ppermute | solution.py:344
  376.4 24.0 %collective-permute-start.51 = (bf16[1024,1024]{1,0:T(8,128)(2,1)}, bf16[1024,1024]{1,0:T(8,128)(2,1)S(1)}, u32[]{:S(2)}, u32[]{:S(2)}) collective-permute-start(bf16[1024,1024]{1,0:T(8,128)(2,1)} %source_grad.1.refs_4_.refs_1_), channel_id=1, source_target_pairs={{0,4},{1,5},{2,6},{3,7},{4,0},{5,1},{6,2},{7,3},{8,12},{9,13},{10,... | collective-permute-start | bytes 6291464 | tf_op jit(solution)/shard_map/ppermute | solution.py:344
  378.2 15.6 %collective-permute-start.52 = (bf16[2,256,512]{2,1,0:T(8,128)(2,1)}, bf16[2,256,512]{2,1,0:T(8,128)(2,1)S(1)}, u32[]{:S(2)}, u32[]{:S(2)}) collective-permute-start(bf16[2,256,512]{2,1,0:T(8,128)(2,1)} %get-tuple-element.174), channel_id=1, source_target_pairs={{0,8},{1,9},{2,10},{3,11},{4,12},{5,13},{6,14},{7,15},{8,0},{9,1},... | collective-permute-start | bytes 1572872 | tf_op jit(solution)/shard_map/ppermute | solution.py:344
  378.6 15.3 %collective-permute-start.53 = (bf16[2,256,512]{2,1,0:T(8,128)(2,1)}, bf16[2,256,512]{2,1,0:T(8,128)(2,1)S(1)}, u32[]{:S(2)}, u32[]{:S(2)}) collective-permute-start(bf16[2,256,512]{2,1,0:T(8,128)(2,1)} %get-tuple-element.175), channel_id=1, source_target_pairs={{0,16},{1,17},{2,18},{3,19},{4,20},{5,21},{6,22},{7,23},{8,24},{9,... | collective-permute-start | bytes 1572872 | tf_op jit(solution)/shard_map/ppermute | solution.py:344
  388.8 23.4 %collective-permute-start.63 = (bf16[64,2048]{1,0:T(8,128)(2,1)}, bf16[64,2048]{1,0:T(8,128)(2,1)S(1)}, u32[]{:S(2)}, u32[]{:S(2)}) collective-permute-start(bf16[64,2048]{1,0:T(8,128)(2,1)} %get-tuple-element.180.refs_4_), channel_id=1, source_target_pairs={{0,1},{1,2},{2,3},{3,0},{4,5},{5,6},{6,7},{7,4},{8,9},{9,10},{10,1... | collective-permute-start | bytes 786440 | tf_op jit(solution)/shard_map/ppermute | solution.py:344
  393.6 18.9 %collective-permute-start.64 = (bf16[64,2048]{1,0:T(8,128)(2,1)}, bf16[64,2048]{1,0:T(8,128)(2,1)}, u32[]{:S(2)}, u32[]{:S(2)}) collective-permute-start(bf16[64,2048]{1,0:T(8,128)(2,1)} %get-tuple-element.188), channel_id=1, source_target_pairs={{0,3},{1,0},{2,1},{3,2},{4,7},{5,4},{6,5},{7,6},{8,11},{9,8},{10,9... | collective-permute-start | bytes 786440 | tf_op jit(solution)/shard_map/ppermute | solution.py:344
  398.1 23.3 %collective-permute-start.58 = (bf16[4,256,512]{2,1,0:T(8,128)(2,1)}, bf16[4,256,512]{2,1,0:T(8,128)(2,1)S(1)}, u32[]{:S(2)}, u32[]{:S(2)}) collective-permute-start(bf16[4,256,512]{2,1,0:T(8,128)(2,1)} %get-tuple-element.181.refs_6_), channel_id=1, source_target_pairs={{0,8},{1,9},{2,10},{3,11},{4,12},{5,13},{6,14},{7,15},{8,0},{9,1},... | collective-permute-start | bytes 3145736 | tf_op jit(solution)/shard_map/ppermute | solution.py:344
  399.2 23.1 %collective-permute-start.59 = (bf16[4,256,512]{2,1,0:T(8,128)(2,1)}, bf16[4,256,512]{2,1,0:T(8,128)(2,1)}, u32[]{:S(2)}, u32[]{:S(2)}) collective-permute-start(bf16[4,256,512]{2,1,0:T(8,128)(2,1)} %get-tuple-element.184), channel_id=1, source_target_pairs={{0,16},{1,17},{2,18},{3,19},{4,20},{5,21},{6,22},{7,23},{8,24},{9,... | collective-permute-start | bytes 3145736 | tf_op jit(solution)/shard_map/ppermute | solution.py:344
  411.6 11.2 %collective-permute-start.60 = (bf16[4,16,512]{2,1,0:T(8,128)(2,1)S(1)}, bf16[4,16,512]{2,1,0:T(8,128)(2,1)S(1)}, u32[]{:S(2)}, u32[]{:S(2)}) collective-permute-start(bf16[4,16,512]{2,1,0:T(8,128)(2,1)S(1)} %bitcast.85), channel_id=1, source_target_pairs={{0,8},{1,9},{2,10},{3,11},{4,12},{5,13},{6,14},{7,15},{8,0},{9,1},... | collective-permute-start | bytes 196616 | tf_op jit(solution)/shard_map/ppermute | solution.py:344
  412.2 11.5 %collective-permute-start.61 = (bf16[4,16,512]{2,1,0:T(8,128)(2,1)S(1)}, bf16[4,16,512]{2,1,0:T(8,128)(2,1)S(1)}, u32[]{:S(2)}, u32[]{:S(2)}) collective-permute-start(bf16[4,16,512]{2,1,0:T(8,128)(2,1)S(1)} %bitcast.87), channel_id=1, source_target_pairs={{0,16},{1,17},{2,18},{3,19},{4,20},{5,21},{6,22},{7,23},{8,24},{9,... | collective-permute-start | bytes 196616 | tf_op jit(solution)/shard_map/ppermute | solution.py:344
  412.5 12.3 %collective-permute-start.62 = (bf16[4,16,512]{2,1,0:T(8,128)(2,1)S(1)}, bf16[4,16,512]{2,1,0:T(8,128)(2,1)S(1)}, u32[]{:S(2)}, u32[]{:S(2)}) collective-permute-start(bf16[4,16,512]{2,1,0:T(8,128)(2,1)S(1)} %bitcast.86), channel_id=1, source_target_pairs={{0,24},{1,25},{2,26},{3,27},{4,28},{5,29},{6,30},{7,31},{8,16},{9,... | collective-permute-start | bytes 196616 | tf_op jit(solution)/shard_map/ppermute | solution.py:344
  430.4 21.2 %collective-permute-start.70 = (f32[32,2048]{1,0:T(8,128)}, f32[32,2048]{1,0:T(8,128)S(1)}, u32[]{:S(2)}, u32[]{:S(2)}) collective-permute-start(f32[32,2048]{1,0:T(8,128)} %get-tuple-element.202), channel_id=1, source_target_pairs={{0,4},{1,5},{2,6},{3,7},{4,0},{5,1},{6,2},{7,3},{8,12},{9,13},{10,... | collective-permute-start | bytes 786440 | tf_op jit(solution)/shard_map/ppermute | solution.py:344
  437.8 15.8 %collective-permute-start.67 = (bf16[272,512]{1,0:T(8,128)(2,1)}, bf16[272,512]{1,0:T(8,128)(2,1)S(1)}, u32[]{:S(2)}, u32[]{:S(2)}) collective-permute-start(bf16[272,512]{1,0:T(8,128)(2,1)} %get-tuple-element.195), channel_id=1, source_target_pairs={{0,1},{1,2},{2,3},{3,0},{4,5},{5,6},{6,7},{7,4},{8,9},{9,10},{10,1... | collective-permute-start | bytes 835592 | tf_op jit(solution)/shard_map/ppermute | solution.py:344
  438.7 14.8 %collective-permute-start.68 = (bf16[272,512]{1,0:T(8,128)(2,1)}, bf16[272,512]{1,0:T(8,128)(2,1)S(1)}, u32[]{:S(2)}, u32[]{:S(2)}) collective-permute-start(bf16[272,512]{1,0:T(8,128)(2,1)} %get-tuple-element.196), channel_id=1, source_target_pairs={{0,3},{1,0},{2,1},{3,2},{4,7},{5,4},{6,5},{7,6},{8,11},{9,8},{10,9... | collective-permute-start | bytes 835592 | tf_op jit(solution)/shard_map/ppermute | solution.py:344
  442.2 23.8 %collective-permute-start.56 = (bf16[256,1024]{1,0:T(8,128)(2,1)S(1)}, bf16[256,1024]{1,0:T(8,128)(2,1)S(1)}, u32[]{:S(2)}, u32[]{:S(2)}) collective-permute-start(bf16[256,1024]{1,0:T(8,128)(2,1)S(1)} %copy-done.24), channel_id=1, source_target_pairs={{0,0},{1,1},{2,4},{3,5},{4,2},{5,3},{6,6},{7,7},{8,8},{9,9},{10,12... | collective-permute-start | bytes 1572872 | tf_op jit(solution)/shard_map/ppermute | solution.py:344
  451.5 24.3 %collective-permute-start.57 = (bf16[256,1024]{1,0:T(8,128)(2,1)S(1)}, bf16[256,1024]{1,0:T(8,128)(2,1)S(1)}, u32[]{:S(2)}, u32[]{:S(2)}) collective-permute-start(bf16[256,1024]{1,0:T(8,128)(2,1)S(1)} %copy-done.59), channel_id=1, source_target_pairs={{0,1},{1,0},{2,5},{3,4},{4,3},{5,2},{6,7},{7,6},{8,9},{9,8},{10,13... | collective-permute-start | bytes 1572872 | tf_op jit(solution)/shard_map/ppermute | solution.py:344
  456.5 20.8 %collective-permute-start.69 = (f32[3,32,512]{2,1,0:T(8,128)}, f32[3,32,512]{2,1,0:T(8,128)S(1)}, u32[]{:S(2)}, u32[]{:S(2)}) collective-permute-start(f32[3,32,512]{2,1,0:T(8,128)} %get-tuple-element.199), channel_id=1, source_target_pairs={{0,4},{1,5},{2,6},{3,7},{4,0},{5,1},{6,2},{7,3},{8,12},{9,13},{10,... | collective-permute-start | bytes 589832 | tf_op jit(solution)/shard_map/ppermute | solution.py:344
  (68 other events, 447.3 us)

commit v4 on v3

--- a/solution.py
+++ b/solution.py
@@ -1273,6 +1273,8 @@
     aa, ab = ring_first(attn_all, X_SWAP, Y_SWAP)
     da, db = ring_first(down_own, Z_UP, Z_DOWN)
     dc = ring_second(da, db, Z_UP, Z_DOWN)
+    ac = ring_outer_second(aa, ab, Y_SWAP, X_SWAP)
+
     in0, in1 = call(
         inputs_kernel,
         [inputs, segment_ids],
@@ -1280,10 +1282,9 @@
         "inputs_own",
         in_specs=[ANY, VMEM],
         scratch=[pltpu.SemaphoreType.DMA((2,))],
-        after=[attn_all],
+        after=[aa, ab, *dc],
     )
     got = [send(in0, SEQUENCE[0]), send(in1, SEQUENCE[1])]
-    ac = ring_outer_second(aa, ab, Y_SWAP, X_SWAP)
 
     def sequence_moves(ins, outs):
         _, cc, zz = place()
@@ -1296,27 +1297,33 @@
                 todo.append((piece.at[pl.ds(0, rows)], outs[0].at[at]))
                 if len(outs) > 1:
                     todo.append((piece.at[pl.ds(rows, 16)], outs[1].at[at]))
-        return todo
-
-    def whole_sequence(pieces, name, after=()):
-        more = pieces[0].shape[0] > rows
-        outs = [shape((2, 2, rows, width))] + [shape((2, 2, 16, width))] * more
-        return copies(pieces, outs, sequence_moves, 8 if more else 4, name, after=after)
-
-    x, segments = whole_sequence(got + [send(g, CORE_SWAP) for g in got], "inputs_whole")
+        return todo + ([(ins[4], outs[2])] if len(outs) > 1 else [])
+
+    def whole_sequence(pieces, name, after=(), more=()):
+        outs = [shape((2, 2, rows, width))]
+        if more:
+            outs += [shape((2, 2, 16, width)), shape(more[0].shape)]
+        return copies(
+            pieces + list(more), outs, sequence_moves, 9 if more else 4, name, after=after
+        )
+
+    down_all = copies(
+        [down_own, da, db, *dc],
+        [shape((4,) + down_own.shape)],
+        inner_moves,
+        5,
+        "down_inner",
+        after=[*ac, in0],
+    )[0]
+    ea, eb = ring_first(down_all, X_SWAP, Y_SWAP)
+    *got, _ = lax.optimization_barrier((*got, down_all))
+    x, segments, up_own = whole_sequence(
+        got + [send(g, CORE_SWAP) for g in got], "inputs_whole", more=[up_pay]
+    )
     x = x.reshape(total, width)
     segments = segments[:, :, 0, :rows].reshape(total).astype(F32)
     seg_col, seg_row = segments.reshape(total, 1), segments.reshape(1, total)
 
-    down_all, up_own = copies(
-        [down_own, da, db, *dc, up_pay],
-        [shape((4,) + down_own.shape), shape(up_pay.shape)],
-        lambda ins, outs: inner_moves(ins, outs) + [(ins[5], outs[1])],
-        6,
-        "down_inner",
-        after=ac,
-    )
-    ea, eb = ring_first(down_all, X_SWAP, Y_SWAP)
     ua, ub = ring_first(up_own, Z_UP, Z_DOWN)
 
     def attn_blocks(src, outs, yx, zz):
@@ -1360,20 +1367,20 @@
         cotangent_moves,
         2,
         "cotangent_own",
-        after=[ua, ub, normed],
+        after=[*uc, normed],
     )
     cot_got = [send(block, pairs) for block, pairs in zip(cots, SEQUENCE)]
-    heads = attend(qkv, seg_col, seg_row, size, 0, [], cots)
     ec = ring_outer_second(ea, eb, Y_SWAP, X_SWAP)
-    mixed, log = attend(qkv, seg_col, seg_row, size, 1, heads, [ea, eb])
     up_all = copies(
         [up_own, ua, ub, *uc],
         [shape((4,) + up_pay.shape)],
         inner_moves,
         5,
         "up_inner",
-        after=[*ec, mixed],
+        after=[*ec, normed],
     )[0]
+    heads = attend(qkv, seg_col, seg_row, size, 0, [], [up_all, *cots])
+    mixed, log = attend(qkv, seg_col, seg_row, size, 1, heads, [])
     fa, fb = ring_first(up_all, X_SWAP, Y_SWAP)
 
     def down_blocks(src, outs, yx, zz):
@@ -1388,10 +1395,10 @@
         lambda ins, outs: final_moves(ins, outs, down_blocks),
         32,
         "down_whole",
-        after=[up_all],
+        after=[mixed],
     )
     wdown, wout = wdown.reshape(units, width), wout.reshape(half, width)
-    part = rows_matmul(mixed, wout, NN, "attend_out")
+    part = rows_matmul(mixed, wout, NN, "attend_out", after=[fa, fb, *cot_got])
     middle, second = middle_norm(x, part, send(part, CORE_SWAP), bias_o, gain2, shift2)
     cot = whole_sequence(
         cot_got + [send(g, CORE_SWAP) for g in cot_got], "cotangent_whole", [part]
@@ -1414,52 +1421,41 @@
         return jnp.where((z & 1) == 0, jnp.stack(got), jnp.stack(got[::-1]))
 
     theirs, mine = output_rows(pos, hidden, wdown, middle, bias_d, [])
-    d = down_grads(pos, hidden, cot, down_rows, [mine])
+    part = rows_matmul(pre_grad, wup, NT, "second_grad", after=[mine])
+    d = down_grads(pos, hidden, cot, down_rows, [part])
     d_far = far_round(d)
+    u = up_grads(pos, second, pre_grad, lead, [d[4]])
+    u_far = far_round(u)
+    passed, d_got = near_round(d, d_far, "down", [u[4]])
     blocks = call(
         result_kernel,
         [mine, send(theirs, CORE_SWAP)],
         [shape((rows, width))] * 2,
         "result",
-        after=[d[4]],
+        after=[passed],
     )
     out_got = [send(block, pairs) for block, pairs in zip(blocks, SEQUENCE)]
-    u = up_grads(pos, second, pre_grad, lead, [blocks[0]])
-    u_far = far_round(u)
-    passed, d_got = near_round(d, d_far, "down", [u[4]])
-    part = rows_matmul(pre_grad, wup, NT, "second_grad", after=[passed])
-    passed, u_got = near_round(u, u_far, "up", [part])
     branch, middle_grad, mixed_grad, sums2 = middle_back(
-        part, send(part, CORE_SWAP), middle, cot, gain2, wout, [passed]
-    )
-
-    back = attend_back(qkv, log, mixed_grad, seg_col, seg_row, size, 0, [], out_got)
+        part, send(part, CORE_SWAP), middle, cot, gain2, wout, [blocks[0]]
+    )
+
+    passed, u_got = near_round(u, u_far, "up", [branch])
+    back = attend_back(qkv, log, mixed_grad, seg_col, seg_row, size, 0, [], [passed])
     output = to_tokens(out_got)
     d_joined = join(d, d_got, "down", after=[back[1]])
     d_came = inner_far(d_joined)
     grads, qv_bias_grad = attend_back(
         qkv, log, mixed_grad, seg_col, seg_row, size, 1, back, [d_joined[4]]
     )
-    passed, d_last = inner_near(d_joined, d_came, "down", [qv_bias_grad])
-    a = attn_grads(pos, normed, grads, mixed, branch, lead, [passed])
-    a_far = far_round(a)
-    u_joined = join(u, u_got, "up", after=[a[4], *d_last[1:]])
-    u_came = inner_far(u_joined)
+    passed, d_last = inner_near(d_joined, d_came, "down", [qv_bias_grad, *out_got])
+    u_joined = list(join(u, u_got, "up", after=[passed]))
     part = source_grad(grads, wqkv, [u_joined[4]])
     got = send(part, CORE_SWAP)
-    passed, u_last = inner_near(u_joined, u_came, "up", [part])
-    passed, a_got = near_round(a, a_far, "attn", [passed])
-    in0, in1, sums1 = input_back(pos, part, got, x, middle_grad, gain1, [passed])
+    a = attn_grads(pos, normed, grads, mixed, branch, lead, [part])
+    a_far = far_round(a)
+    in0, in1, sums1 = input_back(pos, part, got, x, middle_grad, gain1, [a[4], *d_last[1:]])
     in_got = [send(block, pairs) for block, pairs in zip((in0, in1), SEQUENCE)]
     input_grad = to_tokens(in_got).astype(F32)
-    down_out, up_kept, up_given = call(
-        feed_last_kernel,
-        d_last + u_last,
-        [shape(down_weight.shape, F32)] + [shape((lead, units), F32)] * 2,
-        "feed_last",
-        scratch=[pltpu.VMEM((2 * lead, units), F32)],
-        after=[in0],
-    )
 
     wide = jnp.stack([sums1[0], sums1[1], sums2[2], sums2[0], sums2[1], sums2[3]])
     wide = lax.dynamic_index_in_dim(wide.reshape(6, 4, 2, 4, lead), c, 2, keepdims=False)
@@ -1477,14 +1473,28 @@
     pick = lambda k: lax.dynamic_index_in_dim(tiny, o ^ k, 1, keepdims=False)
     extra = [pick(0), send(pick(1), X_SWAP), send(pick(2), Y_SWAP), send(pick(3), XY_FAR)]
 
-    joined = join(a, a_got, "attn", extra, [down_out])
-    _, attn_last = inner_near(joined, inner_far(joined), "attn")
+    passed, a_got = near_round(a, a_far, "attn", [in0, *extra[1:]])
+    joined = join(a, a_got, "attn", extra, in_got)
+    came = inner_far(joined)
+    *u_joined[:2], _ = lax.optimization_barrier((*u_joined[:2], joined[4]))
+    u_came = inner_far(u_joined)
+    passed, attn_last = inner_near(joined, came, "attn")
+    _, u_last = inner_near(u_joined, u_came, "up", [passed])
     qkv_kept, qkv_given, out_out, small_sum = call(
         attn_last_kernel,
         attn_last,
         [shape((3, lead, half), F32)] * 2 + [shape((lead, width), F32), shape((16, half), F32)],
         "attn_last",
         scratch=[pltpu.VMEM((8 * lead + 16, half), F32)],
+    )
+
+    down_out, up_kept, up_given = call(
+        feed_last_kernel,
+        d_last + u_last,
+        [shape(down_weight.shape, F32)] + [shape((lead, units), F32)] * 2,
+        "feed_last",
+        scratch=[pltpu.VMEM((2 * lead, units), F32)],
+        after=[small_sum],
     )
 
     def whole_columns(kept, got):

time: 488 us -> 473 us (0.969)
  starting transfers between devices: 81.9 us -> 73 us
  waiting for transfers between devices: 115 us -> 110 us
    ppermute x71, starting transfers between devices: 81.9 us -> 73 us  [send(): return lax.ppermute(value, AXES, pairs)]
    ppermute x71, waiting for transfers between devices: 115 us -> 110 us  [send(): return lax.ppermute(value, AXES, pairs)]
    unnamed x124 -> x140, local copies, waits for them, and re-layouts: 16.5 us -> 17.7 us
  transfers between devices with their start and end apart: 71 -> 71, of which waited for: 23 -> 22; matrix products, arithmetic and copies ran while one was open for 6% -> 6% of each run, Pallas kernels for 31% -> 33%
where the time goes in v4:
time: 473 us; the launch traced here: 465 us
  Pallas kernels  230 us (49%)
  waiting for transfers between devices  110 us (23%)
  starting transfers between devices  73 us (15%)
  local copies, waits for them, and re-layouts  42.4 us (9%)
  other arithmetic  7.21 us (2%)
    pallas_call x35, Pallas kernels, call(): pl.pallas_call(without(body, len(ins), len(after)), grid=grid, in_specs=l...  180 us
    ppermute x71, waiting for transfers between devices, send(): return lax.ppermute(value, AXES, pairs)  110 us
    ppermute x71, starting transfers between devices, send(): return lax.ppermute(value, AXES, pairs)  73 us
    pallas_call x5, Pallas kernels, placed_call(): pl.pallas_call(without(body, len(ins) + 1, len(after)), grid_spec=pltpu.P...  50.7 us
    unnamed x140, local copies, waits for them, and re-layouts  17.7 us
  transfers between devices with their start and end apart: 71, of which 22 were waited for; matrix products, arithmetic and copies ran while one was open for 6% of the time, Pallas kernels for 33%

profile of v4, /device:TPU:13, one launch (start us, length us, event | category | flops | bytes accessed | tf_op | source)
XLA Modules:
  0.0 465.1 jit_solution(2228154111124023583)
XLA Ops:
  7.3 2.0 second.1
  10.8 5.4 %collective-permute-done.3.refs_2_ = bf16[208,512]{1,0:T(8,128)(2,1)S(1)} collective-permute-done((bf16[208,512]{1,0:T(8,128)(2,1)}, bf16[208,512]{1,0:T(8,128)(2,1)S(1)}, u32[]{:S(2)}, u32[]{:S(2)}) %collective-permute-start.3) | collective-permute-done | bytes 213024 | tf_op jit(solution)/shard_map/ppermute | solution.py:344
  17.7 5.1 %collective-permute-done.2.refs_1_ = bf16[208,512]{1,0:T(8,128)(2,1)S(1)} collective-permute-done((bf16[208,512]{1,0:T(8,128)(2,1)}, bf16[208,512]{1,0:T(8,128)(2,1)S(1)}, u32[]{:S(2)}, u32[]{:S(2)}) %collective-permute-start.2) | collective-permute-done | bytes 213024 | tf_op jit(solution)/shard_map/ppermute | solution.py:344
  22.9 4.1 collective-permute-done.4.refs_3_
  28.2 2.4 attn_inner.2
  33.8 15.4 %collective-permute-done.6.refs_2_.refs_1_ = bf16[4,208,512]{2,1,0:T(8,128)(2,1)S(1)} collective-permute-done((bf16[4,208,512]{2,1,0:T(8,128)(2,1)}, bf16[4,208,512]{2,1,0:T(8,128)(2,1)S(1)}, u32[]{:S(2)}, u32[]{:S(2)}) %collective-permute-start.6) | collective-permute-done | bytes 852000 | tf_op jit(solution)/shard_map/ppermute | solution.py:344
  53.2 2.2 collective-permute-start.9
  55.4 2.9 collective-permute-done.11.refs_5_.refs_4_
  58.3 4.6 collective-permute-done.9.refs_4_.refs_3_
  62.9 2.9 inputs_own.1
  66.7 2.4 down_inner.2.refs_5_.refs_0_
  70.7 6.6 %collective-permute-start.12 = (bf16[272,1024]{1,0:T(8,128)(2,1)}, bf16[272,1024]{1,0:T(8,128)(2,1)}, u32[]{:S(2)}, u32[]{:S(2)}) collective-permute-start(bf16[272,1024]{1,0:T(8,128)(2,1)} %get-tuple-element.118.refs_7_), channel_id=1, source_target_pairs={{0,0},{1,1},{2,4},{3,5},{4,2},{5,3},{6,6},{7,7},{8,8},{9,9},{10,12... | collective-permute-start | bytes 1671176 | tf_op jit(solution)/shard_map/ppermute | solution.py:344
  77.4 4.7 %attn_whole.1 = (bf16[3,4,2,4,32,512]{5,4,3,2,1,0:T(8,128)(2,1)}, bf16[4,4,16,512]{3,2,1,0:T(8,128)(2,1)}) custom-call(bf16[4,208,512]{2,1,0:T(8,128)(2,1)} %get-tuple-element.116.refs_0_, bf16[4,208,512]{2,1,0:T(8,128)(2,1)} %copy-done.2, bf16[4,208,512]{2,1,0:T(8,128)(2,1)} %copy-done.3, bf16[2,208,512]{2,1,0:T(8,128)(2,1)} %copy-done.20, ...), custom_call_target="tpu_custom_call" | custom-call | bytes 6815744 | tf_op jit(solution)/shard_map/attn_whole/pallas_call | solution.py:385
  83.2 11.3 %collective-permute-done.12.refs_0_ = bf16[272,1024]{1,0:T(8,128)(2,1)} collective-permute-done((bf16[272,1024]{1,0:T(8,128)(2,1)}, bf16[272,1024]{1,0:T(8,128)(2,1)}, u32[]{:S(2)}, u32[]{:S(2)}) %collective-permute-start.12) | collective-permute-done | bytes 557088 | tf_op jit(solution)/shard_map/ppermute | solution.py:344
  94.5 7.6 %collective-permute-done.13.refs_1_ = bf16[272,1024]{1,0:T(8,128)(2,1)} collective-permute-done((bf16[272,1024]{1,0:T(8,128)(2,1)}, bf16[272,1024]{1,0:T(8,128)(2,1)}, u32[]{:S(2)}, u32[]{:S(2)}) %collective-permute-start.13) | collective-permute-done | bytes 557088 | tf_op jit(solution)/shard_map/ppermute | solution.py:344
  106.1 3.2 inputs_whole.1
  113.1 3.9 collective-permute-done.18.refs_1_
  117.5 4.5 collective-permute-done.19.refs_2_
  122.0 2.3 collective-permute-start.21
  124.3 8.2 %project.1 = (bf16[1024,1024]{1,0:T(8,128)(2,1)}, bf16[3,1024,512]{2,1,0:T(8,128)(2,1)}) custom-call(bf16[1024,1024]{1,0:T(8,128)(2,1)} %bitcast.73, f32[1,1024]{1,0:T(1,128)} %slice.210.gain.refs_5_, f32[1,1024]{1,0:T(1,128)} %slice.212.shift, bf16[3,1024,512]{2,1,0:T(8,128)(2,1)} %bitcast.101, f32[3,512]{1,0:T(4,128)} %maximum_convert_fusion.bias), custom_call_target="tpu_custom_call" | custom-call | flops 3221225472 | bytes 10500096 | tf_op jit(solution)/shard_map/project/pallas_call | solution.py:385
  133.5 2.2 up_inner.2.refs_5_.refs_0_
  139.0 2.2 cotangent_own.1
  141.2 5.1 %collective-permute-start.28 = (bf16[256,1024]{1,0:T(8,128)(2,1)}, bf16[256,1024]{1,0:T(8,128)(2,1)S(1)}, u32[]{:S(2)}, u32[]{:S(2)}) collective-permute-start(bf16[256,1024]{1,0:T(8,128)(2,1)} %get-tuple-element.130.refs_6_), channel_id=1, source_target_pairs={{0,0},{1,1},{2,4},{3,5},{4,2},{5,3},{6,6},{7,7},{8,8},{9,9},{10,12... | collective-permute-start | bytes 1572872 | tf_op jit(solution)/shard_map/ppermute | solution.py:344
  146.4 10.4 %attend.2 = (bf16[1024,512]{1,0:T(8,128)(2,1)}, f32[1024,512]{1,0:T(8,128)}) custom-call(f32[1024,1]{1,0:T(8,128)} %copy.72.refs_0_.column, f32[1,1024]{1,0:T(1,128)} %bitcast.92, bf16[3,1024,512]{2,1,0:T(8,128)(2,1)} %get-tuple-element.127.refs_2_.refs_3_.refs_4_.q_ref.k_ref.v_ref, ...), custom_call_target="tpu_custom_call" | custom-call | flops 4294967296 | bytes 12591104 | tf_op jit(solution)/shard_map/attend/pallas_call | solution.py:385
  156.8 10.2 %attend.3 = (bf16[1024,512]{1,0:T(8,128)(2,1)}, f32[1024,512]{1,0:T(8,128)}) custom-call(f32[1024,1]{1,0:T(8,128)} %copy.72.refs_0_.column, f32[1,1024]{1,0:T(1,128)} %bitcast.93, bf16[3,1024,512]{2,1,0:T(8,128)(2,1)} %get-tuple-element.127.refs_2_.refs_3_.refs_4_.q_ref.k_ref.v_ref, ...), custom_call_target="tpu_custom_call", output_to_operand_aliasing={{0}: (5, {}), {1}: (6, {})} | custom-call | flops 4294967296 | bytes 15736832 | tf_op jit(solution)/shard_map/attend/pallas_call | solution.py:385
  167.0 5.1 %down_whole.1 = (bf16[4,4,128,1024]{3,2,1,0:T(8,128)(2,1)}, bf16[4,4,32,1024]{3,2,1,0:T(8,128)(2,1)}) custom-call(bf16[4,160,1024]{2,1,0:T(8,128)(2,1)} %down_inner.2.refs_5_.refs_0_, bf16[4,160,1024]{2,1,0:T(8,128)(2,1)} %copy-done.4, bf16[4,160,1024]{2,1,0:T(8,128)(2,1)} %copy-done.5, bf16[2,160,1024]{2,1,0:T(8,128)(2,1)} %copy-done.6, ...), custom_call_target="tpu_custom_call" | custom-call | bytes 10485760 | tf_op jit(solution)/shard_map/down_whole/pallas_call | solution.py:385
  173.8 4.8 %attend_out.1.part.refs_4_ = bf16[1024,1024]{1,0:T(8,128)(2,1)} custom-call(bf16[1024,512]{1,0:T(8,128)(2,1)} %get-tuple-element.134.refs_5_.refs_0_.refs_3_, bf16[512,1024]{1,0:T(8,128)(2,1)} %bitcast.78, bf16[4,64,2048]{2,1,0:T(8,128)(2,1)} %copy-done, bf16[4,64,2048]{2,1,0:T(8,128)(2,1)} %copy-done.1, bf16[256,1024]{1,0:T(8,128)(2,1)} %copy-done.7, ...), custom_call_target="tpu_custom_call" | custom-call | flops 1073741824 | bytes 4194304 | tf_op jit(solution)/shard_map/attend_out/pallas_call | solution.py:385
  180.7 1.9 slice.279
  182.8 1.9 slice.280
  189.9 2.9 cotangent_whole.1
  194.1 6.1 %middle.1 = (f32[1024,1024]{1,0:T(8,128)}, bf16[1024,1024]{1,0:T(8,128)(2,1)}) custom-call(bf16[1024,1024]{1,0:T(8,128)(2,1)} %bitcast.74, bf16[1024,1024]{1,0:T(8,128)(2,1)} %attend_out.1.part.refs_4_, bf16[1024,1024]{1,0:T(8,128)(2,1)} %copy-done.13, f32[1,1024]{1,0:T(1,128)} %slice.222.bias, f32[1,1024]{1,0:T(1,128)} %slice.224.gain.refs_4_, ...), custom_call_target="tpu_custom_call" | custom-call | bytes 12595200 | tf_op jit(solution)/shard_map/middle/pallas_call | solution.py:385
  201.2 4.5 up_whole.1
  205.7 16.3 %feed.1 = (bf16[1024,2048]{1,0:T(8,128)(2,1)}, bf16[1024,2048]{1,0:T(8,128)(2,1)}, f32[1,2048]{1,0:T(1,128)}) custom-call(bf16[1024,1024]{1,0:T(8,128)(2,1)} %get-tuple-element.136.refs_5_.second.refs_1_, bf16[1024,1024]{1,0:T(8,128)(2,1)} %bitcast.70, bf16[1024,2048]{1,0:T(8,128)(2,1)} %bitcast.76, f32[1,2048]{1,0:T(1,128)} %convert.28.bias, ...), custom_call_target="tpu_custom_call" | custom-call | flops 8589934592 | bytes 20987904 | tf_op jit(solution)/shard_map/feed/pallas_call | solution.py:385
  222.0 10.5 %output_rows.1 = (bf16[512,1024]{1,0:T(8,128)(2,1)}, f32[512,1024]{1,0:T(8,128)}) custom-call(s32[3]{0:T(128)} %pad_add_fusion.1.pos.refs_0_, bf16[1024,2048]{1,0:T(8,128)(2,1)} %get-tuple-element.138.hidden.refs_1_, bf16[2048,1024]{1,0:T(8,128)(2,1)} %bitcast.100, f32[1024,1024]{1,0:T(8,128)} %get-tuple-element.139.middle.refs_2_, f32[1,1024]{1,0:T(1,128)} %slice.231.bias), custom_call_target="tpu_custom_call" | custom-call | flops 4294967296 | bytes 15732736 | tf_op jit(solution)/shard_map/output_rows/pallas_call | solution.py:401
  232.6 8.8 %second_grad.1.refs_3_.refs_0_ = bf16[1024,1024]{1,0:T(8,128)(2,1)} custom-call(bf16[1024,2048]{1,0:T(8,128)(2,1)} %get-tuple-element.142.refs_0_.refs_2_, bf16[1024,2048]{1,0:T(8,128)(2,1)} %bitcast.77, f32[512,1024]{1,0:T(8,128)} %get-tuple-element.140.refs_2_.refs_0_), custom_call_target="tpu_custom_call" | custom-call | flops 4294967296 | bytes 10485760 | tf_op jit(solution)/shard_map/second_grad/pallas_call | solution.py:385
  242.1 10.3 %down_grads.1 = (bf16[2,128,1024]{2,1,0:T(8,128)(2,1)}, bf16[2,128,1024]{2,1,0:T(8,128)(2,1)}, bf16[4,128,1024]{2,1,0:T(8,128)(2,1)}, bf16[4,128,1024]{2,1,0:T(8,128)(2,1)}, bf16[4,128,1024]{2,1,0:T(8,128)(2,1)}) custom-call(s32[3]{0:T(128)} %pad_add_fusion.1.pos.refs_0_, bf16[1024,2048]{1,0:T(8,128)(2,1)} %get-tuple-element.138.hidden.refs_1_, ...), custom_call_target="tpu_custom_call" | custom-call | flops 4294967296 | bytes 10485760 | tf_op jit(solution)/shard_map/down_grads/pallas_call | solution.py:401
  253.8 10.6 %up_grads.1 = (bf16[2,64,2048]{2,1,0:T(8,128)(2,1)}, bf16[2,64,2048]{2,1,0:T(8,128)(2,1)}, bf16[4,64,2048]{2,1,0:T(8,128)(2,1)}, bf16[4,64,2048]{2,1,0:T(8,128)(2,1)}, bf16[4,64,2048]{2,1,0:T(8,128)(2,1)}) custom-call(s32[3]{0:T(128)} %pad_add_fusion.1.pos.refs_0_, bf16[1024,1024]{1,0:T(8,128)(2,1)} %get-tuple-element.136.refs_5_.second.refs_1_, ...), custom_call_target="tpu_custom_call" | custom-call | flops 4294967296 | bytes 10485760 | tf_op jit(solution)/shard_map/up_grads/pallas_call | solution.py:401
  267.0 3.3 down_pass.1
  271.4 3.0 result.1
  274.4 4.5 collective-permute-start.38
  278.9 9.9 %middle_back.1 = (bf16[1024,1024]{1,0:T(8,128)(2,1)}, f32[1024,1024]{1,0:T(8,128)}, bf16[1024,512]{1,0:T(8,128)(2,1)}, f32[4,1024]{1,0:T(4,128)}) custom-call(bf16[1024,1024]{1,0:T(8,128)(2,1)} %second_grad.1.refs_3_.refs_0_, bf16[1024,1024]{1,0:T(8,128)(2,1)} %copy-done.19, f32[1024,1024]{1,0:T(8,128)} %get-tuple-element.139.middle.refs_2_, ...), custom_call_target="tpu_custom_call" | custom-call | flops 1073741824 | bytes 18894848 | tf_op jit(solution)/shard_map/middle_back/pallas_call | solution.py:385
  289.6 3.3 up_pass.1
  294.5 13.6 %attend_back.2 = (bf16[3,1024,512]{2,1,0:T(8,128)(2,1)}, f32[2,512]{1,0:T(2,128)}) custom-call(f32[1024,1]{1,0:T(8,128)} %copy.72.refs_0_.column, f32[1,1024]{1,0:T(1,128)} %bitcast.94, bf16[3,1024,512]{2,1,0:T(8,128)(2,1)} %get-tuple-element.127.refs_2_.refs_3_.refs_4_.q_ref.k_ref.v_ref, ...), custom_call_target="tpu_custom_call" | custom-call | flops 6442450944 | bytes 15740928 | tf_op jit(solution)/shard_map/attend_back/pallas_call | solution.py:385
  308.6 3.4 down_join.1
  313.6 14.0 %attend_back.3 = (bf16[3,1024,512]{2,1,0:T(8,128)(2,1)}, f32[2,512]{1,0:T(2,128)}) custom-call(f32[1024,1]{1,0:T(8,128)} %copy.72.refs_0_.column, f32[1,1024]{1,0:T(1,128)} %bitcast.95, bf16[3,1024,512]{2,1,0:T(8,128)(2,1)} %get-tuple-element.127.refs_2_.refs_3_.refs_4_.q_ref.k_ref.v_ref, ...), custom_call_target="tpu_custom_call", output_to_operand_aliasing={{0}: (7, {}), {1}: (8, {})} | custom-call | flops 6442450944 | bytes 18890752 | tf_op jit(solution)/shard_map/attend_back/pallas_call | solution.py:385
  328.4 2.0 down_inner.3
  331.7 3.4 up_join.1
  335.1 7.4 %source_grad.1.refs_5_.refs_1_ = bf16[1024,1024]{1,0:T(8,128)(2,1)} custom-call(bf16[3,1024,512]{2,1,0:T(8,128)(2,1)} %get-tuple-element.164.refs_0_.refs_2_, bf16[3,1024,512]{2,1,0:T(8,128)(2,1)} %bitcast.102, f32[64,2048]{1,0:T(8,128)} %get-tuple-element.172.refs_2_.refs_3_), custom_call_target="tpu_custom_call" | custom-call | flops 3221225472 | bytes 8388608 | tf_op jit(solution)/shard_map/source_grad/pallas_call | solution.py:385
  346.5 11.2 %attn_grads.1 = (bf16[2,256,512]{2,1,0:T(8,128)(2,1)}, bf16[2,256,512]{2,1,0:T(8,128)(2,1)}, bf16[4,256,512]{2,1,0:T(8,128)(2,1)}, bf16[4,256,512]{2,1,0:T(8,128)(2,1)}, bf16[4,256,512]{2,1,0:T(8,128)(2,1)}) custom-call(s32[3]{0:T(128)} %pad_add_fusion.1.pos.refs_0_, bf16[1024,1024]{1,0:T(8,128)(2,1)} %get-tuple-element.129.refs_7_.refs_3_.refs_1_, ...), custom_call_target="tpu_custom_call" | custom-call | flops 4294967296 | bytes 12582912 | tf_op jit(solution)/shard_map/attn_grads/pallas_call | solution.py:401
  360.4 8.2 %input_back.1 = (bf16[256,1024]{1,0:T(8,128)(2,1)}, bf16[256,1024]{1,0:T(8,128)(2,1)}, f32[2,1024]{1,0:T(2,128)}) custom-call(s32[3]{0:T(128)} %pad_add_fusion.1.pos.refs_0_, bf16[1024,1024]{1,0:T(8,128)(2,1)} %source_grad.1.refs_5_.refs_1_, bf16[1024,1024]{1,0:T(8,128)(2,1)} %copy-done.18, bf16[1024,1024]{1,0:T(8,128)(2,1)} %bitcast.75, ...), custom_call_target="tpu_custom_call" | custom-call | bytes 11546624 | tf_op jit(solution)/shard_map/input_back/pallas_call | solution.py:401
  374.7 1.8 collective-permute-done.58.refs_7_.refs_6_
  377.1 3.3 attn_pass.1
  381.9 6.8 %collective-permute-start.52 = (bf16[256,1024]{1,0:T(8,128)(2,1)S(1)}, bf16[256,1024]{1,0:T(8,128)(2,1)S(1)}, u32[]{:S(2)}, u32[]{:S(2)}) collective-permute-start(bf16[256,1024]{1,0:T(8,128)(2,1)S(1)} %copy-done.36), channel_id=1, source_target_pairs={{0,0},{1,1},{2,4},{3,5},{4,2},{5,3},{6,6},{7,7},{8,8},{9,9},{10,12... | collective-permute-start | bytes 1572872 | tf_op jit(solution)/shard_map/ppermute | solution.py:344
  389.6 9.7 %collective-permute-done.52.refs_7_ = bf16[256,1024]{1,0:T(8,128)(2,1)S(1)} collective-permute-done((bf16[256,1024]{1,0:T(8,128)(2,1)S(1)}, bf16[256,1024]{1,0:T(8,128)(2,1)S(1)}, u32[]{:S(2)}, u32[]{:S(2)}) %collective-permute-start.52) | collective-permute-done | bytes 524320 | tf_op jit(solution)/shard_map/ppermute | solution.py:344
  399.4 13.0 %collective-permute-done.53.refs_8_ = bf16[256,1024]{1,0:T(8,128)(2,1)S(1)} collective-permute-done((bf16[256,1024]{1,0:T(8,128)(2,1)}, bf16[256,1024]{1,0:T(8,128)(2,1)S(1)}, u32[]{:S(2)}, u32[]{:S(2)}) %collective-permute-start.53) | collective-permute-done | bytes 524320 | tf_op jit(solution)/shard_map/ppermute | solution.py:344
  413.9 3.6 attn_join.1
  420.4 2.4 collective-permute-done.61.t1
  424.6 2.0 attn_inner.3
  429.2 2.6 collective-permute-done.67.refs_3_
  432.4 2.0 up_inner.3
  437.3 7.5 %collective-permute-done.64.p2 = bf16[272,512]{1,0:T(8,128)(2,1)S(1)} collective-permute-done((bf16[272,512]{1,0:T(8,128)(2,1)}, bf16[272,512]{1,0:T(8,128)(2,1)S(1)}, u32[]{:S(2)}, u32[]{:S(2)}) %collective-permute-start.64) | collective-permute-done | bytes 278560 | tf_op jit(solution)/shard_map/ppermute | solution.py:344
  445.6 2.1 attn_last.1
  449.2 4.1 collective-permute-done.69.refs_5_
  454.0 2.6 feed_last.1
  (341 shorter events, 97.4 us)
Async XLA Ops:
  9.3 6.8 %collective-permute-start.3 = (bf16[208,512]{1,0:T(8,128)(2,1)}, bf16[208,512]{1,0:T(8,128)(2,1)S(1)}, u32[]{:S(2)}, u32[]{:S(2)}) collective-permute-start(bf16[208,512]{1,0:T(8,128)(2,1)} %get-tuple-element.115.refs_0_), channel_id=1, source_target_pairs={{0,3},{1,0},{2,1},{3,2},{4,7},{5,4},{6,5},{7,6},{8,11},{9,8},{10,9... | collective-permute-start | bytes 638984 | tf_op jit(solution)/shard_map/ppermute | solution.py:344
  9.5 13.3 %collective-permute-start.2 = (bf16[208,512]{1,0:T(8,128)(2,1)}, bf16[208,512]{1,0:T(8,128)(2,1)S(1)}, u32[]{:S(2)}, u32[]{:S(2)}) collective-permute-start(bf16[208,512]{1,0:T(8,128)(2,1)} %get-tuple-element.115.refs_0_), channel_id=1, source_target_pairs={{0,1},{1,2},{2,3},{3,0},{4,5},{5,6},{6,7},{7,4},{8,9},{9,10},{10,1... | collective-permute-start | bytes 638984 | tf_op jit(solution)/shard_map/ppermute | solution.py:344
  16.2 10.8 %collective-permute-start.5 = (bf16[112,512]{1,0:T(8,128)(2,1)S(1)}, bf16[112,512]{1,0:T(8,128)(2,1)S(1)}, u32[]{:S(2)}, u32[]{:S(2)}) collective-permute-start(bf16[112,512]{1,0:T(8,128)(2,1)S(1)} %slice.261), channel_id=1, source_target_pairs={{0,3},{1,0},{2,1},{3,2},{4,7},{5,4},{6,5},{7,6},{8,11},{9,8},{10,9... | collective-permute-start | bytes 344072 | tf_op jit(solution)/shard_map/ppermute | solution.py:344
  22.8 4.1 collective-permute-start.4
  30.7 18.6 %collective-permute-start.6 = (bf16[4,208,512]{2,1,0:T(8,128)(2,1)}, bf16[4,208,512]{2,1,0:T(8,128)(2,1)S(1)}, u32[]{:S(2)}, u32[]{:S(2)}) collective-permute-start(bf16[4,208,512]{2,1,0:T(8,128)(2,1)} %get-tuple-element.116.refs_0_), channel_id=1, source_target_pairs={{0,8},{1,9},{2,10},{3,11},{4,12},{5,13},{6,14},{7,15},{8,0},{9,1},... | collective-permute-start | bytes 2555912 | tf_op jit(solution)/shard_map/ppermute | solution.py:344
  31.9 18.4 %collective-permute-start.7 = (bf16[4,208,512]{2,1,0:T(8,128)(2,1)}, bf16[4,208,512]{2,1,0:T(8,128)(2,1)S(1)}, u32[]{:S(2)}, u32[]{:S(2)}) collective-permute-start(bf16[4,208,512]{2,1,0:T(8,128)(2,1)} %get-tuple-element.116.refs_0_), channel_id=1, source_target_pairs={{0,16},{1,17},{2,18},{3,19},{4,20},{5,21},{6,22},{7,23},{8,24},{9,... | collective-permute-start | bytes 2555912 | tf_op jit(solution)/shard_map/ppermute | solution.py:344
  32.2 20.2 %collective-permute-start.10 = (bf16[160,1024]{1,0:T(8,128)(2,1)}, bf16[160,1024]{1,0:T(8,128)(2,1)S(1)}, u32[]{:S(2)}, u32[]{:S(2)}) collective-permute-start(bf16[160,1024]{1,0:T(8,128)(2,1)} %get-tuple-element.117.refs_0_), channel_id=1, source_target_pairs={{0,3},{1,0},{2,1},{3,2},{4,7},{5,4},{6,5},{7,6},{8,11},{9,8},{10,9... | collective-permute-start | bytes 983048 | tf_op jit(solution)/shard_map/ppermute | solution.py:344
  33.5 19.6 %collective-permute-start.8 = (bf16[160,1024]{1,0:T(8,128)(2,1)}, bf16[160,1024]{1,0:T(8,128)(2,1)S(1)}, u32[]{:S(2)}, u32[]{:S(2)}) collective-permute-start(bf16[160,1024]{1,0:T(8,128)(2,1)} %get-tuple-element.117.refs_0_), channel_id=1, source_target_pairs={{0,1},{1,2},{2,3},{3,0},{4,5},{5,6},{6,7},{7,4},{8,9},{9,10},{10,1... | collective-permute-start | bytes 983048 | tf_op jit(solution)/shard_map/ppermute | solution.py:344
  50.1 15.7 %collective-permute-start.14 = (bf16[2,208,512]{2,1,0:T(8,128)(2,1)}, bf16[2,208,512]{2,1,0:T(8,128)(2,1)S(1)}, u32[]{:S(2)}, u32[]{:S(2)}) collective-permute-start(bf16[2,208,512]{2,1,0:T(8,128)(2,1)} %slice.264), channel_id=1, source_target_pairs={{0,16},{1,17},{2,18},{3,19},{4,20},{5,21},{6,22},{7,23},{8,24},{9,... | collective-permute-start | bytes 1277960 | tf_op jit(solution)/shard_map/ppermute | solution.py:344
  51.1 14.7 %collective-permute-start.15 = (bf16[2,208,512]{2,1,0:T(8,128)(2,1)}, bf16[2,208,512]{2,1,0:T(8,128)(2,1)S(1)}, u32[]{:S(2)}, u32[]{:S(2)}) collective-permute-start(bf16[2,208,512]{2,1,0:T(8,128)(2,1)} %slice.265), channel_id=1, source_target_pairs={{0,8},{1,9},{2,10},{3,11},{4,12},{5,13},{6,14},{7,15},{8,0},{9,1},... | collective-permute-start | bytes 1277960 | tf_op jit(solution)/shard_map/ppermute | solution.py:344
  52.4 5.9 %collective-permute-start.11 = (bf16[80,1024]{1,0:T(8,128)(2,1)S(1)}, bf16[80,1024]{1,0:T(8,128)(2,1)S(1)}, u32[]{:S(2)}, u32[]{:S(2)}) collective-permute-start(bf16[80,1024]{1,0:T(8,128)(2,1)S(1)} %slice.263), channel_id=1, source_target_pairs={{0,3},{1,0},{2,1},{3,2},{4,7},{5,4},{6,5},{7,6},{8,11},{9,8},{10,9... | collective-permute-start | bytes 491528 | tf_op jit(solution)/shard_map/ppermute | solution.py:344
  53.2 9.7 %collective-permute-start.9 = (bf16[80,1024]{1,0:T(8,128)(2,1)S(1)}, bf16[80,1024]{1,0:T(8,128)(2,1)}, u32[]{:S(2)}, u32[]{:S(2)}) collective-permute-start(bf16[80,1024]{1,0:T(8,128)(2,1)S(1)} %slice.262), channel_id=1, source_target_pairs={{0,1},{1,2},{2,3},{3,0},{4,5},{5,6},{6,7},{7,4},{8,9},{9,10},{10,1... | collective-permute-start | bytes 491528 | tf_op jit(solution)/shard_map/ppermute | solution.py:344
  69.1 33.6 %collective-permute-start.22 = (bf16[4,160,1024]{2,1,0:T(8,128)(2,1)}, bf16[4,160,1024]{2,1,0:T(8,128)(2,1)S(1)}, u32[]{:S(2)}, u32[]{:S(2)}) collective-permute-start(bf16[4,160,1024]{2,1,0:T(8,128)(2,1)} %down_inner.2.refs_5_.refs_0_), channel_id=1, source_target_pairs={{0,8},{1,9},{2,10},{3,11},{4,12},{5,13},{6,14},{7,15},{8,0},{9,1},... | collective-permute-start | bytes 3932168 | tf_op jit(solution)/shard_map/ppermute | solution.py:344
  69.4 34.5 %collective-permute-start.24 = (bf16[4,160,1024]{2,1,0:T(8,128)(2,1)}, bf16[4,160,1024]{2,1,0:T(8,128)(2,1)S(1)}, u32[]{:S(2)}, u32[]{:S(2)}) collective-permute-start(bf16[4,160,1024]{2,1,0:T(8,128)(2,1)} %down_inner.2.refs_5_.refs_0_), channel_id=1, source_target_pairs={{0,16},{1,17},{2,18},{3,19},{4,20},{5,21},{6,22},{7,23},{8,24},{9,... | collective-permute-start | bytes 3932168 | tf_op jit(solution)/shard_map/ppermute | solution.py:344
  70.7 23.9 %collective-permute-start.12 = (bf16[272,1024]{1,0:T(8,128)(2,1)}, bf16[272,1024]{1,0:T(8,128)(2,1)}, u32[]{:S(2)}, u32[]{:S(2)}) collective-permute-start(bf16[272,1024]{1,0:T(8,128)(2,1)} %get-tuple-element.118.refs_7_), channel_id=1, source_target_pairs={{0,0},{1,1},{2,4},{3,5},{4,2},{5,3},{6,6},{7,7},{8,8},{9,9},{10,12... | collective-permute-start | bytes 1671176 | tf_op jit(solution)/shard_map/ppermute | solution.py:344
  77.3 24.8 %collective-permute-start.13 = (bf16[272,1024]{1,0:T(8,128)(2,1)}, bf16[272,1024]{1,0:T(8,128)(2,1)}, u32[]{:S(2)}, u32[]{:S(2)}) collective-permute-start(bf16[272,1024]{1,0:T(8,128)(2,1)} %get-tuple-element.119), channel_id=1, source_target_pairs={{0,1},{1,0},{2,5},{3,4},{4,3},{5,2},{6,7},{7,6},{8,9},{9,8},{10,13... | collective-permute-start | bytes 1671176 | tf_op jit(solution)/shard_map/ppermute | solution.py:344
  103.7 28.9 %collective-permute-start.23 = (bf16[2,160,1024]{2,1,0:T(8,128)(2,1)}, bf16[2,160,1024]{2,1,0:T(8,128)(2,1)S(1)}, u32[]{:S(2)}, u32[]{:S(2)}) collective-permute-start(bf16[2,160,1024]{2,1,0:T(8,128)(2,1)} %slice.274), channel_id=1, source_target_pairs={{0,16},{1,17},{2,18},{3,19},{4,20},{5,21},{6,22},{7,23},{8,24},{9,... | collective-permute-start | bytes 1966088 | tf_op jit(solution)/shard_map/ppermute | solution.py:344
  104.8 27.7 %collective-permute-start.25 = (bf16[2,160,1024]{2,1,0:T(8,128)(2,1)}, bf16[2,160,1024]{2,1,0:T(8,128)(2,1)}, u32[]{:S(2)}, u32[]{:S(2)}) collective-permute-start(bf16[2,160,1024]{2,1,0:T(8,128)(2,1)} %slice.275), channel_id=1, source_target_pairs={{0,8},{1,9},{2,10},{3,11},{4,12},{5,13},{6,14},{7,15},{8,0},{9,1},... | collective-permute-start | bytes 1966088 | tf_op jit(solution)/shard_map/ppermute | solution.py:344
  109.3 7.7 %collective-permute-start.18 = (bf16[64,2048]{1,0:T(8,128)(2,1)}, bf16[64,2048]{1,0:T(8,128)(2,1)S(1)}, u32[]{:S(2)}, u32[]{:S(2)}) collective-permute-start(bf16[64,2048]{1,0:T(8,128)(2,1)} %get-tuple-element.128.refs_0_), channel_id=1, source_target_pairs={{0,1},{1,2},{2,3},{3,0},{4,5},{5,6},{6,7},{7,4},{8,9},{9,10},{10,1... | collective-permute-start | bytes 786440 | tf_op jit(solution)/shard_map/ppermute | solution.py:344
  110.3 11.7 %collective-permute-start.19 = (bf16[64,2048]{1,0:T(8,128)(2,1)}, bf16[64,2048]{1,0:T(8,128)(2,1)S(1)}, u32[]{:S(2)}, u32[]{:S(2)}) collective-permute-start(bf16[64,2048]{1,0:T(8,128)(2,1)} %get-tuple-element.128.refs_0_), channel_id=1, source_target_pairs={{0,3},{1,0},{2,1},{3,2},{4,7},{5,4},{6,5},{7,6},{8,11},{9,8},{10,9... | collective-permute-start | bytes 786440 | tf_op jit(solution)/shard_map/ppermute | solution.py:344
  117.0 15.5 %collective-permute-start.20 = (bf16[32,2048]{1,0:T(8,128)(2,1)S(1)}, bf16[32,2048]{1,0:T(8,128)(2,1)S(1)}, u32[]{:S(2)}, u32[]{:S(2)}) collective-permute-start(bf16[32,2048]{1,0:T(8,128)(2,1)S(1)} %slice.272), channel_id=1, source_target_pairs={{0,1},{1,2},{2,3},{3,0},{4,5},{5,6},{6,7},{7,4},{8,9},{9,10},{10,1... | collective-permute-start | bytes 393224 | tf_op jit(solution)/shard_map/ppermute | solution.py:344
  122.0 10.5 %collective-permute-start.21 = (bf16[32,2048]{1,0:T(8,128)(2,1)S(1)}, bf16[32,2048]{1,0:T(8,128)(2,1)S(1)}, u32[]{:S(2)}, u32[]{:S(2)}) collective-permute-start(bf16[32,2048]{1,0:T(8,128)(2,1)S(1)} %slice.273), channel_id=1, source_target_pairs={{0,3},{1,0},{2,1},{3,2},{4,7},{5,4},{6,5},{7,6},{8,11},{9,8},{10,9... | collective-permute-start | bytes 393224 | tf_op jit(solution)/shard_map/ppermute | solution.py:344
  135.6 36.5 %collective-permute-start.26 = (bf16[4,64,2048]{2,1,0:T(8,128)(2,1)}, bf16[4,64,2048]{2,1,0:T(8,128)(2,1)S(1)}, u32[]{:S(2)}, u32[]{:S(2)}) collective-permute-start(bf16[4,64,2048]{2,1,0:T(8,128)(2,1)} %up_inner.2.refs_5_.refs_0_), channel_id=1, source_target_pairs={{0,8},{1,9},{2,10},{3,11},{4,12},{5,13},{6,14},{7,15},{8,0},{9,1},... | collective-permute-start | bytes 3145736 | tf_op jit(solution)/shard_map/ppermute | solution.py:344
  136.9 35.3 %collective-permute-start.27 = (bf16[4,64,2048]{2,1,0:T(8,128)(2,1)}, bf16[4,64,2048]{2,1,0:T(8,128)(2,1)S(1)}, u32[]{:S(2)}, u32[]{:S(2)}) collective-permute-start(bf16[4,64,2048]{2,1,0:T(8,128)(2,1)} %up_inner.2.refs_5_.refs_0_), channel_id=1, source_target_pairs={{0,16},{1,17},{2,18},{3,19},{4,20},{5,21},{6,22},{7,23},{8,24},{9,... | collective-permute-start | bytes 3145736 | tf_op jit(solution)/shard_map/ppermute | solution.py:344
  141.2 31.0 %collective-permute-start.28 = (bf16[256,1024]{1,0:T(8,128)(2,1)}, bf16[256,1024]{1,0:T(8,128)(2,1)S(1)}, u32[]{:S(2)}, u32[]{:S(2)}) collective-permute-start(bf16[256,1024]{1,0:T(8,128)(2,1)} %get-tuple-element.130.refs_6_), channel_id=1, source_target_pairs={{0,0},{1,1},{2,4},{3,5},{4,2},{5,3},{6,6},{7,7},{8,8},{9,9},{10,12... | collective-permute-start | bytes 1572872 | tf_op jit(solution)/shard_map/ppermute | solution.py:344
  146.3 25.8 %collective-permute-start.29 = (bf16[256,1024]{1,0:T(8,128)(2,1)}, bf16[256,1024]{1,0:T(8,128)(2,1)S(1)}, u32[]{:S(2)}, u32[]{:S(2)}) collective-permute-start(bf16[256,1024]{1,0:T(8,128)(2,1)} %get-tuple-element.131.refs_7_), channel_id=1, source_target_pairs={{0,1},{1,0},{2,5},{3,4},{4,3},{5,2},{6,7},{7,6},{8,9},{9,8},{10,13... | collective-permute-start | bytes 1572872 | tf_op jit(solution)/shard_map/ppermute | solution.py:344
  178.6 14.2 %collective-permute-start.30 = (bf16[1024,1024]{1,0:T(8,128)(2,1)}, bf16[1024,1024]{1,0:T(8,128)(2,1)S(1)}, u32[]{:S(2)}, u32[]{:S(2)}) collective-permute-start(bf16[1024,1024]{1,0:T(8,128)(2,1)} %attend_out.1.part.refs_4_), channel_id=1, source_target_pairs={{0,4},{1,5},{2,6},{3,7},{4,0},{5,1},{6,2},{7,3},{8,12},{9,13},{10,... | collective-permute-start | bytes 6291464 | tf_op jit(solution)/shard_map/ppermute | solution.py:344
  180.1 9.8 %collective-permute-start.31 = (bf16[256,1024]{1,0:T(8,128)(2,1)}, bf16[256,1024]{1,0:T(8,128)(2,1)}, u32[]{:S(2)}, u32[]{:S(2)}) collective-permute-start(bf16[256,1024]{1,0:T(8,128)(2,1)} %copy-done.7), channel_id=1, source_target_pairs={{0,4},{1,5},{2,6},{3,7},{4,0},{5,1},{6,2},{7,3},{8,12},{9,13},{10,... | collective-permute-start | bytes 1572872 | tf_op jit(solution)/shard_map/ppermute | solution.py:344
  180.1 9.8 %collective-permute-start.32 = (bf16[256,1024]{1,0:T(8,128)(2,1)}, bf16[256,1024]{1,0:T(8,128)(2,1)}, u32[]{:S(2)}, u32[]{:S(2)}) collective-permute-start(bf16[256,1024]{1,0:T(8,128)(2,1)} %copy-done.8), channel_id=1, source_target_pairs={{0,4},{1,5},{2,6},{3,7},{4,0},{5,1},{6,2},{7,3},{8,12},{9,13},{10,... | collective-permute-start | bytes 1572872 | tf_op jit(solution)/shard_map/ppermute | solution.py:344
  182.6 17.6 %collective-permute-start.33 = (bf16[2,64,2048]{2,1,0:T(8,128)(2,1)}, bf16[2,64,2048]{2,1,0:T(8,128)(2,1)S(1)}, u32[]{:S(2)}, u32[]{:S(2)}) collective-permute-start(bf16[2,64,2048]{2,1,0:T(8,128)(2,1)} %slice.279), channel_id=1, source_target_pairs={{0,16},{1,17},{2,18},{3,19},{4,20},{5,21},{6,22},{7,23},{8,24},{9,... | collective-permute-start | bytes 1572872 | tf_op jit(solution)/shard_map/ppermute | solution.py:344
  184.7 15.5 %collective-permute-start.34 = (bf16[2,64,2048]{2,1,0:T(8,128)(2,1)}, bf16[2,64,2048]{2,1,0:T(8,128)(2,1)S(1)}, u32[]{:S(2)}, u32[]{:S(2)}) collective-permute-start(bf16[2,64,2048]{2,1,0:T(8,128)(2,1)} %slice.280), channel_id=1, source_target_pairs={{0,8},{1,9},{2,10},{3,11},{4,12},{5,13},{6,14},{7,15},{8,0},{9,1},... | collective-permute-start | bytes 1572872 | tf_op jit(solution)/shard_map/ppermute | solution.py:344
  241.4 33.0 %collective-permute-start.40 = (bf16[1024,1024]{1,0:T(8,128)(2,1)}, bf16[1024,1024]{1,0:T(8,128)(2,1)S(1)}, u32[]{:S(2)}, u32[]{:S(2)}) collective-permute-start(bf16[1024,1024]{1,0:T(8,128)(2,1)} %second_grad.1.refs_3_.refs_0_), channel_id=1, source_target_pairs={{0,4},{1,5},{2,6},{3,7},{4,0},{5,1},{6,2},{7,3},{8,12},{9,13},{10,... | collective-permute-start | bytes 6291464 | tf_op jit(solution)/shard_map/ppermute | solution.py:344
  242.0 28.5 %collective-permute-start.35 = (bf16[512,1024]{1,0:T(8,128)(2,1)}, bf16[512,1024]{1,0:T(8,128)(2,1)}, u32[]{:S(2)}, u32[]{:S(2)}) collective-permute-start(bf16[512,1024]{1,0:T(8,128)(2,1)} %get-tuple-element.141), channel_id=1, source_target_pairs={{0,4},{1,5},{2,6},{3,7},{4,0},{5,1},{6,2},{7,3},{8,12},{9,13},{10,... | collective-permute-start | bytes 3145736 | tf_op jit(solution)/shard_map/ppermute | solution.py:344
  252.3 13.4 %collective-permute-start.36 = (bf16[2,128,1024]{2,1,0:T(8,128)(2,1)}, bf16[2,128,1024]{2,1,0:T(8,128)(2,1)S(1)}, u32[]{:S(2)}, u32[]{:S(2)}) collective-permute-start(bf16[2,128,1024]{2,1,0:T(8,128)(2,1)} %get-tuple-element.145), channel_id=1, source_target_pairs={{0,8},{1,9},{2,10},{3,11},{4,12},{5,13},{6,14},{7,15},{8,0},{9,1},... | collective-permute-start | bytes 1572872 | tf_op jit(solution)/shard_map/ppermute | solution.py:344
  252.6 14.4 %collective-permute-start.37 = (bf16[2,128,1024]{2,1,0:T(8,128)(2,1)}, bf16[2,128,1024]{2,1,0:T(8,128)(2,1)}, u32[]{:S(2)}, u32[]{:S(2)}) collective-permute-start(bf16[2,128,1024]{2,1,0:T(8,128)(2,1)} %get-tuple-element.146), channel_id=1, source_target_pairs={{0,16},{1,17},{2,18},{3,19},{4,20},{5,21},{6,22},{7,23},{8,24},{9,... | collective-permute-start | bytes 1572872 | tf_op jit(solution)/shard_map/ppermute | solution.py:344
  264.5 24.3 %collective-permute-start.41 = (bf16[2,64,2048]{2,1,0:T(8,128)(2,1)}, bf16[2,64,2048]{2,1,0:T(8,128)(2,1)S(1)}, u32[]{:S(2)}, u32[]{:S(2)}) collective-permute-start(bf16[2,64,2048]{2,1,0:T(8,128)(2,1)} %get-tuple-element.156), channel_id=1, source_target_pairs={{0,8},{1,9},{2,10},{3,11},{4,12},{5,13},{6,14},{7,15},{8,0},{9,1},... | collective-permute-start | bytes 1572872 | tf_op jit(solution)/shard_map/ppermute | solution.py:344
  265.7 23.1 %collective-permute-start.42 = (bf16[2,64,2048]{2,1,0:T(8,128)(2,1)}, bf16[2,64,2048]{2,1,0:T(8,128)(2,1)}, u32[]{:S(2)}, u32[]{:S(2)}) collective-permute-start(bf16[2,64,2048]{2,1,0:T(8,128)(2,1)} %get-tuple-element.157), channel_id=1, source_target_pairs={{0,16},{1,17},{2,18},{3,19},{4,20},{5,21},{6,22},{7,23},{8,24},{9,... | collective-permute-start | bytes 1572872 | tf_op jit(solution)/shard_map/ppermute | solution.py:344
  270.3 37.8 %collective-permute-start.43 = (bf16[4,128,1024]{2,1,0:T(8,128)(2,1)}, bf16[4,128,1024]{2,1,0:T(8,128)(2,1)}, u32[]{:S(2)}, u32[]{:S(2)}) collective-permute-start(bf16[4,128,1024]{2,1,0:T(8,128)(2,1)} %get-tuple-element.149.refs_2_), channel_id=1, source_target_pairs={{0,8},{1,9},{2,10},{3,11},{4,12},{5,13},{6,14},{7,15},{8,0},{9,1},... | collective-permute-start | bytes 3145736 | tf_op jit(solution)/shard_map/ppermute | solution.py:344
  270.5 38.1 %collective-permute-start.44 = (bf16[4,128,1024]{2,1,0:T(8,128)(2,1)}, bf16[4,128,1024]{2,1,0:T(8,128)(2,1)}, u32[]{:S(2)}, u32[]{:S(2)}) collective-permute-start(bf16[4,128,1024]{2,1,0:T(8,128)(2,1)} %get-tuple-element.162), channel_id=1, source_target_pairs={{0,16},{1,17},{2,18},{3,19},{4,20},{5,21},{6,22},{7,23},{8,24},{9,... | collective-permute-start | bytes 3145736 | tf_op jit(solution)/shard_map/ppermute | solution.py:344
  274.4 37.6 %collective-permute-start.38 = (bf16[256,1024]{1,0:T(8,128)(2,1)}, bf16[256,1024]{1,0:T(8,128)(2,1)S(1)}, u32[]{:S(2)}, u32[]{:S(2)}) collective-permute-start(bf16[256,1024]{1,0:T(8,128)(2,1)} %get-tuple-element.150.refs_6_), channel_id=1, source_target_pairs={{0,0},{1,1},{2,4},{3,5},{4,2},{5,3},{6,6},{7,7},{8,8},{9,9},{10,12... | collective-permute-start | bytes 1572872 | tf_op jit(solution)/shard_map/ppermute | solution.py:344
  292.9 37.5 %collective-permute-start.45 = (bf16[4,64,2048]{2,1,0:T(8,128)(2,1)}, bf16[4,64,2048]{2,1,0:T(8,128)(2,1)S(1)}, u32[]{:S(2)}, u32[]{:S(2)}) collective-permute-start(bf16[4,64,2048]{2,1,0:T(8,128)(2,1)} %get-tuple-element.159.refs_7_), channel_id=1, source_target_pairs={{0,8},{1,9},{2,10},{3,11},{4,12},{5,13},{6,14},{7,15},{8,0},{9,1},... | collective-permute-start | bytes 3145736 | tf_op jit(solution)/shard_map/ppermute | solution.py:344
  293.6 36.8 %collective-permute-start.46 = (bf16[4,64,2048]{2,1,0:T(8,128)(2,1)}, bf16[4,64,2048]{2,1,0:T(8,128)(2,1)S(1)}, u32[]{:S(2)}, u32[]{:S(2)}) collective-permute-start(bf16[4,64,2048]{2,1,0:T(8,128)(2,1)} %get-tuple-element.165), channel_id=1, source_target_pairs={{0,16},{1,17},{2,18},{3,19},{4,20},{5,21},{6,22},{7,23},{8,24},{9,... | collective-permute-start | bytes 3145736 | tf_op jit(solution)/shard_map/ppermute | solution.py:344
  308.1 19.4 %collective-permute-start.39 = (bf16[256,1024]{1,0:T(8,128)(2,1)}, bf16[256,1024]{1,0:T(8,128)(2,1)S(1)}, u32[]{:S(2)}, u32[]{:S(2)}) collective-permute-start(bf16[256,1024]{1,0:T(8,128)(2,1)} %get-tuple-element.151), channel_id=1, source_target_pairs={{0,1},{1,0},{2,5},{3,4},{4,3},{5,2},{6,7},{7,6},{8,9},{9,8},{10,13... | collective-permute-start | bytes 1572872 | tf_op jit(solution)/shard_map/ppermute | solution.py:344
  312.0 15.6 %collective-permute-start.47 = (bf16[64,1024]{1,0:T(8,128)(2,1)}, bf16[64,1024]{1,0:T(8,128)(2,1)S(1)}, u32[]{:S(2)}, u32[]{:S(2)}) collective-permute-start(bf16[64,1024]{1,0:T(8,128)(2,1)} %get-tuple-element.168), channel_id=1, source_target_pairs={{0,1},{1,2},{2,3},{3,0},{4,5},{5,6},{6,7},{7,4},{8,9},{9,10},{10,1... | collective-permute-start | bytes 393224 | tf_op jit(solution)/shard_map/ppermute | solution.py:344
  312.0 15.6 %collective-permute-start.48 = (bf16[64,1024]{1,0:T(8,128)(2,1)}, bf16[64,1024]{1,0:T(8,128)(2,1)S(1)}, u32[]{:S(2)}, u32[]{:S(2)}) collective-permute-start(bf16[64,1024]{1,0:T(8,128)(2,1)} %get-tuple-element.169), channel_id=1, source_target_pairs={{0,3},{1,0},{2,1},{3,2},{4,7},{5,4},{6,5},{7,6},{8,11},{9,8},{10,9... | collective-permute-start | bytes 393224 | tf_op jit(solution)/shard_map/ppermute | solution.py:344
  342.6 16.3 %collective-permute-start.49 = (bf16[1024,1024]{1,0:T(8,128)(2,1)}, bf16[1024,1024]{1,0:T(8,128)(2,1)S(1)}, u32[]{:S(2)}, u32[]{:S(2)}) collective-permute-start(bf16[1024,1024]{1,0:T(8,128)(2,1)} %source_grad.1.refs_5_.refs_1_), channel_id=1, source_target_pairs={{0,4},{1,5},{2,6},{3,7},{4,0},{5,1},{6,2},{7,3},{8,12},{9,13},{10,... | collective-permute-start | bytes 6291464 | tf_op jit(solution)/shard_map/ppermute | solution.py:344
  343.9 15.0 %collective-permute-start.50 = (bf16[128,1024]{1,0:T(8,128)(2,1)S(1)}, bf16[128,1024]{1,0:T(8,128)(2,1)S(1)}, u32[]{:S(2)}, u32[]{:S(2)}) collective-permute-start(bf16[128,1024]{1,0:T(8,128)(2,1)S(1)} %copy-done.48), channel_id=1, source_target_pairs={{0,1},{1,2},{2,3},{3,0},{4,5},{5,6},{6,7},{7,4},{8,9},{9,10},{10,1... | collective-permute-start | bytes 786440 | tf_op jit(solution)/shard_map/ppermute | solution.py:344
  345.0 13.9 %collective-permute-start.51 = (bf16[128,1024]{1,0:T(8,128)(2,1)}, bf16[128,1024]{1,0:T(8,128)(2,1)S(1)}, u32[]{:S(2)}, u32[]{:S(2)}) collective-permute-start(bf16[128,1024]{1,0:T(8,128)(2,1)} %get-tuple-element.175), channel_id=1, source_target_pairs={{0,3},{1,0},{2,1},{3,2},{4,7},{5,4},{6,5},{7,6},{8,11},{9,8},{10,9... | collective-permute-start | bytes 786440 | tf_op jit(solution)/shard_map/ppermute | solution.py:344
  357.7 15.6 %collective-permute-start.54 = (bf16[2,256,512]{2,1,0:T(8,128)(2,1)}, bf16[2,256,512]{2,1,0:T(8,128)(2,1)S(1)}, u32[]{:S(2)}, u32[]{:S(2)}) collective-permute-start(bf16[2,256,512]{2,1,0:T(8,128)(2,1)} %get-tuple-element.180), channel_id=1, source_target_pairs={{0,8},{1,9},{2,10},{3,11},{4,12},{5,13},{6,14},{7,15},{8,0},{9,1},... | collective-permute-start | bytes 1572872 | tf_op jit(solution)/shard_map/ppermute | solution.py:344
  357.8 15.5 %collective-permute-start.55 = (bf16[2,256,512]{2,1,0:T(8,128)(2,1)}, bf16[2,256,512]{2,1,0:T(8,128)(2,1)}, u32[]{:S(2)}, u32[]{:S(2)}) collective-permute-start(bf16[2,256,512]{2,1,0:T(8,128)(2,1)} %get-tuple-element.181), channel_id=1, source_target_pairs={{0,16},{1,17},{2,18},{3,19},{4,20},{5,21},{6,22},{7,23},{8,24},{9,... | collective-permute-start | bytes 1572872 | tf_op jit(solution)/shard_map/ppermute | solution.py:344
  372.3 4.2 collective-permute-start.58
  380.5 31.9 %collective-permute-start.59 = (bf16[4,256,512]{2,1,0:T(8,128)(2,1)}, bf16[4,256,512]{2,1,0:T(8,128)(2,1)S(1)}, u32[]{:S(2)}, u32[]{:S(2)}) collective-permute-start(bf16[4,256,512]{2,1,0:T(8,128)(2,1)} %get-tuple-element.185), channel_id=1, source_target_pairs={{0,8},{1,9},{2,10},{3,11},{4,12},{5,13},{6,14},{7,15},{8,0},{9,1},... | collective-permute-start | bytes 3145736 | tf_op jit(solution)/shard_map/ppermute | solution.py:344
  381.1 31.3 %collective-permute-start.60 = (bf16[4,256,512]{2,1,0:T(8,128)(2,1)}, bf16[4,256,512]{2,1,0:T(8,128)(2,1)S(1)}, u32[]{:S(2)}, u32[]{:S(2)}) collective-permute-start(bf16[4,256,512]{2,1,0:T(8,128)(2,1)} %get-tuple-element.186), channel_id=1, source_target_pairs={{0,16},{1,17},{2,18},{3,19},{4,20},{5,21},{6,22},{7,23},{8,24},{9,... | collective-permute-start | bytes 3145736 | tf_op jit(solution)/shard_map/ppermute | solution.py:344
  381.9 17.4 %collective-permute-start.52 = (bf16[256,1024]{1,0:T(8,128)(2,1)S(1)}, bf16[256,1024]{1,0:T(8,128)(2,1)S(1)}, u32[]{:S(2)}, u32[]{:S(2)}) collective-permute-start(bf16[256,1024]{1,0:T(8,128)(2,1)S(1)} %copy-done.36), channel_id=1, source_target_pairs={{0,0},{1,1},{2,4},{3,5},{4,2},{5,3},{6,6},{7,7},{8,8},{9,9},{10,12... | collective-permute-start | bytes 1572872 | tf_op jit(solution)/shard_map/ppermute | solution.py:344
  388.7 23.7 %collective-permute-start.53 = (bf16[256,1024]{1,0:T(8,128)(2,1)}, bf16[256,1024]{1,0:T(8,128)(2,1)S(1)}, u32[]{:S(2)}, u32[]{:S(2)}) collective-permute-start(bf16[256,1024]{1,0:T(8,128)(2,1)} %get-tuple-element.177), channel_id=1, source_target_pairs={{0,1},{1,0},{2,5},{3,4},{4,3},{5,2},{6,7},{7,6},{8,9},{9,8},{10,13... | collective-permute-start | bytes 1572872 | tf_op jit(solution)/shard_map/ppermute | solution.py:344
  417.5 6.5 %collective-permute-start.62 = (bf16[144,512]{1,0:T(8,128)(2,1)}, bf16[144,512]{1,0:T(8,128)(2,1)S(1)}, u32[]{:S(2)}, u32[]{:S(2)}) collective-permute-start(bf16[144,512]{1,0:T(8,128)(2,1)} %get-tuple-element.191), channel_id=1, source_target_pairs={{0,3},{1,0},{2,1},{3,2},{4,7},{5,4},{6,5},{7,6},{8,11},{9,8},{10,9... | collective-permute-start | bytes 442376 | tf_op jit(solution)/shard_map/ppermute | solution.py:344
  417.5 5.4 %collective-permute-start.61 = (bf16[128,512]{1,0:T(8,128)(2,1)}, bf16[128,512]{1,0:T(8,128)(2,1)S(1)}, u32[]{:S(2)}, u32[]{:S(2)}) collective-permute-start(bf16[128,512]{1,0:T(8,128)(2,1)} %get-tuple-element.190), channel_id=1, source_target_pairs={{0,1},{1,2},{2,3},{3,0},{4,5},{5,6},{6,7},{7,4},{8,9},{9,10},{10,1... | collective-permute-start | bytes 393224 | tf_op jit(solution)/shard_map/ppermute | solution.py:344
  418.9 10.2 %collective-permute-start.66 = (bf16[32,2048]{1,0:T(8,128)(2,1)S(1)}, bf16[32,2048]{1,0:T(8,128)(2,1)S(1)}, u32[]{:S(2)}, u32[]{:S(2)}) collective-permute-start(bf16[32,2048]{1,0:T(8,128)(2,1)S(1)} %copy-done.68), channel_id=1, source_target_pairs={{0,1},{1,2},{2,3},{3,0},{4,5},{5,6},{6,7},{7,4},{8,9},{9,10},{10,1... | collective-permute-start | bytes 393224 | tf_op jit(solution)/shard_map/ppermute | solution.py:344
  419.0 12.8 %collective-permute-start.67 = (bf16[32,2048]{1,0:T(8,128)(2,1)S(1)}, bf16[32,2048]{1,0:T(8,128)(2,1)S(1)}, u32[]{:S(2)}, u32[]{:S(2)}) collective-permute-start(bf16[32,2048]{1,0:T(8,128)(2,1)S(1)} %copy-done.67), channel_id=1, source_target_pairs={{0,3},{1,0},{2,1},{3,2},{4,7},{5,4},{6,5},{7,6},{8,11},{9,8},{10,9... | collective-permute-start | bytes 393224 | tf_op jit(solution)/shard_map/ppermute | solution.py:344
  426.6 10.8 %collective-permute-start.63 = (bf16[272,512]{1,0:T(8,128)(2,1)}, bf16[272,512]{1,0:T(8,128)(2,1)S(1)}, u32[]{:S(2)}, u32[]{:S(2)}) collective-permute-start(bf16[272,512]{1,0:T(8,128)(2,1)} %get-tuple-element.192.refs_4_), channel_id=1, source_target_pairs={{0,1},{1,2},{2,3},{3,0},{4,5},{5,6},{6,7},{7,4},{8,9},{9,10},{10,1... | collective-permute-start | bytes 835592 | tf_op jit(solution)/shard_map/ppermute | solution.py:344
  426.6 18.3 %collective-permute-start.64 = (bf16[272,512]{1,0:T(8,128)(2,1)}, bf16[272,512]{1,0:T(8,128)(2,1)S(1)}, u32[]{:S(2)}, u32[]{:S(2)}) collective-permute-start(bf16[272,512]{1,0:T(8,128)(2,1)} %get-tuple-element.193), channel_id=1, source_target_pairs={{0,3},{1,0},{2,1},{3,2},{4,7},{5,4},{6,5},{7,6},{8,11},{9,8},{10,9... | collective-permute-start | bytes 835592 | tf_op jit(solution)/shard_map/ppermute | solution.py:344
  434.4 14.8 %collective-permute-start.68 = (bf16[64,2048]{1,0:T(8,128)(2,1)}, bf16[64,2048]{1,0:T(8,128)(2,1)S(1)}, u32[]{:S(2)}, u32[]{:S(2)}) collective-permute-start(bf16[64,2048]{1,0:T(8,128)(2,1)} %get-tuple-element.204), channel_id=1, source_target_pairs={{0,1},{1,2},{2,3},{3,0},{4,5},{5,6},{6,7},{7,4},{8,9},{9,10},{10,1... | collective-permute-start | bytes 786440 | tf_op jit(solution)/shard_map/ppermute | solution.py:344
  434.4 19.0 %collective-permute-start.69 = (bf16[64,2048]{1,0:T(8,128)(2,1)}, bf16[64,2048]{1,0:T(8,128)(2,1)S(1)}, u32[]{:S(2)}, u32[]{:S(2)}) collective-permute-start(bf16[64,2048]{1,0:T(8,128)(2,1)} %get-tuple-element.205), channel_id=1, source_target_pairs={{0,3},{1,0},{2,1},{3,2},{4,7},{5,4},{6,5},{7,6},{8,11},{9,8},{10,9... | collective-permute-start | bytes 786440 | tf_op jit(solution)/shard_map/ppermute | solution.py:344
  456.6 6.3 %collective-permute-start.70 = (f32[32,2048]{1,0:T(8,128)}, f32[32,2048]{1,0:T(8,128)S(1)}, u32[]{:S(2)}, u32[]{:S(2)}) collective-permute-start(f32[32,2048]{1,0:T(8,128)} %get-tuple-element.207), channel_id=1, source_target_pairs={{0,4},{1,5},{2,6},{3,7},{4,0},{5,1},{6,2},{7,3},{8,12},{9,13},{10,... | collective-permute-start | bytes 786440 | tf_op jit(solution)/shard_map/ppermute | solution.py:344
  (76 other events, 376.5 us)

commit v5 on v4

--- a/solution.py
+++ b/solution.py
@@ -1398,12 +1398,12 @@
         after=[mixed],
     )
     wdown, wout = wdown.reshape(units, width), wout.reshape(half, width)
-    part = rows_matmul(mixed, wout, NN, "attend_out", after=[fa, fb, *cot_got])
+    *cot_got, _ = lax.optimization_barrier((*cot_got, mixed))
+    cot = whole_sequence(
+        cot_got + [send(g, CORE_SWAP) for g in cot_got], "cotangent_whole", [wout]
+    )[0].reshape(total, width)
+    part = rows_matmul(mixed, wout, NN, "attend_out", after=[fa, fb, cot])
     middle, second = middle_norm(x, part, send(part, CORE_SWAP), bias_o, gain2, shift2)
-    cot = whole_sequence(
-        cot_got + [send(g, CORE_SWAP) for g in cot_got], "cotangent_whole", [part]
-    )[0].reshape(total, width)
-
     def up_blocks(src, outs, yx, zz):
         return [(src.at[pl.ds(cc * lead, lead)], outs[0].at[yx, cc, zz]) for cc in range(2)]
 

time: 473 us -> 475 us (level)
    unnamed x140 -> x138, local copies, waits for them, and re-layouts: 17.7 us -> 18.7 us
  transfers between devices with their start and end apart: 71 -> 71, of which waited for: 22 -> 24; matrix products, arithmetic and copies ran while one was open for 6% -> 6% of each run, Pallas kernels for 33% -> 34%
where the time goes in v5:
time: 475 us; the launch traced here: 466 us
  Pallas kernels  230 us (48%)
  waiting for transfers between devices  106 us (22%)
  starting transfers between devices  77.4 us (16%)
  local copies, waits for them, and re-layouts  43.4 us (9%)
  other arithmetic  7.21 us (2%)
    pallas_call x35, Pallas kernels, call(): pl.pallas_call(without(body, len(ins), len(after)), grid=grid, in_specs=l...  180 us
    ppermute x71, waiting for transfers between devices, send(): return lax.ppermute(value, AXES, pairs)  106 us
    ppermute x71, starting transfers between devices, send(): return lax.ppermute(value, AXES, pairs)  77.4 us
    pallas_call x5, Pallas kernels, placed_call(): pl.pallas_call(without(body, len(ins) + 1, len(after)), grid_spec=pltpu.P...  50.7 us
    unnamed x138, local copies, waits for them, and re-layouts  18.7 us
  transfers between devices with their start and end apart: 71, of which 24 were waited for; matrix products, arithmetic and copies ran while one was open for 6% of the time, Pallas kernels for 34%

profile of v5, /device:TPU:13, one launch (start us, length us, event | category | flops | bytes accessed | tf_op | source)
XLA Modules:
  0.0 466.2 jit_solution(5671525149596143303)
XLA Ops:
  2.1 1.7 first.1
  7.3 2.0 second.1
  10.8 5.4 %collective-permute-done.3.refs_2_ = bf16[208,512]{1,0:T(8,128)(2,1)S(1)} collective-permute-done((bf16[208,512]{1,0:T(8,128)(2,1)}, bf16[208,512]{1,0:T(8,128)(2,1)S(1)}, u32[]{:S(2)}, u32[]{:S(2)}) %collective-permute-start.3) | collective-permute-done | bytes 213024 | tf_op jit(solution)/shard_map/ppermute | solution.py:344
  17.7 5.1 %collective-permute-done.2.refs_1_ = bf16[208,512]{1,0:T(8,128)(2,1)S(1)} collective-permute-done((bf16[208,512]{1,0:T(8,128)(2,1)}, bf16[208,512]{1,0:T(8,128)(2,1)S(1)}, u32[]{:S(2)}, u32[]{:S(2)}) %collective-permute-start.2) | collective-permute-done | bytes 213024 | tf_op jit(solution)/shard_map/ppermute | solution.py:344
  22.9 4.1 collective-permute-done.4.refs_3_
  28.2 2.4 attn_inner.2
  33.8 15.4 %collective-permute-done.6.refs_2_.refs_1_ = bf16[4,208,512]{2,1,0:T(8,128)(2,1)S(1)} collective-permute-done((bf16[4,208,512]{2,1,0:T(8,128)(2,1)}, bf16[4,208,512]{2,1,0:T(8,128)(2,1)S(1)}, u32[]{:S(2)}, u32[]{:S(2)}) %collective-permute-start.6) | collective-permute-done | bytes 852000 | tf_op jit(solution)/shard_map/ppermute | solution.py:344
  53.2 2.2 collective-permute-start.9
  55.4 2.9 collective-permute-done.11.refs_5_.refs_4_
  58.3 4.6 collective-permute-done.9.refs_4_.refs_3_
  62.9 2.9 inputs_own.1
  66.7 2.4 down_inner.2.refs_5_.refs_0_
  70.7 6.6 %collective-permute-start.12 = (bf16[272,1024]{1,0:T(8,128)(2,1)}, bf16[272,1024]{1,0:T(8,128)(2,1)}, u32[]{:S(2)}, u32[]{:S(2)}) collective-permute-start(bf16[272,1024]{1,0:T(8,128)(2,1)} %get-tuple-element.120.refs_7_), channel_id=1, source_target_pairs={{0,0},{1,1},{2,4},{3,5},{4,2},{5,3},{6,6},{7,7},{8,8},{9,9},{10,12... | collective-permute-start | bytes 1671176 | tf_op jit(solution)/shard_map/ppermute | solution.py:344
  77.4 4.7 %attn_whole.1 = (bf16[3,4,2,4,32,512]{5,4,3,2,1,0:T(8,128)(2,1)}, bf16[4,4,16,512]{3,2,1,0:T(8,128)(2,1)}) custom-call(bf16[4,208,512]{2,1,0:T(8,128)(2,1)} %get-tuple-element.118.refs_0_, bf16[4,208,512]{2,1,0:T(8,128)(2,1)} %copy-done.2, bf16[4,208,512]{2,1,0:T(8,128)(2,1)} %copy-done.3, bf16[2,208,512]{2,1,0:T(8,128)(2,1)} %copy-done.18, ...), custom_call_target="tpu_custom_call" | custom-call | bytes 6815744 | tf_op jit(solution)/shard_map/attn_whole/pallas_call | solution.py:385
  83.3 11.2 %collective-permute-done.12.refs_0_ = bf16[272,1024]{1,0:T(8,128)(2,1)} collective-permute-done((bf16[272,1024]{1,0:T(8,128)(2,1)}, bf16[272,1024]{1,0:T(8,128)(2,1)}, u32[]{:S(2)}, u32[]{:S(2)}) %collective-permute-start.12) | collective-permute-done | bytes 557088 | tf_op jit(solution)/shard_map/ppermute | solution.py:344
  94.5 7.6 %collective-permute-done.13.refs_1_ = bf16[272,1024]{1,0:T(8,128)(2,1)} collective-permute-done((bf16[272,1024]{1,0:T(8,128)(2,1)}, bf16[272,1024]{1,0:T(8,128)(2,1)}, u32[]{:S(2)}, u32[]{:S(2)}) %collective-permute-start.13) | collective-permute-done | bytes 557088 | tf_op jit(solution)/shard_map/ppermute | solution.py:344
  108.3 3.2 inputs_whole.1
  113.0 8.2 %project.1 = (bf16[1024,1024]{1,0:T(8,128)(2,1)}, bf16[3,1024,512]{2,1,0:T(8,128)(2,1)}) custom-call(bf16[1024,1024]{1,0:T(8,128)(2,1)} %bitcast.77, f32[1,1024]{1,0:T(1,128)} %slice.210.gain.refs_5_, f32[1,1024]{1,0:T(1,128)} %slice.212.shift, bf16[3,1024,512]{2,1,0:T(8,128)(2,1)} %bitcast.103, f32[3,512]{1,0:T(4,128)} %maximum_convert_fusion.bias), custom_call_target="tpu_custom_call" | custom-call | flops 3221225472 | bytes 10500096 | tf_op jit(solution)/shard_map/project/pallas_call | solution.py:385
  127.5 2.8 collective-permute-done.21.refs_4_.refs_2_
  130.9 2.2 cotangent_own.1
  133.1 7.6 %collective-permute-start.28 = (bf16[256,1024]{1,0:T(8,128)(2,1)}, bf16[256,1024]{1,0:T(8,128)(2,1)S(1)}, u32[]{:S(2)}, u32[]{:S(2)}) collective-permute-start(bf16[256,1024]{1,0:T(8,128)(2,1)} %get-tuple-element.132.refs_6_), channel_id=1, source_target_pairs={{0,0},{1,1},{2,4},{3,5},{4,2},{5,3},{6,6},{7,7},{8,8},{9,9},{10,12... | collective-permute-start | bytes 1572872 | tf_op jit(solution)/shard_map/ppermute | solution.py:344
  141.6 2.2 up_inner.2.refs_5_.refs_0_
  145.4 10.4 %attend.2 = (bf16[1024,512]{1,0:T(8,128)(2,1)}, f32[1024,512]{1,0:T(8,128)}) custom-call(f32[1024,1]{1,0:T(8,128)} %copy.72.refs_0_.column, f32[1,1024]{1,0:T(1,128)} %bitcast.94, bf16[3,1024,512]{2,1,0:T(8,128)(2,1)} %get-tuple-element.129.refs_2_.refs_3_.refs_4_.q_ref.k_ref.v_ref, ...), custom_call_target="tpu_custom_call" | custom-call | flops 4294967296 | bytes 12591104 | tf_op jit(solution)/shard_map/attend/pallas_call | solution.py:385
  155.8 10.2 %attend.3 = (bf16[1024,512]{1,0:T(8,128)(2,1)}, f32[1024,512]{1,0:T(8,128)}) custom-call(f32[1024,1]{1,0:T(8,128)} %copy.72.refs_0_.column, f32[1,1024]{1,0:T(1,128)} %bitcast.95, bf16[3,1024,512]{2,1,0:T(8,128)(2,1)} %get-tuple-element.129.refs_2_.refs_3_.refs_4_.q_ref.k_ref.v_ref, ...), custom_call_target="tpu_custom_call", output_to_operand_aliasing={{0}: (5, {}), {1}: (6, {})} | custom-call | flops 4294967296 | bytes 15736832 | tf_op jit(solution)/shard_map/attend/pallas_call | solution.py:385
  166.6 5.1 %down_whole.1 = (bf16[4,4,128,1024]{3,2,1,0:T(8,128)(2,1)}, bf16[4,4,32,1024]{3,2,1,0:T(8,128)(2,1)}) custom-call(bf16[4,160,1024]{2,1,0:T(8,128)(2,1)} %down_inner.2.refs_5_.refs_0_, bf16[4,160,1024]{2,1,0:T(8,128)(2,1)} %copy-done.4, bf16[4,160,1024]{2,1,0:T(8,128)(2,1)} %copy-done.5, bf16[2,160,1024]{2,1,0:T(8,128)(2,1)} %copy-done.6, ...), custom_call_target="tpu_custom_call" | custom-call | bytes 10485760 | tf_op jit(solution)/shard_map/down_whole/pallas_call | solution.py:385
  172.5 2.9 cotangent_whole.1
  176.8 4.8 %attend_out.1.part = bf16[1024,1024]{1,0:T(8,128)(2,1)} custom-call(bf16[1024,512]{1,0:T(8,128)(2,1)} %get-tuple-element.136.refs_5_.refs_0_.refs_3_, bf16[512,1024]{1,0:T(8,128)(2,1)} %bitcast.75, bf16[4,64,2048]{2,1,0:T(8,128)(2,1)} %copy-done, bf16[4,64,2048]{2,1,0:T(8,128)(2,1)} %copy-done.1, bf16[1024,1024]{1,0:T(8,128)(2,1)} %bitcast.70), custom_call_target="tpu_custom_call" | custom-call | flops 1073741824 | bytes 4194304 | tf_op jit(solution)/shard_map/attend_out/pallas_call | solution.py:385
  181.7 1.9 slice.279
  183.8 1.9 slice.280
  192.2 6.1 %middle.1 = (f32[1024,1024]{1,0:T(8,128)}, bf16[1024,1024]{1,0:T(8,128)(2,1)}) custom-call(bf16[1024,1024]{1,0:T(8,128)(2,1)} %bitcast.78, bf16[1024,1024]{1,0:T(8,128)(2,1)} %attend_out.1.part, bf16[1024,1024]{1,0:T(8,128)(2,1)} %copy-done.11, f32[1,1024]{1,0:T(1,128)} %slice.222.bias, f32[1,1024]{1,0:T(1,128)} %slice.224.gain.refs_4_, f32[1,1024]{1,0:T(1,128)} %slice.226.shift), custom_call_target="tpu_custom_call" | custom-call | bytes 12595200 | tf_op jit(solution)/shard_map/middle/pallas_call | solution.py:385
  199.5 4.5 up_whole.1
  204.0 16.3 %feed.1 = (bf16[1024,2048]{1,0:T(8,128)(2,1)}, bf16[1024,2048]{1,0:T(8,128)(2,1)}, f32[1,2048]{1,0:T(1,128)}) custom-call(bf16[1024,1024]{1,0:T(8,128)(2,1)} %get-tuple-element.140.refs_5_.second.refs_1_, bf16[1024,1024]{1,0:T(8,128)(2,1)} %bitcast.71, bf16[1024,2048]{1,0:T(8,128)(2,1)} %bitcast.80, f32[1,2048]{1,0:T(1,128)} %convert.28.bias, ...), custom_call_target="tpu_custom_call" | custom-call | flops 8589934592 | bytes 20987904 | tf_op jit(solution)/shard_map/feed/pallas_call | solution.py:385
  220.4 10.5 %output_rows.1 = (bf16[512,1024]{1,0:T(8,128)(2,1)}, f32[512,1024]{1,0:T(8,128)}) custom-call(s32[3]{0:T(128)} %pad_add_fusion.1.pos.refs_0_, bf16[1024,2048]{1,0:T(8,128)(2,1)} %get-tuple-element.142.hidden.refs_1_, bf16[2048,1024]{1,0:T(8,128)(2,1)} %bitcast.102, f32[1024,1024]{1,0:T(8,128)} %get-tuple-element.143.middle.refs_2_, f32[1,1024]{1,0:T(1,128)} %slice.231.bias), custom_call_target="tpu_custom_call" | custom-call | flops 4294967296 | bytes 15732736 | tf_op jit(solution)/shard_map/output_rows/pallas_call | solution.py:401
  230.9 8.8 %second_grad.1.refs_3_.refs_0_ = bf16[1024,1024]{1,0:T(8,128)(2,1)} custom-call(bf16[1024,2048]{1,0:T(8,128)(2,1)} %get-tuple-element.146.refs_0_.refs_2_, bf16[1024,2048]{1,0:T(8,128)(2,1)} %bitcast.81, f32[512,1024]{1,0:T(8,128)} %get-tuple-element.144.refs_2_.refs_0_), custom_call_target="tpu_custom_call" | custom-call | flops 4294967296 | bytes 10485760 | tf_op jit(solution)/shard_map/second_grad/pallas_call | solution.py:385
  241.4 10.2 %down_grads.1 = (bf16[2,128,1024]{2,1,0:T(8,128)(2,1)}, bf16[2,128,1024]{2,1,0:T(8,128)(2,1)}, bf16[4,128,1024]{2,1,0:T(8,128)(2,1)}, bf16[4,128,1024]{2,1,0:T(8,128)(2,1)}, bf16[4,128,1024]{2,1,0:T(8,128)(2,1)}) custom-call(s32[3]{0:T(128)} %pad_add_fusion.1.pos.refs_0_, bf16[1024,2048]{1,0:T(8,128)(2,1)} %get-tuple-element.142.hidden.refs_1_, ...), custom_call_target="tpu_custom_call" | custom-call | flops 4294967296 | bytes 10485760 | tf_op jit(solution)/shard_map/down_grads/pallas_call | solution.py:401
  254.1 10.6 %up_grads.1 = (bf16[2,64,2048]{2,1,0:T(8,128)(2,1)}, bf16[2,64,2048]{2,1,0:T(8,128)(2,1)}, bf16[4,64,2048]{2,1,0:T(8,128)(2,1)}, bf16[4,64,2048]{2,1,0:T(8,128)(2,1)}, bf16[4,64,2048]{2,1,0:T(8,128)(2,1)}) custom-call(s32[3]{0:T(128)} %pad_add_fusion.1.pos.refs_0_, bf16[1024,1024]{1,0:T(8,128)(2,1)} %get-tuple-element.140.refs_5_.second.refs_1_, ...), custom_call_target="tpu_custom_call" | custom-call | flops 4294967296 | bytes 10485760 | tf_op jit(solution)/shard_map/up_grads/pallas_call | solution.py:401
  266.3 3.3 down_pass.1
  271.6 2.9 result.1
  274.6 4.5 collective-permute-start.38
  279.0 9.9 %middle_back.1 = (bf16[1024,1024]{1,0:T(8,128)(2,1)}, f32[1024,1024]{1,0:T(8,128)}, bf16[1024,512]{1,0:T(8,128)(2,1)}, f32[4,1024]{1,0:T(4,128)}) custom-call(bf16[1024,1024]{1,0:T(8,128)(2,1)} %second_grad.1.refs_3_.refs_0_, bf16[1024,1024]{1,0:T(8,128)(2,1)} %copy-done.17, f32[1024,1024]{1,0:T(8,128)} %get-tuple-element.143.middle.refs_2_, ...), custom_call_target="tpu_custom_call" | custom-call | flops 1073741824 | bytes 18894848 | tf_op jit(solution)/shard_map/middle_back/pallas_call | solution.py:385
  289.7 3.3 up_pass.1
  294.2 13.6 %attend_back.2 = (bf16[3,1024,512]{2,1,0:T(8,128)(2,1)}, f32[2,512]{1,0:T(2,128)}) custom-call(f32[1024,1]{1,0:T(8,128)} %copy.72.refs_0_.column, f32[1,1024]{1,0:T(1,128)} %bitcast.96, bf16[3,1024,512]{2,1,0:T(8,128)(2,1)} %get-tuple-element.129.refs_2_.refs_3_.refs_4_.q_ref.k_ref.v_ref, ...), custom_call_target="tpu_custom_call" | custom-call | flops 6442450944 | bytes 15740928 | tf_op jit(solution)/shard_map/attend_back/pallas_call | solution.py:385
  307.8 2.1 collective-permute-start.39
  309.9 3.4 down_join.1
  314.7 14.0 %attend_back.3 = (bf16[3,1024,512]{2,1,0:T(8,128)(2,1)}, f32[2,512]{1,0:T(2,128)}) custom-call(f32[1024,1]{1,0:T(8,128)} %copy.72.refs_0_.column, f32[1,1024]{1,0:T(1,128)} %bitcast.97, bf16[3,1024,512]{2,1,0:T(8,128)(2,1)} %get-tuple-element.129.refs_2_.refs_3_.refs_4_.q_ref.k_ref.v_ref, ...), custom_call_target="tpu_custom_call", output_to_operand_aliasing={{0}: (7, {}), {1}: (8, {})} | custom-call | flops 6442450944 | bytes 18890752 | tf_op jit(solution)/shard_map/attend_back/pallas_call | solution.py:385
  329.6 1.9 down_inner.3
  332.9 3.4 up_join.1
  336.3 7.4 %source_grad.1.refs_5_.refs_1_ = bf16[1024,1024]{1,0:T(8,128)(2,1)} custom-call(bf16[3,1024,512]{2,1,0:T(8,128)(2,1)} %get-tuple-element.168.refs_0_.refs_2_, bf16[3,1024,512]{2,1,0:T(8,128)(2,1)} %bitcast.104, f32[64,2048]{1,0:T(8,128)} %get-tuple-element.176.refs_2_.refs_3_), custom_call_target="tpu_custom_call" | custom-call | flops 3221225472 | bytes 8388608 | tf_op jit(solution)/shard_map/source_grad/pallas_call | solution.py:385
  343.9 2.3 collective-permute-start.50
  347.2 11.2 %attn_grads.1 = (bf16[2,256,512]{2,1,0:T(8,128)(2,1)}, bf16[2,256,512]{2,1,0:T(8,128)(2,1)}, bf16[4,256,512]{2,1,0:T(8,128)(2,1)}, bf16[4,256,512]{2,1,0:T(8,128)(2,1)}, bf16[4,256,512]{2,1,0:T(8,128)(2,1)}) custom-call(s32[3]{0:T(128)} %pad_add_fusion.1.pos.refs_0_, bf16[1024,1024]{1,0:T(8,128)(2,1)} %get-tuple-element.131.refs_7_.refs_3_.refs_1_, ...), custom_call_target="tpu_custom_call" | custom-call | flops 4294967296 | bytes 12582912 | tf_op jit(solution)/shard_map/attn_grads/pallas_call | solution.py:401
  361.8 8.1 %input_back.1 = (bf16[256,1024]{1,0:T(8,128)(2,1)}, bf16[256,1024]{1,0:T(8,128)(2,1)}, f32[2,1024]{1,0:T(2,128)}) custom-call(s32[3]{0:T(128)} %pad_add_fusion.1.pos.refs_0_, bf16[1024,1024]{1,0:T(8,128)(2,1)} %source_grad.1.refs_5_.refs_1_, bf16[1024,1024]{1,0:T(8,128)(2,1)} %copy-done.16, bf16[1024,1024]{1,0:T(8,128)(2,1)} %bitcast.79, ...), custom_call_target="tpu_custom_call" | custom-call | bytes 11546624 | tf_op jit(solution)/shard_map/input_back/pallas_call | solution.py:401
  378.3 3.3 attn_pass.1
  383.3 6.8 %collective-permute-start.52 = (bf16[256,1024]{1,0:T(8,128)(2,1)}, bf16[256,1024]{1,0:T(8,128)(2,1)S(1)}, u32[]{:S(2)}, u32[]{:S(2)}) collective-permute-start(bf16[256,1024]{1,0:T(8,128)(2,1)} %get-tuple-element.180.refs_4_), channel_id=1, source_target_pairs={{0,0},{1,1},{2,4},{3,5},{4,2},{5,3},{6,6},{7,7},{8,8},{9,9},{10,12... | collective-permute-start | bytes 1572872 | tf_op jit(solution)/shard_map/ppermute | solution.py:344
  390.9 12.3 %collective-permute-done.52.refs_7_ = bf16[256,1024]{1,0:T(8,128)(2,1)S(1)} collective-permute-done((bf16[256,1024]{1,0:T(8,128)(2,1)}, bf16[256,1024]{1,0:T(8,128)(2,1)S(1)}, u32[]{:S(2)}, u32[]{:S(2)}) %collective-permute-start.52) | collective-permute-done | bytes 524320 | tf_op jit(solution)/shard_map/ppermute | solution.py:344
  403.2 10.3 %collective-permute-done.53.refs_8_ = bf16[256,1024]{1,0:T(8,128)(2,1)S(1)} collective-permute-done((bf16[256,1024]{1,0:T(8,128)(2,1)}, bf16[256,1024]{1,0:T(8,128)(2,1)S(1)}, u32[]{:S(2)}, u32[]{:S(2)}) %collective-permute-start.53) | collective-permute-done | bytes 524320 | tf_op jit(solution)/shard_map/ppermute | solution.py:344
  415.0 3.6 attn_join.1
  421.5 2.0 collective-permute-done.61.t1
  425.1 2.0 attn_inner.3
  429.7 2.2 collective-permute-done.67.refs_3_
  432.5 1.9 up_inner.3
  437.5 8.0 %collective-permute-done.64.p2 = bf16[272,512]{1,0:T(8,128)(2,1)S(1)} collective-permute-done((bf16[272,512]{1,0:T(8,128)(2,1)}, bf16[272,512]{1,0:T(8,128)(2,1)S(1)}, u32[]{:S(2)}, u32[]{:S(2)}) %collective-permute-start.64) | collective-permute-done | bytes 278560 | tf_op jit(solution)/shard_map/ppermute | solution.py:344
  446.2 2.1 attn_last.1
  449.8 4.1 collective-permute-done.69.refs_5_
  454.6 2.6 feed_last.1
  (339 shorter events, 100.2 us)
Async XLA Ops:
  9.3 6.8 %collective-permute-start.3 = (bf16[208,512]{1,0:T(8,128)(2,1)}, bf16[208,512]{1,0:T(8,128)(2,1)S(1)}, u32[]{:S(2)}, u32[]{:S(2)}) collective-permute-start(bf16[208,512]{1,0:T(8,128)(2,1)} %get-tuple-element.117.refs_0_), channel_id=1, source_target_pairs={{0,3},{1,0},{2,1},{3,2},{4,7},{5,4},{6,5},{7,6},{8,11},{9,8},{10,9... | collective-permute-start | bytes 638984 | tf_op jit(solution)/shard_map/ppermute | solution.py:344
  9.5 13.3 %collective-permute-start.2 = (bf16[208,512]{1,0:T(8,128)(2,1)}, bf16[208,512]{1,0:T(8,128)(2,1)S(1)}, u32[]{:S(2)}, u32[]{:S(2)}) collective-permute-start(bf16[208,512]{1,0:T(8,128)(2,1)} %get-tuple-element.117.refs_0_), channel_id=1, source_target_pairs={{0,1},{1,2},{2,3},{3,0},{4,5},{5,6},{6,7},{7,4},{8,9},{9,10},{10,1... | collective-permute-start | bytes 638984 | tf_op jit(solution)/shard_map/ppermute | solution.py:344
  16.2 10.8 %collective-permute-start.5 = (bf16[112,512]{1,0:T(8,128)(2,1)S(1)}, bf16[112,512]{1,0:T(8,128)(2,1)S(1)}, u32[]{:S(2)}, u32[]{:S(2)}) collective-permute-start(bf16[112,512]{1,0:T(8,128)(2,1)S(1)} %slice.261), channel_id=1, source_target_pairs={{0,3},{1,0},{2,1},{3,2},{4,7},{5,4},{6,5},{7,6},{8,11},{9,8},{10,9... | collective-permute-start | bytes 344072 | tf_op jit(solution)/shard_map/ppermute | solution.py:344
  30.7 18.6 %collective-permute-start.6 = (bf16[4,208,512]{2,1,0:T(8,128)(2,1)}, bf16[4,208,512]{2,1,0:T(8,128)(2,1)S(1)}, u32[]{:S(2)}, u32[]{:S(2)}) collective-permute-start(bf16[4,208,512]{2,1,0:T(8,128)(2,1)} %get-tuple-element.118.refs_0_), channel_id=1, source_target_pairs={{0,8},{1,9},{2,10},{3,11},{4,12},{5,13},{6,14},{7,15},{8,0},{9,1},... | collective-permute-start | bytes 2555912 | tf_op jit(solution)/shard_map/ppermute | solution.py:344
  31.9 18.4 %collective-permute-start.7 = (bf16[4,208,512]{2,1,0:T(8,128)(2,1)}, bf16[4,208,512]{2,1,0:T(8,128)(2,1)S(1)}, u32[]{:S(2)}, u32[]{:S(2)}) collective-permute-start(bf16[4,208,512]{2,1,0:T(8,128)(2,1)} %get-tuple-element.118.refs_0_), channel_id=1, source_target_pairs={{0,16},{1,17},{2,18},{3,19},{4,20},{5,21},{6,22},{7,23},{8,24},{9,... | collective-permute-start | bytes 2555912 | tf_op jit(solution)/shard_map/ppermute | solution.py:344
  32.2 20.2 %collective-permute-start.10 = (bf16[160,1024]{1,0:T(8,128)(2,1)}, bf16[160,1024]{1,0:T(8,128)(2,1)S(1)}, u32[]{:S(2)}, u32[]{:S(2)}) collective-permute-start(bf16[160,1024]{1,0:T(8,128)(2,1)} %get-tuple-element.119.refs_0_), channel_id=1, source_target_pairs={{0,3},{1,0},{2,1},{3,2},{4,7},{5,4},{6,5},{7,6},{8,11},{9,8},{10,9... | collective-permute-start | bytes 983048 | tf_op jit(solution)/shard_map/ppermute | solution.py:344
  33.5 19.6 %collective-permute-start.8 = (bf16[160,1024]{1,0:T(8,128)(2,1)}, bf16[160,1024]{1,0:T(8,128)(2,1)S(1)}, u32[]{:S(2)}, u32[]{:S(2)}) collective-permute-start(bf16[160,1024]{1,0:T(8,128)(2,1)} %get-tuple-element.119.refs_0_), channel_id=1, source_target_pairs={{0,1},{1,2},{2,3},{3,0},{4,5},{5,6},{6,7},{7,4},{8,9},{9,10},{10,1... | collective-permute-start | bytes 983048 | tf_op jit(solution)/shard_map/ppermute | solution.py:344
  50.1 15.7 %collective-permute-start.14 = (bf16[2,208,512]{2,1,0:T(8,128)(2,1)}, bf16[2,208,512]{2,1,0:T(8,128)(2,1)S(1)}, u32[]{:S(2)}, u32[]{:S(2)}) collective-permute-start(bf16[2,208,512]{2,1,0:T(8,128)(2,1)} %slice.264), channel_id=1, source_target_pairs={{0,16},{1,17},{2,18},{3,19},{4,20},{5,21},{6,22},{7,23},{8,24},{9,... | collective-permute-start | bytes 1277960 | tf_op jit(solution)/shard_map/ppermute | solution.py:344
  51.2 14.7 %collective-permute-start.15 = (bf16[2,208,512]{2,1,0:T(8,128)(2,1)}, bf16[2,208,512]{2,1,0:T(8,128)(2,1)S(1)}, u32[]{:S(2)}, u32[]{:S(2)}) collective-permute-start(bf16[2,208,512]{2,1,0:T(8,128)(2,1)} %slice.265), channel_id=1, source_target_pairs={{0,8},{1,9},{2,10},{3,11},{4,12},{5,13},{6,14},{7,15},{8,0},{9,1},... | collective-permute-start | bytes 1277960 | tf_op jit(solution)/shard_map/ppermute | solution.py:344
  52.4 5.9 %collective-permute-start.11 = (bf16[80,1024]{1,0:T(8,128)(2,1)S(1)}, bf16[80,1024]{1,0:T(8,128)(2,1)S(1)}, u32[]{:S(2)}, u32[]{:S(2)}) collective-permute-start(bf16[80,1024]{1,0:T(8,128)(2,1)S(1)} %slice.263), channel_id=1, source_target_pairs={{0,3},{1,0},{2,1},{3,2},{4,7},{5,4},{6,5},{7,6},{8,11},{9,8},{10,9... | collective-permute-start | bytes 491528 | tf_op jit(solution)/shard_map/ppermute | solution.py:344
  53.2 9.7 %collective-permute-start.9 = (bf16[80,1024]{1,0:T(8,128)(2,1)S(1)}, bf16[80,1024]{1,0:T(8,128)(2,1)}, u32[]{:S(2)}, u32[]{:S(2)}) collective-permute-start(bf16[80,1024]{1,0:T(8,128)(2,1)S(1)} %slice.262), channel_id=1, source_target_pairs={{0,1},{1,2},{2,3},{3,0},{4,5},{5,6},{6,7},{7,4},{8,9},{9,10},{10,1... | collective-permute-start | bytes 491528 | tf_op jit(solution)/shard_map/ppermute | solution.py:344
  69.1 35.2 %collective-permute-start.22 = (bf16[4,160,1024]{2,1,0:T(8,128)(2,1)}, bf16[4,160,1024]{2,1,0:T(8,128)(2,1)S(1)}, u32[]{:S(2)}, u32[]{:S(2)}) collective-permute-start(bf16[4,160,1024]{2,1,0:T(8,128)(2,1)} %down_inner.2.refs_5_.refs_0_), channel_id=1, source_target_pairs={{0,8},{1,9},{2,10},{3,11},{4,12},{5,13},{6,14},{7,15},{8,0},{9,1},... | collective-permute-start | bytes 3932168 | tf_op jit(solution)/shard_map/ppermute | solution.py:344
  69.4 36.0 %collective-permute-start.24 = (bf16[4,160,1024]{2,1,0:T(8,128)(2,1)}, bf16[4,160,1024]{2,1,0:T(8,128)(2,1)S(1)}, u32[]{:S(2)}, u32[]{:S(2)}) collective-permute-start(bf16[4,160,1024]{2,1,0:T(8,128)(2,1)} %down_inner.2.refs_5_.refs_0_), channel_id=1, source_target_pairs={{0,16},{1,17},{2,18},{3,19},{4,20},{5,21},{6,22},{7,23},{8,24},{9,... | collective-permute-start | bytes 3932168 | tf_op jit(solution)/shard_map/ppermute | solution.py:344
  70.7 23.8 %collective-permute-start.12 = (bf16[272,1024]{1,0:T(8,128)(2,1)}, bf16[272,1024]{1,0:T(8,128)(2,1)}, u32[]{:S(2)}, u32[]{:S(2)}) collective-permute-start(bf16[272,1024]{1,0:T(8,128)(2,1)} %get-tuple-element.120.refs_7_), channel_id=1, source_target_pairs={{0,0},{1,1},{2,4},{3,5},{4,2},{5,3},{6,6},{7,7},{8,8},{9,9},{10,12... | collective-permute-start | bytes 1671176 | tf_op jit(solution)/shard_map/ppermute | solution.py:344
  77.3 24.8 %collective-permute-start.13 = (bf16[272,1024]{1,0:T(8,128)(2,1)}, bf16[272,1024]{1,0:T(8,128)(2,1)}, u32[]{:S(2)}, u32[]{:S(2)}) collective-permute-start(bf16[272,1024]{1,0:T(8,128)(2,1)} %get-tuple-element.121), channel_id=1, source_target_pairs={{0,1},{1,0},{2,5},{3,4},{4,3},{5,2},{6,7},{7,6},{8,9},{9,8},{10,13... | collective-permute-start | bytes 1671176 | tf_op jit(solution)/shard_map/ppermute | solution.py:344
  102.1 6.2 %collective-permute-start.16 = (bf16[272,1024]{1,0:T(8,128)(2,1)}, bf16[272,1024]{1,0:T(8,128)(2,1)}, u32[]{:S(2)}, u32[]{:S(2)}) collective-permute-start(bf16[272,1024]{1,0:T(8,128)(2,1)} %collective-permute-done.12.refs_0_), channel_id=1, source_target_pairs={{0,4},{1,5},{2,6},{3,7},{4,0},{5,1},{6,2},{7,3},{8,12},{9,13},{10,... | collective-permute-start | bytes 1671176 | tf_op jit(solution)/shard_map/ppermute | solution.py:344
  102.1 6.2 %collective-permute-start.17 = (bf16[272,1024]{1,0:T(8,128)(2,1)}, bf16[272,1024]{1,0:T(8,128)(2,1)}, u32[]{:S(2)}, u32[]{:S(2)}) collective-permute-start(bf16[272,1024]{1,0:T(8,128)(2,1)} %collective-permute-done.13.refs_1_), channel_id=1, source_target_pairs={{0,4},{1,5},{2,6},{3,7},{4,0},{5,1},{6,2},{7,3},{8,12},{9,13},{10,... | collective-permute-start | bytes 1671176 | tf_op jit(solution)/shard_map/ppermute | solution.py:344
  105.2 35.5 %collective-permute-start.23 = (bf16[2,160,1024]{2,1,0:T(8,128)(2,1)}, bf16[2,160,1024]{2,1,0:T(8,128)(2,1)S(1)}, u32[]{:S(2)}, u32[]{:S(2)}) collective-permute-start(bf16[2,160,1024]{2,1,0:T(8,128)(2,1)} %slice.274), channel_id=1, source_target_pairs={{0,16},{1,17},{2,18},{3,19},{4,20},{5,21},{6,22},{7,23},{8,24},{9,... | collective-permute-start | bytes 1966088 | tf_op jit(solution)/shard_map/ppermute | solution.py:344
  106.4 34.4 %collective-permute-start.25 = (bf16[2,160,1024]{2,1,0:T(8,128)(2,1)}, bf16[2,160,1024]{2,1,0:T(8,128)(2,1)}, u32[]{:S(2)}, u32[]{:S(2)}) collective-permute-start(bf16[2,160,1024]{2,1,0:T(8,128)(2,1)} %slice.275), channel_id=1, source_target_pairs={{0,8},{1,9},{2,10},{3,11},{4,12},{5,13},{6,14},{7,15},{8,0},{9,1},... | collective-permute-start | bytes 1966088 | tf_op jit(solution)/shard_map/ppermute | solution.py:344
  111.5 9.7 %collective-permute-start.18 = (bf16[64,2048]{1,0:T(8,128)(2,1)}, bf16[64,2048]{1,0:T(8,128)(2,1)S(1)}, u32[]{:S(2)}, u32[]{:S(2)}) collective-permute-start(bf16[64,2048]{1,0:T(8,128)(2,1)} %get-tuple-element.130.refs_0_), channel_id=1, source_target_pairs={{0,1},{1,2},{2,3},{3,0},{4,5},{5,6},{6,7},{7,4},{8,9},{9,10},{10,1... | collective-permute-start | bytes 786440 | tf_op jit(solution)/shard_map/ppermute | solution.py:344
  112.5 11.2 %collective-permute-start.19 = (bf16[64,2048]{1,0:T(8,128)(2,1)}, bf16[64,2048]{1,0:T(8,128)(2,1)S(1)}, u32[]{:S(2)}, u32[]{:S(2)}) collective-permute-start(bf16[64,2048]{1,0:T(8,128)(2,1)} %get-tuple-element.130.refs_0_), channel_id=1, source_target_pairs={{0,3},{1,0},{2,1},{3,2},{4,7},{5,4},{6,5},{7,6},{8,11},{9,8},{10,9... | collective-permute-start | bytes 786440 | tf_op jit(solution)/shard_map/ppermute | solution.py:344
  121.2 6.3 %collective-permute-start.20 = (bf16[32,2048]{1,0:T(8,128)(2,1)S(1)}, bf16[32,2048]{1,0:T(8,128)(2,1)S(1)}, u32[]{:S(2)}, u32[]{:S(2)}) collective-permute-start(bf16[32,2048]{1,0:T(8,128)(2,1)S(1)} %slice.272), channel_id=1, source_target_pairs={{0,1},{1,2},{2,3},{3,0},{4,5},{5,6},{6,7},{7,4},{8,9},{9,10},{10,1... | collective-permute-start | bytes 393224 | tf_op jit(solution)/shard_map/ppermute | solution.py:344
  123.8 6.5 %collective-permute-start.21 = (bf16[32,2048]{1,0:T(8,128)(2,1)S(1)}, bf16[32,2048]{1,0:T(8,128)(2,1)S(1)}, u32[]{:S(2)}, u32[]{:S(2)}) collective-permute-start(bf16[32,2048]{1,0:T(8,128)(2,1)S(1)} %slice.273), channel_id=1, source_target_pairs={{0,3},{1,0},{2,1},{3,2},{4,7},{5,4},{6,5},{7,6},{8,11},{9,8},{10,9... | collective-permute-start | bytes 393224 | tf_op jit(solution)/shard_map/ppermute | solution.py:344
  133.1 32.9 %collective-permute-start.28 = (bf16[256,1024]{1,0:T(8,128)(2,1)}, bf16[256,1024]{1,0:T(8,128)(2,1)S(1)}, u32[]{:S(2)}, u32[]{:S(2)}) collective-permute-start(bf16[256,1024]{1,0:T(8,128)(2,1)} %get-tuple-element.132.refs_6_), channel_id=1, source_target_pairs={{0,0},{1,1},{2,4},{3,5},{4,2},{5,3},{6,6},{7,7},{8,8},{9,9},{10,12... | collective-permute-start | bytes 1572872 | tf_op jit(solution)/shard_map/ppermute | solution.py:344
  140.7 25.3 %collective-permute-start.29 = (bf16[256,1024]{1,0:T(8,128)(2,1)}, bf16[256,1024]{1,0:T(8,128)(2,1)}, u32[]{:S(2)}, u32[]{:S(2)}) collective-permute-start(bf16[256,1024]{1,0:T(8,128)(2,1)} %get-tuple-element.133.refs_7_), channel_id=1, source_target_pairs={{0,1},{1,0},{2,5},{3,4},{4,3},{5,2},{6,7},{7,6},{8,9},{9,8},{10,13... | collective-permute-start | bytes 1572872 | tf_op jit(solution)/shard_map/ppermute | solution.py:344
  143.8 31.6 %collective-permute-start.26 = (bf16[4,64,2048]{2,1,0:T(8,128)(2,1)}, bf16[4,64,2048]{2,1,0:T(8,128)(2,1)S(1)}, u32[]{:S(2)}, u32[]{:S(2)}) collective-permute-start(bf16[4,64,2048]{2,1,0:T(8,128)(2,1)} %up_inner.2.refs_5_.refs_0_), channel_id=1, source_target_pairs={{0,8},{1,9},{2,10},{3,11},{4,12},{5,13},{6,14},{7,15},{8,0},{9,1},... | collective-permute-start | bytes 3145736 | tf_op jit(solution)/shard_map/ppermute | solution.py:344
  144.1 31.3 %collective-permute-start.27 = (bf16[4,64,2048]{2,1,0:T(8,128)(2,1)}, bf16[4,64,2048]{2,1,0:T(8,128)(2,1)S(1)}, u32[]{:S(2)}, u32[]{:S(2)}) collective-permute-start(bf16[4,64,2048]{2,1,0:T(8,128)(2,1)} %up_inner.2.refs_5_.refs_0_), channel_id=1, source_target_pairs={{0,16},{1,17},{2,18},{3,19},{4,20},{5,21},{6,22},{7,23},{8,24},{9,... | collective-permute-start | bytes 3145736 | tf_op jit(solution)/shard_map/ppermute | solution.py:344
  166.0 5.7 %collective-permute-start.30 = (bf16[256,1024]{1,0:T(8,128)(2,1)S(1)}, bf16[256,1024]{1,0:T(8,128)(2,1)S(1)}, u32[]{:S(2)}, u32[]{:S(2)}) collective-permute-start(bf16[256,1024]{1,0:T(8,128)(2,1)S(1)} %collective-permute-done.28.refs_0_), channel_id=1, source_target_pairs={{0,4},{1,5},{2,6},{3,7},{4,0},{5,1},{6,2},{7,3},{8,12},{9,13},{10,... | collective-permute-start | bytes 1572872 | tf_op jit(solution)/shard_map/ppermute | solution.py:344
  166.1 5.6 %collective-permute-start.31 = (bf16[256,1024]{1,0:T(8,128)(2,1)}, bf16[256,1024]{1,0:T(8,128)(2,1)}, u32[]{:S(2)}, u32[]{:S(2)}) collective-permute-start(bf16[256,1024]{1,0:T(8,128)(2,1)} %collective-permute-done.29.refs_1_), channel_id=1, source_target_pairs={{0,4},{1,5},{2,6},{3,7},{4,0},{5,1},{6,2},{7,3},{8,12},{9,13},{10,... | collective-permute-start | bytes 1572872 | tf_op jit(solution)/shard_map/ppermute | solution.py:344
  181.6 9.3 %collective-permute-start.32 = (bf16[1024,1024]{1,0:T(8,128)(2,1)}, bf16[1024,1024]{1,0:T(8,128)(2,1)S(1)}, u32[]{:S(2)}, u32[]{:S(2)}) collective-permute-start(bf16[1024,1024]{1,0:T(8,128)(2,1)} %attend_out.1.part), channel_id=1, source_target_pairs={{0,4},{1,5},{2,6},{3,7},{4,0},{5,1},{6,2},{7,3},{8,12},{9,13},{10,... | collective-permute-start | bytes 6291464 | tf_op jit(solution)/shard_map/ppermute | solution.py:344
  183.6 14.7 %collective-permute-start.33 = (bf16[2,64,2048]{2,1,0:T(8,128)(2,1)}, bf16[2,64,2048]{2,1,0:T(8,128)(2,1)S(1)}, u32[]{:S(2)}, u32[]{:S(2)}) collective-permute-start(bf16[2,64,2048]{2,1,0:T(8,128)(2,1)} %slice.279), channel_id=1, source_target_pairs={{0,16},{1,17},{2,18},{3,19},{4,20},{5,21},{6,22},{7,23},{8,24},{9,... | collective-permute-start | bytes 1572872 | tf_op jit(solution)/shard_map/ppermute | solution.py:344
  185.7 13.0 %collective-permute-start.34 = (bf16[2,64,2048]{2,1,0:T(8,128)(2,1)}, bf16[2,64,2048]{2,1,0:T(8,128)(2,1)S(1)}, u32[]{:S(2)}, u32[]{:S(2)}) collective-permute-start(bf16[2,64,2048]{2,1,0:T(8,128)(2,1)} %slice.280), channel_id=1, source_target_pairs={{0,8},{1,9},{2,10},{3,11},{4,12},{5,13},{6,14},{7,15},{8,0},{9,1},... | collective-permute-start | bytes 1572872 | tf_op jit(solution)/shard_map/ppermute | solution.py:344
  239.7 34.8 %collective-permute-start.40 = (bf16[1024,1024]{1,0:T(8,128)(2,1)}, bf16[1024,1024]{1,0:T(8,128)(2,1)S(1)}, u32[]{:S(2)}, u32[]{:S(2)}) collective-permute-start(bf16[1024,1024]{1,0:T(8,128)(2,1)} %second_grad.1.refs_3_.refs_0_), channel_id=1, source_target_pairs={{0,4},{1,5},{2,6},{3,7},{4,0},{5,1},{6,2},{7,3},{8,12},{9,13},{10,... | collective-permute-start | bytes 6291464 | tf_op jit(solution)/shard_map/ppermute | solution.py:344
  241.3 29.5 %collective-permute-start.35 = (bf16[512,1024]{1,0:T(8,128)(2,1)}, bf16[512,1024]{1,0:T(8,128)(2,1)}, u32[]{:S(2)}, u32[]{:S(2)}) collective-permute-start(bf16[512,1024]{1,0:T(8,128)(2,1)} %get-tuple-element.145), channel_id=1, source_target_pairs={{0,4},{1,5},{2,6},{3,7},{4,0},{5,1},{6,2},{7,3},{8,12},{9,13},{10,... | collective-permute-start | bytes 3145736 | tf_op jit(solution)/shard_map/ppermute | solution.py:344
  251.7 13.4 %collective-permute-start.36 = (bf16[2,128,1024]{2,1,0:T(8,128)(2,1)}, bf16[2,128,1024]{2,1,0:T(8,128)(2,1)S(1)}, u32[]{:S(2)}, u32[]{:S(2)}) collective-permute-start(bf16[2,128,1024]{2,1,0:T(8,128)(2,1)} %get-tuple-element.149), channel_id=1, source_target_pairs={{0,8},{1,9},{2,10},{3,11},{4,12},{5,13},{6,14},{7,15},{8,0},{9,1},... | collective-permute-start | bytes 1572872 | tf_op jit(solution)/shard_map/ppermute | solution.py:344
  252.9 13.4 %collective-permute-start.37 = (bf16[2,128,1024]{2,1,0:T(8,128)(2,1)}, bf16[2,128,1024]{2,1,0:T(8,128)(2,1)}, u32[]{:S(2)}, u32[]{:S(2)}) collective-permute-start(bf16[2,128,1024]{2,1,0:T(8,128)(2,1)} %get-tuple-element.150), channel_id=1, source_target_pairs={{0,16},{1,17},{2,18},{3,19},{4,20},{5,21},{6,22},{7,23},{8,24},{9,... | collective-permute-start | bytes 1572872 | tf_op jit(solution)/shard_map/ppermute | solution.py:344
  264.8 24.1 %collective-permute-start.41 = (bf16[2,64,2048]{2,1,0:T(8,128)(2,1)}, bf16[2,64,2048]{2,1,0:T(8,128)(2,1)S(1)}, u32[]{:S(2)}, u32[]{:S(2)}) collective-permute-start(bf16[2,64,2048]{2,1,0:T(8,128)(2,1)} %get-tuple-element.160), channel_id=1, source_target_pairs={{0,8},{1,9},{2,10},{3,11},{4,12},{5,13},{6,14},{7,15},{8,0},{9,1},... | collective-permute-start | bytes 1572872 | tf_op jit(solution)/shard_map/ppermute | solution.py:344
  265.0 23.9 %collective-permute-start.42 = (bf16[2,64,2048]{2,1,0:T(8,128)(2,1)}, bf16[2,64,2048]{2,1,0:T(8,128)(2,1)}, u32[]{:S(2)}, u32[]{:S(2)}) collective-permute-start(bf16[2,64,2048]{2,1,0:T(8,128)(2,1)} %get-tuple-element.161), channel_id=1, source_target_pairs={{0,16},{1,17},{2,18},{3,19},{4,20},{5,21},{6,22},{7,23},{8,24},{9,... | collective-permute-start | bytes 1572872 | tf_op jit(solution)/shard_map/ppermute | solution.py:344
  269.6 38.2 %collective-permute-start.43 = (bf16[4,128,1024]{2,1,0:T(8,128)(2,1)}, bf16[4,128,1024]{2,1,0:T(8,128)(2,1)}, u32[]{:S(2)}, u32[]{:S(2)}) collective-permute-start(bf16[4,128,1024]{2,1,0:T(8,128)(2,1)} %get-tuple-element.153.refs_2_), channel_id=1, source_target_pairs={{0,8},{1,9},{2,10},{3,11},{4,12},{5,13},{6,14},{7,15},{8,0},{9,1},... | collective-permute-start | bytes 3145736 | tf_op jit(solution)/shard_map/ppermute | solution.py:344
  270.8 39.1 %collective-permute-start.44 = (bf16[4,128,1024]{2,1,0:T(8,128)(2,1)}, bf16[4,128,1024]{2,1,0:T(8,128)(2,1)}, u32[]{:S(2)}, u32[]{:S(2)}) collective-permute-start(bf16[4,128,1024]{2,1,0:T(8,128)(2,1)} %get-tuple-element.166), channel_id=1, source_target_pairs={{0,16},{1,17},{2,18},{3,19},{4,20},{5,21},{6,22},{7,23},{8,24},{9,... | collective-permute-start | bytes 3145736 | tf_op jit(solution)/shard_map/ppermute | solution.py:344
  274.6 38.7 %collective-permute-start.38 = (bf16[256,1024]{1,0:T(8,128)(2,1)}, bf16[256,1024]{1,0:T(8,128)(2,1)S(1)}, u32[]{:S(2)}, u32[]{:S(2)}) collective-permute-start(bf16[256,1024]{1,0:T(8,128)(2,1)} %get-tuple-element.154.refs_6_), channel_id=1, source_target_pairs={{0,0},{1,1},{2,4},{3,5},{4,2},{5,3},{6,6},{7,7},{8,8},{9,9},{10,12... | collective-permute-start | bytes 1572872 | tf_op jit(solution)/shard_map/ppermute | solution.py:344
  293.0 38.5 %collective-permute-start.45 = (bf16[4,64,2048]{2,1,0:T(8,128)(2,1)}, bf16[4,64,2048]{2,1,0:T(8,128)(2,1)S(1)}, u32[]{:S(2)}, u32[]{:S(2)}) collective-permute-start(bf16[4,64,2048]{2,1,0:T(8,128)(2,1)} %get-tuple-element.163.refs_7_), channel_id=1, source_target_pairs={{0,8},{1,9},{2,10},{3,11},{4,12},{5,13},{6,14},{7,15},{8,0},{9,1},... | collective-permute-start | bytes 3145736 | tf_op jit(solution)/shard_map/ppermute | solution.py:344
  293.7 37.8 %collective-permute-start.46 = (bf16[4,64,2048]{2,1,0:T(8,128)(2,1)}, bf16[4,64,2048]{2,1,0:T(8,128)(2,1)S(1)}, u32[]{:S(2)}, u32[]{:S(2)}) collective-permute-start(bf16[4,64,2048]{2,1,0:T(8,128)(2,1)} %get-tuple-element.169), channel_id=1, source_target_pairs={{0,16},{1,17},{2,18},{3,19},{4,20},{5,21},{6,22},{7,23},{8,24},{9,... | collective-permute-start | bytes 3145736 | tf_op jit(solution)/shard_map/ppermute | solution.py:344
  307.8 20.9 %collective-permute-start.39 = (bf16[256,1024]{1,0:T(8,128)(2,1)}, bf16[256,1024]{1,0:T(8,128)(2,1)S(1)}, u32[]{:S(2)}, u32[]{:S(2)}) collective-permute-start(bf16[256,1024]{1,0:T(8,128)(2,1)} %get-tuple-element.155), channel_id=1, source_target_pairs={{0,1},{1,0},{2,5},{3,4},{4,3},{5,2},{6,7},{7,6},{8,9},{9,8},{10,13... | collective-permute-start | bytes 1572872 | tf_op jit(solution)/shard_map/ppermute | solution.py:344
  313.2 15.5 %collective-permute-start.47 = (bf16[64,1024]{1,0:T(8,128)(2,1)}, bf16[64,1024]{1,0:T(8,128)(2,1)S(1)}, u32[]{:S(2)}, u32[]{:S(2)}) collective-permute-start(bf16[64,1024]{1,0:T(8,128)(2,1)} %get-tuple-element.172), channel_id=1, source_target_pairs={{0,1},{1,2},{2,3},{3,0},{4,5},{5,6},{6,7},{7,4},{8,9},{9,10},{10,1... | collective-permute-start | bytes 393224 | tf_op jit(solution)/shard_map/ppermute | solution.py:344
  313.3 15.5 %collective-permute-start.48 = (bf16[64,1024]{1,0:T(8,128)(2,1)}, bf16[64,1024]{1,0:T(8,128)(2,1)S(1)}, u32[]{:S(2)}, u32[]{:S(2)}) collective-permute-start(bf16[64,1024]{1,0:T(8,128)(2,1)} %get-tuple-element.173), channel_id=1, source_target_pairs={{0,3},{1,0},{2,1},{3,2},{4,7},{5,4},{6,5},{7,6},{8,11},{9,8},{10,9... | collective-permute-start | bytes 393224 | tf_op jit(solution)/shard_map/ppermute | solution.py:344
  343.7 16.5 %collective-permute-start.49 = (bf16[1024,1024]{1,0:T(8,128)(2,1)}, bf16[1024,1024]{1,0:T(8,128)(2,1)S(1)}, u32[]{:S(2)}, u32[]{:S(2)}) collective-permute-start(bf16[1024,1024]{1,0:T(8,128)(2,1)} %source_grad.1.refs_5_.refs_1_), channel_id=1, source_target_pairs={{0,4},{1,5},{2,6},{3,7},{4,0},{5,1},{6,2},{7,3},{8,12},{9,13},{10,... | collective-permute-start | bytes 6291464 | tf_op jit(solution)/shard_map/ppermute | solution.py:344
  343.9 16.3 %collective-permute-start.50 = (bf16[128,1024]{1,0:T(8,128)(2,1)S(1)}, bf16[128,1024]{1,0:T(8,128)(2,1)S(1)}, u32[]{:S(2)}, u32[]{:S(2)}) collective-permute-start(bf16[128,1024]{1,0:T(8,128)(2,1)S(1)} %copy-done.47), channel_id=1, source_target_pairs={{0,1},{1,2},{2,3},{3,0},{4,5},{5,6},{6,7},{7,4},{8,9},{9,10},{10,1... | collective-permute-start | bytes 786440 | tf_op jit(solution)/shard_map/ppermute | solution.py:344
  346.2 14.0 %collective-permute-start.51 = (bf16[128,1024]{1,0:T(8,128)(2,1)}, bf16[128,1024]{1,0:T(8,128)(2,1)S(1)}, u32[]{:S(2)}, u32[]{:S(2)}) collective-permute-start(bf16[128,1024]{1,0:T(8,128)(2,1)} %get-tuple-element.179), channel_id=1, source_target_pairs={{0,3},{1,0},{2,1},{3,2},{4,7},{5,4},{6,5},{7,6},{8,11},{9,8},{10,9... | collective-permute-start | bytes 786440 | tf_op jit(solution)/shard_map/ppermute | solution.py:344
  358.4 16.2 %collective-permute-start.54 = (bf16[2,256,512]{2,1,0:T(8,128)(2,1)}, bf16[2,256,512]{2,1,0:T(8,128)(2,1)S(1)}, u32[]{:S(2)}, u32[]{:S(2)}) collective-permute-start(bf16[2,256,512]{2,1,0:T(8,128)(2,1)} %get-tuple-element.184), channel_id=1, source_target_pairs={{0,8},{1,9},{2,10},{3,11},{4,12},{5,13},{6,14},{7,15},{8,0},{9,1},... | collective-permute-start | bytes 1572872 | tf_op jit(solution)/shard_map/ppermute | solution.py:344
  359.7 14.9 %collective-permute-start.55 = (bf16[2,256,512]{2,1,0:T(8,128)(2,1)}, bf16[2,256,512]{2,1,0:T(8,128)(2,1)}, u32[]{:S(2)}, u32[]{:S(2)}) collective-permute-start(bf16[2,256,512]{2,1,0:T(8,128)(2,1)} %get-tuple-element.185), channel_id=1, source_target_pairs={{0,16},{1,17},{2,18},{3,19},{4,20},{5,21},{6,22},{7,23},{8,24},{9,... | collective-permute-start | bytes 1572872 | tf_op jit(solution)/shard_map/ppermute | solution.py:344
  381.6 31.9 %collective-permute-start.59 = (bf16[4,256,512]{2,1,0:T(8,128)(2,1)}, bf16[4,256,512]{2,1,0:T(8,128)(2,1)S(1)}, u32[]{:S(2)}, u32[]{:S(2)}) collective-permute-start(bf16[4,256,512]{2,1,0:T(8,128)(2,1)} %get-tuple-element.189), channel_id=1, source_target_pairs={{0,8},{1,9},{2,10},{3,11},{4,12},{5,13},{6,14},{7,15},{8,0},{9,1},... | collective-permute-start | bytes 3145736 | tf_op jit(solution)/shard_map/ppermute | solution.py:344
  382.5 31.1 %collective-permute-start.60 = (bf16[4,256,512]{2,1,0:T(8,128)(2,1)}, bf16[4,256,512]{2,1,0:T(8,128)(2,1)S(1)}, u32[]{:S(2)}, u32[]{:S(2)}) collective-permute-start(bf16[4,256,512]{2,1,0:T(8,128)(2,1)} %get-tuple-element.190), channel_id=1, source_target_pairs={{0,16},{1,17},{2,18},{3,19},{4,20},{5,21},{6,22},{7,23},{8,24},{9,... | collective-permute-start | bytes 3145736 | tf_op jit(solution)/shard_map/ppermute | solution.py:344
  383.3 19.8 %collective-permute-start.52 = (bf16[256,1024]{1,0:T(8,128)(2,1)}, bf16[256,1024]{1,0:T(8,128)(2,1)S(1)}, u32[]{:S(2)}, u32[]{:S(2)}) collective-permute-start(bf16[256,1024]{1,0:T(8,128)(2,1)} %get-tuple-element.180.refs_4_), channel_id=1, source_target_pairs={{0,0},{1,1},{2,4},{3,5},{4,2},{5,3},{6,6},{7,7},{8,8},{9,9},{10,12... | collective-permute-start | bytes 1572872 | tf_op jit(solution)/shard_map/ppermute | solution.py:344
  390.1 23.4 %collective-permute-start.53 = (bf16[256,1024]{1,0:T(8,128)(2,1)}, bf16[256,1024]{1,0:T(8,128)(2,1)S(1)}, u32[]{:S(2)}, u32[]{:S(2)}) collective-permute-start(bf16[256,1024]{1,0:T(8,128)(2,1)} %get-tuple-element.181), channel_id=1, source_target_pairs={{0,1},{1,0},{2,5},{3,4},{4,3},{5,2},{6,7},{7,6},{8,9},{9,8},{10,13... | collective-permute-start | bytes 1572872 | tf_op jit(solution)/shard_map/ppermute | solution.py:344
  418.6 5.9 %collective-permute-start.62 = (bf16[144,512]{1,0:T(8,128)(2,1)}, bf16[144,512]{1,0:T(8,128)(2,1)S(1)}, u32[]{:S(2)}, u32[]{:S(2)}) collective-permute-start(bf16[144,512]{1,0:T(8,128)(2,1)} %get-tuple-element.195), channel_id=1, source_target_pairs={{0,3},{1,0},{2,1},{3,2},{4,7},{5,4},{6,5},{7,6},{8,11},{9,8},{10,9... | collective-permute-start | bytes 442376 | tf_op jit(solution)/shard_map/ppermute | solution.py:344
  418.6 5.0 %collective-permute-start.61 = (bf16[128,512]{1,0:T(8,128)(2,1)}, bf16[128,512]{1,0:T(8,128)(2,1)S(1)}, u32[]{:S(2)}, u32[]{:S(2)}) collective-permute-start(bf16[128,512]{1,0:T(8,128)(2,1)} %get-tuple-element.194), channel_id=1, source_target_pairs={{0,1},{1,2},{2,3},{3,0},{4,5},{5,6},{6,7},{7,4},{8,9},{9,10},{10,1... | collective-permute-start | bytes 393224 | tf_op jit(solution)/shard_map/ppermute | solution.py:344
  420.0 9.7 %collective-permute-start.66 = (bf16[32,2048]{1,0:T(8,128)(2,1)S(1)}, bf16[32,2048]{1,0:T(8,128)(2,1)S(1)}, u32[]{:S(2)}, u32[]{:S(2)}) collective-permute-start(bf16[32,2048]{1,0:T(8,128)(2,1)S(1)} %copy-done.67), channel_id=1, source_target_pairs={{0,1},{1,2},{2,3},{3,0},{4,5},{5,6},{6,7},{7,4},{8,9},{9,10},{10,1... | collective-permute-start | bytes 393224 | tf_op jit(solution)/shard_map/ppermute | solution.py:344
  420.1 11.8 %collective-permute-start.67 = (bf16[32,2048]{1,0:T(8,128)(2,1)S(1)}, bf16[32,2048]{1,0:T(8,128)(2,1)S(1)}, u32[]{:S(2)}, u32[]{:S(2)}) collective-permute-start(bf16[32,2048]{1,0:T(8,128)(2,1)S(1)} %copy-done.66), channel_id=1, source_target_pairs={{0,3},{1,0},{2,1},{3,2},{4,7},{5,4},{6,5},{7,6},{8,11},{9,8},{10,9... | collective-permute-start | bytes 393224 | tf_op jit(solution)/shard_map/ppermute | solution.py:344
  427.1 10.4 %collective-permute-start.63 = (bf16[272,512]{1,0:T(8,128)(2,1)}, bf16[272,512]{1,0:T(8,128)(2,1)S(1)}, u32[]{:S(2)}, u32[]{:S(2)}) collective-permute-start(bf16[272,512]{1,0:T(8,128)(2,1)} %get-tuple-element.196.refs_4_), channel_id=1, source_target_pairs={{0,1},{1,2},{2,3},{3,0},{4,5},{5,6},{6,7},{7,4},{8,9},{9,10},{10,1... | collective-permute-start | bytes 835592 | tf_op jit(solution)/shard_map/ppermute | solution.py:344
  427.2 18.3 %collective-permute-start.64 = (bf16[272,512]{1,0:T(8,128)(2,1)}, bf16[272,512]{1,0:T(8,128)(2,1)S(1)}, u32[]{:S(2)}, u32[]{:S(2)}) collective-permute-start(bf16[272,512]{1,0:T(8,128)(2,1)} %get-tuple-element.197), channel_id=1, source_target_pairs={{0,3},{1,0},{2,1},{3,2},{4,7},{5,4},{6,5},{7,6},{8,11},{9,8},{10,9... | collective-permute-start | bytes 835592 | tf_op jit(solution)/shard_map/ppermute | solution.py:344
  434.5 15.3 %collective-permute-start.68 = (bf16[64,2048]{1,0:T(8,128)(2,1)}, bf16[64,2048]{1,0:T(8,128)(2,1)S(1)}, u32[]{:S(2)}, u32[]{:S(2)}) collective-permute-start(bf16[64,2048]{1,0:T(8,128)(2,1)} %get-tuple-element.208), channel_id=1, source_target_pairs={{0,1},{1,2},{2,3},{3,0},{4,5},{5,6},{6,7},{7,4},{8,9},{9,10},{10,1... | collective-permute-start | bytes 786440 | tf_op jit(solution)/shard_map/ppermute | solution.py:344
  434.5 19.4 %collective-permute-start.69 = (bf16[64,2048]{1,0:T(8,128)(2,1)}, bf16[64,2048]{1,0:T(8,128)(2,1)S(1)}, u32[]{:S(2)}, u32[]{:S(2)}) collective-permute-start(bf16[64,2048]{1,0:T(8,128)(2,1)} %get-tuple-element.209), channel_id=1, source_target_pairs={{0,3},{1,0},{2,1},{3,2},{4,7},{5,4},{6,5},{7,6},{8,11},{9,8},{10,9... | collective-permute-start | bytes 786440 | tf_op jit(solution)/shard_map/ppermute | solution.py:344
  457.2 6.8 %collective-permute-start.70 = (f32[32,2048]{1,0:T(8,128)}, f32[32,2048]{1,0:T(8,128)S(1)}, u32[]{:S(2)}, u32[]{:S(2)}) collective-permute-start(f32[32,2048]{1,0:T(8,128)} %get-tuple-element.211), channel_id=1, source_target_pairs={{0,4},{1,5},{2,6},{3,7},{4,0},{5,1},{6,2},{7,3},{8,12},{9,13},{10,... | collective-permute-start | bytes 786440 | tf_op jit(solution)/shard_map/ppermute | solution.py:344
  (75 other events, 369.7 us)
